TPU v7x, 32 devices: a whole 2x2x4 slice. The times are simulated.
32 devices in a mesh: dp: 4 (over y, x), expert: 8 (over z, core).
Axes of the slice: x: 2, y: 2, z: 4, core: 2. Of those that a mesh axis runs over, the one named last changes fastest.
Arguments:
- inputs: bfloat16 [1, 4096, 2048], P(None, 'expert'), may hold values from -6 to 6
- attention_norm_gain: float32 [2048], replicated, may hold values from 0.5 to 1.5
- w_query: bfloat16 [2048, 2048], P(None, 'dp'), may hold values from -0.125 to 0.125
- w_key: bfloat16 [2048, 2048], P(None, 'dp'), may hold values from -0.125 to 0.125
- w_value: bfloat16 [2048, 2048], P(None, 'dp'), may hold values from -0.125 to 0.125
- w_out: bfloat16 [2048, 2048], P('dp'), may hold values from -1 to 1
- q_gain: float32 [2048], P('dp'), may hold values from 0.5 to 1.5
- k_gain: float32 [2048], P('dp'), may hold values from 0.5 to 1.5
- expert_norm_gain: float32 [2048], replicated, may hold values from 0.5 to 1.5
- w_router: float32 [2048, 16], replicated, may hold values from -0.125 to 0.125
- w_gate: bfloat16 [16, 2048, 1024], P('expert', None, 'dp'), may hold values from -0.125 to 0.125
- w_up: bfloat16 [16, 2048, 1024], P('expert', None, 'dp'), may hold values from -0.125 to 0.125
- w_down: bfloat16 [16, 1024, 2048], P('expert', 'dp'), may hold values from -4 to 4
- routes: int32 [4096, 1, 8], P('expert'), may hold values from 0 to 15, all different within a row; in each aligned block of 512 rows (0 to 511, 512 to 1023, ..., all dimensions but the last counted through in order) at most 512 rows name the same one
- lengths: int32 [1, 16], replicated, may hold values from 1 to 3072, 4096 in all within a row
- d_output: bfloat16 [1, 4096, 2048], P(None, 'expert'), may hold values from -6 to 6
Outputs:
- output: bfloat16 [1, 4096, 2048], P(None, 'expert')
- grad_input: float32 [1, 4096, 2048], P(None, 'expert')
- grad_attn_gain: float32 [2048], P('expert')
- grad_query: float32 [2048, 2048], P('expert', 'dp')
- grad_key: float32 [2048, 2048], P('expert', 'dp')
- grad_value: float32 [2048, 2048], P('expert', 'dp')
- grad_out: float32 [2048, 2048], P(('dp', 'expert'))
- grad_q_gain: float32 [2048], P(('dp', 'expert'))
- grad_k_gain: float32 [2048], P(('dp', 'expert'))
- grad_expert_norm_gain: float32 [2048], P('expert')
- grad_router: float32 [2048, 16], P('expert')
- grad_gate: float32 [16, 2048, 1024], P('expert', None, 'dp')
- grad_up: float32 [16, 2048, 1024], P('expert', None, 'dp')
- grad_down: float32 [16, 1024, 2048], P('expert', 'dp')
Inputs may be any that keep to these rules, and one draw needn't show every extreme that they name: `routes`: each token names 8 different experts; of the rows of one index of the expert axis at most 512 name any one expert, a bound that some block reaches of them. `lengths`: each row sums to 4096; its largest entry is 3072.
All inputs are finite; a program needn't handle non-finite values.
Results may differ from a plain program's by a relative error of at most 0.025.
Values may be sent and summed in bfloat16 or wider, within the bound.
A program may use at most 576 MiB of HBM per device.

v0:
```python
import jax
import jax.numpy as jnp
from jax import lax
from jax.sharding import PartitionSpec as P

HD = 128


epsilon = 1e-05
rope_base = 10000.0
masked_score = -1e30


def doc_layout(lengths, pack_span):
    doc_ends = jnp.cumsum(lengths, axis=1)
    starts = doc_ends - lengths
    places = jnp.arange(pack_span, dtype=jnp.int32)
    segment = jnp.sum((places[None, :, None] >= doc_ends[:, None, :]).astype(jnp.int32), axis=2)
    member = segment[:, :, None] == jnp.arange(lengths.shape[1], dtype=jnp.int32)[None, None, :]
    begins = jnp.sum(jnp.where(member, starts[:, None, :], 0), axis=2)
    return (segment, places[None, :] - begins)


def rope_tables(positions, head_size):
    half_size = head_size // 2
    frequency = rope_base ** (-2.0 * jnp.arange(half_size, dtype=jnp.float32) / head_size)
    angles = positions.astype(jnp.float32)[..., None] * frequency
    return (jnp.cos(angles), jnp.sin(angles))


def rotate(heads_in, cos_table, sin_table):
    half_size = heads_in.shape[-1] // 2
    first_half = heads_in[..., :half_size]
    second_half = heads_in[..., half_size:]
    cos_head = cos_table[..., None, :]
    sin_head = sin_table[..., None, :]
    return jnp.concatenate(
        [
            first_half * cos_head - second_half * sin_head,
            second_half * cos_head + first_half * sin_head,
        ],
        axis=-1,
    )


def dp_total(partial_value):
    return lax.psum(partial_value, "dp")


def head_totals(first_sum, second_sum):
    return lax.psum((first_sum, second_sum), "dp")


def dispatch(routed, placing, experts, capacity, groups):
    buffer = jnp.zeros((experts * capacity, routed.shape[1]), routed.dtype).at[placing].set(routed)
    buffer = buffer.reshape(groups, experts // groups * capacity, routed.shape[1])
    return lax.all_to_all(buffer, "expert", split_axis=0, concat_axis=0, tiled=True)


def send_rows(routed, placing, experts, capacity, groups):
    return dispatch(routed, placing, experts, capacity, groups)


def collect(returned):
    return lax.all_to_all(returned, "expert", split_axis=0, concat_axis=0, tiled=True)


def per_device(
    inputs,
    attention_norm_gain,
    w_query,
    w_key,
    w_value,
    w_out,
    q_gain,
    k_gain,
    expert_norm_gain,
    w_router,
    w_gate,
    w_up,
    w_down,
    routes,
    lengths,
    d_output,
):
    pack_count, seg_rows, model_width = inputs.shape
    local_width = w_query.shape[1]
    local_heads = local_width // HD
    experts = w_router.shape[1]
    groups = lax.axis_size("expert")
    pack_span = seg_rows * groups
    top_routes = routes.shape[2]
    route_count = pack_count * seg_rows * top_routes
    capacity = 2 * route_count // experts
    local_experts = w_gate.shape[0]
    scale_factor = HD ** (-0.5)
    offset_rows = lax.axis_index("expert") * seg_rows
    segment, positions = doc_layout(lengths, pack_span)
    seg_query = lax.dynamic_slice_in_dim(segment, offset_rows, seg_rows, 1)
    pos_query = lax.dynamic_slice_in_dim(positions, offset_rows, seg_rows, 1)
    cos_table, sin_table = rope_tables(pos_query, HD)
    key_places = jnp.arange(pack_span, dtype=jnp.int32)
    query_places = offset_rows + jnp.arange(seg_rows, dtype=jnp.int32)
    allowed = (seg_query[:, :, None] == segment[:, None, :]) & (
        key_places[None, None, :] <= query_places[None, :, None]
    )
    head_shape = (pack_count, seg_rows, local_heads, HD)
    inputs_single_float = inputs.astype(jnp.float32)
    first_inverse_norm = lax.rsqrt(
        jnp.mean(inputs_single_float * inputs_single_float, axis=-1, keepdims=True) + epsilon
    )
    first_unit_input = inputs_single_float * first_inverse_norm
    first_normed_input = (first_unit_input * attention_norm_gain).astype(jnp.bfloat16)
    q_raw = jnp.dot(first_normed_input, w_query, preferred_element_type=jnp.float32)
    k_raw = jnp.dot(first_normed_input, w_key, preferred_element_type=jnp.float32)
    value_rows = jnp.dot(first_normed_input, w_value, preferred_element_type=jnp.float32).astype(
        jnp.bfloat16
    )
    q_sum, k_sum = head_totals(jnp.sum(q_raw * q_raw, axis=-1), jnp.sum(k_raw * k_raw, axis=-1))
    q_inv = lax.rsqrt(q_sum[..., None] / model_width + epsilon)
    k_inv = lax.rsqrt(k_sum[..., None] / model_width + epsilon)
    q_hat = q_raw * q_inv
    k_hat = k_raw * k_inv
    queries = rotate((q_hat * q_gain).reshape(head_shape), cos_table, sin_table).astype(
        jnp.bfloat16
    )
    key_rows = (
        rotate((k_hat * k_gain).reshape(head_shape), cos_table, sin_table)
        .astype(jnp.bfloat16)
        .reshape(pack_count, seg_rows, local_width)
    )
    keys_all, values_all = (
        lax.all_gather(key_rows, "expert", axis=1, tiled=True),
        lax.all_gather(value_rows, "expert", axis=1, tiled=True),
    )
    keys_heads = keys_all.reshape(pack_count, pack_span, local_heads, HD)
    values_heads = values_all.reshape(pack_count, pack_span, local_heads, HD)

    def score_block(query_block):
        scores = (
            jnp.einsum(
                "pshd,plhd->phsl", query_block, keys_heads, preferred_element_type=jnp.float32
            )
            * scale_factor
        )
        return jnp.where(allowed[:, None], scores, masked_score)

    scores = score_block(queries)
    largest = jnp.max(scores, axis=-1, keepdims=True)
    log_total = largest + jnp.log(jnp.sum(jnp.exp(scores - largest), axis=-1, keepdims=True))
    weights = jnp.exp(scores - log_total)
    attended = jnp.einsum(
        "phsl,plhd->pshd",
        weights.astype(jnp.bfloat16),
        values_heads,
        preferred_element_type=jnp.float32,
    )
    attended = attended.astype(jnp.bfloat16).reshape(pack_count, seg_rows, local_width)
    hidden_state = inputs_single_float + dp_total(
        jnp.dot(attended, w_out, preferred_element_type=jnp.float32)
    )
    second_inverse_norm = lax.rsqrt(
        jnp.mean(hidden_state * hidden_state, axis=-1, keepdims=True) + epsilon
    )
    second_unit_input = hidden_state * second_inverse_norm
    second_normed_input = second_unit_input * expert_norm_gain
    router = jax.nn.softmax(
        jnp.dot(second_normed_input, w_router, precision=lax.Precision.HIGHEST), axis=-1
    )
    chosen = jnp.transpose(routes, (1, 0, 2))
    gate_values = jnp.take_along_axis(router, chosen, axis=-1)
    route_ids = chosen.reshape(-1)
    expert_range = jnp.arange(experts, dtype=jnp.int32)
    one_hot = (route_ids[:, None] == expert_range[None, :]).astype(jnp.int32)
    earlier = jnp.cumsum(one_hot, axis=0) - one_hot
    slot_index = jnp.sum(earlier * one_hot, axis=1)
    placing = route_ids * capacity + slot_index
    token_of = jnp.arange(route_count, dtype=jnp.int32) // top_routes
    rows_out = second_normed_input.astype(jnp.bfloat16).reshape(pack_count * seg_rows, model_width)[
        token_of
    ]
    grid_shape = (groups, local_experts, capacity, model_width)
    expert_rows = send_rows(rows_out, placing, experts, capacity, groups).reshape(grid_shape)

    def expert_inner(routed_rows):
        gate_pre = jnp.einsum(
            "gjcd,jdf->gjcf", routed_rows, w_gate, preferred_element_type=jnp.float32
        )
        up_pre = jnp.einsum("gjcd,jdf->gjcf", routed_rows, w_up, preferred_element_type=jnp.float32)
        return (gate_pre, up_pre)

    gate_pre, up_pre = expert_inner(expert_rows)
    activated = (jax.nn.silu(gate_pre) * up_pre).astype(jnp.bfloat16)
    pieces = jnp.einsum(
        "gjcf,jfd->gjcd", activated, w_down, preferred_element_type=jnp.float32
    ).astype(jnp.bfloat16)
    returned = collect(pieces.reshape(groups, local_experts * capacity, model_width))
    route_out = (
        returned.reshape(experts * capacity, model_width)[placing]
        .astype(jnp.float32)
        .reshape(pack_count, seg_rows, top_routes, model_width)
    )
    moe_out = dp_total(jnp.sum(gate_values[..., None] * route_out, axis=2))
    output = (hidden_state + moe_out).astype(jnp.bfloat16)
    grad_top = d_output.astype(jnp.float32)
    gate_part = jnp.sum(grad_top[:, :, None, :] * route_out, axis=-1)
    grad_rows = (
        (gate_values[..., None] * grad_top[:, :, None, :])
        .astype(jnp.bfloat16)
        .reshape(route_count, model_width)
    )
    grad_arrived = send_rows(grad_rows, placing, experts, capacity, groups).reshape(grid_shape)
    gate_pre, up_pre = expert_inner(expert_rows)
    sigmoid_gate = jax.nn.sigmoid(gate_pre)
    silu_gate = jax.nn.silu(gate_pre)
    activated = (silu_gate * up_pre).astype(jnp.bfloat16)
    grad_act = jnp.einsum(
        "gjcd,jfd->gjcf", grad_arrived, w_down, preferred_element_type=jnp.float32
    )
    grad_down = jnp.einsum(
        "gjcf,gjcd->jfd", activated, grad_arrived, preferred_element_type=jnp.float32
    )
    grad_gate_pre = (
        grad_act * up_pre * sigmoid_gate * (1.0 + gate_pre * (1.0 - sigmoid_gate))
    ).astype(jnp.bfloat16)
    grad_up_pre = (grad_act * silu_gate).astype(jnp.bfloat16)
    grad_gate = jnp.einsum(
        "gjcd,gjcf->jdf", expert_rows, grad_gate_pre, preferred_element_type=jnp.float32
    )
    grad_up = jnp.einsum(
        "gjcd,gjcf->jdf", expert_rows, grad_up_pre, preferred_element_type=jnp.float32
    )
    grad_expert_rows = jnp.einsum(
        "gjcf,jdf->gjcd", grad_gate_pre, w_gate, preferred_element_type=jnp.float32
    )
    grad_expert_rows = grad_expert_rows + jnp.einsum(
        "gjcf,jdf->gjcd", grad_up_pre, w_up, preferred_element_type=jnp.float32
    )
    grad_back = collect(
        grad_expert_rows.astype(jnp.bfloat16).reshape(groups, local_experts * capacity, model_width)
    )
    grad_route = (
        grad_back.reshape(experts * capacity, model_width)[placing]
        .astype(jnp.float32)
        .reshape(pack_count, seg_rows, top_routes, model_width)
    )
    grad_xn_exp, grad_gates = (
        lax.psum(jnp.sum(grad_route, axis=2).astype(jnp.bfloat16), "dp").astype(jnp.float32),
        lax.psum(gate_part.astype(jnp.bfloat16), "dp").astype(jnp.float32),
    )
    grad_router_probs = jnp.sum(
        jnp.where(chosen[..., None] == expert_range, grad_gates[..., None], 0.0), axis=2
    )
    grad_logits = router * (
        grad_router_probs - jnp.sum(router * grad_router_probs, axis=-1, keepdims=True)
    )
    grad_second_normed_input = grad_xn_exp + jnp.einsum(
        "pse,de->psd", grad_logits, w_router, precision=lax.Precision.HIGHEST
    )
    grad_router = jnp.einsum(
        "psd,pse->de", second_normed_input, grad_logits, precision=lax.Precision.HIGHEST
    )
    grad_expert_norm_gain = jnp.sum(grad_second_normed_input * second_unit_input, axis=(0, 1))
    grad_second_unit_input = grad_second_normed_input * expert_norm_gain
    grad_hidden = grad_top + second_inverse_norm * (
        grad_second_unit_input
        - second_unit_input
        * jnp.mean(grad_second_unit_input * second_unit_input, axis=-1, keepdims=True)
    )
    grad_attn = grad_hidden.astype(jnp.bfloat16)
    grad_out = jnp.einsum("psk,psd->kd", attended, grad_attn, preferred_element_type=jnp.float32)
    grad_heads = (
        jnp.einsum("psd,kd->psk", grad_attn, w_out, preferred_element_type=jnp.float32)
        .astype(jnp.bfloat16)
        .reshape(head_shape)
    )
    scores = score_block(queries)
    weights = jnp.exp(scores - log_total)
    grad_weights = jnp.einsum(
        "pshd,plhd->phsl", grad_heads, values_heads, preferred_element_type=jnp.float32
    )
    row_delta = jnp.sum(weights * grad_weights, axis=-1, keepdims=True)
    grad_scores = (weights * (grad_weights - row_delta)).astype(jnp.bfloat16)
    grad_queries = (
        jnp.einsum("phsl,plhd->pshd", grad_scores, keys_heads, preferred_element_type=jnp.float32)
        * scale_factor
    )
    key_part = (
        jnp.einsum("phsl,pshd->plhd", grad_scores, queries, preferred_element_type=jnp.float32)
        * scale_factor
    )
    value_part = jnp.einsum(
        "phsl,pshd->plhd",
        weights.astype(jnp.bfloat16),
        grad_heads,
        preferred_element_type=jnp.float32,
    )
    grad_keys, grad_values = (
        lax.psum_scatter(
            key_part.reshape(pack_count, pack_span, local_width).astype(jnp.bfloat16),
            "expert",
            scatter_dimension=1,
            tiled=True,
        ).astype(jnp.float32),
        lax.psum_scatter(
            value_part.reshape(pack_count, pack_span, local_width).astype(jnp.bfloat16),
            "expert",
            scatter_dimension=1,
            tiled=True,
        ).astype(jnp.float32),
    )
    grad_q_normed = rotate(grad_queries, cos_table, -sin_table).reshape(
        pack_count, seg_rows, local_width
    )
    grad_k_normed = rotate(grad_keys.reshape(head_shape), cos_table, -sin_table).reshape(
        pack_count, seg_rows, local_width
    )
    grad_q_gain = jnp.sum(grad_q_normed * q_hat, axis=(0, 1))
    grad_k_gain = jnp.sum(grad_k_normed * k_hat, axis=(0, 1))
    grad_q_hat = grad_q_normed * q_gain
    grad_k_hat = grad_k_normed * k_gain
    q_dot, k_dot = head_totals(
        jnp.sum(grad_q_hat * q_hat, axis=-1), jnp.sum(grad_k_hat * k_hat, axis=-1)
    )
    grad_q_raw = (q_inv * (grad_q_hat - q_hat * q_dot[..., None] / model_width)).astype(
        jnp.bfloat16
    )
    grad_k_raw = (k_inv * (grad_k_hat - k_hat * k_dot[..., None] / model_width)).astype(
        jnp.bfloat16
    )
    grad_v_raw = grad_values.astype(jnp.bfloat16)
    grad_query = jnp.einsum(
        "psd,psk->dk", first_normed_input, grad_q_raw, preferred_element_type=jnp.float32
    )
    grad_key = jnp.einsum(
        "psd,psk->dk", first_normed_input, grad_k_raw, preferred_element_type=jnp.float32
    )
    grad_value = jnp.einsum(
        "psd,psk->dk", first_normed_input, grad_v_raw, preferred_element_type=jnp.float32
    )
    grad_first_normed_input = jnp.einsum(
        "psk,dk->psd", grad_q_raw, w_query, preferred_element_type=jnp.float32
    )
    grad_first_normed_input = grad_first_normed_input + jnp.einsum(
        "psk,dk->psd", grad_k_raw, w_key, preferred_element_type=jnp.float32
    )
    grad_first_normed_input = grad_first_normed_input + jnp.einsum(
        "psk,dk->psd", grad_v_raw, w_value, preferred_element_type=jnp.float32
    )
    gain_portion = jnp.sum(grad_first_normed_input * first_unit_input, axis=(0, 1))
    grad_first_unit_input = grad_first_normed_input * attention_norm_gain
    input_part = first_inverse_norm * (
        grad_first_unit_input
        - first_unit_input
        * jnp.mean(grad_first_unit_input * first_unit_input, axis=-1, keepdims=True)
    )
    input_total, grad_attn_gain = (
        lax.psum(input_part.astype(jnp.bfloat16), "dp").astype(jnp.float32),
        lax.psum(gain_portion.astype(jnp.bfloat16), "dp").astype(jnp.float32),
    )
    grad_input = grad_hidden + input_total
    reduced_dense = (
        lax.psum_scatter(
            grad_query.astype(jnp.bfloat16), "expert", scatter_dimension=0, tiled=True
        ).astype(jnp.float32),
        lax.psum_scatter(
            grad_key.astype(jnp.bfloat16), "expert", scatter_dimension=0, tiled=True
        ).astype(jnp.float32),
        lax.psum_scatter(
            grad_value.astype(jnp.bfloat16), "expert", scatter_dimension=0, tiled=True
        ).astype(jnp.float32),
        lax.psum_scatter(
            grad_out.astype(jnp.bfloat16), "expert", scatter_dimension=0, tiled=True
        ).astype(jnp.float32),
        lax.psum_scatter(
            grad_q_gain.astype(jnp.bfloat16), "expert", scatter_dimension=0, tiled=True
        ).astype(jnp.float32),
        lax.psum_scatter(
            grad_k_gain.astype(jnp.bfloat16), "expert", scatter_dimension=0, tiled=True
        ).astype(jnp.float32),
        lax.psum_scatter(
            grad_attn_gain.astype(jnp.bfloat16), "expert", scatter_dimension=0, tiled=True
        ).astype(jnp.float32),
        lax.psum_scatter(
            grad_expert_norm_gain.astype(jnp.bfloat16), "expert", scatter_dimension=0, tiled=True
        ).astype(jnp.float32),
        lax.psum_scatter(
            grad_router.astype(jnp.bfloat16), "expert", scatter_dimension=0, tiled=True
        ).astype(jnp.float32),
    )
    return (
        output,
        grad_input,
        reduced_dense[6],
        reduced_dense[0],
        reduced_dense[1],
        reduced_dense[2],
        reduced_dense[3],
        reduced_dense[4],
        reduced_dense[5],
        reduced_dense[7],
        reduced_dense[8],
        grad_gate,
        grad_up,
        grad_down,
    )


def solution(mesh):
    placed = (
        P(None, "expert", None),
        P(),
        P(None, "dp"),
        P(None, "dp"),
        P(None, "dp"),
        P("dp", None),
        P("dp"),
        P("dp"),
        P(),
        P(),
        P("expert", None, "dp"),
        P("expert", None, "dp"),
        P("expert", "dp", None),
        P("expert", None, None),
        P(),
        P(None, "expert", None),
    )
    return jax.shard_map(
        per_device,
        mesh=mesh,
        in_specs=placed,
        out_specs=(
            P(None, "expert", None),
            P(None, "expert", None),
            P("expert"),
            P("expert", "dp"),
            P("expert", "dp"),
            P("expert", "dp"),
            P(("dp", "expert"), None),
            P(("dp", "expert")),
            P(("dp", "expert")),
            P("expert"),
            P("expert", None),
            P("expert", None, "dp"),
            P("expert", None, "dp"),
            P("expert", "dp", None),
        ),
        check_vma=False,
    )
```

profile of v0, /device:TPU:24, one launch (start us, length us, event | category | flops | bytes accessed | tf_op | source)
XLA Modules:
  0.0 4495.4 jit_solution(1720066278517942681)
XLA Ops:
  54.3 35.8 all-gather.4.cloned.1.call-done
  170.6 92.5 %all-reduce.12.cloned.1.call-done = f32[1,512,2048]{2,1,0:T(8,128)} async-done(((f32[1,512,2048]{2,1,0:T(8,128)}), f32[1,512,2048]{2,1,0:T(8,128)}) %all-reduce.12.cloned.1.call-update) | async-done | bytes 4194320 | tf_op jit(solution)/shard_map/psum | solution.py:47
  270.4 33.2 gather_fusion
  303.6 95.4 %scatter_custom_fusion = bf16[8192,2048]{1,0:T(8,128)(2,1)} fusion(s32[4096]{0:T(1024)S(1)} %get-tuple-element.14, bf16[4096,2048]{1,0:T(8,128)(2,1)} %gather_fusion, s32[4096]{0:T(1024)S(1)} %broadcast_clamp_fusion.1, bf16[]{:T(256)} %constant.85.clone.1), kind=kCustom, calls=%fused_computation.36 | custom fusion | bytes 33554944 | tf_op jit(solution)/shard_map/scatter | solution.py:55
  398.9 732.7 %all_to_all.20 = bf16[8,1024,2048]{2,1,0:T(8,128)(2,1)} all-to-all(bf16[8,1024,2048]{2,1,0:T(8,128)(2,1)} %bitcast.293), channel_id=1, replica_groups=mesh['dp'=4,'expert'=8] {'expert'}, dimensions={0} | all-to-all | bytes 67108864 | tf_op jit(solution)/shard_map/all_to_all | solution.py:57
  1188.0 22.9 copy.186
  1230.4 711.8 %all-to-all-done.1 = bf16[8,1024,2048]{2,1,0:T(8,128)(2,1)} async-done(((bf16[8,1024,2048]{2,1,0:T(8,128)(2,1)}), bf16[8,1024,2048]{2,1,0:T(8,128)(2,1)}, u32[]{:S(2)}, u32[]{:S(2)}) %all-to-all-start.1) | async-done | bytes 33554464 | tf_op jit(solution)/shard_map/all_to_all | solution.py:65
  1942.2 95.9 %gather_fusion.1 = bf16[4096,2048]{1,0:T(8,128)(2,1)} fusion(bf16[8192,2048]{1,0:T(8,128)(2,1)} %bitcast.39, s32[4096]{0:T(1024)S(1)} %broadcast_clamp_fusion), kind=kCustom, calls=%fused_computation.1 | custom fusion | bytes 33570816 | tf_op jit(solution)/shard_map/gather | solution.py:199
  2058.0 33.0 gather_fusion.3
  2101.0 95.8 %scatter_custom_fusion.1 = bf16[8192,2048]{1,0:T(8,128)(2,1)} fusion(s32[4096]{0:T(1024)} %copy-done.70, bf16[4096,2048]{1,0:T(8,128)(2,1)} %fusion.6, s32[4096]{0:T(1024)} %copy-done.69, bf16[]{:T(256)} %constant.85.clone.1), kind=kCustom, calls=%fused_computation.34 | custom fusion | bytes 33554944 | tf_op jit(solution)/shard_map/scatter | solution.py:55
  2196.8 734.4 %all_to_all.21 = bf16[8,1024,2048]{2,1,0:T(8,128)(2,1)} all-to-all(bf16[8,1024,2048]{2,1,0:T(8,128)(2,1)} %bitcast.292), channel_id=1, replica_groups=mesh['dp'=4,'expert'=8] {'expert'}, dimensions={0} | all-to-all | bytes 67108864 | tf_op jit(solution)/shard_map/all_to_all | solution.py:57
  2931.2 23.7 fusion.31
  2954.9 26.7 fusion.86
  2981.7 34.1 fusion.16
  3038.7 735.4 %all_to_all.22 = bf16[8,1024,2048]{2,1,0:T(8,128)(2,1)} all-to-all(bf16[8,1024,2048]{2,1,0:T(8,128)(2,1)} %bitcast.294), channel_id=1, replica_groups=mesh['dp'=4,'expert'=8] {'expert'}, dimensions={0} | all-to-all | bytes 67108864 | tf_op jit(solution)/shard_map/all_to_all | solution.py:65
  3774.0 95.9 %gather_fusion.2 = bf16[4096,2048]{1,0:T(8,128)(2,1)} fusion(bf16[8192,2048]{1,0:T(8,128)(2,1)} %bitcast.290, s32[4096]{0:T(1024)S(1)} %copy-done.47), kind=kCustom, calls=%fused_computation.2 | custom fusion | bytes 33570816 | tf_op jit(solution)/shard_map/gather | solution.py:243
  3902.3 52.1 %all-reduce.16.cloned.1.call-done = bf16[1,512,2048]{2,1,0:T(8,128)(2,1)} async-done(((bf16[1,512,2048]{2,1,0:T(8,128)(2,1)}), bf16[1,512,2048]{2,1,0:T(8,128)(2,1)}) %all-reduce.16.cloned.1.call-update) | async-done | bytes 2097168 | tf_op jit(solution)/shard_map/psum | solution.py:248
  3963.2 98.0 %all-reduce.14.cloned.1.call-done = f32[1,512,2048]{2,1,0:T(8,128)} async-done(((f32[1,512,2048]{2,1,0:T(8,128)}), f32[1,512,2048]{2,1,0:T(8,128)}) %all-reduce.14.cloned.1.call-update) | async-done | bytes 4194320 | tf_op jit(solution)/shard_map/psum | solution.py:47
  4072.0 26.8 multiply_reduce_fusion
  4098.9 28.4 multiply_convert_fusion
  4334.1 24.2 all-reduce.6
  4384.3 28.7 reduce-scatter.16.cloned.1.call-done
  4414.9 34.8 reduce-scatter.12.cloned.1.call-done
  4451.5 35.2 reduce-scatter.14.cloned.1.call-done
  (300 shorter events, 551.5 us)
Async XLA Ops:
  7.2 1164.9 %copy-start = (bf16[2,256,2048]{2,1,0:T(8,128)(2,1)S(1)}, bf16[2,256,2048]{2,1,0:T(8,128)(2,1)}, u32[]{:S(2)}) copy-start(bf16[2,256,2048]{2,1,0:T(8,128)(2,1)} %param.28) | copy-start | bytes 6291460
  7.2 82.9 %all-gather.4.cloned.1.call-start = ((), (), s32[]{:S(2)}) async-start(), calls=%async_computation.11 | async-start | bytes 4718592 | tf_op jit(solution)/shard_map/all_gather | solution.py:133
  45.9 92.1 %all-gather.6.cloned.1.call-start = ((), (), s32[]{:S(2)}) async-start(), calls=%async_computation.23 | async-start | bytes 4718592 | tf_op jit(solution)/shard_map/all_gather | solution.py:134
  50.3 212.8 %all-reduce.12.cloned.1.call-start = ((), (), s32[]{:S(2)}) async-start(), calls=%async_computation.12 | async-start | bytes 8388608 | tf_op jit(solution)/shard_map/psum | solution.py:47
  158.7 107.9 %copy-start.20 = (s32[512,1,8]{2,0,1:T(8,128)}, s32[512,1,8]{2,0,1:T(8,128)S(1)}, u32[]{:S(2)}) copy-start(s32[512,1,8]{2,0,1:T(8,128)S(1)} %copy.179) | copy-start | bytes 49156
  158.8 107.8 %copy-start.48 = (s32[4096]{0:T(1024)}, s32[4096]{0:T(1024)S(1)}, u32[]{:S(2)}) copy-start(s32[4096]{0:T(1024)S(1)} %eq.92) | copy-start | bytes 49156
  170.5 133.0 %copy-start.70 = (s32[4096]{0:T(1024)}, s32[4096]{0:T(1024)S(1)}, u32[]{:S(2)}) copy-start(s32[4096]{0:T(1024)S(1)} %get-tuple-element.14) | copy-start | bytes 49156
  170.6 132.9 %copy-start.69 = (s32[4096]{0:T(1024)}, s32[4096]{0:T(1024)S(1)}, u32[]{:S(2)}) copy-start(s32[4096]{0:T(1024)S(1)} %broadcast_clamp_fusion.1) | copy-start | bytes 49156
  170.6 98.0 %copy-start.43 = (f32[2048]{0:T(1024)S(1)}, f32[2048]{0:T(1024)}, u32[]{:S(2)}) copy-start(f32[2048]{0:T(1024)} %param.24) | copy-start | bytes 24580
  1210.9 731.3 %all-to-all-start.1 = ((bf16[8,1024,2048]{2,1,0:T(8,128)(2,1)}), bf16[8,1024,2048]{2,1,0:T(8,128)(2,1)}, u32[]{:S(2)}, u32[]{:S(2)}) async-start(bf16[8,1024,2048]{2,1,0:T(8,128)(2,1)} %bitcast.291), calls=%async_computation.1 | async-start | bytes 67108864 | tf_op jit(solution)/shard_map/all_to_all | solution.py:65
  1221.5 2732.9 %all-reduce.16.cloned.1.call-start = ((), (), s32[]{:S(2)}) async-start(), calls=%async_computation.14 | async-start | bytes 4194304 | tf_op jit(solution)/shard_map/psum | solution.py:248
  1222.1 720.1 %copy-start.46 = (s32[4096]{0:T(1024)}, s32[4096]{0:T(1024)S(1)}, u32[]{:S(2)}) copy-start(s32[4096]{0:T(1024)S(1)} %broadcast_clamp_fusion) | copy-start | bytes 49156
  3038.7 735.4 %copy-start.47 = (s32[4096]{0:T(1024)S(1)}, s32[4096]{0:T(1024)}, u32[]{:S(2)}) copy-start(s32[4096]{0:T(1024)} %copy-done.46) | copy-start | bytes 49156
  3884.8 176.4 %all-reduce.14.cloned.1.call-start = ((), (), s32[]{:S(2)}) async-start(), calls=%async_computation.13 | async-start | bytes 8388608 | tf_op jit(solution)/shard_map/psum | solution.py:47
  3902.2 52.2 %copy-start.61 = (f32[512]{0:T(512)S(1)}, f32[512]{0:T(512)}, u32[]{:S(2)}) copy-start(f32[512]{0:T(512)} %get-tuple-element.34) | copy-start | bytes 6148
  3902.3 283.1 %reduce-scatter.8.cloned.1.call-start = ((), (), s32[]{:S(2)}) async-start(), calls=%async_computation.15 | async-start | bytes 4718592 | tf_op jit(solution)/shard_map/reduce_scatter | solution.py:299
  4137.7 98.9 %reduce-scatter.10.cloned.1.call-start = ((), (), s32[]{:S(2)}) async-start(), calls=%async_computation.16 | async-start | bytes 4718592 | tf_op jit(solution)/shard_map/reduce_scatter | solution.py:305
  4155.9 111.4 %reduce-scatter.20.cloned.1.call-start = ((), (), s32[]{:S(2)}) async-start(), calls=%async_computation.22 | async-start | bytes 73728 | tf_op jit(solution)/shard_map/reduce_scatter | solution.py:387
  4161.5 170.9 %reduce-scatter.18.cloned.1.call-start = ((), (), s32[]{:S(2)}) async-start(), calls=%async_computation.21 | async-start | bytes 2359296 | tf_op jit(solution)/shard_map/reduce_scatter | solution.py:372
  4174.0 204.6 %all-reduce.18.cloned.1.call-start = ((), (), s32[]{:S(2)}) async-start(), calls=%async_computation.17 | async-start | bytes 4194304 | tf_op jit(solution)/shard_map/psum | solution.py:358
  4245.8 167.3 %reduce-scatter.16.cloned.1.call-start = ((), (), s32[]{:S(2)}) async-start(), calls=%async_computation.20 | async-start | bytes 2359296 | tf_op jit(solution)/shard_map/reduce_scatter | solution.py:369
  4248.7 201.0 %reduce-scatter.12.cloned.1.call-start = ((), (), s32[]{:S(2)}) async-start(), calls=%async_computation.18 | async-start | bytes 2359296 | tf_op jit(solution)/shard_map/reduce_scatter | solution.py:363
  4251.8 234.8 %reduce-scatter.14.cloned.1.call-start = ((), (), s32[]{:S(2)}) async-start(), calls=%async_computation.19 | async-start | bytes 2359296 | tf_op jit(solution)/shard_map/reduce_scatter | solution.py:366
  4370.1 118.4 %copy-start.1 = (bf16[2,256,2048]{2,1,0:T(8,128)(2,1)S(1)}, bf16[2,256,2048]{2,1,0:T(8,128)(2,1)}, u32[]{:S(2)}) copy-start(bf16[2,256,2048]{2,1,0:T(8,128)(2,1)} %param.28) | copy-start | bytes 6291460
  (62 other events, 977.4 us)
Sparse Core Ops, SparseCore 0:
  46.1 44.0 all-gather.3
  92.3 45.6 all-gather.5
  158.7 104.4 all-reduce.11
  3884.9 69.4 all-reduce.15
  3957.5 103.5 all-reduce.13
  4137.9 47.4 reduce-scatter.7
  4188.2 48.3 reduce-scatter.9
  4239.5 27.8 reduce-scatter.19
  4269.6 33.9 reduce-scatter.17
  4306.5 71.9 all-reduce.17
  4380.9 32.1 reduce-scatter.15
  4415.2 34.4 reduce-scatter.11
  4452.0 34.6 reduce-scatter.13
where the time goes:
time: 4510 us; the launch traced here: 4500 us
  blocking collectives  2270 us (50%)
  waiting for transfers between devices  1150 us (25%)
  local copies, waits for them, and re-layouts  520 us (12%)
  matrix products  359 us (8%)
  other arithmetic  168 us (4%)
    all_to_all x2, blocking collectives, dispatch(): lax.all_to_all(buffer, 'expert', split_axis=0, concat_axis=0, tiled=True)  1470 us
    all_to_all x1, blocking collectives, collect(): lax.all_to_all(returned, 'expert', split_axis=0, concat_axis=0, tiled=True)  735 us
    all_to_all x1, waiting for transfers between devices, collect(): lax.all_to_all(returned, 'expert', split_axis=0, concat_axis=0, tiled=True)  712 us
    scatter x3, local copies, waits for them, and re-layouts, dispatch(): jnp.zeros((experts * capacity, routed.shape[1]), routed.dtype).at[placing]  191 us
    psum x2, waiting for transfers between devices, dp_total(): return lax.psum(partial_value, 'dp')  190 us
    gather x1, local copies, waits for them, and re-layouts, per_device(): returned.reshape(experts * capacity, model_width)[placing]  95.9 us
    gather x1, local copies, waits for them, and re-layouts, per_device(): grad_back.reshape(experts * capacity, model_width)[placing]  95.9 us
  transfers between devices with their start and end apart: 14, of which 13 were waited for; matrix products, arithmetic and copies ran while one was open for 5% of the time, Pallas kernels for 0%

commit v1 on v0

--- a/solution.py
+++ b/solution.py
@@ -43,26 +43,32 @@
     )
 
 
-def dp_total(partial_value):
-    return lax.psum(partial_value, "dp")
+ALL = ("dp", "expert")
+
+
+def gather_all(rows):
+    return lax.all_gather(rows, ALL, axis=0, tiled=True)
+
+
+def gather_dp(rows):
+    return lax.all_gather(rows, "dp", axis=0, tiled=True)
+
+
+def scatter_all(rows):
+    return lax.psum_scatter(rows, ALL, scatter_dimension=0, tiled=True).astype(jnp.float32)
+
+
+def scatter_dp(rows):
+    return lax.psum_scatter(rows, "dp", scatter_dimension=0, tiled=True).astype(jnp.float32)
+
+
+def scatter_sum(value):
+    total = lax.psum(value.astype(jnp.bfloat16), "dp")
+    return lax.psum_scatter(total, "expert", scatter_dimension=0, tiled=True).astype(jnp.float32)
 
 
 def head_totals(first_sum, second_sum):
     return lax.psum((first_sum, second_sum), "dp")
-
-
-def dispatch(routed, placing, experts, capacity, groups):
-    buffer = jnp.zeros((experts * capacity, routed.shape[1]), routed.dtype).at[placing].set(routed)
-    buffer = buffer.reshape(groups, experts // groups * capacity, routed.shape[1])
-    return lax.all_to_all(buffer, "expert", split_axis=0, concat_axis=0, tiled=True)
-
-
-def send_rows(routed, placing, experts, capacity, groups):
-    return dispatch(routed, placing, experts, capacity, groups)
-
-
-def collect(returned):
-    return lax.all_to_all(returned, "expert", split_axis=0, concat_axis=0, tiled=True)
 
 
 def per_device(
@@ -89,9 +95,6 @@
     experts = w_router.shape[1]
     groups = lax.axis_size("expert")
     pack_span = seg_rows * groups
-    top_routes = routes.shape[2]
-    route_count = pack_count * seg_rows * top_routes
-    capacity = 2 * route_count // experts
     local_experts = w_gate.shape[0]
     scale_factor = HD ** (-0.5)
     offset_rows = lax.axis_index("expert") * seg_rows
@@ -156,9 +159,16 @@
         preferred_element_type=jnp.float32,
     )
     attended = attended.astype(jnp.bfloat16).reshape(pack_count, seg_rows, local_width)
-    hidden_state = inputs_single_float + dp_total(
-        jnp.dot(attended, w_out, preferred_element_type=jnp.float32)
-    )
+    attn_part = jnp.dot(
+        attended.reshape(seg_rows, local_width), w_out, preferred_element_type=jnp.float32
+    )
+    own = lax.axis_index("dp")
+    part_rows = seg_rows // lax.axis_size("dp")
+
+    def own_rows(rows):
+        return lax.dynamic_slice_in_dim(rows, own * part_rows, part_rows, 0)
+
+    hidden_state = own_rows(inputs_single_float[0]) + scatter_dp(attn_part.astype(jnp.bfloat16))
     second_inverse_norm = lax.rsqrt(
         jnp.mean(hidden_state * hidden_state, axis=-1, keepdims=True) + epsilon
     )
@@ -167,107 +177,62 @@
     router = jax.nn.softmax(
         jnp.dot(second_normed_input, w_router, precision=lax.Precision.HIGHEST), axis=-1
     )
-    chosen = jnp.transpose(routes, (1, 0, 2))
-    gate_values = jnp.take_along_axis(router, chosen, axis=-1)
-    route_ids = chosen.reshape(-1)
+    chosen = own_rows(routes[:, 0, :])
     expert_range = jnp.arange(experts, dtype=jnp.int32)
-    one_hot = (route_ids[:, None] == expert_range[None, :]).astype(jnp.int32)
-    earlier = jnp.cumsum(one_hot, axis=0) - one_hot
-    slot_index = jnp.sum(earlier * one_hot, axis=1)
-    placing = route_ids * capacity + slot_index
-    token_of = jnp.arange(route_count, dtype=jnp.int32) // top_routes
-    rows_out = second_normed_input.astype(jnp.bfloat16).reshape(pack_count * seg_rows, model_width)[
-        token_of
-    ]
-    grid_shape = (groups, local_experts, capacity, model_width)
-    expert_rows = send_rows(rows_out, placing, experts, capacity, groups).reshape(grid_shape)
-
-    def expert_inner(routed_rows):
-        gate_pre = jnp.einsum(
-            "gjcd,jdf->gjcf", routed_rows, w_gate, preferred_element_type=jnp.float32
-        )
-        up_pre = jnp.einsum("gjcd,jdf->gjcf", routed_rows, w_up, preferred_element_type=jnp.float32)
-        return (gate_pre, up_pre)
-
-    gate_pre, up_pre = expert_inner(expert_rows)
-    activated = (jax.nn.silu(gate_pre) * up_pre).astype(jnp.bfloat16)
-    pieces = jnp.einsum(
-        "gjcf,jfd->gjcd", activated, w_down, preferred_element_type=jnp.float32
-    ).astype(jnp.bfloat16)
-    returned = collect(pieces.reshape(groups, local_experts * capacity, model_width))
-    route_out = (
-        returned.reshape(experts * capacity, model_width)[placing]
-        .astype(jnp.float32)
-        .reshape(pack_count, seg_rows, top_routes, model_width)
-    )
-    moe_out = dp_total(jnp.sum(gate_values[..., None] * route_out, axis=2))
-    output = (hidden_state + moe_out).astype(jnp.bfloat16)
-    grad_top = d_output.astype(jnp.float32)
-    gate_part = jnp.sum(grad_top[:, :, None, :] * route_out, axis=-1)
-    grad_rows = (
-        (gate_values[..., None] * grad_top[:, :, None, :])
-        .astype(jnp.bfloat16)
-        .reshape(route_count, model_width)
-    )
-    grad_arrived = send_rows(grad_rows, placing, experts, capacity, groups).reshape(grid_shape)
-    gate_pre, up_pre = expert_inner(expert_rows)
+    named = jnp.any(chosen[:, :, None] == expert_range, axis=1)
+    gate_table = gather_all(jnp.where(named, router, 0.0))
+    first_expert = lax.axis_index("expert") * local_experts
+    gates = lax.dynamic_slice_in_dim(gate_table, first_expert, local_experts, 1)
+    xn_all = gather_all(second_normed_input.astype(jnp.bfloat16))
+    top_own = own_rows(d_output[0])
+    top_all = gather_all(top_own)
+
+    gate_pre = jnp.einsum("td,jdf->tjf", xn_all, w_gate, preferred_element_type=jnp.float32)
+    up_pre = jnp.einsum("td,jdf->tjf", xn_all, w_up, preferred_element_type=jnp.float32)
+    top_down = jnp.einsum("td,jfd->tjf", top_all, w_down, preferred_element_type=jnp.float32)
     sigmoid_gate = jax.nn.sigmoid(gate_pre)
-    silu_gate = jax.nn.silu(gate_pre)
-    activated = (silu_gate * up_pre).astype(jnp.bfloat16)
-    grad_act = jnp.einsum(
-        "gjcd,jfd->gjcf", grad_arrived, w_down, preferred_element_type=jnp.float32
-    )
-    grad_down = jnp.einsum(
-        "gjcf,gjcd->jfd", activated, grad_arrived, preferred_element_type=jnp.float32
-    )
+    silu_gate = gate_pre * sigmoid_gate
+    activated = silu_gate * up_pre
+    scaled = (activated * gates[:, :, None]).astype(jnp.bfloat16)
+    gate_part = jnp.sum(activated * top_down, axis=-1)
+    grad_act = top_down * gates[:, :, None]
     grad_gate_pre = (
         grad_act * up_pre * sigmoid_gate * (1.0 + gate_pre * (1.0 - sigmoid_gate))
     ).astype(jnp.bfloat16)
     grad_up_pre = (grad_act * silu_gate).astype(jnp.bfloat16)
-    grad_gate = jnp.einsum(
-        "gjcd,gjcf->jdf", expert_rows, grad_gate_pre, preferred_element_type=jnp.float32
-    )
-    grad_up = jnp.einsum(
-        "gjcd,gjcf->jdf", expert_rows, grad_up_pre, preferred_element_type=jnp.float32
-    )
-    grad_expert_rows = jnp.einsum(
-        "gjcf,jdf->gjcd", grad_gate_pre, w_gate, preferred_element_type=jnp.float32
-    )
-    grad_expert_rows = grad_expert_rows + jnp.einsum(
-        "gjcf,jdf->gjcd", grad_up_pre, w_up, preferred_element_type=jnp.float32
-    )
-    grad_back = collect(
-        grad_expert_rows.astype(jnp.bfloat16).reshape(groups, local_experts * capacity, model_width)
-    )
-    grad_route = (
-        grad_back.reshape(experts * capacity, model_width)[placing]
-        .astype(jnp.float32)
-        .reshape(pack_count, seg_rows, top_routes, model_width)
-    )
-    grad_xn_exp, grad_gates = (
-        lax.psum(jnp.sum(grad_route, axis=2).astype(jnp.bfloat16), "dp").astype(jnp.float32),
-        lax.psum(gate_part.astype(jnp.bfloat16), "dp").astype(jnp.float32),
-    )
-    grad_router_probs = jnp.sum(
-        jnp.where(chosen[..., None] == expert_range, grad_gates[..., None], 0.0), axis=2
-    )
+    moe_part = jnp.einsum("tjf,jfd->td", scaled, w_down, preferred_element_type=jnp.float32)
+    grad_rows = jnp.einsum("tjf,jdf->td", grad_gate_pre, w_gate, preferred_element_type=jnp.float32)
+    grad_rows = grad_rows + jnp.einsum(
+        "tjf,jdf->td", grad_up_pre, w_up, preferred_element_type=jnp.float32
+    )
+    grad_down = jnp.einsum("tjf,td->jfd", scaled, top_all, preferred_element_type=jnp.float32)
+    grad_gate = jnp.einsum("td,tjf->jdf", xn_all, grad_gate_pre, preferred_element_type=jnp.float32)
+    grad_up = jnp.einsum("td,tjf->jdf", xn_all, grad_up_pre, preferred_element_type=jnp.float32)
+
+    moe_out = scatter_all(moe_part.astype(jnp.bfloat16))
+    output = gather_dp((hidden_state + moe_out).astype(jnp.bfloat16))[None]
+
+    gate_columns = jnp.zeros((gate_part.shape[0], experts), jnp.float32)
+    gate_columns = lax.dynamic_update_slice_in_dim(gate_columns, gate_part, first_expert, 1)
+    grad_router_probs = jnp.where(named, scatter_all(gate_columns), 0.0)
+    grad_xn_exp = scatter_all(grad_rows.astype(jnp.bfloat16))
     grad_logits = router * (
         grad_router_probs - jnp.sum(router * grad_router_probs, axis=-1, keepdims=True)
     )
     grad_second_normed_input = grad_xn_exp + jnp.einsum(
-        "pse,de->psd", grad_logits, w_router, precision=lax.Precision.HIGHEST
+        "se,de->sd", grad_logits, w_router, precision=lax.Precision.HIGHEST
     )
     grad_router = jnp.einsum(
-        "psd,pse->de", second_normed_input, grad_logits, precision=lax.Precision.HIGHEST
-    )
-    grad_expert_norm_gain = jnp.sum(grad_second_normed_input * second_unit_input, axis=(0, 1))
+        "sd,se->de", second_normed_input, grad_logits, precision=lax.Precision.HIGHEST
+    )
+    grad_expert_norm_gain = jnp.sum(grad_second_normed_input * second_unit_input, axis=0)
     grad_second_unit_input = grad_second_normed_input * expert_norm_gain
-    grad_hidden = grad_top + second_inverse_norm * (
+    grad_hidden = top_own.astype(jnp.float32) + second_inverse_norm * (
         grad_second_unit_input
         - second_unit_input
         * jnp.mean(grad_second_unit_input * second_unit_input, axis=-1, keepdims=True)
     )
-    grad_attn = grad_hidden.astype(jnp.bfloat16)
+    grad_attn = gather_dp(grad_hidden.astype(jnp.bfloat16))[None]
     grad_out = jnp.einsum("psk,psd->kd", attended, grad_attn, preferred_element_type=jnp.float32)
     grad_heads = (
         jnp.einsum("psd,kd->psk", grad_attn, w_out, preferred_element_type=jnp.float32)
@@ -354,11 +319,9 @@
         - first_unit_input
         * jnp.mean(grad_first_unit_input * first_unit_input, axis=-1, keepdims=True)
     )
-    input_total, grad_attn_gain = (
-        lax.psum(input_part.astype(jnp.bfloat16), "dp").astype(jnp.float32),
-        lax.psum(gain_portion.astype(jnp.bfloat16), "dp").astype(jnp.float32),
-    )
-    grad_input = grad_hidden + input_total
+    input_total = scatter_dp(input_part[0].astype(jnp.bfloat16))
+    grad_input = gather_dp((grad_hidden + input_total).astype(jnp.bfloat16))
+    grad_input = grad_input.astype(jnp.float32)[None]
     reduced_dense = (
         lax.psum_scatter(
             grad_query.astype(jnp.bfloat16), "expert", scatter_dimension=0, tiled=True
@@ -378,15 +341,9 @@
         lax.psum_scatter(
             grad_k_gain.astype(jnp.bfloat16), "expert", scatter_dimension=0, tiled=True
         ).astype(jnp.float32),
-        lax.psum_scatter(
-            grad_attn_gain.astype(jnp.bfloat16), "expert", scatter_dimension=0, tiled=True
-        ).astype(jnp.float32),
-        lax.psum_scatter(
-            grad_expert_norm_gain.astype(jnp.bfloat16), "expert", scatter_dimension=0, tiled=True
-        ).astype(jnp.float32),
-        lax.psum_scatter(
-            grad_router.astype(jnp.bfloat16), "expert", scatter_dimension=0, tiled=True
-        ).astype(jnp.float32),
+        scatter_sum(gain_portion),
+        scatter_sum(grad_expert_norm_gain),
+        scatter_sum(grad_router),
     )
     return (
         output,

time: 4510 us -> 1490 us (0.33)
  blocking collectives: 2270 us -> 89.8 us
  local copies, waits for them, and re-layouts: 520 us -> 43.8 us
  waiting for transfers between devices: 1150 us -> 906 us
  other arithmetic: 168 us -> 104 us
    all_to_all x3 -> x0, blocking collectives: 2200 us -> none  [the longest x2 1470 us: dispatch(): lax.all_to_all(buffer, 'expert', split_axis=0, concat_axis=0, tiled=True)]
    all_to_all x1 -> x0, waiting for transfers between devices: 712 us -> none  [collect(): lax.all_to_all(returned, 'expert', split_axis=0, concat_axis=0, tiled=True)]
    reduce_scatter x1 -> x6, waiting for transfers between devices: 13.6 us -> 502 us  [the longest x3 429 us: scatter_all(): lax.psum_scatter(rows, ALL, scatter_dimension=0, tiled=True)]
    all_gather x0 -> x5, waiting for transfers between devices: none -> 272 us  [the longest x2 159 us: gather_all(): return lax.all_gather(rows, ALL, axis=0, tiled=True)]
    gather x7 -> x0, local copies, waits for them, and re-layouts: 258 us -> none  [the longest x1 95.9 us: per_device(): returned.reshape(experts * capacity, model_width)[placing]]
    psum x4 -> x0, waiting for transfers between devices: 250 us -> none  [the longest x2 190 us: dp_total(): return lax.psum(partial_value, 'dp')]
    scatter x3 -> x0, local copies, waits for them, and re-layouts: 191 us -> none  [dispatch(): jnp.zeros((experts * capacity, routed.shape[1]), routed.dtype).at[placing]]
    dot_general x12, matrix products: 219 us -> 163 us  [the longest x1 24.6 us: per_device(): jnp.einsum('td,jfd->tjf', top_all, w_down, preferred_element_type=jnp.flo...]
  transfers between devices with their start and end apart: 14 -> 19, of which waited for: 13 -> 17; matrix products, arithmetic and copies ran while one was open for 5% -> 20% of each run, Pallas kernels for 0% -> 0%
where the time goes in v1:
time: 1490 us; the launch traced here: 1480 us
  waiting for transfers between devices  906 us (61%)
  matrix products  317 us (21%)
  other arithmetic  104 us (7%)
  blocking collectives  89.8 us (6%)
  local copies, waits for them, and re-layouts  43.8 us (3%)
  between operations  16.1 us (1%)
    reduce_scatter x3, waiting for transfers between devices, scatter_all(): lax.psum_scatter(rows, ALL, scatter_dimension=0, tiled=True)  429 us
    all_gather x2, waiting for transfers between devices, gather_all(): return lax.all_gather(rows, ALL, axis=0, tiled=True)  159 us
    all_gather x3, waiting for transfers between devices, gather_dp(): return lax.all_gather(rows, 'dp', axis=0, tiled=True)  113 us
    reduce_scatter x2, waiting for transfers between devices, scatter_dp(): lax.psum_scatter(rows, 'dp', scatter_dimension=0, tiled=True)  73.3 us
    all_gather x1, blocking collectives, gather_all(): return lax.all_gather(rows, ALL, axis=0, tiled=True)  36.2 us
    all_gather x1, waiting for transfers between devices, per_device(): lax.all_gather(key_rows, 'expert', axis=1, tiled=True)  35.6 us
    reduce_scatter x1, waiting for transfers between devices, per_device(): lax.psum_scatter(grad_query.astype(jnp.bfloat16), 'expert', scatter_dimen...  35.2 us
    reduce_scatter x1, waiting for transfers between devices, per_device(): lax.psum_scatter(grad_key.astype(jnp.bfloat16), 'expert', scatter_dimensi...  34.9 us
  transfers between devices with their start and end apart: 19, of which 17 were waited for; matrix products, arithmetic and copies ran while one was open for 20% of the time, Pallas kernels for 0%

profile of v1, /device:TPU:24, one launch (start us, length us, event | category | flops | bytes accessed | tf_op | source)
XLA Modules:
  0.0 1478.7 jit_solution(10479653903484946769)
XLA Ops:
  54.6 35.6 %all-gather.10.cloned.1.call-done = bf16[1,4096,512]{1,2,0:T(8,128)(2,1)} async-done(((bf16[1,512,512]{1,2,0:T(8,128)(2,1)}), bf16[1,4096,512]{1,2,0:T(8,128)(2,1)}) %all-gather.10.cloned.1.call-update) | async-done | bytes 4194320 | tf_op jit(solution)/shard_map/all_gather | solution.py:136
  90.2 18.1 %fusion.1 = (f32[4,512]{1,0:T(4,128)S(1)}, f32[4,512,4096]{2,1,0:T(8,128)}) fusion(pred[512,4096]{1,0:T(8,128)(4,1)} %fusion.16, bf16[4096,4,128]{0,2,1:T(8,128)(2,1)} %bitcast.196, bf16[512,4,64]{2,0,1:T(8,128)(2,1)S(1)} %get-tuple-element.98, bf16[512,4,64]{2,0,1:T(8,128)(2,1)S(1)} %get-tuple-element.97), kind=kOutput, calls=%fused_computation.8 | convolution fusion | flops 2173696000 | bytes 40378368 | tf_op jit(solution)/shard_map/pshd,plhd->phsl/dot_general | solution.py:144
  108.3 15.4 %exponential_reduce_fusion = f32[4,512]{1,0:T(4,128)S(1)} fusion(f32[4,512,4096]{2,1,0:T(8,128)} %get-tuple-element.123, f32[4,512]{1,0:T(4,128)S(1)} %get-tuple-element.122, pred[512,4096]{1,0:T(8,128)(4,1)S(1)} %copy-done.1), kind=kLoop, calls=%fused_computation.6 | loop fusion | flops 33552384 | bytes 35667968 | tf_op jit(solution)/shard_map/reduce_sum | solution.py:153
  138.1 16.4 %fusion.36 = bf16[4,128,512]{2,1,0:T(8,128)(2,1)S(1)} fusion(f32[4,512,4096]{2,1,0:T(8,128)} %get-tuple-element.123, f32[4,512]{1,0:T(4,128)S(1)} %log_add_fusion, pred[512,4096]{1,0:T(8,128)(4,1)} %fusion.16, bf16[4096,512]{1,0:T(8,128)(2,1)} %all-gather.20.cloned.1.call-done), kind=kOutput, calls=%fused_computation.64 | convolution fusion | flops 2181300224 | bytes 40378368 | tf_op jit(solution)/shard_map/phsl,plhd->pshd/dot_general | solution.py:155
  162.1 31.9 %reduce-scatter.13.cloned.1.call-done = bf16[128,2048]{1,0:T(8,128)(2,1)} async-done(((bf16[512,2048]{1,0:T(8,128)(2,1)}), bf16[128,2048]{1,0:T(8,128)(2,1)}) %reduce-scatter.13.cloned.1.call-update) | async-done | bytes 524304 | tf_op jit(solution)/shard_map/reduce_scatter | solution.py:62
  201.7 36.2 %all_gather.27 = f32[4096,16]{0,1:T(8,128)S(1)} all-gather(f32[128,16]{0,1:T(8,128)S(1)} %broadcast_select_fusion.1), channel_id=1, replica_groups=mesh['dp'=4,'expert'=8] {'dp','expert'}, dimensions={0}, use_global_device_ids=true | all-gather | bytes 270336 | tf_op jit(solution)/shard_map/all_gather | solution.py:50
  238.6 72.7 %all-gather.12.cloned.1.call-done = bf16[4096,2048]{1,0:T(8,128)(2,1)} async-done(((bf16[128,2048]{1,0:T(8,128)(2,1)}), bf16[4096,2048]{1,0:T(8,128)(2,1)}) %all-gather.12.cloned.1.call-update) | async-done | bytes 16777232 | tf_op jit(solution)/shard_map/all_gather | solution.py:50
  341.4 86.0 %all-gather.22.cloned.1.call-done = bf16[1,4096,2048]{2,1,0:T(8,128)(2,1)} async-done(((bf16[1,128,2048]{2,1,0:T(8,128)(2,1)}), bf16[1,4096,2048]{2,1,0:T(8,128)(2,1)}) %all-gather.22.cloned.1.call-update) | async-done | bytes 16777232 | tf_op jit(solution)/shard_map/all_gather | solution.py:50
  427.3 24.6 %multiply_reduce_fusion.1 = (f32[4096,2]{0,1:T(2,128)}, bf16[4096,2,256]{0,2,1:T(8,128)(2,1)}, bf16[4096,2,256]{0,2,1:T(8,128)(2,1)}, bf16[4096,2,256]{0,2,1:T(8,128)(2,1)}) fusion(f32[4096,2,256]{0,2,1:T(8,128)} %fusion.11, f32[4096,2,256]{0,2,1:T(8,128)} %fusion.13, f32[4096,2]{0,1:T(2,128)S(1)} %copy-done.28, bf16[2,256,2048]{2,1,0:T(8,128)(2,1)S(1)} %copy-done, ...), kind=kOutput, calls=%fused_computation.23 | convolution fusion | flops 8629772288 | bytes 48300032 | tf_op jit(solution)/shard_map/td,jfd->tjf/dot_general | solution.py:192
  453.5 18.3 %fusion.81 = f32[4096,2048,1]{1,0,2:T(8,128)} fusion(bf16[4096,2,256]{0,2,1:T(8,128)(2,1)} %get-tuple-element.92, bf16[2,2048,256]{2,1,0:T(8,128)(2,1)} %param.26), kind=kOutput, calls=%fused_computation.158 | convolution fusion | flops 8589934592 | bytes 39845888 | tf_op jit(solution)/shard_map/tjf,jdf->td/dot_general | solution.py:204
  471.8 22.8 %fusion = bf16[4096,2048]{1,0:T(8,128)(2,1)} fusion(f32[4096,2048,1]{1,0,2:T(8,128)} %fusion.81, bf16[4096,2,256]{0,2,1:T(8,128)(2,1)} %get-tuple-element.94, bf16[2,2048,256]{2,1,0:T(8,128)(2,1)} %param.27), kind=kOutput, calls=%fused_computation.1 | convolution fusion | flops 8606711808 | bytes 56623104 | tf_op jit(solution)/shard_map/tjf,jdf->td/dot_general | solution.py:205
  494.6 78.7 %reduce-scatter.19.cloned.1.call-done = f32[128,16]{0,1:T(8,128)} async-done(((f32[4096,16]{0,1:T(8,128)}), f32[128,16]{0,1:T(8,128)}) %reduce-scatter.19.cloned.1.call-update) | async-done | bytes 8208 | tf_op jit(solution)/shard_map/reduce_scatter | solution.py:58
  574.0 195.3 %reduce-scatter.17.cloned.1.call-done = bf16[128,2048]{1,0:T(8,128)(2,1)} async-done(((bf16[4096,2048]{1,0:T(8,128)(2,1)}), bf16[128,2048]{1,0:T(8,128)(2,1)}) %reduce-scatter.17.cloned.1.call-update) | async-done | bytes 524304 | tf_op jit(solution)/shard_map/reduce_scatter | solution.py:58
  775.6 38.1 %all-gather.16.cloned.1.call-done = bf16[512,2048]{1,0:T(8,128)(2,1)} async-done(((bf16[128,2048]{1,0:T(8,128)(2,1)}), bf16[512,2048]{1,0:T(8,128)(2,1)}) %all-gather.16.cloned.1.call-update) | async-done | bytes 2097168 | tf_op jit(solution)/shard_map/all_gather | solution.py:54
  818.1 30.8 %multiply_reduce_fusion = (f32[4,512]{1,0:T(4,128)S(1)}, f32[4,512,4096]{2,1,0:T(8,128)}) fusion(f32[4,512,4096]{2,1,0:T(8,128)} %get-tuple-element.123, f32[4,512]{1,0:T(4,128)S(1)} %log_add_fusion, pred[512,4096]{1,0:T(8,128)(4,1)} %fusion.16, bf16[512,4,128]{0,2,1:T(8,128)(2,1)} %bitcast.204, bf16[4096,512]{1,0:T(8,128)(2,1)} %all-gather.20.cloned.1.call-done), kind=kOutput, calls=%fused_computation.4 | convolution fusion | flops 2189424640 | bytes 73940992 | tf_op jit(solution)/shard_map/pshd,plhd->phsl/dot_general | solution.py:244
  848.9 28.4 %multiply_convert_fusion = bf16[4,512,4096]{2,1,0:T(8,128)(2,1)} fusion(f32[4,512,4096]{2,1,0:T(8,128)} %get-tuple-element.128, f32[4,512,4096]{2,1,0:T(8,128)} %get-tuple-element.123, f32[4,512]{1,0:T(4,128)S(1)} %get-tuple-element.127, f32[4,512]{1,0:T(4,128)S(1)} %log_add_fusion, pred[512,4096]{1,0:T(8,128)(4,1)} %fusion.16), kind=kLoop, calls=%fused_computation.3 | loop fusion | flops 50331648 | bytes 85999616 | tf_op jit(solution)/shard_map/convert_element_type | solution.py:248
  888.3 18.0 %convolution_convert_fusion = bf16[4,128,4096]{2,1,0:T(8,128)(2,1)} fusion(bf16[512,4,128]{0,2,1:T(8,128)(2,1)} %bitcast.205, f32[4,512,4096]{2,1,0:T(8,128)} %get-tuple-element.123, f32[4,512]{1,0:T(4,128)S(1)} %log_add_fusion, pred[512,4096]{1,0:T(8,128)(4,1)} %fusion.16), kind=kOutput, calls=%fused_computation.31 | convolution fusion | flops 2183135232 | bytes 40378368 | tf_op jit(solution)/shard_map/phsl,pshd->plhd/dot_general | solution.py:257
  1016.8 154.9 %reduce-scatter.15.cloned.1.call-done = bf16[128,2048]{1,0:T(8,128)(2,1)} async-done(((bf16[4096,2048]{1,0:T(8,128)(2,1)}), bf16[128,2048]{1,0:T(8,128)(2,1)}) %reduce-scatter.15.cloned.1.call-update) | async-done | bytes 524304 | tf_op jit(solution)/shard_map/reduce_scatter | solution.py:58
  1171.8 41.4 %reduce-scatter.25.cloned.1.call-done = bf16[128,2048]{1,0:T(8,128)(2,1)} async-done(((bf16[512,2048]{1,0:T(8,128)(2,1)}), bf16[128,2048]{1,0:T(8,128)(2,1)}) %reduce-scatter.25.cloned.1.call-update) | async-done | bytes 524304 | tf_op jit(solution)/shard_map/reduce_scatter | solution.py:62
  1276.1 23.9 %all-reduce.6 = (bf16[2048]{0:T(1024)(128)(2,1)S(1)}, bf16[512]{0:T(512)(128)(2,1)S(1)}, bf16[512]{0:T(512)(128)(2,1)S(1)}, bf16[2048]{0:T(1024)(128)(2,1)S(1)}) all-reduce(bf16[2048]{0:T(1024)(128)(2,1)S(1)} %get-tuple-element.70, bf16[512]{0:T(512)(128)(2,1)S(1)} %get-tuple-element.74, ...), channel_id=11, replica_groups=mesh['dp'=4,'expert'=8] {'expert'}, use_global_device_ids=true, to_apply=%region_32.33.clone | all-reduce | flops 5120 | bytes 20480
  1317.6 35.2 %reduce-scatter.27.cloned.1.call-done = bf16[256,512]{1,0:T(8,128)(2,1)} async-done(((bf16[2048,512]{1,0:T(8,128)(2,1)}), bf16[256,512]{1,0:T(8,128)(2,1)}) %reduce-scatter.27.cloned.1.call-update) | async-done | bytes 262160 | tf_op jit(solution)/shard_map/reduce_scatter | solution.py:326
  1354.6 34.9 %reduce-scatter.29.cloned.1.call-done = bf16[256,512]{1,0:T(8,128)(2,1)} async-done(((bf16[2048,512]{1,0:T(8,128)(2,1)}), bf16[256,512]{1,0:T(8,128)(2,1)}) %reduce-scatter.29.cloned.1.call-update) | async-done | bytes 262160 | tf_op jit(solution)/shard_map/reduce_scatter | solution.py:329
  1391.3 37.5 %all-gather.14.cloned.1.call-done = bf16[512,2048]{1,0:T(8,128)(2,1)} async-done(((bf16[128,2048]{1,0:T(8,128)(2,1)}), bf16[512,2048]{1,0:T(8,128)(2,1)}) %all-gather.14.cloned.1.call-update) | async-done | bytes 2097168 | tf_op jit(solution)/shard_map/all_gather | solution.py:54
  1428.7 37.6 %all-gather.18.cloned.1.call-done = bf16[512,2048]{1,0:T(8,128)(2,1)} async-done(((bf16[128,2048]{1,0:T(8,128)(2,1)}), bf16[512,2048]{1,0:T(8,128)(2,1)}) %all-gather.18.cloned.1.call-update) | async-done | bytes 2097168 | tf_op jit(solution)/shard_map/all_gather | solution.py:54
  (251 shorter events, 330.1 us)
Async XLA Ops:
  7.2 420.2 %copy-start = (bf16[2,256,2048]{2,1,0:T(8,128)(2,1)S(1)}, bf16[2,256,2048]{2,1,0:T(8,128)(2,1)}, u32[]{:S(2)}) copy-start(bf16[2,256,2048]{2,1,0:T(8,128)(2,1)} %param.28) | copy-start | bytes 6291460
  7.2 83.0 %all-gather.10.cloned.1.call-start = ((), (), s32[]{:S(2)}) async-start(), calls=%async_computation.12 | async-start | bytes 4718592 | tf_op jit(solution)/shard_map/all_gather | solution.py:136
  46.0 92.1 %all-gather.20.cloned.1.call-start = ((), (), s32[]{:S(2)}) async-start(), calls=%async_computation.28 | async-start | bytes 4718592 | tf_op jit(solution)/shard_map/all_gather | solution.py:137
  50.4 143.6 %reduce-scatter.13.cloned.1.call-start = ((), (), s32[]{:S(2)}) async-start(), calls=%async_computation.13 | async-start | bytes 2621440 | tf_op jit(solution)/shard_map/reduce_scatter | solution.py:62
  157.9 153.3 %all-gather.12.cloned.1.call-start = ((), (), s32[]{:S(2)}) async-start(), calls=%async_computation.14 | async-start | bytes 17301504 | tf_op jit(solution)/shard_map/all_gather | solution.py:50
  196.7 230.7 %all-gather.22.cloned.1.call-start = ((), (), s32[]{:S(2)}) async-start(), calls=%async_computation.29 | async-start | bytes 17301504 | tf_op jit(solution)/shard_map/all_gather | solution.py:50
  198.6 374.7 %reduce-scatter.19.cloned.1.call-start = ((), (), s32[]{:S(2)}) async-start(), calls=%async_computation.18 | async-start | bytes 270336 | tf_op jit(solution)/shard_map/reduce_scatter | solution.py:58
  326.6 100.8 %copy-start.28 = (f32[4096,2]{0,1:T(2,128)S(1)}, f32[4096,2]{0,1:T(2,128)}, u32[]{:S(2)}) copy-start(f32[4096,2]{0,1:T(2,128)} %constant_dynamic-slice_fusion.1) | copy-start | bytes 98308
  453.4 315.9 %reduce-scatter.17.cloned.1.call-start = ((), (), s32[]{:S(2)}) async-start(), calls=%async_computation.17 | async-start | bytes 17301504 | tf_op jit(solution)/shard_map/reduce_scatter | solution.py:58
  494.5 274.8 %copy-start.34 = (f32[128]{0:T(128)S(1)}, f32[128]{0:T(128)}, u32[]{:S(2)}) copy-start(f32[128]{0:T(128)} %copy-done.33) | copy-start | bytes 1540
  494.6 319.2 %all-gather.16.cloned.1.call-start = ((), (), s32[]{:S(2)}) async-start(), calls=%async_computation.19 | async-start | bytes 2621440 | tf_op jit(solution)/shard_map/all_gather | solution.py:54
  574.0 244.0 %copy-start.49 = (f32[128]{0:T(128)}, f32[128]{0:T(128)S(1)}, u32[]{:S(2)}) copy-start(f32[128]{0:T(128)S(1)} %multiply_reduce_fusion.10) | copy-start | bytes 1540
  775.6 160.3 %reduce-scatter.21.cloned.1.call-start = ((), (), s32[]{:S(2)}) async-start(), calls=%async_computation.20 | async-start | bytes 4718592 | tf_op jit(solution)/shard_map/reduce_scatter | solution.py:264
  888.2 98.8 %reduce-scatter.23.cloned.1.call-start = ((), (), s32[]{:S(2)}) async-start(), calls=%async_computation.21 | async-start | bytes 4718592 | tf_op jit(solution)/shard_map/reduce_scatter | solution.py:270
  906.3 265.5 %reduce-scatter.15.cloned.1.call-start = ((), (), s32[]{:S(2)}) async-start(), calls=%async_computation.15 | async-start | bytes 17301504 | tf_op jit(solution)/shard_map/reduce_scatter | solution.py:58
  921.1 292.1 %reduce-scatter.25.cloned.1.call-start = ((), (), s32[]{:S(2)}) async-start(), calls=%async_computation.22 | async-start | bytes 2621440 | tf_op jit(solution)/shard_map/reduce_scatter | solution.py:62
  997.0 277.3 %reduce-scatter.33.cloned.1.call-start = ((), (), s32[]{:S(2)}) async-start(), calls=%async_computation.27 | async-start | bytes 2359296 | tf_op jit(solution)/shard_map/reduce_scatter | solution.py:335
  1001.4 298.7 %reduce-scatter.35.cloned.1.call-start = ((), (), s32[]{:S(2)}) async-start(), calls=%async_computation.30 | async-start | bytes 73728 | tf_op jit(solution)/shard_map/reduce_scatter | solution.py:67
  1003.0 312.8 %reduce-scatter.31.cloned.1.call-start = ((), (), s32[]{:S(2)}) async-start(), calls=%async_computation.26 | async-start | bytes 2359296 | tf_op jit(solution)/shard_map/reduce_scatter | solution.py:332
  1007.5 345.3 %reduce-scatter.27.cloned.1.call-start = ((), (), s32[]{:S(2)}) async-start(), calls=%async_computation.24 | async-start | bytes 2359296 | tf_op jit(solution)/shard_map/reduce_scatter | solution.py:326
  1012.1 377.3 %reduce-scatter.29.cloned.1.call-start = ((), (), s32[]{:S(2)}) async-start(), calls=%async_computation.25 | async-start | bytes 2359296 | tf_op jit(solution)/shard_map/reduce_scatter | solution.py:329
  1016.8 199.8 %copy-start.54 = (u32[32]{0:T(128)S(1)}, u32[32]{0:T(128)}, u32[]{:S(2)}) copy-start(u32[32]{0:T(128)} %constant.69) | copy-start | bytes 388
  1016.8 411.9 %all-gather.14.cloned.1.call-start = ((), (), s32[]{:S(2)}) async-start(), calls=%async_computation.16 | async-start | bytes 2621440 | tf_op jit(solution)/shard_map/all_gather | solution.py:54
  1216.3 250.0 %all-gather.18.cloned.1.call-start = ((), (), s32[]{:S(2)}) async-start(), calls=%async_computation.23 | async-start | bytes 2621440 | tf_op jit(solution)/shard_map/all_gather | solution.py:54
  (50 other events, 783.9 us)
Sparse Core Ops, SparseCore 0:
  46.1 44.0 all-gather.9
  92.4 45.6 all-gather.19
  158.1 35.9 reduce-scatter.12
  197.5 113.7 all-gather.11
  314.7 112.5 all-gather.21
  453.6 119.6 reduce-scatter.18
  575.6 193.7 reduce-scatter.16
  775.7 38.0 all-gather.15
  888.3 47.4 reduce-scatter.20
  938.6 48.3 reduce-scatter.22
  989.3 182.4 reduce-scatter.14
  1175.2 37.9 reduce-scatter.24
  1215.5 32.2 reduce-scatter.32
  1250.4 29.2 reduce-scatter.34
  1281.9 33.8 reduce-scatter.30
  1317.9 34.8 reduce-scatter.26
  1354.9 34.4 reduce-scatter.28
  1391.2 37.5 all-gather.13
  1431.1 35.1 all-gather.17

commit v2 on v1

--- a/solution.py
+++ b/solution.py
@@ -1,6 +1,10 @@
+import functools
+
 import jax
 import jax.numpy as jnp
 from jax import lax
+from jax.experimental import pallas as pl
+from jax.experimental.pallas import tpu as pltpu
 from jax.sharding import PartitionSpec as P
 
 HD = 128
@@ -46,25 +50,505 @@
 ALL = ("dp", "expert")
 
 
-def gather_all(rows):
-    return lax.all_gather(rows, ALL, axis=0, tiled=True)
+DEVICES = pl.DeviceIdType.MESH
+
+
+def greet(device):
+    pl.semaphore_signal(
+        pltpu.get_barrier_semaphore(), inc=1, device_id=device, device_id_type=DEVICES
+    )
+
+
+def send(source, target, send_sem, arrive_sem, device):
+    return pltpu.make_async_remote_copy(
+        src_ref=source,
+        dst_ref=target,
+        send_sem=send_sem,
+        recv_sem=arrive_sem,
+        device_id=device,
+        device_id_type=DEVICES,
+    )
+
+
+def corners(dp):
+    return dp + 1 - 2 * (dp % 2), (dp + 2) % 4
+
+
+def gather_all_kernel(line, x_ref, g_ref, out_ref, table_ref, sent, arrived, own_sem):
+    dp, place = lax.axis_index("dp"), lax.axis_index("expert")
+    z, c = place // 2, place % 2
+    side_x, side_y = corners(dp)
+    far = 3 - dp
+    devices = (
+        (dp, place + 2),
+        (dp, place - 2),
+        (side_x, place),
+        (side_y, place),
+        (dp, 2 * z + 1 - c),
+    )
+    up, down, along_x, along_y, pair = range(5)
+    has_up, has_down = z < line - 1, z > 0
+    for way in (along_x, along_y, pair):
+        greet(devices[way])
+    pl.when(has_up)(lambda: greet(devices[up]))
+    pl.when(has_down)(lambda: greet(devices[down]))
+    greeted = 3 + has_up.astype(jnp.int32) + has_down.astype(jnp.int32)
+    pl.semaphore_wait(pltpu.get_barrier_semaphore(), greeted)
+
+    pieces = (0, 1, 2)
+
+    def slot(corner, height, core):
+        return corner * (2 * line) + 2 * height + core
+
+    def part(s, p):
+        return table_ref.at[s] if p == 2 else out_ref.at[s, p]
+
+    def copy(s, p, way, source=None):
+        target = part(s, p)
+        return send(
+            target if source is None else source,
+            target,
+            sent.at[s, p, way],
+            arrived.at[s, p],
+            devices[way],
+        )
+
+    def arrive(s, p):
+        copy(s, p, pair).wait_recv()
+
+    mine = slot(dp, z, c)
+    for p in pieces:
+        source = g_ref if p == 2 else x_ref.at[p]
+        pltpu.make_async_copy(source, part(mine, p), own_sem.at[p]).start()
+        pl.when(has_up)(lambda: copy(mine, p, up, source).start())
+        pl.when(has_down)(lambda: copy(mine, p, down, source).start())
+        for way in (along_x, along_y, pair):
+            copy(mine, p, way, source).start()
+
+    def spread(s, p):
+        for way in (along_x, along_y, pair):
+            copy(s, p, way).start()
+
+    def column(away):
+        def below():
+            s = slot(dp, z - away, c)
+            for p in pieces:
+                arrive(s, p)
+                pl.when(has_up)(lambda: copy(s, p, up).start())
+                spread(s, p)
+
+        def above():
+            s = slot(dp, z + away, c)
+            for p in pieces:
+                arrive(s, p)
+                pl.when(has_down)(lambda: copy(s, p, down).start())
+                spread(s, p)
+
+        pl.when((away > 0) & (away < line) & (z - away >= 0))(below)
+        pl.when((away > 0) & (away < line) & (z + away < line))(above)
+
+    def sides(height):
+        for p in pieces:
+            s = slot(side_x, height, c)
+            arrive(s, p)
+            if p != 1:
+                copy(s, p, along_y).start()
+            copy(s, p, pair).start()
+            s = slot(side_y, height, c)
+            arrive(s, p)
+            if p == 1:
+                copy(s, p, along_x).start()
+            copy(s, p, pair).start()
+
+    def opposite(height):
+        for p in pieces:
+            s = slot(far, height, c)
+            arrive(s, p)
+            copy(s, p, pair).start()
+
+    def both(away, visit):
+        pl.when((away >= 0) & (away < line) & (z - away >= 0))(lambda: visit(z - away))
+        pl.when((away > 0) & (away < line) & (z + away < line))(lambda: visit(z + away))
+
+    def step(k, carry):
+        column(k)
+        both(k - 1, sides)
+        both(k - 2, opposite)
+        return carry
+
+    lax.fori_loop(1, line + 2, step, 0)
+
+    def finish(height, carry):
+        for p in pieces:
+            for corner in range(4):
+                arrive(slot(corner, height, 1 - c), p)
+                copy(slot(corner, height, c), p, pair).wait_send()
+            s = slot(dp, height, c)
+            copy(s, p, along_x).wait_send()
+            copy(s, p, along_y).wait_send()
+            if p == 1:
+                copy(slot(side_y, height, c), p, along_x).wait_send()
+            else:
+                copy(slot(side_x, height, c), p, along_y).wait_send()
+            pl.when(has_up & (height <= z))(lambda: copy(s, p, up).wait_send())
+            pl.when(has_down & (height >= z))(lambda: copy(s, p, down).wait_send())
+        return carry
+
+    lax.fori_loop(0, line, finish, 0)
+    for p in pieces:
+        source = g_ref if p == 2 else x_ref.at[p]
+        pltpu.make_async_copy(source, part(mine, p), own_sem.at[p]).wait()
+
+
+def gather_all(rows, table, line):
+    count, width = rows.shape
+    slots = 8 * line
+    gathered, tables = pl.pallas_call(
+        functools.partial(gather_all_kernel, line),
+        out_shape=(
+            jax.ShapeDtypeStruct((slots, 2, count // 2, width), rows.dtype),
+            jax.ShapeDtypeStruct((slots, *table.shape), table.dtype),
+        ),
+        in_specs=[pl.BlockSpec(memory_space=pltpu.VMEM)] * 2,
+        out_specs=[pl.BlockSpec(memory_space=pl.ANY)] * 2,
+        scratch_shapes=[
+            pltpu.SemaphoreType.DMA((slots, 3, 5)),
+            pltpu.SemaphoreType.DMA((slots, 3)),
+            pltpu.SemaphoreType.DMA((3,)),
+        ],
+        compiler_params=pltpu.CompilerParams(collective_id=1, has_side_effects=True),
+        name="gather_all",
+    )(rows.reshape(2, count // 2, width), table)
+    return gathered.reshape(slots * count, width), tables
+
+
+def gather_square_kernel(x_ref, out_ref, sent, arrived, own_sem):
+    dp, place = lax.axis_index("dp"), lax.axis_index("expert")
+    side_x, side_y = corners(dp)
+    devices = ((side_x, place), (side_y, place))
+    for device in devices:
+        greet(device)
+    pl.semaphore_wait(pltpu.get_barrier_semaphore(), 2)
+
+    def copy(corner, p, way, source=None):
+        target = out_ref.at[corner, p]
+        return send(
+            target if source is None else source,
+            target,
+            sent.at[corner, p, way],
+            arrived.at[corner, p],
+            devices[way],
+        )
+
+    for p in (0, 1):
+        pltpu.make_async_copy(x_ref.at[p], out_ref.at[dp, p], own_sem.at[p]).start()
+        for way in (0, 1):
+            copy(dp, p, way, x_ref.at[p]).start()
+    copy(side_x, 0, 0).wait_recv()
+    copy(side_x, 0, 1).start()
+    copy(side_y, 0, 0).wait_recv()
+    copy(side_x, 1, 0).wait_recv()
+    copy(side_y, 1, 0).wait_recv()
+    copy(side_y, 1, 0).start()
+    for p in (0, 1):
+        copy(3 - dp, p, 0).wait_recv()
+        for way in (0, 1):
+            copy(dp, p, way).wait_send()
+        pltpu.make_async_copy(x_ref.at[p], out_ref.at[dp, p], own_sem.at[p]).wait()
+    copy(side_x, 0, 1).wait_send()
+    copy(side_y, 1, 0).wait_send()
 
 
 def gather_dp(rows):
-    return lax.all_gather(rows, "dp", axis=0, tiled=True)
-
-
-def scatter_all(rows):
-    return lax.psum_scatter(rows, ALL, scatter_dimension=0, tiled=True).astype(jnp.float32)
+    count, width = rows.shape
+    gathered = pl.pallas_call(
+        gather_square_kernel,
+        out_shape=jax.ShapeDtypeStruct((4, 2, count // 2, width), rows.dtype),
+        in_specs=[pl.BlockSpec(memory_space=pltpu.VMEM)],
+        out_specs=pl.BlockSpec(memory_space=pl.ANY),
+        scratch_shapes=[
+            pltpu.SemaphoreType.DMA((4, 2, 2)),
+            pltpu.SemaphoreType.DMA((4, 2)),
+            pltpu.SemaphoreType.DMA((2,)),
+        ],
+        compiler_params=pltpu.CompilerParams(collective_id=2, has_side_effects=True),
+        name="gather_dp",
+    )(rows.reshape(2, count // 2, width))
+    return gathered.reshape(4 * count, width)
+
+
+def farthest(line, z, k):
+    total = jnp.int32(0)
+    for at in range(line):
+        order = sorted(range(line), key=lambda place: (-abs(place - at), place))
+        place = sum([jnp.where(k == i, order[i], 0) for i in range(line)])
+        total = total + jnp.where(z == at, place, 0)
+    return total
+
+
+def reduce_kernel(
+    square,
+    line,
+    paired,
+    x_ref,
+    out_ref,
+    acc,
+    got_pair,
+    got_x,
+    got_y,
+    got_far_x,
+    got_far_y,
+    got_below,
+    got_above,
+    load_sem,
+    pair_sem,
+    x_sem,
+    y_sem,
+    far_x_sem,
+    far_y_sem,
+    below_sem,
+    above_sem,
+):
+    dp, place = lax.axis_index("dp"), lax.axis_index("expert")
+    z, c = place // 2, place % 2
+    side_x, side_y = corners(dp)
+    core = c if paired else 0
+    own = dp if square else 0
+    quarters = (3 - dp, side_x, side_y, dp) if square else (0,)
+    to_x, to_y = (side_x, place), (side_y, place)
+    to_pair, to_up, to_down = (dp, 2 * z + 1 - c), (dp, place + 2), (dp, place - 2)
+    greeted = 0
+    if square:
+        greet(to_x)
+        greet(to_y)
+        greeted += 2
+    if paired:
+        greet(to_pair)
+        greeted += 1
+    if line > 1:
+        pl.when(z > 0)(lambda: greet(to_down))
+        pl.when(z < line - 1)(lambda: greet(to_up))
+        greeted = greeted + (z > 0).astype(jnp.int32) + (z < line - 1).astype(jnp.int32)
+    pl.semaphore_wait(pltpu.get_barrier_semaphore(), greeted)
+
+    def load(q, height, p):
+        return pltpu.make_async_copy(
+            x_ref.at[q, height, core, p], acc.at[q, height, p], load_sem.at[q, height, p]
+        )
+
+    def hand(q, height, p):
+        at = (q, height, p)
+        source = x_ref.at[q, height, 1 - core, p]
+        return send(source, got_pair.at[at], pair_sem.at[0, *at], pair_sem.at[1, *at], to_pair)
+
+    def along_x(height, p):
+        at = (height, p)
+        return send(
+            acc.at[side_x, height, p], got_x.at[at], x_sem.at[0, *at], x_sem.at[1, *at], to_x
+        )
+
+    def along_y(height, p):
+        at = (height, p)
+        return send(
+            acc.at[side_y, height, p], got_y.at[at], y_sem.at[0, *at], y_sem.at[1, *at], to_y
+        )
+
+    def far_x(height):
+        return send(
+            acc.at[3 - dp, height, 0],
+            got_far_x.at[height],
+            far_x_sem.at[0, height],
+            far_x_sem.at[1, height],
+            to_x,
+        )
+
+    def far_y(height):
+        return send(
+            acc.at[3 - dp, height, 1],
+            got_far_y.at[height],
+            far_y_sem.at[0, height],
+            far_y_sem.at[1, height],
+            to_y,
+        )
+
+    def climb(height, p):
+        at = (height, p)
+        return send(
+            acc.at[own, height, p], got_below.at[at], below_sem.at[0, *at], below_sem.at[1, *at], to_up
+        )
+
+    def descend(height, p):
+        at = (height, p)
+        return send(
+            acc.at[own, height, p],
+            got_above.at[at],
+            above_sem.at[0, *at],
+            above_sem.at[1, *at],
+            to_down,
+        )
+
+    def height_of(k):
+        return farthest(line, z, k) if line > 1 else 0
+
+    def start(k, carry):
+        for q in quarters:
+            for p in (0, 1):
+                load(q, height_of(k), p).start()
+                if paired:
+                    hand(q, height_of(k), p).start()
+        return carry
+
+    lax.fori_loop(0, line, start, 0)
+
+    def step(k, carry):
+        def cores():
+            height = height_of(k)
+            for q in quarters:
+                for p in (0, 1):
+                    load(q, height, p).wait()
+                    if paired:
+                        hand(q, height, p).wait_recv()
+                        acc[q, height, p] = acc[q, height, p] + got_pair[q, height, p]
+                if square and q is quarters[0]:
+                    far_x(height).start()
+                    far_y(height).start()
+
+        def sides():
+            height = height_of(k - 1)
+            along_x(height, 0).start()
+            along_y(height, 1).start()
+            far_x(height).wait_recv()
+            acc[side_y, height, 0] = acc[side_y, height, 0] + got_far_x[height]
+            along_y(height, 0).start()
+            far_y(height).wait_recv()
+            acc[side_x, height, 1] = acc[side_x, height, 1] + got_far_y[height]
+            along_x(height, 1).start()
+
+        def column():
+            height = height_of(k - 2)
+            for p in (0, 1):
+                if square:
+                    along_x(height, p).wait_recv()
+                    along_y(height, p).wait_recv()
+                    total = acc[own, height, p].astype(jnp.float32)
+                    total = total + got_x[height, p].astype(jnp.float32)
+                    total = total + got_y[height, p].astype(jnp.float32)
+                    acc[own, height, p] = total.astype(acc.dtype)
+                if line > 1:
+                    pl.when((z == 0) & (height > z))(lambda: climb(height, p).start())
+                    pl.when((z == line - 1) & (height < z))(lambda: descend(height, p).start())
+
+        def pass_on():
+            height = height_of(k - 3)
+            for p in (0, 1):
+
+                def upwards():
+                    climb(height, p).wait_recv()
+                    acc[own, height, p] = acc[own, height, p] + got_below[height, p]
+                    climb(height, p).start()
+
+                def downwards():
+                    descend(height, p).wait_recv()
+                    acc[own, height, p] = acc[own, height, p] + got_above[height, p]
+                    descend(height, p).start()
+
+                pl.when((height > z) & (z > 0))(upwards)
+                pl.when((height < z) & (z < line - 1))(downwards)
+
+        pl.when(k < line)(cores)
+        if square:
+            pl.when((k >= 1) & (k < line + 1))(sides)
+        pl.when((k >= 2) & (k < line + 2))(column)
+        if line > 1:
+            pl.when(k >= 3)(pass_on)
+        return carry
+
+    lax.fori_loop(0, line + (3 if line > 1 else 2), step, 0)
+    home = z if line > 1 else 0
+    for p in (0, 1):
+        out_ref[p] = acc[own, home, p].astype(jnp.float32)
+        if line > 1:
+
+            def from_below():
+                climb(z, p).wait_recv()
+                out_ref[p] = out_ref[p] + got_below[z, p].astype(jnp.float32)
+
+            def from_above():
+                descend(z, p).wait_recv()
+                out_ref[p] = out_ref[p] + got_above[z, p].astype(jnp.float32)
+
+            pl.when(z > 0)(from_below)
+            pl.when(z < line - 1)(from_above)
+
+    def finish(height, carry):
+        if square:
+            far_x(height).wait_send()
+            far_y(height).wait_send()
+        for p in (0, 1):
+            if paired:
+                for q in quarters:
+                    hand(q, height, p).wait_send()
+            if square:
+                along_x(height, p).wait_send()
+                along_y(height, p).wait_send()
+            if line > 1:
+                pl.when(height > z)(lambda: climb(height, p).wait_send())
+                pl.when(height < z)(lambda: descend(height, p).wait_send())
+        return carry
+
+    lax.fori_loop(0, line, finish, 0)
+
+
+def reduce_to(parts, square, line, paired, name, number):
+    _, rows, width = parts.shape
+    quarters, cores, half = (4 if square else 1), (2 if paired else 1), rows // 2
+
+    def space(used, *shape):
+        return pltpu.VMEM((*shape, half, width) if used else (*shape, 16, 128), parts.dtype)
+
+    sems = pltpu.SemaphoreType.DMA
+    total = pl.pallas_call(
+        functools.partial(reduce_kernel, square, line, paired),
+        out_shape=jax.ShapeDtypeStruct((2, half, width), jnp.float32),
+        in_specs=[pl.BlockSpec(memory_space=pl.ANY)],
+        out_specs=pl.BlockSpec(memory_space=pltpu.VMEM),
+        scratch_shapes=[
+            space(True, quarters, line, 2),
+            space(paired, quarters, line, 2),
+            space(square, line, 2),
+            space(square, line, 2),
+            space(square, line),
+            space(square, line),
+            space(line > 1, line, 2),
+            space(line > 1, line, 2),
+            sems((quarters, line, 2)),
+            sems((2, quarters, line, 2)),
+            sems((2, line, 2)),
+            sems((2, line, 2)),
+            sems((2, line)),
+            sems((2, line)),
+            sems((2, line, 2)),
+            sems((2, line, 2)),
+        ],
+        compiler_params=pltpu.CompilerParams(
+            collective_id=number, has_side_effects=True, vmem_limit_bytes=60 << 20
+        ),
+        name=name,
+    )(parts.reshape(quarters, line, cores, 2, half, width))
+    return total.reshape(rows, width)
 
 
 def scatter_dp(rows):
-    return lax.psum_scatter(rows, "dp", scatter_dimension=0, tiled=True).astype(jnp.float32)
-
-
-def scatter_sum(value):
-    total = lax.psum(value.astype(jnp.bfloat16), "dp")
-    return lax.psum_scatter(total, "expert", scatter_dimension=0, tiled=True).astype(jnp.float32)
+    return reduce_to(rows.reshape(4, -1, rows.shape[1]), True, 1, False, "scatter_dp", 3)
+
+
+def scatter_all(rows, line):
+    parts = rows.reshape(8 * line, -1, rows.shape[1])
+    return reduce_to(parts, True, line, True, "scatter_all", 4)
+
+
+def scatter_expert(parts, line):
+    return reduce_to(parts, False, line, True, "scatter_expert", 5)
 
 
 def head_totals(first_sum, second_sum):
@@ -94,6 +578,7 @@
     local_heads = local_width // HD
     experts = w_router.shape[1]
     groups = lax.axis_size("expert")
+    line = groups // 2
     pack_span = seg_rows * groups
     local_experts = w_gate.shape[0]
     scale_factor = HD ** (-0.5)
@@ -180,12 +665,14 @@
     chosen = own_rows(routes[:, 0, :])
     expert_range = jnp.arange(experts, dtype=jnp.int32)
     named = jnp.any(chosen[:, :, None] == expert_range, axis=1)
-    gate_table = gather_all(jnp.where(named, router, 0.0))
     first_expert = lax.axis_index("expert") * local_experts
+    top_own = own_rows(d_output[0])
+    top_all = lax.all_gather(top_own, ALL, axis=0, tiled=True)
+    xn_all, gate_table = gather_all(
+        second_normed_input.astype(jnp.bfloat16), jnp.where(named, router, 0.0).T, line
+    )
     gates = lax.dynamic_slice_in_dim(gate_table, first_expert, local_experts, 1)
-    xn_all = gather_all(second_normed_input.astype(jnp.bfloat16))
-    top_own = own_rows(d_output[0])
-    top_all = gather_all(top_own)
+    gates = jnp.transpose(gates, (0, 2, 1)).reshape(-1, local_experts)
 
     gate_pre = jnp.einsum("td,jdf->tjf", xn_all, w_gate, preferred_element_type=jnp.float32)
     up_pre = jnp.einsum("td,jdf->tjf", xn_all, w_up, preferred_element_type=jnp.float32)
@@ -209,13 +696,16 @@
     grad_gate = jnp.einsum("td,tjf->jdf", xn_all, grad_gate_pre, preferred_element_type=jnp.float32)
     grad_up = jnp.einsum("td,tjf->jdf", xn_all, grad_up_pre, preferred_element_type=jnp.float32)
 
-    moe_out = scatter_all(moe_part.astype(jnp.bfloat16))
+    moe_out = lax.psum_scatter(
+        moe_part.astype(jnp.bfloat16), ALL, scatter_dimension=0, tiled=True
+    ).astype(jnp.float32)
     output = gather_dp((hidden_state + moe_out).astype(jnp.bfloat16))[None]
 
     gate_columns = jnp.zeros((gate_part.shape[0], experts), jnp.float32)
     gate_columns = lax.dynamic_update_slice_in_dim(gate_columns, gate_part, first_expert, 1)
-    grad_router_probs = jnp.where(named, scatter_all(gate_columns), 0.0)
-    grad_xn_exp = scatter_all(grad_rows.astype(jnp.bfloat16))
+    gate_sums = lax.psum_scatter(gate_columns, ALL, scatter_dimension=0, tiled=True)
+    grad_router_probs = jnp.where(named, gate_sums, 0.0)
+    grad_xn_exp = scatter_all(grad_rows.astype(jnp.bfloat16), line)
     grad_logits = router * (
         grad_router_probs - jnp.sum(router * grad_router_probs, axis=-1, keepdims=True)
     )
@@ -294,14 +784,9 @@
         jnp.bfloat16
     )
     grad_v_raw = grad_values.astype(jnp.bfloat16)
-    grad_query = jnp.einsum(
-        "psd,psk->dk", first_normed_input, grad_q_raw, preferred_element_type=jnp.float32
-    )
-    grad_key = jnp.einsum(
-        "psd,psk->dk", first_normed_input, grad_k_raw, preferred_element_type=jnp.float32
-    )
-    grad_value = jnp.einsum(
-        "psd,psk->dk", first_normed_input, grad_v_raw, preferred_element_type=jnp.float32
+    grad_heads_raw = jnp.concatenate([grad_q_raw[0], grad_k_raw[0], grad_v_raw[0]], axis=1)
+    grad_projections = jnp.einsum(
+        "sd,sk->dk", first_normed_input[0], grad_heads_raw, preferred_element_type=jnp.float32
     )
     grad_first_normed_input = jnp.einsum(
         "psk,dk->psd", grad_q_raw, w_query, preferred_element_type=jnp.float32
@@ -312,51 +797,58 @@
     grad_first_normed_input = grad_first_normed_input + jnp.einsum(
         "psk,dk->psd", grad_v_raw, w_value, preferred_element_type=jnp.float32
     )
-    gain_portion = jnp.sum(grad_first_normed_input * first_unit_input, axis=(0, 1))
-    grad_first_unit_input = grad_first_normed_input * attention_norm_gain
-    input_part = first_inverse_norm * (
-        grad_first_unit_input
-        - first_unit_input
-        * jnp.mean(grad_first_unit_input * first_unit_input, axis=-1, keepdims=True)
-    )
-    input_total = scatter_dp(input_part[0].astype(jnp.bfloat16))
-    grad_input = gather_dp((grad_hidden + input_total).astype(jnp.bfloat16))
-    grad_input = grad_input.astype(jnp.float32)[None]
-    reduced_dense = (
-        lax.psum_scatter(
-            grad_query.astype(jnp.bfloat16), "expert", scatter_dimension=0, tiled=True
-        ).astype(jnp.float32),
-        lax.psum_scatter(
-            grad_key.astype(jnp.bfloat16), "expert", scatter_dimension=0, tiled=True
-        ).astype(jnp.float32),
-        lax.psum_scatter(
-            grad_value.astype(jnp.bfloat16), "expert", scatter_dimension=0, tiled=True
-        ).astype(jnp.float32),
-        lax.psum_scatter(
-            grad_out.astype(jnp.bfloat16), "expert", scatter_dimension=0, tiled=True
-        ).astype(jnp.float32),
-        lax.psum_scatter(
-            grad_q_gain.astype(jnp.bfloat16), "expert", scatter_dimension=0, tiled=True
-        ).astype(jnp.float32),
-        lax.psum_scatter(
-            grad_k_gain.astype(jnp.bfloat16), "expert", scatter_dimension=0, tiled=True
-        ).astype(jnp.float32),
-        scatter_sum(gain_portion),
-        scatter_sum(grad_expert_norm_gain),
-        scatter_sum(grad_router),
-    )
+    grad_first = scatter_dp(grad_first_normed_input[0].astype(jnp.bfloat16))
+    unit_own = own_rows(first_unit_input[0])
+    grad_attn_gain = jnp.sum(grad_first * unit_own, axis=0)
+    grad_first = grad_first * attention_norm_gain
+    grad_input = grad_hidden + own_rows(first_inverse_norm[0]) * (
+        grad_first - unit_own * jnp.mean(grad_first * unit_own, axis=-1, keepdims=True)
+    )
+    grad_input = gather_dp(grad_input.astype(jnp.bfloat16)).astype(jnp.float32)[None]
+
+    wide = grad_projections.shape[1]
+    small = jnp.concatenate(
+        [
+            grad_q_gain.reshape(groups, -1),
+            grad_k_gain.reshape(groups, -1),
+            grad_attn_gain.reshape(groups, -1),
+            grad_expert_norm_gain.reshape(groups, -1),
+            grad_router.reshape(groups, -1),
+        ],
+        axis=1,
+    )
+    small_rows = 32
+    filled = small.shape[1]
+    small = jnp.pad(small, ((0, 0), (0, small_rows * wide - filled)))
+    parts = jnp.concatenate(
+        [
+            grad_projections.astype(jnp.bfloat16).reshape(groups, -1, wide),
+            small.astype(jnp.bfloat16).reshape(groups, small_rows, wide),
+        ],
+        axis=1,
+    )
+    summed = scatter_expert(parts, line)
+    large_rows = summed.shape[0] - small_rows
+    small = summed[large_rows:].reshape(-1)
+    gain_size, norm_size = local_width // groups, model_width // groups
+    own_gains = small[: 2 * gain_size]
+    shared = lax.psum(small[2 * gain_size : filled].astype(jnp.bfloat16), "dp")
+    shared = shared.astype(jnp.float32)
+    grad_out = lax.psum_scatter(
+        grad_out.astype(jnp.bfloat16), "expert", scatter_dimension=0, tiled=True
+    ).astype(jnp.float32)
     return (
         output,
         grad_input,
-        reduced_dense[6],
-        reduced_dense[0],
-        reduced_dense[1],
-        reduced_dense[2],
-        reduced_dense[3],
-        reduced_dense[4],
-        reduced_dense[5],
-        reduced_dense[7],
-        reduced_dense[8],
+        shared[:norm_size],
+        summed[:large_rows, :local_width],
+        summed[:large_rows, local_width : 2 * local_width],
+        summed[:large_rows, 2 * local_width :],
+        grad_out,
+        own_gains[:gain_size],
+        own_gains[gain_size:],
+        shared[norm_size : 2 * norm_size],
+        shared[2 * norm_size :].reshape(norm_size, experts),
         grad_gate,
         grad_up,
         grad_down,

time: 1490 us -> 1030 us (0.69)
  waiting for transfers between devices: 906 us -> 43.5 us
  Pallas kernels: 0 us -> 454 us
  blocking collectives: 89.8 us -> 35.2 us
    reduce_scatter x9 -> x2, waiting for transfers between devices: 576 us -> 0.02 us  [the longest x1 0.02 us: per_device(): lax.psum_scatter(gate_columns, ALL, scatter_dimension=0, tiled=True)]
    pallas_call x0 -> x8, Pallas kernels: none -> 454 us  [the longest x4 278 us: reduce_to(): pl.pallas_call(functools.partial(reduce_kernel, square, line, paired), ou...]
    all_gather x5 -> x1, waiting for transfers between devices: 272 us -> 0.01 us  [per_device(): top_all = lax.all_gather(top_own, ALL, axis=0, tiled=True)]
    all_gather x1 -> x0, blocking collectives: 36.2 us -> none  [gather_all(): return lax.all_gather(rows, ALL, axis=0, tiled=True)]
    unnamed x1 -> x0, blocking collectives: 23.9 us -> none
  transfers between devices with their start and end apart: 19 -> 8, of which waited for: 17 -> 2; matrix products, arithmetic and copies ran while one was open for 20% -> 39% of each run, Pallas kernels for 0% -> 38%
where the time goes in v2:
time: 1030 us; the launch traced here: 1020 us
  Pallas kernels  454 us (44%)
  matrix products  308 us (30%)
  other arithmetic  111 us (11%)
  local copies, waits for them, and re-layouts  53.9 us (5%)
  waiting for transfers between devices  43.5 us (4%)
  blocking collectives  35.2 us (3%)
  between operations  15 us (1%)
    pallas_call x4, Pallas kernels, reduce_to(): pl.pallas_call(functools.partial(reduce_kernel, square, line, paired), ou...  278 us
    pallas_call x1, Pallas kernels, gather_all(): pl.pallas_call(functools.partial(gather_all_kernel, line), out_shape=(jax...  113 us
    pallas_call x3, Pallas kernels, gather_dp(): pl.pallas_call(gather_square_kernel, out_shape=jax.ShapeDtypeStruct((4, 2...  63 us
    dot_general x1, matrix products, per_device(): jnp.einsum('pshd,plhd->phsl', grad_heads, values_heads, preferred_element...  30.4 us
    unnamed x110, local copies, waits for them, and re-layouts  29.4 us
    all_gather x1, waiting for transfers between devices, per_device(): lax.all_gather(key_rows, 'expert', axis=1, tiled=True)  28.9 us
    convert_element_type x1, other arithmetic, per_device(): grad_scores = (weights * (grad_weights - row_delta)).astype(jnp.bfloat16)  28.5 us
    dot_general x1, matrix products, per_device(): jnp.einsum('td,jfd->tjf', top_all, w_down, preferred_element_type=jnp.flo...  25 us
  transfers between devices with their start and end apart: 8, of which 2 were waited for; matrix products, arithmetic and copies ran while one was open for 39% of the time, Pallas kernels for 38%

profile of v2, /device:TPU:24, one launch (start us, length us, event | category | flops | bytes accessed | tf_op | source)
XLA Modules:
  0.0 1021.3 jit_solution(9337076117170003784)
XLA Ops:
  60.2 28.9 %all-gather.6.cloned.1.call-done = bf16[1,4096,512]{1,2,0:T(8,128)(2,1)} async-done(((bf16[1,512,512]{1,2,0:T(8,128)(2,1)}), bf16[1,4096,512]{1,2,0:T(8,128)(2,1)}) %all-gather.6.cloned.1.call-update) | async-done | bytes 4194320 | tf_op jit(solution)/shard_map/all_gather | solution.py:621
  89.1 18.1 %fusion.1 = (f32[4,512]{1,0:T(4,128)S(1)}, f32[4,512,4096]{2,1,0:T(8,128)}) fusion(pred[512,4096]{1,0:T(8,128)(4,1)} %fusion.8, bf16[4096,4,128]{0,2,1:T(8,128)(2,1)} %bitcast.214, bf16[512,4,64]{2,0,1:T(8,128)(2,1)S(1)} %get-tuple-element.82, bf16[512,4,64]{2,0,1:T(8,128)(2,1)S(1)} %get-tuple-element.81), kind=kOutput, calls=%fused_computation.8 | convolution fusion | flops 2173696000 | bytes 40378368 | tf_op jit(solution)/shard_map/pshd,plhd->phsl/dot_general | solution.py:629
  107.1 15.4 %exponential_reduce_fusion = f32[4,512]{1,0:T(4,128)S(1)} fusion(f32[4,512,4096]{2,1,0:T(8,128)} %get-tuple-element.114, f32[4,512]{1,0:T(4,128)S(1)} %get-tuple-element.113, pred[512,4096]{1,0:T(8,128)(4,1)S(1)} %copy-done.1), kind=kLoop, calls=%fused_computation.6 | loop fusion | flops 33552384 | bytes 35667968 | tf_op jit(solution)/shard_map/reduce_sum | solution.py:638
  136.9 16.5 %fusion.22 = bf16[4,128,512]{2,1,0:T(8,128)(2,1)S(1)} fusion(f32[4,512,4096]{2,1,0:T(8,128)} %get-tuple-element.114, f32[4,512]{1,0:T(4,128)S(1)} %log_add_fusion, pred[512,4096]{1,0:T(8,128)(4,1)} %fusion.8, bf16[4096,512]{1,0:T(8,128)(2,1)} %all-gather.8.cloned.1.call-done), kind=kOutput, calls=%fused_computation.52 | convolution fusion | flops 2181300224 | bytes 40378368 | tf_op jit(solution)/shard_map/phsl,plhd->pshd/dot_general | solution.py:640
  156.1 28.7 %scatter_dp.2 = f32[2,64,2048]{2,1,0:T(8,128)} custom-call(bf16[4,1,1,2,64,2048]{5,4,3,2,1,0:T(8,128)(2,1)} %bitcast.227), custom_call_target="tpu_custom_call" | custom-call | tf_op jit(solution)/shard_map/scatter_dp/pallas_call | solution.py:510
  191.9 112.8 %gather_all.1 = (bf16[32,2,64,2048]{3,2,1,0:T(8,128)(2,1)}, f32[32,16,128]{2,1,0:T(8,128)}) custom-call(bf16[2,64,2048]{2,1,0:T(8,128)(2,1)} %multiply_convert_fusion.8.x_ref, f32[16,128]{1,0:T(8,128)} %select_bitcast_fusion.g_ref), custom_call_target="tpu_custom_call" | custom-call | tf_op jit(solution)/shard_map/gather_all/pallas_call | solution.py:206
  305.6 15.3 %fusion.74 = f32[4096,2,256]{0,2,1:T(8,128)} fusion(bf16[4096,2048,1]{1,0,2:T(8,128)(2,1)} %bitcast.244, bf16[2,2048,256]{2,1,0:T(8,128)(2,1)} %param.27), kind=kOutput, calls=%fused_computation.159 | convolution fusion | flops 8589934592 | bytes 27262976 | tf_op jit(solution)/shard_map/td,jdf->tjf/dot_general | solution.py:678
  320.9 14.8 %fusion.73 = f32[4096,2,256]{0,2,1:T(8,128)} fusion(bf16[4096,2048,1]{1,0,2:T(8,128)(2,1)} %bitcast.245, bf16[2,2048,256]{2,1,0:T(8,128)(2,1)S(1)} %copy-done.45), kind=kOutput, calls=%fused_computation.158 | convolution fusion | flops 8589934592 | bytes 27262976 | tf_op jit(solution)/shard_map/td,jdf->tjf/dot_general | solution.py:677
  335.7 25.0 %multiply_reduce_fusion.1 = (f32[4096,2]{0,1:T(2,128)}, bf16[4096,2,256]{0,2,1:T(8,128)(2,1)}, bf16[4096,2,256]{0,2,1:T(8,128)(2,1)}, bf16[4096,2,256]{0,2,1:T(8,128)(2,1)}) fusion(f32[4096,2,256]{0,2,1:T(8,128)} %fusion.74, f32[4096,2,256]{0,2,1:T(8,128)} %fusion.73, f32[4096,2]{0,1:T(2,128)S(1)} %dynamic-slice_bitcast_fusion, ...), kind=kOutput, calls=%fused_computation.15 | convolution fusion | flops 8629772288 | bytes 48300032 | tf_op jit(solution)/shard_map/td,jfd->tjf/dot_general | solution.py:679
  362.3 18.2 %fusion.75 = f32[4096,2048,1]{1,0,2:T(8,128)} fusion(bf16[4096,2,256]{0,2,1:T(8,128)(2,1)} %get-tuple-element.76, bf16[2,2048,256]{2,1,0:T(8,128)(2,1)} %param.26), kind=kOutput, calls=%fused_computation.160 | convolution fusion | flops 8589934592 | bytes 39845888 | tf_op jit(solution)/shard_map/tjf,jdf->td/dot_general | solution.py:691
  380.6 22.7 %fusion = bf16[4096,2048]{1,0:T(8,128)(2,1)} fusion(f32[4096,2048,1]{1,0,2:T(8,128)} %fusion.75, bf16[4096,2,256]{0,2,1:T(8,128)(2,1)} %get-tuple-element.78, bf16[2,2048,256]{2,1,0:T(8,128)(2,1)} %param.27), kind=kOutput, calls=%fused_computation.1 | convolution fusion | flops 8606711808 | bytes 56623104 | tf_op jit(solution)/shard_map/tjf,jdf->td/dot_general | solution.py:692
  403.3 89.8 %scatter_all.1 = f32[2,64,2048]{2,1,0:T(8,128)} custom-call(bf16[4,4,2,2,64,2048]{5,4,3,2,1,0:T(8,128)(2,1)} %bitcast.205), custom_call_target="tpu_custom_call" | custom-call | tf_op jit(solution)/shard_map/scatter_all/pallas_call | solution.py:510
  499.7 22.8 %gather_dp.4 = bf16[4,2,64,2048]{3,2,1,0:T(8,128)(2,1)} custom-call(bf16[2,64,2048]{2,1,0:T(8,128)(2,1)} %bitcast.224), custom_call_target="tpu_custom_call" | custom-call | tf_op jit(solution)/shard_map/gather_dp/pallas_call | solution.py:264
  529.7 30.4 %multiply_reduce_fusion = (f32[4,512]{1,0:T(4,128)S(1)}, f32[4,512,4096]{2,1,0:T(8,128)}) fusion(f32[4,512,4096]{2,1,0:T(8,128)} %get-tuple-element.114, f32[4,512]{1,0:T(4,128)S(1)} %log_add_fusion, pred[512,4096]{1,0:T(8,128)(4,1)} %fusion.8, bf16[512,4,128]{0,2,1:T(8,128)(2,1)} %bitcast.230, bf16[4096,512]{1,0:T(8,128)(2,1)} %all-gather.8.cloned.1.call-done), kind=kOutput, calls=%fused_computation.4 | convolution fusion | flops 2189424640 | bytes 73940992 | tf_op jit(solution)/shard_map/pshd,plhd->phsl/dot_general | solution.py:734
  560.1 28.5 %multiply_convert_fusion = bf16[4,512,4096]{2,1,0:T(8,128)(2,1)} fusion(f32[4,512,4096]{2,1,0:T(8,128)} %get-tuple-element.119, f32[4,512,4096]{2,1,0:T(8,128)} %get-tuple-element.114, f32[4,512]{1,0:T(4,128)S(1)} %get-tuple-element.118, f32[4,512]{1,0:T(4,128)S(1)} %log_add_fusion, pred[512,4096]{1,0:T(8,128)(4,1)} %fusion.8), kind=kLoop, calls=%fused_computation.3 | loop fusion | flops 50331648 | bytes 85999616 | tf_op jit(solution)/shard_map/convert_element_type | solution.py:738
  599.5 18.1 %convolution_convert_fusion.1 = bf16[4,128,4096]{2,1,0:T(8,128)(2,1)} fusion(bf16[512,4,128]{0,2,1:T(8,128)(2,1)} %bitcast.231, f32[4,512,4096]{2,1,0:T(8,128)} %get-tuple-element.114, f32[4,512]{1,0:T(4,128)S(1)} %log_add_fusion, pred[512,4096]{1,0:T(8,128)(4,1)} %fusion.8), kind=kOutput, calls=%fused_computation.25 | convolution fusion | flops 2183135232 | bytes 40378368 | tf_op jit(solution)/shard_map/phsl,pshd->plhd/dot_general | solution.py:747
  617.7 14.7 %bitcast_convert_fusion = bf16[4096,2048]{1,0:T(8,128)(2,1)} fusion(bf16[4096,2,256]{0,2,1:T(8,128)(2,1)} %get-tuple-element.77, bf16[2,256,2048]{2,1,0:T(8,128)(2,1)S(1)} %copy-done), kind=kOutput, calls=%fused_computation.2 | convolution fusion | flops 8598323200 | bytes 23068672 | tf_op jit(solution)/shard_map/tjf,jfd->td/dot_general | solution.py:690
  657.2 15.2 %convolution_bitcast_fusion.1 = f32[2,2048,256]{1,2,0:T(8,128)} fusion(bf16[4096,2,256]{0,2,1:T(8,128)(2,1)} %get-tuple-element.76, bf16[4096,2048,1]{1,0,2:T(8,128)(2,1)} %bitcast.247), kind=kOutput, calls=%fused_computation.36 | convolution fusion | flops 8589934592 | bytes 25165824 | tf_op jit(solution)/shard_map/td,tjf->jdf/dot_general | solution.py:696
  678.3 15.0 %fusion.3 = f32[2,256,2048]{2,1,0:T(8,128)} fusion(bf16[4096,2,256]{0,2,1:T(8,128)(2,1)} %get-tuple-element.77, bf16[1,4096,2048]{2,1,0:T(8,128)(2,1)} %all-gather.10.cloned.1.call-done), kind=kOutput, calls=%fused_computation.10 | convolution fusion | flops 8589934592 | bytes 25165824 | tf_op jit(solution)/shard_map/tjf,td->jfd/dot_general | solution.py:695
  763.3 36.8 %scatter_dp.3 = f32[2,64,2048]{2,1,0:T(8,128)} custom-call(bf16[4,1,1,2,64,2048]{5,4,3,2,1,0:T(8,128)(2,1)} %bitcast.209), custom_call_target="tpu_custom_call" | custom-call | tf_op jit(solution)/shard_map/scatter_dp/pallas_call | solution.py:510
  820.9 122.8 %scatter_expert.1 = f32[2,144,1536]{2,1,0:T(8,128)} custom-call(bf16[1,4,2,2,144,1536]{5,4,3,2,1,0:T(8,128)(2,1)} %bitcast.204), custom_call_target="tpu_custom_call" | custom-call | tf_op jit(solution)/shard_map/scatter_expert/pallas_call | solution.py:510
  944.7 15.0 %psum.39 = bf16[4608]{0:T(1024)(128)(2,1)S(1)} all-reduce(bf16[4608]{0:T(1024)(128)(2,1)S(1)} %slice.110), channel_id=1, replica_groups=mesh['dp'=4,'expert'=8] {'dp'}, use_global_device_ids=true, to_apply=%region_31.32 | all-reduce | flops 4608 | bytes 18432 | tf_op jit(solution)/shard_map/psum | solution.py:835
  968.4 21.3 %gather_dp.3 = bf16[4,2,64,2048]{3,2,1,0:T(8,128)(2,1)} custom-call(bf16[2,64,2048]{2,1,0:T(8,128)(2,1)} %bitcast.223), custom_call_target="tpu_custom_call" | custom-call | tf_op jit(solution)/shard_map/gather_dp/pallas_call | solution.py:264
  989.8 18.9 %gather_dp.5 = bf16[4,2,64,2048]{3,2,1,0:T(8,128)(2,1)} custom-call(bf16[2,64,2048]{2,1,0:T(8,128)(2,1)} %bitcast.222), custom_call_target="tpu_custom_call" | custom-call | tf_op jit(solution)/shard_map/gather_dp/pallas_call | solution.py:264
  (224 shorter events, 240.3 us)
Async XLA Ops:
  7.2 328.5 %copy-start = (bf16[2,256,2048]{2,1,0:T(8,128)(2,1)S(1)}, bf16[2,256,2048]{2,1,0:T(8,128)(2,1)}, u32[]{:S(2)}) copy-start(bf16[2,256,2048]{2,1,0:T(8,128)(2,1)} %param.28) | copy-start | bytes 6291460
  7.2 81.9 %all-gather.6.cloned.1.call-start = ((), (), s32[]{:S(2)}) async-start(), calls=%async_computation.5 | async-start | bytes 4718592 | tf_op jit(solution)/shard_map/all_gather | solution.py:621
  11.0 34.0 %copy-start.42 = (f32[512]{0:T(512)}, f32[512]{0:T(512)S(1)}, u32[]{:S(2)}) copy-start(f32[512]{0:T(512)S(1)} %add_rsqrt_fusion.2) | copy-start | bytes 6148
  41.7 47.4 %copy-start.8 = (bf16[512,4,64]{2,0,1:T(8,128)(2,1)}, bf16[512,4,64]{2,0,1:T(8,128)(2,1)S(1)}, u32[]{:S(2)}) copy-start(bf16[512,4,64]{2,0,1:T(8,128)(2,1)S(1)} %get-tuple-element.81) | copy-start | bytes 786436
  41.7 47.4 %copy-start.9 = (bf16[512,4,64]{2,0,1:T(8,128)(2,1)}, bf16[512,4,64]{2,0,1:T(8,128)(2,1)S(1)}, u32[]{:S(2)}) copy-start(bf16[512,4,64]{2,0,1:T(8,128)(2,1)S(1)} %get-tuple-element.82) | copy-start | bytes 786436
  44.9 92.1 %all-gather.8.cloned.1.call-start = ((), (), s32[]{:S(2)}) async-start(), calls=%async_computation.11 | async-start | bytes 4718592 | tf_op jit(solution)/shard_map/all_gather | solution.py:622
  49.3 286.4 %all-gather.10.cloned.1.call-start = ((), (), s32[]{:S(2)}) async-start(), calls=%async_computation.12 | async-start | bytes 17301504 | tf_op jit(solution)/shard_map/all_gather | solution.py:670
  51.3 441.9 %reduce-scatter.8.cloned.1.call-start = ((), (), s32[]{:S(2)}) async-start(), calls=%async_computation.7 | async-start | bytes 270336 | tf_op jit(solution)/shard_map/reduce_scatter | solution.py:706
  56.5 132.2 %copy-start.24 = (pred[128,16]{0,1:T(8,128)(4,1)}, pred[128,16]{0,1:T(8,128)(4,1)S(1)}, u32[]{:S(2)}) copy-start(pred[128,16]{0,1:T(8,128)(4,1)S(1)} %fusion.45) | copy-start | bytes 6148
  156.1 31.5 %copy-start.20 = (f32[2048]{0:T(1024)S(1)}, f32[2048]{0:T(1024)}, u32[]{:S(2)}) copy-start(f32[2048]{0:T(1024)} %param.24) | copy-start | bytes 24580
  187.5 117.1 %copy-start.38 = (f32[128]{0:T(128)}, f32[128]{0:T(128)S(1)}, u32[]{:S(2)}) copy-start(f32[128]{0:T(128)S(1)} %add_rsqrt_fusion.3) | copy-start | bytes 1540
  188.7 116.0 %copy-start.36 = (f32[128]{0:T(128)}, f32[128]{0:T(128)S(1)}, u32[]{:S(2)}) copy-start(f32[128]{0:T(128)S(1)} %get-tuple-element.115) | copy-start | bytes 1540
  188.7 132.3 %copy-start.21 = (f32[128,16]{0,1:T(8,128)}, f32[128,16]{0,1:T(8,128)S(1)}, u32[]{:S(2)}) copy-start(f32[128,16]{0,1:T(8,128)S(1)} %get-tuple-element.116) | copy-start | bytes 24580
  188.7 115.9 %copy-start.40 = (f32[128]{0:T(128)}, f32[128]{0:T(128)S(1)}, u32[]{:S(2)}) copy-start(f32[128]{0:T(128)S(1)} %fusion.47) | copy-start | bytes 1540
  362.3 347.2 %reduce-scatter.14.cloned.1.call-start = ((), (), s32[]{:S(2)}) async-start(), calls=%async_computation.10 | async-start | bytes 2359296 | tf_op jit(solution)/shard_map/reduce_scatter | solution.py:837
  403.3 89.9 %copy-start.22 = (f32[128,16]{0,1:T(8,128)S(1)}, f32[128,16]{0,1:T(8,128)}, u32[]{:S(2)}) copy-start(f32[128,16]{0,1:T(8,128)} %copy-done.21) | copy-start | bytes 24580
  403.3 89.9 %copy-start.25 = (pred[128,16]{0,1:T(8,128)(4,1)S(1)}, pred[128,16]{0,1:T(8,128)(4,1)}, u32[]{:S(2)}) copy-start(pred[128,16]{0,1:T(8,128)(4,1)} %copy-done.24) | copy-start | bytes 6148
  403.3 89.9 %copy-start.37 = (f32[128]{0:T(128)S(1)}, f32[128]{0:T(128)}, u32[]{:S(2)}) copy-start(f32[128]{0:T(128)} %copy-done.36) | copy-start | bytes 1540
  403.3 89.9 %copy-start.41 = (f32[128]{0:T(128)S(1)}, f32[128]{0:T(128)}, u32[]{:S(2)}) copy-start(f32[128]{0:T(128)} %copy-done.40) | copy-start | bytes 1540
  403.3 90.6 %copy-start.39 = (f32[128]{0:T(128)S(1)}, f32[128]{0:T(128)}, u32[]{:S(2)}) copy-start(f32[128]{0:T(128)} %copy-done.38) | copy-start | bytes 1540
  529.6 181.7 %reduce-scatter.10.cloned.1.call-start = ((), (), s32[]{:S(2)}) async-start(), calls=%async_computation.8 | async-start | bytes 4718592 | tf_op jit(solution)/shard_map/reduce_scatter | solution.py:754
  599.4 156.9 %reduce-scatter.12.cloned.1.call-start = ((), (), s32[]{:S(2)}) async-start(), calls=%async_computation.9 | async-start | bytes 4718592 | tf_op jit(solution)/shard_map/reduce_scatter | solution.py:760
  617.6 347.2 %reduce-scatter.6.cloned.1.call-start = ((), (), s32[]{:S(2)}) async-start(), calls=%async_computation.6 | async-start | bytes 17301504 | tf_op jit(solution)/shard_map/reduce_scatter | solution.py:699
  756.3 43.8 %copy-start.27 = (f32[2048]{0:T(1024)S(1)}, f32[2048]{0:T(1024)}, u32[]{:S(2)}) copy-start(f32[2048]{0:T(1024)} %param.17) | copy-start | bytes 24580
  (34 other events, 264.9 us)
Sparse Core Ops, SparseCore 0:
  45.0 44.0 all-gather.5
  91.2 45.6 all-gather.7
  140.5 154.6 all-gather.9
  362.4 120.0 reduce-scatter.7
  529.7 33.2 reduce-scatter.13
  599.5 48.4 reduce-scatter.9
  650.3 48.3 reduce-scatter.11
  701.0 237.3 reduce-scatter.5

commit v3 on v2

--- a/solution.py
+++ b/solution.py
@@ -551,6 +551,427 @@
     return reduce_to(parts, False, line, True, "scatter_expert", 5)
 
 
+def visit_others(line, z, visit):
+    def turn(k, carry):
+        visit((z + k) % line)
+        return carry
+
+    lax.fori_loop(1, line, turn, 0)
+
+
+def greet_line(line, dp, z, c):
+    visit_others(line, z, lambda other: greet((dp, 2 * other + c)))
+    greet((dp, 2 * z + 1 - c))
+    pl.semaphore_wait(pltpu.get_barrier_semaphore(), line)
+
+
+def columns(z):
+    return pl.ds(pl.multiple_of(z * HD, HD), HD)
+
+
+def to_heads_kernel(line, shared, *refs):
+    count = len(shared)
+    ins, outs = refs[:count], refs[count : 2 * count]
+    sent, arrived, pair_sent, pair_arrived, own_sem = refs[2 * count :]
+    dp, place = lax.axis_index("dp"), lax.axis_index("expert")
+    z, c = place // 2, place % 2
+    pair = (dp, 2 * z + 1 - c)
+    greet_line(line, dp, z, c)
+
+    def block(i, origin):
+        return outs[i].at[origin, c] if shared[i] else outs[i].at[origin]
+
+    def out(i, other):
+        source = ins[i].at[:, columns(other)]
+        device = (dp, 2 * other + c)
+        return send(source, block(i, z), sent.at[i, other], arrived.at[i, z], device)
+
+    def into(i, origin):
+        part = block(i, origin)
+        return send(part, part, sent.at[i, origin], arrived.at[i, origin], pair)
+
+    def share(i, origin, source=None):
+        part = block(i, origin)
+        return send(
+            part if source is None else source,
+            part,
+            pair_sent.at[i, origin],
+            pair_arrived.at[i, origin],
+            pair,
+        )
+
+    def own(i):
+        return pltpu.make_async_copy(ins[i].at[:, columns(z)], block(i, z), own_sem.at[i])
+
+    def dispatch(other):
+        for i in range(count):
+            out(i, other).start()
+
+    visit_others(line, z, dispatch)
+    for i in range(count):
+        own(i).start()
+        if shared[i]:
+            share(i, z, ins[i].at[:, columns(z)]).start()
+
+    def receive(origin):
+        for i in range(count):
+            into(i, origin).wait_recv()
+            if shared[i]:
+                share(i, origin).start()
+
+    visit_others(line, z, receive)
+
+    def finish(other):
+        for i in range(count):
+            out(i, other).wait_send()
+
+    visit_others(line, z, finish)
+    for i in range(count):
+        own(i).wait()
+        if shared[i]:
+
+            def settle(origin, carry):
+                share(i, origin).wait()
+                return carry
+
+            lax.fori_loop(0, line, settle, 0)
+
+
+def to_heads(arrays, shared, line, name, number):
+    rows = arrays[0].shape[0]
+    count = len(arrays)
+    sems = pltpu.SemaphoreType.DMA
+    return pl.pallas_call(
+        functools.partial(to_heads_kernel, line, shared),
+        out_shape=[
+            jax.ShapeDtypeStruct((line, 2, rows, HD) if both else (line, rows, HD), array.dtype)
+            for array, both in zip(arrays, shared)
+        ],
+        in_specs=[pl.BlockSpec(memory_space=pltpu.VMEM)] * count,
+        out_specs=[pl.BlockSpec(memory_space=pl.ANY)] * count,
+        scratch_shapes=[sems((count, line))] * 4 + [sems((count,))],
+        compiler_params=pltpu.CompilerParams(collective_id=number, has_side_effects=True),
+        name=name,
+    )(*arrays)
+
+
+def to_tokens_kernel(line, summed, *refs):
+    count, sums = len(summed), sum(summed)
+    ins, outs = refs[:count], refs[count : 2 * count]
+    mine, theirs = refs[2 * count : 2 * count + 2]
+    sent, arrived, pair_sem, load_sem, own_sem = refs[2 * count + 2 :]
+    dp, place = lax.axis_index("dp"), lax.axis_index("expert")
+    z, c = place // 2, place % 2
+    pair = (dp, 2 * z + 1 - c)
+    greet_line(line, dp, z, c)
+    at_sum = [sum(summed[:i]) for i in range(count)]
+
+    def load(i, other):
+        return pltpu.make_async_copy(
+            ins[i].at[other, c], mine.at[at_sum[i], other], load_sem.at[at_sum[i], other]
+        )
+
+    def hand(i, other):
+        s = at_sum[i]
+        return send(
+            ins[i].at[other, 1 - c],
+            theirs.at[s, other],
+            pair_sem.at[0, s, other],
+            pair_sem.at[1, s, other],
+            pair,
+        )
+
+    def source(i, other):
+        return mine.at[at_sum[i], other] if summed[i] else ins[i].at[other]
+
+    def out(i, other):
+        target = outs[i].at[:, columns(z)]
+        device = (dp, 2 * other + c)
+        return send(source(i, other), target, sent.at[i, other], arrived.at[i, z], device)
+
+    def into(i, origin):
+        part = outs[i].at[:, columns(origin)]
+        return send(part, part, sent.at[i, origin], arrived.at[i, origin], pair)
+
+    def own(i):
+        return pltpu.make_async_copy(source(i, z), outs[i].at[:, columns(z)], own_sem.at[i])
+
+    def prepare(other):
+        for i in range(count):
+            if summed[i]:
+                load(i, other).start()
+                hand(i, other).start()
+
+    def add(i, other):
+        if summed[i]:
+            load(i, other).wait()
+            hand(i, other).wait_recv()
+            s = at_sum[i]
+            mine[s, other] = mine[s, other] + theirs[s, other]
+
+    def dispatch(other):
+        for i in range(count):
+            add(i, other)
+            out(i, other).start()
+
+    if sums:
+        visit_others(line, z, prepare)
+        prepare(z)
+    visit_others(line, z, dispatch)
+    for i in range(count):
+        add(i, z)
+        own(i).start()
+
+    def finish(other):
+        for i in range(count):
+            into(i, other).wait_recv()
+            out(i, other).wait_send()
+            if summed[i]:
+                hand(i, other).wait_send()
+
+    visit_others(line, z, finish)
+    for i in range(count):
+        own(i).wait()
+        if summed[i]:
+            hand(i, z).wait_send()
+
+
+def to_tokens(arrays, summed, line, name, number):
+    rows = arrays[0].shape[-2]
+    count, sums = len(arrays), max(sum(summed), 1)
+    sems = pltpu.SemaphoreType.DMA
+    dtype = arrays[0].dtype
+    held = (sums, line, rows, HD) if sum(summed) else (1, 1, 16, HD)
+    return pl.pallas_call(
+        functools.partial(to_tokens_kernel, line, summed),
+        out_shape=[jax.ShapeDtypeStruct((rows, line * HD), dtype)] * count,
+        in_specs=[pl.BlockSpec(memory_space=pl.ANY)] * count,
+        out_specs=[pl.BlockSpec(memory_space=pl.ANY)] * count,
+        scratch_shapes=[pltpu.VMEM(held, dtype)] * 2
+        + [
+            sems((count, line)),
+            sems((count, line)),
+            sems((2, sums, line)),
+            sems((sums, line)),
+            sems((count,)),
+        ],
+        compiler_params=pltpu.CompilerParams(collective_id=number, has_side_effects=True),
+        name=name,
+    )(*arrays)
+
+
+KEY_TILE = 512
+
+
+def contract(a, b, a_dim, b_dim):
+    return lax.dot_general(
+        a, b, (((a_dim,), (b_dim,)), ((), ())), preferred_element_type=jnp.float32
+    )
+
+
+def masked_scores(keys, queries, tile, first, starts):
+    scores = contract(keys, queries, 1, 1) * HD ** (-0.5)
+    key_at = tile * KEY_TILE + lax.broadcasted_iota(jnp.int32, scores.shape, 0)
+    query_at = first + lax.broadcasted_iota(jnp.int32, (1, scores.shape[1]), 1)
+    return jnp.where((key_at >= starts) & (key_at <= query_at), scores, masked_score)
+
+
+def attend_kernel(bounds, q_ref, k_ref, v_ref, start_ref, o_ref, total_ref):
+    i = pl.program_id(0)
+    queries, starts = q_ref[0], start_ref[0]
+    span = queries.shape[0]
+
+    def tile_step(tile, carry):
+        largest, total, acc = carry
+        rows = pl.ds(pl.multiple_of(tile * KEY_TILE, KEY_TILE), KEY_TILE)
+        scores = masked_scores(k_ref[rows, :], queries, tile, bounds[2, i], starts)
+        new = jnp.maximum(largest, jnp.max(scores, axis=0, keepdims=True))
+        weights = jnp.exp(scores - new)
+        fade = jnp.exp(largest - new)
+        total = fade * total + jnp.sum(weights, axis=0, keepdims=True)
+        acc = fade * acc + contract(v_ref[rows, :], weights.astype(jnp.bfloat16), 0, 0)
+        return new, total, acc
+
+    largest, total, acc = lax.fori_loop(
+        bounds[0, i],
+        bounds[1, i],
+        tile_step,
+        (
+            jnp.full((1, span), masked_score, jnp.float32),
+            jnp.zeros((1, span), jnp.float32),
+            jnp.zeros((HD, span), jnp.float32),
+        ),
+    )
+    o_ref[0] = (acc / total).T.astype(o_ref.dtype)
+    total_ref[0] = largest + jnp.log(total)
+
+
+def attend_back_kernel(
+    bounds, q_ref, k_ref, v_ref, start_ref, total_ref, delta_ref, d_ref, dq_ref, dk_ref, dv_ref, dk, dv
+):
+    i = pl.program_id(0)
+    queries, starts, grad = q_ref[0], start_ref[0], d_ref[0]
+    total, delta = total_ref[0], delta_ref[0]
+
+    @pl.when(i == 0)
+    def _():
+        dk[...] = jnp.zeros_like(dk)
+        dv[...] = jnp.zeros_like(dv)
+
+    def tile_step(tile, acc):
+        rows = pl.ds(pl.multiple_of(tile * KEY_TILE, KEY_TILE), KEY_TILE)
+        keys = k_ref[rows, :]
+        scores = masked_scores(keys, queries, tile, bounds[2, i], starts)
+        weights = jnp.exp(scores - total)
+        grad_weights = contract(v_ref[rows, :], grad, 1, 1)
+        grad_scores = (weights * (grad_weights - delta)).astype(jnp.bfloat16)
+        dv[rows, :] += contract(weights.astype(jnp.bfloat16), grad, 1, 0)
+        dk[rows, :] += contract(grad_scores, queries, 1, 0)
+        return acc + contract(keys, grad_scores, 0, 0)
+
+    acc = jnp.zeros((HD, queries.shape[0]), jnp.float32)
+    acc = lax.fori_loop(bounds[0, i], bounds[1, i], tile_step, acc)
+    dq_ref[0] = (acc * HD ** (-0.5)).T.astype(dq_ref.dtype)
+
+    @pl.when(i == pl.num_programs(0) - 1)
+    def _():
+        dk_ref[...] = (dk[...] * HD ** (-0.5)).astype(dk_ref.dtype)
+        dv_ref[...] = dv[...].astype(dv_ref.dtype)
+
+
+def attend(bounds, queries, keys, values, starts):
+    line, span, _ = queries.shape
+    pack = keys.shape[0]
+    block = pl.BlockSpec((1, span, HD), lambda i, _: (i, 0, 0))
+    row = pl.BlockSpec((1, 1, span), lambda i, _: (i, 0, 0))
+    whole = pl.BlockSpec((pack, HD), lambda i, _: (0, 0))
+    return pl.pallas_call(
+        attend_kernel,
+        grid_spec=pltpu.PrefetchScalarGridSpec(
+            num_scalar_prefetch=1,
+            grid=(line,),
+            in_specs=[block, whole, whole, row],
+            out_specs=[block, row],
+        ),
+        out_shape=[
+            jax.ShapeDtypeStruct(queries.shape, jnp.bfloat16),
+            jax.ShapeDtypeStruct(starts.shape, jnp.float32),
+        ],
+        name="attend",
+    )(bounds, queries, keys, values, starts)
+
+
+def attend_back(bounds, queries, keys, values, starts, total, delta, grad):
+    line, span, _ = queries.shape
+    pack = keys.shape[0]
+    block = pl.BlockSpec((1, span, HD), lambda i, _: (i, 0, 0))
+    row = pl.BlockSpec((1, 1, span), lambda i, _: (i, 0, 0))
+    whole = pl.BlockSpec((pack, HD), lambda i, _: (0, 0))
+    return pl.pallas_call(
+        attend_back_kernel,
+        grid_spec=pltpu.PrefetchScalarGridSpec(
+            num_scalar_prefetch=1,
+            grid=(line,),
+            in_specs=[block, whole, whole, row, row, row, block],
+            out_specs=[block, whole, whole],
+            scratch_shapes=[pltpu.VMEM((pack, HD), jnp.float32)] * 2,
+        ),
+        out_shape=[jax.ShapeDtypeStruct(queries.shape, jnp.bfloat16)]
+        + [jax.ShapeDtypeStruct((pack, HD), jnp.bfloat16)] * 2,
+        name="attend_back",
+    )(bounds, queries, keys, values, starts, total, delta, grad)
+
+
+def by_head(layout, line):
+    positions = layout[1][0]
+    pack = positions.shape[0]
+    span = pack // (2 * line)
+    core = lax.axis_index("expert") % 2
+    starts = (jnp.arange(pack, dtype=jnp.int32) - positions).reshape(line, 2, 1, span)
+    starts = lax.dynamic_index_in_dim(starts, core, 1, keepdims=False)
+    first = (2 * jnp.arange(line, dtype=jnp.int32) + core) * span
+    bounds = jnp.stack(
+        [starts[:, 0, 0] // KEY_TILE, (first + span - 1) // KEY_TILE + 1, first]
+    ).astype(jnp.int32)
+
+    def forward(queries, keys, values):
+        q, k, v = to_heads(
+            [queries, keys, values], (False, True, True), line, "scatter_heads", 6
+        )
+        k, v = k.reshape(pack, HD), v.reshape(pack, HD)
+        out, total = attend(bounds, q, k, v, starts)
+        (attended,) = to_tokens([out], (False,), line, "gather_heads", 7)
+        return attended, (q, k, v, out, total)
+
+    def backward(kept, grad):
+        q, k, v, out, total = kept
+        (grad,) = to_heads([grad], (False,), line, "scatter_grads", 8)
+        delta = jnp.sum(grad.astype(jnp.float32) * out.astype(jnp.float32), axis=-1)
+        dq, dk, dv = attend_back(bounds, q, k, v, starts, total, delta[:, None, :], grad)
+        shape = (line, 2, span, HD)
+        return to_tokens(
+            [dq, dk.reshape(shape), dv.reshape(shape)],
+            (False, True, True),
+            line,
+            "gather_grads",
+            9,
+        )
+
+    return forward, backward
+
+
+def by_query(layout, offset_rows):
+    segment = layout[0][0]
+    pack = segment.shape[0]
+
+    def heads(rows):
+        return rows.reshape(rows.shape[0], -1, HD)
+
+    def score_block(queries, keys):
+        rows = queries.shape[0]
+        scores = jnp.einsum("shd,lhd->hsl", queries, keys, preferred_element_type=jnp.float32)
+        own = lax.dynamic_slice_in_dim(segment, offset_rows, rows, 0)
+        query_places = offset_rows + jnp.arange(rows, dtype=jnp.int32)
+        key_places = jnp.arange(pack, dtype=jnp.int32)
+        allowed = (own[:, None] == segment[None, :]) & (
+            key_places[None, :] <= query_places[:, None]
+        )
+        return jnp.where(allowed[None], scores * HD ** (-0.5), masked_score)
+
+    def forward(queries, keys, values):
+        q = heads(queries)
+        k = heads(lax.all_gather(keys, "expert", axis=0, tiled=True))
+        v = heads(lax.all_gather(values, "expert", axis=0, tiled=True))
+        scores = score_block(q, k)
+        largest = jnp.max(scores, axis=-1, keepdims=True)
+        total = largest + jnp.log(jnp.sum(jnp.exp(scores - largest), axis=-1, keepdims=True))
+        weights = jnp.exp(scores - total).astype(jnp.bfloat16)
+        attended = jnp.einsum("hsl,lhd->shd", weights, v, preferred_element_type=jnp.float32)
+        return attended.astype(jnp.bfloat16).reshape(queries.shape), (q, k, v, total)
+
+    def backward(kept, grad):
+        q, k, v, total = kept
+        shape = grad.shape
+        grad = heads(grad)
+        weights = jnp.exp(score_block(q, k) - total)
+        grad_weights = jnp.einsum("shd,lhd->hsl", grad, v, preferred_element_type=jnp.float32)
+        delta = jnp.sum(weights * grad_weights, axis=-1, keepdims=True)
+        grad_scores = (weights * (grad_weights - delta)).astype(jnp.bfloat16)
+        dq = jnp.einsum("hsl,lhd->shd", grad_scores, k, preferred_element_type=jnp.float32)
+        dk = jnp.einsum("hsl,shd->lhd", grad_scores, q, preferred_element_type=jnp.float32)
+        weights = weights.astype(jnp.bfloat16)
+        dv = jnp.einsum("hsl,shd->lhd", weights, grad, preferred_element_type=jnp.float32)
+
+        def to_owner(part):
+            part = part.astype(jnp.bfloat16).reshape(pack, shape[1])
+            return lax.psum_scatter(part, "expert", scatter_dimension=0, tiled=True)
+
+        scale = HD ** (-0.5)
+        return (dq * scale).reshape(shape), to_owner(dk * scale), to_owner(dv)
+
+    return forward, backward
+
+
 def head_totals(first_sum, second_sum):
     return lax.psum((first_sum, second_sum), "dp")
 
@@ -581,17 +1002,10 @@
     line = groups // 2
     pack_span = seg_rows * groups
     local_experts = w_gate.shape[0]
-    scale_factor = HD ** (-0.5)
     offset_rows = lax.axis_index("expert") * seg_rows
     segment, positions = doc_layout(lengths, pack_span)
-    seg_query = lax.dynamic_slice_in_dim(segment, offset_rows, seg_rows, 1)
     pos_query = lax.dynamic_slice_in_dim(positions, offset_rows, seg_rows, 1)
     cos_table, sin_table = rope_tables(pos_query, HD)
-    key_places = jnp.arange(pack_span, dtype=jnp.int32)
-    query_places = offset_rows + jnp.arange(seg_rows, dtype=jnp.int32)
-    allowed = (seg_query[:, :, None] == segment[:, None, :]) & (
-        key_places[None, None, :] <= query_places[None, :, None]
-    )
     head_shape = (pack_count, seg_rows, local_heads, HD)
     inputs_single_float = inputs.astype(jnp.float32)
     first_inverse_norm = lax.rsqrt(
@@ -617,35 +1031,14 @@
         .astype(jnp.bfloat16)
         .reshape(pack_count, seg_rows, local_width)
     )
-    keys_all, values_all = (
-        lax.all_gather(key_rows, "expert", axis=1, tiled=True),
-        lax.all_gather(value_rows, "expert", axis=1, tiled=True),
-    )
-    keys_heads = keys_all.reshape(pack_count, pack_span, local_heads, HD)
-    values_heads = values_all.reshape(pack_count, pack_span, local_heads, HD)
-
-    def score_block(query_block):
-        scores = (
-            jnp.einsum(
-                "pshd,plhd->phsl", query_block, keys_heads, preferred_element_type=jnp.float32
-            )
-            * scale_factor
-        )
-        return jnp.where(allowed[:, None], scores, masked_score)
-
-    scores = score_block(queries)
-    largest = jnp.max(scores, axis=-1, keepdims=True)
-    log_total = largest + jnp.log(jnp.sum(jnp.exp(scores - largest), axis=-1, keepdims=True))
-    weights = jnp.exp(scores - log_total)
-    attended = jnp.einsum(
-        "phsl,plhd->pshd",
-        weights.astype(jnp.bfloat16),
-        values_heads,
-        preferred_element_type=jnp.float32,
-    )
-    attended = attended.astype(jnp.bfloat16).reshape(pack_count, seg_rows, local_width)
+    layout = (segment, positions)
+    if local_heads == line:
+        attention = by_head(layout, line)
+    else:
+        attention = by_query(layout, offset_rows)
+    attended, kept = attention[0](queries.reshape(seg_rows, local_width), key_rows[0], value_rows[0])
     attn_part = jnp.dot(
-        attended.reshape(seg_rows, local_width), w_out, preferred_element_type=jnp.float32
+        attended, w_out, preferred_element_type=jnp.float32
     )
     own = lax.axis_index("dp")
     part_rows = seg_rows // lax.axis_size("dp")
@@ -722,52 +1115,18 @@
         - second_unit_input
         * jnp.mean(grad_second_unit_input * second_unit_input, axis=-1, keepdims=True)
     )
-    grad_attn = gather_dp(grad_hidden.astype(jnp.bfloat16))[None]
-    grad_out = jnp.einsum("psk,psd->kd", attended, grad_attn, preferred_element_type=jnp.float32)
-    grad_heads = (
-        jnp.einsum("psd,kd->psk", grad_attn, w_out, preferred_element_type=jnp.float32)
-        .astype(jnp.bfloat16)
-        .reshape(head_shape)
-    )
-    scores = score_block(queries)
-    weights = jnp.exp(scores - log_total)
-    grad_weights = jnp.einsum(
-        "pshd,plhd->phsl", grad_heads, values_heads, preferred_element_type=jnp.float32
-    )
-    row_delta = jnp.sum(weights * grad_weights, axis=-1, keepdims=True)
-    grad_scores = (weights * (grad_weights - row_delta)).astype(jnp.bfloat16)
-    grad_queries = (
-        jnp.einsum("phsl,plhd->pshd", grad_scores, keys_heads, preferred_element_type=jnp.float32)
-        * scale_factor
-    )
-    key_part = (
-        jnp.einsum("phsl,pshd->plhd", grad_scores, queries, preferred_element_type=jnp.float32)
-        * scale_factor
-    )
-    value_part = jnp.einsum(
-        "phsl,pshd->plhd",
-        weights.astype(jnp.bfloat16),
-        grad_heads,
-        preferred_element_type=jnp.float32,
-    )
-    grad_keys, grad_values = (
-        lax.psum_scatter(
-            key_part.reshape(pack_count, pack_span, local_width).astype(jnp.bfloat16),
-            "expert",
-            scatter_dimension=1,
-            tiled=True,
-        ).astype(jnp.float32),
-        lax.psum_scatter(
-            value_part.reshape(pack_count, pack_span, local_width).astype(jnp.bfloat16),
-            "expert",
-            scatter_dimension=1,
-            tiled=True,
-        ).astype(jnp.float32),
-    )
+    grad_attn = gather_dp(grad_hidden.astype(jnp.bfloat16))
+    grad_out = jnp.einsum("sk,sd->kd", attended, grad_attn, preferred_element_type=jnp.float32)
+    grad_heads = jnp.einsum(
+        "sd,kd->sk", grad_attn, w_out, preferred_element_type=jnp.float32
+    ).astype(jnp.bfloat16)
+    grad_queries, grad_keys, grad_values = attention[1](kept, grad_heads)
+    grad_queries = grad_queries.astype(jnp.float32).reshape(head_shape)
     grad_q_normed = rotate(grad_queries, cos_table, -sin_table).reshape(
         pack_count, seg_rows, local_width
     )
-    grad_k_normed = rotate(grad_keys.reshape(head_shape), cos_table, -sin_table).reshape(
+    grad_k_normed = rotate(
+        grad_keys.astype(jnp.float32).reshape(head_shape), cos_table, -sin_table).reshape(
         pack_count, seg_rows, local_width
     )
     grad_q_gain = jnp.sum(grad_q_normed * q_hat, axis=(0, 1))
@@ -783,7 +1142,7 @@
     grad_k_raw = (k_inv * (grad_k_hat - k_hat * k_dot[..., None] / model_width)).astype(
         jnp.bfloat16
     )
-    grad_v_raw = grad_values.astype(jnp.bfloat16)
+    grad_v_raw = grad_values.astype(jnp.bfloat16)[None]
     grad_heads_raw = jnp.concatenate([grad_q_raw[0], grad_k_raw[0], grad_v_raw[0]], axis=1)
     grad_projections = jnp.einsum(
         "sd,sk->dk", first_normed_input[0], grad_heads_raw, preferred_element_type=jnp.float32

time: 1030 us -> 929 us (0.902)
  matrix products: 308 us -> 195 us
  Pallas kernels: 454 us -> 567 us
  other arithmetic: 111 us -> 63.3 us
  waiting for transfers between devices: 43.5 us -> 0.09 us
    pallas_call x0 -> x6, Pallas kernels: none -> 207 us  [the longest x2 94.4 us: to_heads(): pl.pallas_call(functools.partial(to_heads_kernel, line, shared), out_shap...]
    dot_general x9 -> x3, matrix products: 116 us -> 13 us  [the longest x1 4.35 us: per_device(): jnp.einsum('sd,kd->sk', grad_attn, w_out, preferred_element_type=jnp.floa...]
    pallas_call x4, Pallas kernels: 278 us -> 218 us  [reduce_to(): pl.pallas_call(functools.partial(reduce_kernel, square, line, paired), ou...]
    all_gather x2 -> x0, waiting for transfers between devices: 43.3 us -> none  [the longest x1 28.9 us: per_device(): lax.all_gather(key_rows, 'expert', axis=1, tiled=True)]
    pallas_call x1, Pallas kernels: 113 us -> 79.1 us  [gather_all(): pl.pallas_call(functools.partial(gather_all_kernel, line), out_shape=(jax...]
    convert_element_type x2 -> x1, other arithmetic: 30.6 us -> 2.19 us  [per_device(): grad_attn = gather_dp(grad_hidden.astype(jnp.bfloat16))]
    reduce_sum x1, other arithmetic: 15.4 us -> 1.55 us  [backward(): delta = jnp.sum(grad.astype(jnp.float32) * out.astype(jnp.float32), axis=-1)]
    unnamed x110 -> x112, local copies, waits for them, and re-layouts: 29.4 us -> 21.9 us
  transfers between devices with their start and end apart: 8 -> 4, of which waited for: 2 -> 0; matrix products, arithmetic and copies ran while one was open for 39% -> 28% of each run, Pallas kernels for 38% -> 54%
where the time goes in v3:
time: 929 us; the launch traced here: 925 us
  Pallas kernels  567 us (61%)
  matrix products  195 us (21%)
  other arithmetic  63.3 us (7%)
  local copies, waits for them, and re-layouts  49.9 us (5%)
  blocking collectives  34.7 us (4%)
  between operations  14.8 us (2%)
    pallas_call x4, Pallas kernels, reduce_to(): pl.pallas_call(functools.partial(reduce_kernel, square, line, paired), ou...  218 us
    pallas_call x2, Pallas kernels, to_heads(): pl.pallas_call(functools.partial(to_heads_kernel, line, shared), out_shap...  94.4 us
    pallas_call x2, Pallas kernels, to_tokens(): pl.pallas_call(functools.partial(to_tokens_kernel, line, summed), out_sha...  80.5 us
    pallas_call x1, Pallas kernels, gather_all(): pl.pallas_call(functools.partial(gather_all_kernel, line), out_shape=(jax...  79.1 us
    pallas_call x3, Pallas kernels, gather_dp(): pl.pallas_call(gather_square_kernel, out_shape=jax.ShapeDtypeStruct((4, 2...  63.4 us
    dot_general x1, matrix products, per_device(): jnp.einsum('td,jfd->tjf', top_all, w_down, preferred_element_type=jnp.flo...  24.7 us
    dot_general x1, matrix products, per_device(): jnp.einsum('tjf,jdf->td', grad_up_pre, w_up, preferred_element_type=jnp.f...  22.9 us
    unnamed x112, local copies, waits for them, and re-layouts  21.9 us
  transfers between devices with their start and end apart: 4, of which 0 were waited for; matrix products, arithmetic and copies ran while one was open for 28% of the time, Pallas kernels for 54%

profile of v3, /device:TPU:24, one launch (start us, length us, event | category | flops | bytes accessed | tf_op | source)
XLA Modules:
  0.0 924.8 jit_solution(282205627604057896)
XLA Ops:
  57.3 68.3 %scatter_heads.1 = (bf16[4,512,128]{2,1,0:T(8,128)(2,1)}, bf16[4,2,512,128]{3,2,1,0:T(8,128)(2,1)}, bf16[4,2,512,128]{3,2,1,0:T(8,128)(2,1)}) custom-call(bf16[512,512]{1,0:T(8,128)(2,1)} %bitcast.204, bf16[512,512]{1,0:T(8,128)(2,1)} %bitcast.203, bf16[512,512]{1,0:T(8,128)(2,1)} %convolution_convert_fusion.5.refs_2_), custom_call_target="tpu_custom_call" | custom-call | tf_op jit(solution)/shard_map/scatter_heads/pallas_call | solution.py:644
  126.5 13.6 %attend.1 = (bf16[4,512,128]{2,1,0:T(8,128)(2,1)}, f32[4,1,512]{2,1,0:T(1,128)}) custom-call(s32[3,4]{1,0:T(4,128)} %pad_add_fusion.bounds, bf16[4,512,128]{2,1,0:T(8,128)(2,1)} %get-tuple-element.27.q_ref, bf16[4096,128]{1,0:T(8,128)(2,1)} %bitcast.193, bf16[4096,128]{1,0:T(8,128)(2,1)} %bitcast.195, s32[4,1,512]{2,1,0:T(1,128)} %copy-done.25), custom_call_target="tpu_custom_call" | custom-call | tf_op jit(solution)/shard_map/attend/pallas_call | solution.py:848
  140.1 18.0 %gather_heads.1 = bf16[512,512]{1,0:T(8,128)(2,1)} custom-call(bf16[4,512,128]{2,1,0:T(8,128)(2,1)} %get-tuple-element.30.refs_0_), custom_call_target="tpu_custom_call" | custom-call | tf_op jit(solution)/shard_map/gather_heads/pallas_call | solution.py:745
  162.5 22.3 %scatter_dp.2 = f32[2,64,2048]{2,1,0:T(8,128)} custom-call(bf16[4,1,1,2,64,2048]{5,4,3,2,1,0:T(8,128)(2,1)} %bitcast.207), custom_call_target="tpu_custom_call" | custom-call | tf_op jit(solution)/shard_map/scatter_dp/pallas_call | solution.py:510
  193.1 79.1 %gather_all.1 = (bf16[32,2,64,2048]{3,2,1,0:T(8,128)(2,1)}, f32[32,16,128]{2,1,0:T(8,128)}) custom-call(bf16[2,64,2048]{2,1,0:T(8,128)(2,1)} %multiply_convert_fusion.6.x_ref, f32[16,128]{1,0:T(8,128)} %select_bitcast_fusion.g_ref), custom_call_target="tpu_custom_call" | custom-call | tf_op jit(solution)/shard_map/gather_all/pallas_call | solution.py:206
  273.2 15.3 %fusion.51 = f32[4096,2,256]{0,2,1:T(8,128)} fusion(bf16[4096,2048,1]{1,0,2:T(8,128)(2,1)} %bitcast.221, bf16[2,2048,256]{2,1,0:T(8,128)(2,1)} %param.27), kind=kOutput, calls=%fused_computation.145 | convolution fusion | flops 8589934592 | bytes 27262976 | tf_op jit(solution)/shard_map/td,jdf->tjf/dot_general | solution.py:1071
  288.5 14.8 %fusion.50 = f32[4096,2,256]{0,2,1:T(8,128)} fusion(bf16[4096,2048,1]{1,0,2:T(8,128)(2,1)} %bitcast.222, bf16[2,2048,256]{2,1,0:T(8,128)(2,1)S(1)} %copy-done.51), kind=kOutput, calls=%fused_computation.144 | convolution fusion | flops 8589934592 | bytes 27262976 | tf_op jit(solution)/shard_map/td,jdf->tjf/dot_general | solution.py:1070
  303.3 24.7 %multiply_reduce_fusion = (f32[4096,2]{0,1:T(2,128)}, bf16[4096,2,256]{0,2,1:T(8,128)(2,1)}, bf16[4096,2,256]{0,2,1:T(8,128)(2,1)}, bf16[4096,2,256]{0,2,1:T(8,128)(2,1)}) fusion(f32[4096,2,256]{0,2,1:T(8,128)} %fusion.51, f32[4096,2,256]{0,2,1:T(8,128)} %fusion.50, f32[4096,2]{0,1:T(2,128)S(1)} %dynamic-slice_bitcast_fusion, ...), kind=kOutput, calls=%fused_computation.7 | convolution fusion | flops 8629772288 | bytes 48300032 | tf_op jit(solution)/shard_map/td,jfd->tjf/dot_general | solution.py:1072
  329.6 18.0 %fusion.52 = f32[4096,2048,1]{1,0,2:T(8,128)} fusion(bf16[4096,2,256]{0,2,1:T(8,128)(2,1)} %get-tuple-element.98, bf16[2,2048,256]{2,1,0:T(8,128)(2,1)} %param.26), kind=kOutput, calls=%fused_computation.146 | convolution fusion | flops 8589934592 | bytes 39845888 | tf_op jit(solution)/shard_map/tjf,jdf->td/dot_general | solution.py:1084
  347.6 22.9 %fusion = bf16[4096,2048]{1,0:T(8,128)(2,1)} fusion(f32[4096,2048,1]{1,0,2:T(8,128)} %fusion.52, bf16[4096,2,256]{0,2,1:T(8,128)(2,1)} %get-tuple-element.100, bf16[2,2048,256]{2,1,0:T(8,128)(2,1)} %param.27), kind=kOutput, calls=%fused_computation.1 | convolution fusion | flops 8606711808 | bytes 56623104 | tf_op jit(solution)/shard_map/tjf,jdf->td/dot_general | solution.py:1085
  370.5 89.1 %scatter_all.1 = f32[2,64,2048]{2,1,0:T(8,128)} custom-call(bf16[4,4,2,2,64,2048]{5,4,3,2,1,0:T(8,128)(2,1)} %bitcast.179), custom_call_target="tpu_custom_call" | custom-call | tf_op jit(solution)/shard_map/scatter_all/pallas_call | solution.py:510
  466.1 23.4 %gather_dp.4 = bf16[4,2,64,2048]{3,2,1,0:T(8,128)(2,1)} custom-call(bf16[2,64,2048]{2,1,0:T(8,128)(2,1)} %bitcast.200), custom_call_target="tpu_custom_call" | custom-call | tf_op jit(solution)/shard_map/gather_dp/pallas_call | solution.py:264
  493.9 15.0 %bitcast_convert_fusion = bf16[4096,2048]{1,0:T(8,128)(2,1)} fusion(bf16[4096,2,256]{0,2,1:T(8,128)(2,1)} %get-tuple-element.99, bf16[2,256,2048]{2,1,0:T(8,128)(2,1)S(1)} %copy-done), kind=kOutput, calls=%fused_computation.2 | convolution fusion | flops 8598323200 | bytes 23068672 | tf_op jit(solution)/shard_map/tjf,jfd->td/dot_general | solution.py:1083
  512.9 13.9 %convolution_bitcast_fusion = f32[2,2048,256]{1,2,0:T(8,128)} fusion(bf16[4096,2,256]{0,2,1:T(8,128)(2,1)S(1)} %copy-done.52, bf16[4096,2048,1]{1,0,2:T(8,128)(2,1)} %bitcast.223), kind=kOutput, calls=%fused_computation.18 | convolution fusion | flops 8589934592 | bytes 25165824 | tf_op jit(solution)/shard_map/td,tjf->jdf/dot_general | solution.py:1090
  532.2 15.1 %convolution_bitcast_fusion.1 = f32[2,2048,256]{1,2,0:T(8,128)} fusion(bf16[4096,2,256]{0,2,1:T(8,128)(2,1)} %get-tuple-element.98, bf16[4096,2048,1]{1,0,2:T(8,128)(2,1)} %bitcast.224), kind=kOutput, calls=%fused_computation.19 | convolution fusion | flops 8589934592 | bytes 25165824 | tf_op jit(solution)/shard_map/td,tjf->jdf/dot_general | solution.py:1089
  552.8 15.0 %fusion.1 = f32[2,256,2048]{2,1,0:T(8,128)} fusion(bf16[4096,2,256]{0,2,1:T(8,128)(2,1)} %get-tuple-element.99, bf16[1,4096,2048]{2,1,0:T(8,128)(2,1)} %all-gather.3.cloned.1.call-done), kind=kOutput, calls=%fused_computation.3 | convolution fusion | flops 8589934592 | bytes 25165824 | tf_op jit(solution)/shard_map/tjf,td->jfd/dot_general | solution.py:1088
  575.7 26.1 %scatter_grads.1.d_ref = bf16[4,512,128]{2,1,0:T(8,128)(2,1)} custom-call(bf16[512,512]{1,0:T(8,128)(2,1)} %convolution_convert_fusion.4.refs_0_), custom_call_target="tpu_custom_call" | custom-call | tf_op jit(solution)/shard_map/scatter_grads/pallas_call | solution.py:644
  604.0 18.4 %attend_back.1 = (bf16[4,512,128]{2,1,0:T(8,128)(2,1)}, bf16[4096,128]{1,0:T(8,128)(2,1)}, bf16[4096,128]{1,0:T(8,128)(2,1)}) custom-call(s32[3,4]{1,0:T(4,128)} %pad_add_fusion.bounds, bf16[4,512,128]{2,1,0:T(8,128)(2,1)} %get-tuple-element.27.q_ref, bf16[4096,128]{1,0:T(8,128)(2,1)} %bitcast.194, bf16[4096,128]{1,0:T(8,128)(2,1)} %bitcast.196, ...), custom_call_target="tpu_custom_call" | custom-call | tf_op jit(solution)/shard_map/attend_back/pallas_call | solution.py:870
  622.4 62.5 %gather_grads.1 = (bf16[512,512]{1,0:T(8,128)(2,1)}, bf16[512,512]{1,0:T(8,128)(2,1)}, bf16[512,512]{1,0:T(8,128)(2,1)}) custom-call(bf16[4,512,128]{2,1,0:T(8,128)(2,1)} %get-tuple-element.34.refs_0_, bf16[4,2,512,128]{3,2,1,0:T(8,128)(2,1)} %bitcast.208, bf16[4,2,512,128]{3,2,1,0:T(8,128)(2,1)} %bitcast.209), custom_call_target="tpu_custom_call" | custom-call | tf_op jit(solution)/shard_map/gather_grads/pallas_call | solution.py:745
  719.5 38.3 %scatter_dp.3 = f32[2,64,2048]{2,1,0:T(8,128)} custom-call(bf16[4,1,1,2,64,2048]{5,4,3,2,1,0:T(8,128)(2,1)} %bitcast.186), custom_call_target="tpu_custom_call" | custom-call | tf_op jit(solution)/shard_map/scatter_dp/pallas_call | solution.py:510
  777.2 67.8 %scatter_expert.1 = f32[2,144,1536]{2,1,0:T(8,128)} custom-call(bf16[1,4,2,2,144,1536]{5,4,3,2,1,0:T(8,128)(2,1)} %bitcast.178), custom_call_target="tpu_custom_call" | custom-call | tf_op jit(solution)/shard_map/scatter_expert/pallas_call | solution.py:510
  846.1 16.3 %psum.39 = bf16[4608]{0:T(1024)(128)(2,1)S(1)} all-reduce(bf16[4608]{0:T(1024)(128)(2,1)S(1)} %slice.128), channel_id=1, replica_groups=mesh['dp'=4,'expert'=8] {'dp'}, use_global_device_ids=true, to_apply=%region_27.28 | all-reduce | flops 4608 | bytes 18432 | tf_op jit(solution)/shard_map/psum | solution.py:1194
  872.5 21.4 %gather_dp.3 = bf16[4,2,64,2048]{3,2,1,0:T(8,128)(2,1)} custom-call(bf16[2,64,2048]{2,1,0:T(8,128)(2,1)} %bitcast.199), custom_call_target="tpu_custom_call" | custom-call | tf_op jit(solution)/shard_map/gather_dp/pallas_call | solution.py:264
  893.9 18.5 %gather_dp.5 = bf16[4,2,64,2048]{3,2,1,0:T(8,128)(2,1)} custom-call(bf16[2,64,2048]{2,1,0:T(8,128)(2,1)} %bitcast.198), custom_call_target="tpu_custom_call" | custom-call | tf_op jit(solution)/shard_map/gather_dp/pallas_call | solution.py:264
  (217 shorter events, 172.0 us)
Async XLA Ops:
  7.2 296.1 %copy-start = (bf16[2,256,2048]{2,1,0:T(8,128)(2,1)S(1)}, bf16[2,256,2048]{2,1,0:T(8,128)(2,1)}, u32[]{:S(2)}) copy-start(bf16[2,256,2048]{2,1,0:T(8,128)(2,1)} %param.28) | copy-start | bytes 6291460
  7.2 296.1 %all-gather.3.cloned.1.call-start = ((), (), s32[]{:S(2)}) async-start(), calls=%async_computation.6 | async-start | bytes 17301504 | tf_op jit(solution)/shard_map/all_gather | solution.py:1063
  9.3 450.3 %reduce-scatter.6.cloned.1.call-start = ((), (), s32[]{:S(2)}) async-start(), calls=%async_computation.4 | async-start | bytes 270336 | tf_op jit(solution)/shard_map/reduce_scatter | solution.py:1099
  16.0 37.0 %copy-start.46 = (f32[512]{0:T(512)}, f32[512]{0:T(512)S(1)}, u32[]{:S(2)}) copy-start(f32[512]{0:T(512)S(1)} %add_rsqrt_fusion.2) | copy-start | bytes 6148
  18.8 17.0 %copy-start.37 = (f32[512]{0:T(512)S(1)}, f32[512]{0:T(512)}, u32[]{:S(2)}) copy-start(f32[512]{0:T(512)} %param.22) | copy-start | bytes 6148
  25.0 19.5 %copy-start.4 = (f32[512,512]{1,0:T(8,128)}, f32[512,512]{1,0:T(8,128)S(1)}, u32[]{:S(2)}) copy-start(f32[512,512]{1,0:T(8,128)S(1)} %copy.52) | copy-start | bytes 3145732
  162.5 25.8 %copy-start.23 = (f32[2048,16]{0,1:T(8,128)S(1)}, f32[2048,16]{0,1:T(8,128)}, u32[]{:S(2)}) copy-start(f32[2048,16]{0,1:T(8,128)} %param.25) | copy-start | bytes 393220
  162.5 25.8 %copy-start.24 = (f32[2048]{0:T(1024)S(1)}, f32[2048]{0:T(1024)}, u32[]{:S(2)}) copy-start(f32[2048]{0:T(1024)} %param.24) | copy-start | bytes 24580
  187.5 84.7 %copy-start.41 = (f32[128]{0:T(128)}, f32[128]{0:T(128)S(1)}, u32[]{:S(2)}) copy-start(f32[128]{0:T(128)S(1)} %add_rsqrt_fusion.3) | copy-start | bytes 1540
  189.3 82.9 %copy-start.44 = (f32[128]{0:T(128)}, f32[128]{0:T(128)S(1)}, u32[]{:S(2)}) copy-start(f32[128]{0:T(128)S(1)} %fusion.31) | copy-start | bytes 1540
  329.5 538.1 %reduce-scatter.8.cloned.1.call-start = ((), (), s32[]{:S(2)}) async-start(), calls=%async_computation.5 | async-start | bytes 2359296 | tf_op jit(solution)/shard_map/reduce_scatter | solution.py:1196
  370.5 89.1 %copy-start.28 = (pred[128,16]{0,1:T(8,128)(4,1)S(1)}, pred[128,16]{0,1:T(8,128)(4,1)}, u32[]{:S(2)}) copy-start(pred[128,16]{0,1:T(8,128)(4,1)} %copy-done.27) | copy-start | bytes 6148
  370.5 89.1 %copy-start.40 = (f32[128]{0:T(128)S(1)}, f32[128]{0:T(128)}, u32[]{:S(2)}) copy-start(f32[128]{0:T(128)} %copy-done.39) | copy-start | bytes 1540
  370.5 89.1 %copy-start.45 = (f32[128]{0:T(128)S(1)}, f32[128]{0:T(128)}, u32[]{:S(2)}) copy-start(f32[128]{0:T(128)} %copy-done.44) | copy-start | bytes 1540
  370.5 89.9 %copy-start.42 = (f32[128]{0:T(128)S(1)}, f32[128]{0:T(128)}, u32[]{:S(2)}) copy-start(f32[128]{0:T(128)} %copy-done.41) | copy-start | bytes 1540
  463.0 30.9 %copy-start.48 = (f32[128]{0:T(128)}, f32[128]{0:T(128)S(1)}, u32[]{:S(2)}) copy-start(f32[128]{0:T(128)S(1)} %broadcast_multiply_fusion.2) | copy-start | bytes 1540
  493.9 375.5 %reduce-scatter.4.cloned.1.call-start = ((), (), s32[]{:S(2)}) async-start(), calls=%async_computation.3 | async-start | bytes 17301504 | tf_op jit(solution)/shard_map/reduce_scatter | solution.py:1092
  604.0 85.6 %copy-start.16 = (f32[512,64]{1,0:T(8,128)S(1)}, f32[512,64]{1,0:T(8,128)}, u32[]{:S(2)}) copy-start(f32[512,64]{1,0:T(8,128)} %copy-done.15) | copy-start | bytes 393220
  716.9 41.0 %copy-start.30 = (f32[2048]{0:T(1024)S(1)}, f32[2048]{0:T(1024)}, u32[]{:S(2)}) copy-start(f32[2048]{0:T(1024)} %param.17) | copy-start | bytes 24580
  845.0 24.4 %copy-start.6 = (f32[2,64,2048]{2,1,0:T(8,128)S(1)}, f32[2,64,2048]{2,1,0:T(8,128)}, u32[]{:S(2)}) copy-start(f32[2,64,2048]{2,1,0:T(8,128)} %scatter_dp.3) | copy-start | bytes 3145732
  845.0 24.4 %copy-start.10 = (f32[128,2048]{1,0:T(8,128)S(1)}, f32[128,2048]{1,0:T(8,128)}, u32[]{:S(2)}) copy-start(f32[128,2048]{1,0:T(8,128)} %copy-done.9) | copy-start | bytes 3145732
  846.1 23.3 %copy-start.43 = (f32[128]{0:T(128)S(1)}, f32[128]{0:T(128)}, u32[]{:S(2)}) copy-start(f32[128]{0:T(128)} %copy-done.41) | copy-start | bytes 1540
  846.1 23.3 %copy-start.49 = (f32[128]{0:T(128)S(1)}, f32[128]{0:T(128)}, u32[]{:S(2)}) copy-start(f32[128]{0:T(128)} %copy-done.48) | copy-start | bytes 1540
  846.1 23.3 %copy-start.50 = (f32[128]{0:T(128)S(1)}, f32[128]{0:T(128)}, u32[]{:S(2)}) copy-start(f32[128]{0:T(128)} %dynamic_slice.44) | copy-start | bytes 1540
  (33 other events, 137.2 us)
Sparse Core Ops, SparseCore 0:
  11.6 139.8 all-gather.2
  329.6 119.7 reduce-scatter.5
  494.0 33.2 reduce-scatter.7
  529.5 228.4 reduce-scatter.3

commit v4 on v3

--- a/solution.py
+++ b/solution.py
@@ -70,156 +70,14 @@
     )
 
 
+def contract(a, b, a_dim, b_dim):
+    return lax.dot_general(
+        a, b, (((a_dim,), (b_dim,)), ((), ())), preferred_element_type=jnp.float32
+    )
+
+
 def corners(dp):
     return dp + 1 - 2 * (dp % 2), (dp + 2) % 4
-
-
-def gather_all_kernel(line, x_ref, g_ref, out_ref, table_ref, sent, arrived, own_sem):
-    dp, place = lax.axis_index("dp"), lax.axis_index("expert")
-    z, c = place // 2, place % 2
-    side_x, side_y = corners(dp)
-    far = 3 - dp
-    devices = (
-        (dp, place + 2),
-        (dp, place - 2),
-        (side_x, place),
-        (side_y, place),
-        (dp, 2 * z + 1 - c),
-    )
-    up, down, along_x, along_y, pair = range(5)
-    has_up, has_down = z < line - 1, z > 0
-    for way in (along_x, along_y, pair):
-        greet(devices[way])
-    pl.when(has_up)(lambda: greet(devices[up]))
-    pl.when(has_down)(lambda: greet(devices[down]))
-    greeted = 3 + has_up.astype(jnp.int32) + has_down.astype(jnp.int32)
-    pl.semaphore_wait(pltpu.get_barrier_semaphore(), greeted)
-
-    pieces = (0, 1, 2)
-
-    def slot(corner, height, core):
-        return corner * (2 * line) + 2 * height + core
-
-    def part(s, p):
-        return table_ref.at[s] if p == 2 else out_ref.at[s, p]
-
-    def copy(s, p, way, source=None):
-        target = part(s, p)
-        return send(
-            target if source is None else source,
-            target,
-            sent.at[s, p, way],
-            arrived.at[s, p],
-            devices[way],
-        )
-
-    def arrive(s, p):
-        copy(s, p, pair).wait_recv()
-
-    mine = slot(dp, z, c)
-    for p in pieces:
-        source = g_ref if p == 2 else x_ref.at[p]
-        pltpu.make_async_copy(source, part(mine, p), own_sem.at[p]).start()
-        pl.when(has_up)(lambda: copy(mine, p, up, source).start())
-        pl.when(has_down)(lambda: copy(mine, p, down, source).start())
-        for way in (along_x, along_y, pair):
-            copy(mine, p, way, source).start()
-
-    def spread(s, p):
-        for way in (along_x, along_y, pair):
-            copy(s, p, way).start()
-
-    def column(away):
-        def below():
-            s = slot(dp, z - away, c)
-            for p in pieces:
-                arrive(s, p)
-                pl.when(has_up)(lambda: copy(s, p, up).start())
-                spread(s, p)
-
-        def above():
-            s = slot(dp, z + away, c)
-            for p in pieces:
-                arrive(s, p)
-                pl.when(has_down)(lambda: copy(s, p, down).start())
-                spread(s, p)
-
-        pl.when((away > 0) & (away < line) & (z - away >= 0))(below)
-        pl.when((away > 0) & (away < line) & (z + away < line))(above)
-
-    def sides(height):
-        for p in pieces:
-            s = slot(side_x, height, c)
-            arrive(s, p)
-            if p != 1:
-                copy(s, p, along_y).start()
-            copy(s, p, pair).start()
-            s = slot(side_y, height, c)
-            arrive(s, p)
-            if p == 1:
-                copy(s, p, along_x).start()
-            copy(s, p, pair).start()
-
-    def opposite(height):
-        for p in pieces:
-            s = slot(far, height, c)
-            arrive(s, p)
-            copy(s, p, pair).start()
-
-    def both(away, visit):
-        pl.when((away >= 0) & (away < line) & (z - away >= 0))(lambda: visit(z - away))
-        pl.when((away > 0) & (away < line) & (z + away < line))(lambda: visit(z + away))
-
-    def step(k, carry):
-        column(k)
-        both(k - 1, sides)
-        both(k - 2, opposite)
-        return carry
-
-    lax.fori_loop(1, line + 2, step, 0)
-
-    def finish(height, carry):
-        for p in pieces:
-            for corner in range(4):
-                arrive(slot(corner, height, 1 - c), p)
-                copy(slot(corner, height, c), p, pair).wait_send()
-            s = slot(dp, height, c)
-            copy(s, p, along_x).wait_send()
-            copy(s, p, along_y).wait_send()
-            if p == 1:
-                copy(slot(side_y, height, c), p, along_x).wait_send()
-            else:
-                copy(slot(side_x, height, c), p, along_y).wait_send()
-            pl.when(has_up & (height <= z))(lambda: copy(s, p, up).wait_send())
-            pl.when(has_down & (height >= z))(lambda: copy(s, p, down).wait_send())
-        return carry
-
-    lax.fori_loop(0, line, finish, 0)
-    for p in pieces:
-        source = g_ref if p == 2 else x_ref.at[p]
-        pltpu.make_async_copy(source, part(mine, p), own_sem.at[p]).wait()
-
-
-def gather_all(rows, table, line):
-    count, width = rows.shape
-    slots = 8 * line
-    gathered, tables = pl.pallas_call(
-        functools.partial(gather_all_kernel, line),
-        out_shape=(
-            jax.ShapeDtypeStruct((slots, 2, count // 2, width), rows.dtype),
-            jax.ShapeDtypeStruct((slots, *table.shape), table.dtype),
-        ),
-        in_specs=[pl.BlockSpec(memory_space=pltpu.VMEM)] * 2,
-        out_specs=[pl.BlockSpec(memory_space=pl.ANY)] * 2,
-        scratch_shapes=[
-            pltpu.SemaphoreType.DMA((slots, 3, 5)),
-            pltpu.SemaphoreType.DMA((slots, 3)),
-            pltpu.SemaphoreType.DMA((3,)),
-        ],
-        compiler_params=pltpu.CompilerParams(collective_id=1, has_side_effects=True),
-        name="gather_all",
-    )(rows.reshape(2, count // 2, width), table)
-    return gathered.reshape(slots * count, width), tables
 
 
 def gather_square_kernel(x_ref, out_ref, sent, arrived, own_sem):
@@ -278,12 +136,7 @@
 
 
 def farthest(line, z, k):
-    total = jnp.int32(0)
-    for at in range(line):
-        order = sorted(range(line), key=lambda place: (-abs(place - at), place))
-        place = sum([jnp.where(k == i, order[i], 0) for i in range(line)])
-        total = total + jnp.where(z == at, place, 0)
-    return total
+    return ranked(line, z, k, lambda place, at: (-abs(place - at), place))
 
 
 def reduce_kernel(
@@ -542,11 +395,6 @@
     return reduce_to(rows.reshape(4, -1, rows.shape[1]), True, 1, False, "scatter_dp", 3)
 
 
-def scatter_all(rows, line):
-    parts = rows.reshape(8 * line, -1, rows.shape[1])
-    return reduce_to(parts, True, line, True, "scatter_all", 4)
-
-
 def scatter_expert(parts, line):
     return reduce_to(parts, False, line, True, "scatter_expert", 5)
 
@@ -763,12 +611,6 @@
 KEY_TILE = 512
 
 
-def contract(a, b, a_dim, b_dim):
-    return lax.dot_general(
-        a, b, (((a_dim,), (b_dim,)), ((), ())), preferred_element_type=jnp.float32
-    )
-
-
 def masked_scores(keys, queries, tile, first, starts):
     scores = contract(keys, queries, 1, 1) * HD ** (-0.5)
     key_at = tile * KEY_TILE + lax.broadcasted_iota(jnp.int32, scores.shape, 0)
@@ -970,6 +812,535 @@
         return (dq * scale).reshape(shape), to_owner(dk * scale), to_owner(dv)
 
     return forward, backward
+
+
+def nearest(line, z, k):
+    return ranked(line, z, k, lambda place, at: (abs(place - at), place))
+
+
+def ranked(line, z, k, rank):
+    total = jnp.int32(0)
+    for at in range(line):
+        order = sorted(range(line), key=lambda place: rank(place, at))
+        place = sum([jnp.where(k == i, order[i], 0) for i in range(line)])
+        total = total + jnp.where(z == at, place, 0)
+    return total
+
+
+def gate_act_kernel(
+    line,
+    x_ref,
+    top_ref,
+    wg_ref,
+    wu_ref,
+    wd_ref,
+    xn_ref,
+    grads_ref,
+    scaled_ref,
+    gates_ref,
+    xbuf,
+    top_buf,
+    grads_buf,
+    scaled_buf,
+    gates_buf,
+    sent,
+    arrived,
+    own_sem,
+    top_sem,
+    xn_sem,
+    grads_sem,
+    scaled_sem,
+    gates_sem,
+):
+    dp, place = lax.axis_index("dp"), lax.axis_index("expert")
+    z, c = place // 2, place % 2
+    side_x, side_y = corners(dp)
+    far = 3 - dp
+    devices = (
+        (dp, place + 2),
+        (dp, place - 2),
+        (side_x, place),
+        (side_y, place),
+        (dp, 2 * z + 1 - c),
+    )
+    up, down, along_x, along_y, pair = range(5)
+    has_up, has_down = z < line - 1, z > 0
+    for way in (along_x, along_y, pair):
+        greet(devices[way])
+    pl.when(has_up)(lambda: greet(devices[up]))
+    pl.when(has_down)(lambda: greet(devices[down]))
+    greeted = 3 + has_up.astype(jnp.int32) + has_down.astype(jnp.int32)
+    pl.semaphore_wait(pltpu.get_barrier_semaphore(), greeted)
+    local, width, units = wg_ref.shape
+    rows = top_buf.shape[1]
+    first = place * local
+
+    def slot(corner, height, core):
+        return corner * (2 * line) + 2 * height + core
+
+    def copy(s, p, way, source=None):
+        target = xbuf.at[s, p]
+        return send(
+            target if source is None else source,
+            target,
+            sent.at[s, p, way],
+            arrived.at[s, p],
+            devices[way],
+        )
+
+    def arrive(s, p):
+        copy(s, p, pair).wait_recv()
+
+    mine = slot(dp, z, c)
+    for p in (0, 1):
+        pltpu.make_async_copy(x_ref.at[p], xbuf.at[mine, p], own_sem.at[p]).start()
+        pl.when(has_up)(lambda: copy(mine, p, up, x_ref.at[p]).start())
+        pl.when(has_down)(lambda: copy(mine, p, down, x_ref.at[p]).start())
+        for way in (along_x, along_y, pair):
+            copy(mine, p, way, x_ref.at[p]).start()
+
+    def decode(i):
+        turn, j = i // 4, i % 4
+        k = turn - (j > 0).astype(jnp.int32) - (j == 3).astype(jnp.int32)
+        valid = (i >= 0) & (k >= 0) & (k < line)
+        corner = jnp.where(j == 0, dp, jnp.where(j == 1, side_x, jnp.where(j == 2, side_y, far)))
+        return j, k, valid, corner, nearest(line, z, k)
+
+    def top_load(i, corner, height):
+        block = corner * line + height
+        return pltpu.make_async_copy(top_ref.at[block], top_buf.at[i % 2], top_sem.at[i % 2])
+
+    def xn_out(block):
+        return pltpu.make_async_copy(
+            xbuf.at[pl.ds(2 * block, 2), :, :, pl.ds(0, width)],
+            xn_ref.at[pl.ds(2 * block, 2)],
+            xn_sem.at[block],
+        )
+
+    def grads_out(block):
+        return pltpu.make_async_copy(grads_buf.at[block], grads_ref.at[block], grads_sem.at[block])
+
+    def scaled_out(block):
+        return pltpu.make_async_copy(
+            scaled_buf.at[block], scaled_ref.at[block], scaled_sem.at[block]
+        )
+
+    def gates_out(block):
+        return pltpu.make_async_copy(gates_buf.at[block], gates_ref.at[block], gates_sem.at[block])
+
+    def compute(i):
+        j, k, _, corner, height = decode(i)
+        block = corner * line + height
+        for p in (0, 1):
+            arrive(slot(corner, height, 1 - c), p)
+        xn_out(block).start()
+        top_load(i, corner, height).wait()
+        lanes = lax.broadcasted_iota(jnp.int32, (rows, 128), 1)
+
+        def tokens():
+            return xbuf[pl.ds(2 * block, 2), :, :, pl.ds(0, width)].reshape(rows, width)
+
+        table = xbuf[pl.ds(2 * block, 2), :, :, pl.ds(width, 128)].reshape(rows, 128)
+        table = table.astype(jnp.float32)
+        gate_grads = jnp.zeros((rows, 128), jnp.float32)
+        for e in range(local):
+            at = (lanes == first + e) | (lanes == first + e + 64)
+            gate = jnp.sum(jnp.where(at, table, 0.0), axis=1, keepdims=True)
+            g = contract(tokens(), wg_ref[e], 1, 0)
+            u = contract(tokens(), wu_ref[e], 1, 0)
+            h = contract(top_buf[i % 2], wd_ref[e], 1, 1)
+            sigmoid = 1.0 / (1.0 + jnp.exp(-g))
+            silu = g * sigmoid
+            act = silu * u
+            gate_grad = jnp.sum(act * h, axis=1, keepdims=True)
+            gate_grads = gate_grads + jnp.where(lanes == first + e, gate_grad, 0.0)
+            grad_act = h * gate
+            dg = grad_act * u * sigmoid * (1.0 + g * (1.0 - sigmoid))
+            du = grad_act * silu
+            scaled_buf[block, :, e * units : (e + 1) * units] = (act * gate).astype(jnp.bfloat16)
+            grads_buf[block, :, e * units : (e + 1) * units] = dg.astype(jnp.bfloat16)
+            at = (local + e) * units
+            grads_buf[block, :, at : at + units] = du.astype(jnp.bfloat16)
+        gates_buf[block] = gate_grads.astype(jnp.bfloat16)
+        grads_out(block).start()
+        scaled_out(block).start()
+        gates_out(block).start()
+
+    def step(i, carry):
+        j, k, valid, corner, height = decode(i)
+        s = slot(corner, height, c)
+
+        def own():
+            for p in (0, 1):
+                pltpu.make_async_copy(x_ref.at[p], xbuf.at[mine, p], own_sem.at[p]).wait()
+
+        def column():
+            for p in (0, 1):
+                arrive(s, p)
+                pl.when(has_up & (height < z))(lambda: copy(s, p, up).start())
+                pl.when(has_down & (height > z))(lambda: copy(s, p, down).start())
+                for way in (along_x, along_y, pair):
+                    copy(s, p, way).start()
+
+        def sides():
+            for p in (0, 1):
+                arrive(s, p)
+                copy(s, p, pair).start()
+            pl.when(j == 1)(lambda: copy(s, 0, along_y).start())
+            pl.when(j == 2)(lambda: copy(s, 1, along_x).start())
+
+        def opposite():
+            for p in (0, 1):
+                arrive(s, p)
+                copy(s, p, pair).start()
+
+        pl.when(valid & (j == 0) & (k == 0))(own)
+        pl.when(valid & (j == 0) & (k > 0))(column)
+        pl.when(valid & ((j == 1) | (j == 2)))(sides)
+        pl.when(valid & (j == 3))(opposite)
+        pl.when(valid)(lambda: top_load(i, corner, height).start())
+        pl.when(decode(i - 1)[2])(lambda: compute(i - 1))
+        return carry
+
+    lax.fori_loop(0, 4 * (line + 2) + 1, step, 0)
+
+    def finish(height, carry):
+        for p in (0, 1):
+            for corner in range(4):
+                copy(slot(corner, height, c), p, pair).wait_send()
+            s = slot(dp, height, c)
+            copy(s, p, along_x).wait_send()
+            copy(s, p, along_y).wait_send()
+            pl.when(has_up & (height <= z))(lambda: copy(s, p, up).wait_send())
+            pl.when(has_down & (height >= z))(lambda: copy(s, p, down).wait_send())
+        copy(slot(side_x, height, c), 0, along_y).wait_send()
+        copy(slot(side_y, height, c), 1, along_x).wait_send()
+        for corner in range(4):
+            block = corner * line + height
+            xn_out(block).wait()
+            grads_out(block).wait()
+            scaled_out(block).wait()
+            gates_out(block).wait()
+        return carry
+
+    lax.fori_loop(0, line, finish, 0)
+
+
+def gate_act(own, tops, w_gate, w_up, w_down, line):
+    count, wide = own.shape
+    local, width, units = w_gate.shape
+    slots, blocks, rows, half = 8 * line, 4 * line, 2 * count, count // 2
+    sems = pltpu.SemaphoreType.DMA
+    dtype = own.dtype
+    xn, grads, scaled, gates = pl.pallas_call(
+        functools.partial(gate_act_kernel, line),
+        out_shape=[
+            jax.ShapeDtypeStruct((slots, 2, half, width), dtype),
+            jax.ShapeDtypeStruct((blocks, rows, 2 * local * units), dtype),
+            jax.ShapeDtypeStruct((blocks, rows, local * units), dtype),
+            jax.ShapeDtypeStruct((blocks, rows, 128), dtype),
+        ],
+        in_specs=[
+            pl.BlockSpec(memory_space=pltpu.VMEM),
+            pl.BlockSpec(memory_space=pl.ANY),
+            pl.BlockSpec(memory_space=pltpu.VMEM),
+            pl.BlockSpec(memory_space=pltpu.VMEM),
+            pl.BlockSpec(memory_space=pltpu.VMEM),
+        ],
+        out_specs=[pl.BlockSpec(memory_space=pl.ANY)] * 4,
+        scratch_shapes=[
+            pltpu.VMEM((slots, 2, half, wide), dtype),
+            pltpu.VMEM((2, rows, width), dtype),
+            pltpu.VMEM((blocks, rows, 2 * local * units), dtype),
+            pltpu.VMEM((blocks, rows, local * units), dtype),
+            pltpu.VMEM((blocks, rows, 128), dtype),
+            sems((slots, 2, 5)),
+            sems((slots, 2)),
+            sems((2,)),
+            sems((2,)),
+            sems((blocks,)),
+            sems((blocks,)),
+            sems((blocks,)),
+            sems((blocks,)),
+        ],
+        compiler_params=pltpu.CompilerParams(
+            collective_id=1, has_side_effects=True, vmem_limit_bytes=60 << 20
+        ),
+        name="gate_act",
+    )(own.reshape(2, half, wide), tops.reshape(blocks, rows, width), w_gate, w_up, w_down)
+    return xn.reshape(slots * count, width), grads, scaled, gates
+
+
+def product_sum_kernel(
+    line,
+    flipped,
+    extra,
+    *refs,
+):
+    a_ref, w_ref = refs[0], refs[1]
+    e_ref = refs[2] if extra else None
+    refs = refs[3:] if extra else refs[2:]
+    (
+        out_ref,
+        made,
+        a_buf,
+        e_buf,
+        got_pair,
+        got_x,
+        got_y,
+        got_far_x,
+        got_far_y,
+        got_below,
+        got_above,
+        load_sem,
+        extra_sem,
+        pair_sem,
+        x_sem,
+        y_sem,
+        far_x_sem,
+        far_y_sem,
+        below_sem,
+        above_sem,
+    ) = refs
+    dp, place = lax.axis_index("dp"), lax.axis_index("expert")
+    z, c = place // 2, place % 2
+    side_x, side_y = corners(dp)
+    far = 3 - dp
+    to_x, to_y, to_pair = (side_x, place), (side_y, place), (dp, 2 * z + 1 - c)
+    to_up, to_down = (dp, place + 2), (dp, place - 2)
+    for device in (to_x, to_y, to_pair):
+        greet(device)
+    pl.when(z > 0)(lambda: greet(to_down))
+    pl.when(z < line - 1)(lambda: greet(to_up))
+    greeted = 3 + (z > 0).astype(jnp.int32) + (z < line - 1).astype(jnp.int32)
+    pl.semaphore_wait(pltpu.get_barrier_semaphore(), greeted)
+    count = 4 * line
+    width = w_ref.shape[0] if flipped else w_ref.shape[1]
+    half = made.shape[4]
+    chunk = 512
+
+    def mine(q, height, p):
+        return made.at[q, height, c, p]
+
+    def hand(q, height, p):
+        at = (q, height, p)
+        source = made.at[q, height, 1 - c, p]
+        return send(source, got_pair.at[at], pair_sem.at[0, *at], pair_sem.at[1, *at], to_pair)
+
+    def along_x(height, p):
+        at = (height, p)
+        source = mine(side_x, height, p)
+        return send(source, got_x.at[at], x_sem.at[0, *at], x_sem.at[1, *at], to_x)
+
+    def along_y(height, p):
+        at = (height, p)
+        source = mine(side_y, height, p)
+        return send(source, got_y.at[at], y_sem.at[0, *at], y_sem.at[1, *at], to_y)
+
+    def far_x(height):
+        source = mine(far, height, 0)
+        return send(
+            source, got_far_x.at[height], far_x_sem.at[0, height], far_x_sem.at[1, height], to_x
+        )
+
+    def far_y(height):
+        source = mine(far, height, 1)
+        return send(
+            source, got_far_y.at[height], far_y_sem.at[0, height], far_y_sem.at[1, height], to_y
+        )
+
+    def climb(height, p):
+        at = (height, p)
+        source = mine(dp, height, p)
+        return send(source, got_below.at[at], below_sem.at[0, *at], below_sem.at[1, *at], to_up)
+
+    def descend(height, p):
+        at = (height, p)
+        source = mine(dp, height, p)
+        return send(source, got_above.at[at], above_sem.at[0, *at], above_sem.at[1, *at], to_down)
+
+    def decode(i):
+        k, j = i // 4, i % 4
+        q = jnp.where(j == 0, far, jnp.where(j == 1, side_x, jnp.where(j == 2, side_y, dp)))
+        return k, j, q, farthest(line, z, k)
+
+    def load(i):
+        _, _, q, height = decode(i)
+        return pltpu.make_async_copy(
+            a_ref.at[q * line + height], a_buf.at[i % 2], load_sem.at[i % 2]
+        )
+
+    def load_extra(i):
+        _, _, q, height = decode(i)
+        return pltpu.make_async_copy(
+            e_ref.at[q * line + height], e_buf.at[i % 2], extra_sem.at[i % 2]
+        )
+
+    def start_load(i):
+        load(i).start()
+        if extra:
+            load_extra(i).start()
+
+    def add(q, height, p, other):
+        at = (q, height, c, p)
+        made[at] = made[at] + other[...]
+
+    def compute(i):
+        _, _, q, height = decode(i)
+        load(i).wait()
+        if extra:
+            load_extra(i).wait()
+        pl.when(i + 1 < count)(lambda: start_load(i + 1))
+        for at in range(0, width, chunk):
+            if flipped:
+                part = contract(a_buf[i % 2], w_ref[at : at + chunk, :], 1, 1)
+            else:
+                part = contract(a_buf[i % 2], w_ref[:, at : at + chunk], 1, 0)
+            part = part.astype(made.dtype).reshape(2, 2, half, chunk)
+            made[q, height, :, :, :, at : at + chunk] = part
+        if extra:
+            made[q, height, :, :, :, width : width + 128] = e_buf[i % 2].reshape(2, 2, half, 128)
+        for p in (0, 1):
+            hand(q, height, p).start()
+
+    def settle(i):
+        _, j, q, height = decode(i)
+        for p in (0, 1):
+            hand(q, height, p).wait_recv()
+            add(q, height, p, got_pair.at[q, height, p])
+
+        def opposite():
+            far_x(height).start()
+            far_y(height).start()
+
+        def side_of_x():
+            along_x(height, 0).start()
+            far_y(height).wait_recv()
+            add(side_x, height, 1, got_far_y.at[height])
+            along_x(height, 1).start()
+
+        def side_of_y():
+            along_y(height, 1).start()
+            far_x(height).wait_recv()
+            add(side_y, height, 0, got_far_x.at[height])
+            along_y(height, 0).start()
+
+        pl.when(j == 0)(opposite)
+        pl.when(j == 1)(side_of_x)
+        pl.when(j == 2)(side_of_y)
+
+    def column(height):
+        for p in (0, 1):
+            along_x(height, p).wait_recv()
+            along_y(height, p).wait_recv()
+            total = made[dp, height, c, p].astype(jnp.float32)
+            total = total + got_x[height, p].astype(jnp.float32)
+            total = total + got_y[height, p].astype(jnp.float32)
+            made[dp, height, c, p] = total.astype(made.dtype)
+            pl.when((z == 0) & (height > z))(lambda: climb(height, p).start())
+            pl.when((z == line - 1) & (height < z))(lambda: descend(height, p).start())
+
+    def pass_on(height):
+        for p in (0, 1):
+
+            def upwards():
+                climb(height, p).wait_recv()
+                add(dp, height, p, got_below.at[height, p])
+                climb(height, p).start()
+
+            def downwards():
+                descend(height, p).wait_recv()
+                add(dp, height, p, got_above.at[height, p])
+                descend(height, p).start()
+
+            pl.when((height > z) & (z > 0))(upwards)
+            pl.when((height < z) & (z < line - 1))(downwards)
+
+    start_load(0)
+
+    def step(i, carry):
+        k, j, _, _ = decode(i)
+        pl.when(i < count)(lambda: compute(i))
+        pl.when((i >= 1) & (i <= count))(lambda: settle(i - 1))
+        late = farthest(line, z, k - 2)
+        pl.when((k >= 2) & (j == 0))(lambda: column(late))
+        pl.when((k >= 2) & (j == 3))(lambda: pass_on(late))
+        return carry
+
+    lax.fori_loop(0, count + 8, step, 0)
+    for p in (0, 1):
+        out_ref[p] = made[dp, z, c, p].astype(jnp.float32)
+
+        def from_below():
+            climb(z, p).wait_recv()
+            out_ref[p] = out_ref[p] + got_below[z, p].astype(jnp.float32)
+
+        def from_above():
+            descend(z, p).wait_recv()
+            out_ref[p] = out_ref[p] + got_above[z, p].astype(jnp.float32)
+
+        pl.when(z > 0)(from_below)
+        pl.when(z < line - 1)(from_above)
+
+    def finish(height, carry):
+        far_x(height).wait_send()
+        far_y(height).wait_send()
+        for p in (0, 1):
+            for q in range(4):
+                hand(q, height, p).wait_send()
+            along_x(height, p).wait_send()
+            along_y(height, p).wait_send()
+            pl.when(height > z)(lambda: climb(height, p).wait_send())
+            pl.when(height < z)(lambda: descend(height, p).wait_send())
+        return carry
+
+    lax.fori_loop(0, line, finish, 0)
+
+
+def product_sum(blocks, weights, flipped, extra, line, name, number):
+    count, rows, depth = blocks.shape
+    width = weights.shape[0] if flipped else weights.shape[1]
+    wide = width + (0 if extra is None else 128)
+    half = rows // 4
+    sems = pltpu.SemaphoreType.DMA
+    dtype = blocks.dtype
+
+    def space(*shape):
+        return pltpu.VMEM((*shape, half, wide), dtype)
+
+    anywhere, inside = pl.BlockSpec(memory_space=pl.ANY), pl.BlockSpec(memory_space=pltpu.VMEM)
+    total = pl.pallas_call(
+        functools.partial(product_sum_kernel, line, flipped, extra is not None),
+        out_shape=jax.ShapeDtypeStruct((2, half, wide), jnp.float32),
+        in_specs=[anywhere, inside] + ([] if extra is None else [anywhere]),
+        out_specs=inside,
+        scratch_shapes=[
+            space(4, line, 2, 2),
+            pltpu.VMEM((2, rows, depth), dtype),
+            pltpu.VMEM((2, rows, 128), dtype),
+            space(4, line, 2),
+            space(line, 2),
+            space(line, 2),
+            space(line),
+            space(line),
+            space(line, 2),
+            space(line, 2),
+            sems((2,)),
+            sems((2,)),
+            sems((2, 4, line, 2)),
+            sems((2, line, 2)),
+            sems((2, line, 2)),
+            sems((2, line)),
+            sems((2, line)),
+            sems((2, line, 2)),
+            sems((2, line, 2)),
+        ],
+        compiler_params=pltpu.CompilerParams(
+            collective_id=number, has_side_effects=True, vmem_limit_bytes=60 << 20
+        ),
+        name=name,
+    )(blocks, weights, *([] if extra is None else [extra]))
+    return total.reshape(2 * half, wide)
 
 
 def head_totals(first_sum, second_sum):
@@ -1058,47 +1429,48 @@
     chosen = own_rows(routes[:, 0, :])
     expert_range = jnp.arange(experts, dtype=jnp.int32)
     named = jnp.any(chosen[:, :, None] == expert_range, axis=1)
-    first_expert = lax.axis_index("expert") * local_experts
     top_own = own_rows(d_output[0])
     top_all = lax.all_gather(top_own, ALL, axis=0, tiled=True)
-    xn_all, gate_table = gather_all(
-        second_normed_input.astype(jnp.bfloat16), jnp.where(named, router, 0.0).T, line
-    )
-    gates = lax.dynamic_slice_in_dim(gate_table, first_expert, local_experts, 1)
-    gates = jnp.transpose(gates, (0, 2, 1)).reshape(-1, local_experts)
-
-    gate_pre = jnp.einsum("td,jdf->tjf", xn_all, w_gate, preferred_element_type=jnp.float32)
-    up_pre = jnp.einsum("td,jdf->tjf", xn_all, w_up, preferred_element_type=jnp.float32)
-    top_down = jnp.einsum("td,jfd->tjf", top_all, w_down, preferred_element_type=jnp.float32)
-    sigmoid_gate = jax.nn.sigmoid(gate_pre)
-    silu_gate = gate_pre * sigmoid_gate
-    activated = silu_gate * up_pre
-    scaled = (activated * gates[:, :, None]).astype(jnp.bfloat16)
-    gate_part = jnp.sum(activated * top_down, axis=-1)
-    grad_act = top_down * gates[:, :, None]
-    grad_gate_pre = (
-        grad_act * up_pre * sigmoid_gate * (1.0 + gate_pre * (1.0 - sigmoid_gate))
-    ).astype(jnp.bfloat16)
-    grad_up_pre = (grad_act * silu_gate).astype(jnp.bfloat16)
-    moe_part = jnp.einsum("tjf,jfd->td", scaled, w_down, preferred_element_type=jnp.float32)
-    grad_rows = jnp.einsum("tjf,jdf->td", grad_gate_pre, w_gate, preferred_element_type=jnp.float32)
-    grad_rows = grad_rows + jnp.einsum(
-        "tjf,jdf->td", grad_up_pre, w_up, preferred_element_type=jnp.float32
-    )
-    grad_down = jnp.einsum("tjf,td->jfd", scaled, top_all, preferred_element_type=jnp.float32)
-    grad_gate = jnp.einsum("td,tjf->jdf", xn_all, grad_gate_pre, preferred_element_type=jnp.float32)
-    grad_up = jnp.einsum("td,tjf->jdf", xn_all, grad_up_pre, preferred_element_type=jnp.float32)
+    gate_table = jnp.where(named, router, 0.0)
+    gate_high = gate_table.astype(jnp.bfloat16)
+    gate_low = (gate_table - gate_high.astype(jnp.float32)).astype(jnp.bfloat16)
+    widen = ((0, 0), (0, 64 - experts))
+    own_tokens = jnp.concatenate(
+        [
+            second_normed_input.astype(jnp.bfloat16),
+            jnp.pad(gate_high, widen),
+            jnp.pad(gate_low, widen),
+        ],
+        axis=1,
+    )
+    xn_all, grad_units, scaled, gate_part = gate_act(
+        own_tokens, top_all, w_gate, w_up, w_down, line
+    )
+    token_count = pack_count * pack_span
+    w_both = jnp.concatenate([*w_gate, *w_up], axis=1)
+    grad_tokens = product_sum(grad_units, w_both, True, gate_part, line, "grad_tokens", 4)
+    grad_units = grad_units.reshape(token_count, -1)
+    scaled = scaled.reshape(token_count, -1)
+    units = w_gate.shape[2]
+    moe_part = jnp.dot(
+        scaled, w_down.reshape(-1, model_width), preferred_element_type=jnp.float32
+    )
+    grad_down = contract(scaled, top_all, 0, 0).reshape(w_down.shape)
+    grad_both = [
+        contract(xn_all, grad_units[:, at : at + units], 0, 0)
+        for at in range(0, grad_units.shape[1], units)
+    ]
+    grad_gate = jnp.stack(grad_both[:local_experts])
+    grad_up = jnp.stack(grad_both[local_experts:])
 
     moe_out = lax.psum_scatter(
         moe_part.astype(jnp.bfloat16), ALL, scatter_dimension=0, tiled=True
     ).astype(jnp.float32)
     output = gather_dp((hidden_state + moe_out).astype(jnp.bfloat16))[None]
 
-    gate_columns = jnp.zeros((gate_part.shape[0], experts), jnp.float32)
-    gate_columns = lax.dynamic_update_slice_in_dim(gate_columns, gate_part, first_expert, 1)
-    gate_sums = lax.psum_scatter(gate_columns, ALL, scatter_dimension=0, tiled=True)
+    grad_xn_exp = grad_tokens[:, :model_width]
+    gate_sums = grad_tokens[:, model_width : model_width + experts]
     grad_router_probs = jnp.where(named, gate_sums, 0.0)
-    grad_xn_exp = scatter_all(grad_rows.astype(jnp.bfloat16), line)
     grad_logits = router * (
         grad_router_probs - jnp.sum(router * grad_router_probs, axis=-1, keepdims=True)
     )

time: 929 us -> 883 us (0.950)
  matrix products: 195 us -> 101 us
  Pallas kernels: 567 us -> 606 us
    pallas_call x1 -> x2, Pallas kernels: 79.1 us -> 181 us  [the longest x1 95.8 us: product_sum(): pl.pallas_call(functools.partial(product_sum_kernel, line, flipped, extra...]
    dot_general x9 -> x6, matrix products: 155 us -> 61.7 us  [the longest x5 46.8 us: contract(): lax.dot_general(a, b, (((a_dim,), (b_dim,)), ((), ())), preferred_element...]
    pallas_call x4 -> x3, Pallas kernels: 218 us -> 160 us  [reduce_to(): pl.pallas_call(functools.partial(reduce_kernel, square, line, paired), ou...]
    unnamed x112 -> x123, local copies, waits for them, and re-layouts: 21.9 us -> 14.3 us
  transfers between devices with their start and end apart: 4 -> 3, of which waited for: 0 -> 0; matrix products, arithmetic and copies ran while one was open for 28% -> 22% of each run, Pallas kernels for 54% -> 41%
where the time goes in v4:
time: 883 us; the launch traced here: 876 us
  Pallas kernels  606 us (69%)
  matrix products  101 us (11%)
  other arithmetic  64.8 us (7%)
  local copies, waits for them, and re-layouts  53.4 us (6%)
  blocking collectives  35.8 us (4%)
  between operations  14.9 us (2%)
    pallas_call x3, Pallas kernels, reduce_to(): pl.pallas_call(functools.partial(reduce_kernel, square, line, paired), ou...  160 us
    pallas_call x1, Pallas kernels, product_sum(): pl.pallas_call(functools.partial(product_sum_kernel, line, flipped, extra...  95.8 us
    pallas_call x2, Pallas kernels, to_heads(): pl.pallas_call(functools.partial(to_heads_kernel, line, shared), out_shap...  87.5 us
    pallas_call x1, Pallas kernels, gate_act(): pl.pallas_call(functools.partial(gate_act_kernel, line), out_shape=[jax.S...  85.3 us
    pallas_call x2, Pallas kernels, to_tokens(): pl.pallas_call(functools.partial(to_tokens_kernel, line, summed), out_sha...  83.8 us
    pallas_call x3, Pallas kernels, gather_dp(): pl.pallas_call(gather_square_kernel, out_shape=jax.ShapeDtypeStruct((4, 2...  61.8 us
    dot_general x5, matrix products, contract(): lax.dot_general(a, b, (((a_dim,), (b_dim,)), ((), ())), preferred_element...  46.8 us
    psum x2, blocking collectives, head_totals(): return lax.psum((first_sum, second_sum), 'dp')  20.2 us
  transfers between devices with their start and end apart: 3, of which 0 were waited for; matrix products, arithmetic and copies ran while one was open for 22% of the time, Pallas kernels for 41%

profile of v4, /device:TPU:24, one launch (start us, length us, event | category | flops | bytes accessed | tf_op | source)
XLA Modules:
  0.0 876.3 jit_solution(13248940944760387205)
XLA Ops:
  22.5 10.2 %all-reduce.4 = (f32[1,512]{1,0:T(1,128)S(1)}, f32[1,512]{1,0:T(1,128)S(1)}) all-reduce(f32[1,512]{1,0:T(1,128)S(1)} %bitcast.220, f32[1,512]{1,0:T(1,128)S(1)} %bitcast.221), channel_id=1, replica_groups=mesh['dp'=4,'expert'=8] {'dp'}, use_global_device_ids=true, to_apply=%region_5.6 | all-reduce | flops 1024 | bytes 8192 | tf_op jit(solution)/shard_map/psum | solution.py:1347
  55.4 68.4 %scatter_heads.1 = (bf16[4,512,128]{2,1,0:T(8,128)(2,1)}, bf16[4,2,512,128]{3,2,1,0:T(8,128)(2,1)}, bf16[4,2,512,128]{3,2,1,0:T(8,128)(2,1)}) custom-call(bf16[512,512]{1,0:T(8,128)(2,1)} %bitcast.206, bf16[512,512]{1,0:T(8,128)(2,1)} %bitcast.205, bf16[512,512]{1,0:T(8,128)(2,1)} %convolution_convert_fusion.6.refs_2_), custom_call_target="tpu_custom_call" | custom-call | tf_op jit(solution)/shard_map/scatter_heads/pallas_call | solution.py:492
  124.6 13.7 %attend.1 = (bf16[4,512,128]{2,1,0:T(8,128)(2,1)}, f32[4,1,512]{2,1,0:T(1,128)}) custom-call(s32[3,4]{1,0:T(4,128)} %pad_add_fusion.bounds, bf16[4,512,128]{2,1,0:T(8,128)(2,1)} %get-tuple-element.29.q_ref, bf16[4096,128]{1,0:T(8,128)(2,1)} %bitcast.193, bf16[4096,128]{1,0:T(8,128)(2,1)} %bitcast.195, s32[4,1,512]{2,1,0:T(1,128)} %copy-done.26), custom_call_target="tpu_custom_call" | custom-call | tf_op jit(solution)/shard_map/attend/pallas_call | solution.py:690
  138.3 18.6 %gather_heads.1 = bf16[512,512]{1,0:T(8,128)(2,1)} custom-call(bf16[4,512,128]{2,1,0:T(8,128)(2,1)} %get-tuple-element.32.refs_0_), custom_call_target="tpu_custom_call" | custom-call | tf_op jit(solution)/shard_map/gather_heads/pallas_call | solution.py:593
  161.3 22.3 %scatter_dp.2 = f32[2,64,2048]{2,1,0:T(8,128)} custom-call(bf16[4,1,1,2,64,2048]{5,4,3,2,1,0:T(8,128)(2,1)} %bitcast.209), custom_call_target="tpu_custom_call" | custom-call | tf_op jit(solution)/shard_map/scatter_dp/pallas_call | solution.py:363
  202.2 85.3 %gate_act.1 = (bf16[32,2,64,2048]{3,2,1,0:T(8,128)(2,1)}, bf16[16,256,1024]{2,1,0:T(8,128)(2,1)}, bf16[16,256,512]{2,1,0:T(8,128)(2,1)}, bf16[16,256,128]{2,1,0:T(8,128)(2,1)}) custom-call(bf16[2,64,2176]{2,1,0:T(8,128)(2,1)} %bitcast.198, bf16[16,256,2048]{2,1,0:T(8,128)(2,1)} %bitcast.168, bf16[2,2048,256]{2,1,0:T(8,128)(2,1)} %wg_ref.1, ...), custom_call_target="tpu_custom_call" | custom-call | tf_op jit(solution)/shard_map/gate_act/pallas_call | solution.py:1035
  287.5 95.8 %grad_tokens.1 = f32[2,64,2176]{2,1,0:T(8,128)} custom-call(bf16[16,256,1024]{2,1,0:T(8,128)(2,1)} %get-tuple-element.34.refs_0_, bf16[2048,1024]{1,0:T(8,128)(2,1)} %pad_maximum_fusion.1.refs_1_, bf16[16,256,128]{2,1,0:T(8,128)(2,1)} %get-tuple-element.35.refs_2_), custom_call_target="tpu_custom_call" | custom-call | tf_op jit(solution)/shard_map/grad_tokens/pallas_call | solution.py:1312
  393.5 23.7 %gather_dp.4 = bf16[4,2,64,2048]{3,2,1,0:T(8,128)(2,1)} custom-call(bf16[2,64,2048]{2,1,0:T(8,128)(2,1)} %bitcast.202), custom_call_target="tpu_custom_call" | custom-call | tf_op jit(solution)/shard_map/gather_dp/pallas_call | solution.py:122
  422.0 14.9 %convolution_convert_fusion = bf16[4096,2048]{1,0:T(8,128)(2,1)} fusion(bf16[4096,512]{1,0:T(8,128)(2,1)} %bitcast.190, bf16[512,2048]{1,0:T(8,128)(2,1)} %bitcast.199), kind=kOutput, calls=%fused_computation.2 | convolution fusion | flops 8598323200 | bytes 23068672 | tf_op jit(solution)/shard_map/dot_general | solution.py:1455
  443.8 19.1 %scatter_grads.1.d_ref = bf16[4,512,128]{2,1,0:T(8,128)(2,1)} custom-call(bf16[512,512]{1,0:T(8,128)(2,1)} %convolution_convert_fusion.5.refs_0_), custom_call_target="tpu_custom_call" | custom-call | tf_op jit(solution)/shard_map/scatter_grads/pallas_call | solution.py:492
  465.1 18.4 %attend_back.1 = (bf16[4,512,128]{2,1,0:T(8,128)(2,1)}, bf16[4096,128]{1,0:T(8,128)(2,1)}, bf16[4096,128]{1,0:T(8,128)(2,1)}) custom-call(s32[3,4]{1,0:T(4,128)} %pad_add_fusion.bounds, bf16[4,512,128]{2,1,0:T(8,128)(2,1)} %get-tuple-element.29.q_ref, bf16[4096,128]{1,0:T(8,128)(2,1)} %bitcast.194, bf16[4096,128]{1,0:T(8,128)(2,1)} %bitcast.196, ...), custom_call_target="tpu_custom_call" | custom-call | tf_op jit(solution)/shard_map/attend_back/pallas_call | solution.py:712
  483.5 65.2 %gather_grads.1 = (bf16[512,512]{1,0:T(8,128)(2,1)}, bf16[512,512]{1,0:T(8,128)(2,1)}, bf16[512,512]{1,0:T(8,128)(2,1)}) custom-call(bf16[4,512,128]{2,1,0:T(8,128)(2,1)} %get-tuple-element.37.refs_0_, bf16[4,2,512,128]{3,2,1,0:T(8,128)(2,1)} %bitcast.210, bf16[4,2,512,128]{3,2,1,0:T(8,128)(2,1)} %bitcast.211), custom_call_target="tpu_custom_call" | custom-call | tf_op jit(solution)/shard_map/gather_grads/pallas_call | solution.py:593
  562.9 10.0 %all-reduce.3 = (f32[512]{0:T(512)S(1)}, f32[512]{0:T(512)S(1)}) all-reduce(f32[512]{0:T(512)S(1)} %get-tuple-element.75, f32[512]{0:T(512)S(1)} %get-tuple-element.73), channel_id=1, replica_groups=mesh['dp'=4,'expert'=8] {'dp'}, use_global_device_ids=true, to_apply=%region_17.18 | all-reduce | flops 1024 | bytes 8192 | tf_op jit(solution)/shard_map/psum | solution.py:1347
  582.9 37.4 %scatter_dp.3 = f32[2,64,2048]{2,1,0:T(8,128)} custom-call(bf16[4,1,1,2,64,2048]{5,4,3,2,1,0:T(8,128)(2,1)} %bitcast.183), custom_call_target="tpu_custom_call" | custom-call | tf_op jit(solution)/shard_map/scatter_dp/pallas_call | solution.py:363
  626.1 6.9 convolution_convert_fusion.1
  639.5 100.2 %scatter_expert.1 = f32[2,144,1536]{2,1,0:T(8,128)} custom-call(bf16[1,4,2,2,144,1536]{5,4,3,2,1,0:T(8,128)(2,1)} %bitcast.167), custom_call_target="tpu_custom_call" | custom-call | tf_op jit(solution)/shard_map/scatter_expert/pallas_call | solution.py:363
  740.7 15.6 %psum.39 = bf16[4608]{0:T(1024)(128)(2,1)S(1)} all-reduce(bf16[4608]{0:T(1024)(128)(2,1)S(1)} %slice.167), channel_id=1, replica_groups=mesh['dp'=4,'expert'=8] {'dp'}, use_global_device_ids=true, to_apply=%region_25.26 | all-reduce | flops 4608 | bytes 18432 | tf_op jit(solution)/shard_map/psum | solution.py:1566
  765.8 9.4 %convolution_bitcast_fusion = f32[1,2048,256]{2,1,0:T(8,128)S(1)} fusion(bf16[4096,2048]{1,0:T(8,128)(2,1)} %bitcast.223, bf16[4096,1024]{1,0:T(8,128)(2,1)} %bitcast.177), kind=kOutput, calls=%fused_computation.13 | convolution fusion | flops 4294967296 | bytes 20971520 | tf_op jit(solution)/shard_map/dot_general | solution.py:74
  775.3 8.3 convolution_bitcast_fusion.1
  785.8 8.5 convolution_bitcast_fusion.2
  794.3 9.9 %convolution_bitcast_fusion.3 = f32[1,2048,256]{2,1,0:T(8,128)} fusion(bf16[4096,2048]{1,0:T(8,128)(2,1)} %bitcast.226, bf16[4096,1024]{1,0:T(8,128)(2,1)S(1)} %bitcast.182), kind=kOutput, calls=%fused_computation.16 | convolution fusion | flops 4294967296 | bytes 20971520 | tf_op jit(solution)/shard_map/dot_general | solution.py:74
  808.4 10.7 %fusion = f32[2,256,2048]{2,1,0:T(8,128)} fusion(bf16[2,256,4096]{2,1,0:T(8,128)(2,1)S(1)} %bitcast.192, bf16[1,4096,2048]{2,1,0:T(8,128)(2,1)S(1)} %bitcast.170), kind=kOutput, calls=%fused_computation | convolution fusion | flops 8589934592 | bytes 25165824 | tf_op jit(solution)/shard_map/dot_general | solution.py:74
  823.9 19.0 %gather_dp.5 = bf16[4,2,64,2048]{3,2,1,0:T(8,128)(2,1)} custom-call(bf16[2,64,2048]{2,1,0:T(8,128)(2,1)} %bitcast.201), custom_call_target="tpu_custom_call" | custom-call | tf_op jit(solution)/shard_map/gather_dp/pallas_call | solution.py:122
  847.2 19.1 %gather_dp.3 = bf16[4,2,64,2048]{3,2,1,0:T(8,128)(2,1)} custom-call(bf16[2,64,2048]{2,1,0:T(8,128)(2,1)} %bitcast.200), custom_call_target="tpu_custom_call" | custom-call | tf_op jit(solution)/shard_map/gather_dp/pallas_call | solution.py:122
  (229 shorter events, 150.8 us)
Async XLA Ops:
  7.2 195.0 %all-gather.3.cloned.1.call-start = ((), (), s32[]{:S(2)}) async-start(), calls=%async_computation.4 | async-start | bytes 17301504 | tf_op jit(solution)/shard_map/all_gather | solution.py:1433
  9.3 809.8 %reduce-scatter.5.cloned.1.call-start = ((), (), s32[]{:S(2)}) async-start(), calls=%async_computation.3 | async-start | bytes 2359296 | tf_op jit(solution)/shard_map/reduce_scatter | solution.py:1568
  14.2 36.9 %copy-start.46 = (f32[512]{0:T(512)}, f32[512]{0:T(512)S(1)}, u32[]{:S(2)}) copy-start(f32[512]{0:T(512)S(1)} %add_rsqrt_fusion.2) | copy-start | bytes 6148
  18.2 14.6 %copy-start.4 = (f32[512,512]{1,0:T(8,128)}, f32[512,512]{1,0:T(8,128)S(1)}, u32[]{:S(2)}) copy-start(f32[512,512]{1,0:T(8,128)S(1)} %copy.46) | copy-start | bytes 3145732
  18.2 14.6 %copy-start.37 = (f32[512]{0:T(512)S(1)}, f32[512]{0:T(512)}, u32[]{:S(2)}) copy-start(f32[512]{0:T(512)} %param.22) | copy-start | bytes 6148
  22.5 15.5 %copy-start.35 = (f32[512]{0:T(512)S(1)}, f32[512]{0:T(512)}, u32[]{:S(2)}) copy-start(f32[512]{0:T(512)} %param.23) | copy-start | bytes 6148
  161.3 24.7 %copy-start.23 = (f32[2048,16]{0,1:T(8,128)S(1)}, f32[2048,16]{0,1:T(8,128)}, u32[]{:S(2)}) copy-start(f32[2048,16]{0,1:T(8,128)} %param.25) | copy-start | bytes 393220
  161.3 24.7 %copy-start.24 = (f32[2048]{0:T(1024)S(1)}, f32[2048]{0:T(1024)}, u32[]{:S(2)}) copy-start(f32[2048]{0:T(1024)} %param.24) | copy-start | bytes 24580
  421.6 399.3 %reduce-scatter.3.cloned.1.call-start = ((), (), s32[]{:S(2)}) async-start(), calls=%async_computation.2 | async-start | bytes 17301504 | tf_op jit(solution)/shard_map/reduce_scatter | solution.py:1466
  465.1 88.3 %copy-start.25 = (f32[128,16]{0,1:T(8,128)S(1)}, f32[128,16]{0,1:T(8,128)}, u32[]{:S(2)}) copy-start(f32[128,16]{0,1:T(8,128)} %copy.55) | copy-start | bytes 24580
  465.1 88.3 %copy-start.28 = (pred[128,16]{0,1:T(8,128)(4,1)S(1)}, pred[128,16]{0,1:T(8,128)(4,1)}, u32[]{:S(2)}) copy-start(pred[128,16]{0,1:T(8,128)(4,1)} %copy-done.27) | copy-start | bytes 6148
  465.1 88.3 %copy-start.40 = (f32[128]{0:T(128)S(1)}, f32[128]{0:T(128)}, u32[]{:S(2)}) copy-start(f32[128]{0:T(128)} %copy-done.39) | copy-start | bytes 1540
  465.1 88.3 %copy-start.42 = (f32[128]{0:T(128)S(1)}, f32[128]{0:T(128)}, u32[]{:S(2)}) copy-start(f32[128]{0:T(128)} %copy-done.41) | copy-start | bytes 1540
  465.1 88.3 %copy-start.45 = (f32[128]{0:T(128)S(1)}, f32[128]{0:T(128)}, u32[]{:S(2)}) copy-start(f32[128]{0:T(128)} %copy-done.44) | copy-start | bytes 1540
  465.1 88.3 %copy-start.49 = (f32[128]{0:T(128)S(1)}, f32[128]{0:T(128)}, u32[]{:S(2)}) copy-start(f32[128]{0:T(128)} %copy-done.48) | copy-start | bytes 1540
  580.3 40.0 %copy-start.30 = (f32[2048]{0:T(1024)S(1)}, f32[2048]{0:T(1024)}, u32[]{:S(2)}) copy-start(f32[2048]{0:T(1024)} %param.17) | copy-start | bytes 24580
  582.9 41.9 %copy-start.43 = (bf16[2048]{0:T(1024)(128)(2,1)S(1)}, bf16[2048]{0:T(1024)(128)(2,1)}, u32[]{:S(2)}) copy-start(bf16[2048]{0:T(1024)(128)(2,1)} %get-tuple-element.76) | copy-start | bytes 12292
  785.8 22.5 %slice-start = ((s8[16777216]{0:T(1024)(128)(4,1)}), s8[4194304]{0:T(1024)(128)(4,1)S(1)}, s32[]{:S(2)}) async-start(s8[16777216]{0:T(1024)(128)(4,1)} %bitcast.169), calls=%async_computation.5 | async-start | bytes 8388608
  785.8 22.5 %slice-start.1 = ((s8[16777216]{0:T(1024)(128)(4,1)}), s8[4194304]{0:T(1024)(128)(4,1)S(1)}, s32[]{:S(2)}) async-start(s8[16777216]{0:T(1024)(128)(4,1)} %bitcast.169), calls=%async_computation.6 | async-start | bytes 8388608
  794.3 14.0 %slice-start.2 = ((s8[16777216]{0:T(1024)(128)(4,1)}), s8[4194304]{0:T(1024)(128)(4,1)S(1)}, s32[]{:S(2)}) async-start(s8[16777216]{0:T(1024)(128)(4,1)} %bitcast.169), calls=%async_computation.7 | async-start | bytes 8388608
  794.3 14.0 %slice-start.3 = ((s8[16777216]{0:T(1024)(128)(4,1)}), s8[4194304]{0:T(1024)(128)(4,1)S(1)}, s32[]{:S(2)}) async-start(s8[16777216]{0:T(1024)(128)(4,1)} %bitcast.169), calls=%async_computation.8 | async-start | bytes 8388608
  808.3 12.5 %copy-start.8 = (f32[2,64,2048]{2,1,0:T(8,128)S(1)}, f32[2,64,2048]{2,1,0:T(8,128)}, u32[]{:S(2)}) copy-start(f32[2,64,2048]{2,1,0:T(8,128)} %scatter_dp.3) | copy-start | bytes 3145732
  808.3 12.5 %copy-start.12 = (f32[128,2048]{1,0:T(8,128)S(1)}, f32[128,2048]{1,0:T(8,128)}, u32[]{:S(2)}) copy-start(f32[128,2048]{1,0:T(8,128)} %copy-done.11) | copy-start | bytes 3145732
  842.9 26.6 %copy-start.1 = (bf16[2048,512]{1,0:T(8,128)(2,1)S(1)}, bf16[2048,512]{1,0:T(8,128)(2,1)}, u32[]{:S(2)}) copy-start(bf16[2048,512]{1,0:T(8,128)(2,1)} %param.19) | copy-start | bytes 6291460
  (37 other events, 135.3 us)
Sparse Core Ops, SparseCore 0:
  11.6 140.0 all-gather.2
  421.7 33.9 reduce-scatter.4
  458.0 252.6 reduce-scatter.2

commit v5 on v4

--- a/solution.py
+++ b/solution.py
@@ -129,7 +129,7 @@
             pltpu.SemaphoreType.DMA((4, 2)),
             pltpu.SemaphoreType.DMA((2,)),
         ],
-        compiler_params=pltpu.CompilerParams(collective_id=2, has_side_effects=True),
+        compiler_params=pltpu.CompilerParams(collective_id=10, has_side_effects=True),
         name="gather_dp",
     )(rows.reshape(2, count // 2, width))
     return gathered.reshape(4 * count, width)
@@ -395,10 +395,6 @@
     return reduce_to(rows.reshape(4, -1, rows.shape[1]), True, 1, False, "scatter_dp", 3)
 
 
-def scatter_expert(parts, line):
-    return reduce_to(parts, False, line, True, "scatter_expert", 5)
-
-
 def visit_others(line, z, visit):
     def turn(k, carry):
         visit((z + k) % line)
@@ -1075,11 +1071,14 @@
     line,
     flipped,
     extra,
+    grads,
     *refs,
 ):
     a_ref, w_ref = refs[0], refs[1]
     e_ref = refs[2] if extra else None
     refs = refs[3:] if extra else refs[2:]
+    if grads:
+        work_refs, refs = (*refs[:3], *refs[4:7], *refs[-12:]), (refs[3], *refs[7:-12])
     (
         out_ref,
         made,
@@ -1257,17 +1256,23 @@
             pl.when((height < z) & (z < line - 1))(downwards)
 
     start_load(0)
+    work, work_end, turns = weight_grads(a_ref, *work_refs) if grads else (None, None, 1)
 
     def step(i, carry):
         k, j, _, _ = decode(i)
         pl.when(i < count)(lambda: compute(i))
         pl.when((i >= 1) & (i <= count))(lambda: settle(i - 1))
+        if grads:
+            every = count // turns
+            pl.when((i < count) & (i % every == 0))(lambda: work(i // every))
         late = farthest(line, z, k - 2)
         pl.when((k >= 2) & (j == 0))(lambda: column(late))
         pl.when((k >= 2) & (j == 3))(lambda: pass_on(late))
         return carry
 
     lax.fori_loop(0, count + 8, step, 0)
+    if grads:
+        work_end()
     for p in (0, 1):
         out_ref[p] = made[dp, z, c, p].astype(jnp.float32)
 
@@ -1297,7 +1302,124 @@
     lax.fori_loop(0, line, finish, 0)
 
 
-def product_sum(blocks, weights, flipped, extra, line, name, number):
+def weight_grads(
+    scaled_ref,
+    xn_ref,
+    top_ref,
+    units_ref,
+    gate_ref,
+    up_ref,
+    down_ref,
+    chunk_buf,
+    units_buf,
+    scaled_buf,
+    total,
+    both_out,
+    down_out,
+    chunk_sem,
+    units_sem,
+    scaled_sem,
+    gate_sem,
+    up_sem,
+    down_sem,
+):
+    local, width, units = gate_ref.shape
+    span = chunk_buf.shape[2]
+    blocks, rows, _ = units_buf.shape
+    step_blocks = max(1, min(blocks, 1024 // rows))
+    turns = 2 * (width // span)
+
+    def at(n):
+        return pl.ds(pl.multiple_of(n // 2 * span, span), span)
+
+    def chunk(n, source):
+        return pltpu.make_async_copy(
+            source.at[:, at(n)], chunk_buf.at[n % 2], chunk_sem.at[n % 2]
+        )
+
+    def start_chunk(n):
+        pl.when(n % 2 == 0)(lambda: chunk(n, xn_ref).start())
+        pl.when(n % 2 == 1)(lambda: chunk(n, top_ref).start())
+
+    def both(n, e):
+        gate = pltpu.make_async_copy(
+            both_out.at[:, pl.ds(e * units, units)], gate_ref.at[e, at(n), :], gate_sem.at[e]
+        )
+        up = pltpu.make_async_copy(
+            both_out.at[:, pl.ds((local + e) * units, units)],
+            up_ref.at[e, at(n), :],
+            up_sem.at[e],
+        )
+        return gate, up
+
+    def down(n, e):
+        return pltpu.make_async_copy(down_out.at[e], down_ref.at[e, :, at(n)], down_sem.at[e])
+
+    units_load = pltpu.make_async_copy(units_ref, units_buf, units_sem.at[0])
+    scaled_load = pltpu.make_async_copy(scaled_ref, scaled_buf, scaled_sem.at[0])
+    start_chunk(0)
+    units_load.start()
+    scaled_load.start()
+
+    def add_up(n, right, lanes):
+        total[:, :lanes] = jnp.zeros((span, lanes), jnp.float32)
+
+        def part(k, carry):
+            depth = step_blocks * rows
+            left = chunk_buf[n % 2, pl.ds(pl.multiple_of(k * depth, depth), depth), :]
+            with_rows = right[pl.ds(k * step_blocks, step_blocks)].reshape(depth, lanes)
+            total[:, :lanes] += contract(left, with_rows, 0, 0)
+            return carry
+
+        lax.fori_loop(0, blocks // step_blocks, part, 0)
+
+    def turn(n):
+        pl.when(n + 1 < turns)(lambda: start_chunk(n + 1))
+
+        def even():
+            chunk(n, xn_ref).wait()
+            pl.when(n == 0)(units_load.wait)
+            add_up(n, units_buf, 2 * local * units)
+
+            @pl.when(n > 1)
+            def _():
+                for e in range(local):
+                    for copy in both(n - 2, e):
+                        copy.wait()
+
+            both_out[...] = total[...].astype(both_out.dtype)
+            for e in range(local):
+                for copy in both(n, e):
+                    copy.start()
+
+        def odd():
+            chunk(n, top_ref).wait()
+            pl.when(n == 1)(scaled_load.wait)
+            add_up(n, scaled_buf, local * units)
+
+            @pl.when(n > 2)
+            def _():
+                for e in range(local):
+                    down(n - 2, e).wait()
+
+            for e in range(local):
+                value = total[:, e * units : (e + 1) * units].T
+                down_out[e] = value.astype(down_out.dtype)
+                down(n, e).start()
+
+        pl.when(n % 2 == 0)(even)
+        pl.when(n % 2 == 1)(odd)
+
+    def end():
+        for e in range(local):
+            for copy in both(turns - 2, e):
+                copy.wait()
+            down(turns - 1, e).wait()
+
+    return turn, end, turns
+
+
+def product_sum(blocks, weights, flipped, extra, line, name, number, grads=None):
     count, rows, depth = blocks.shape
     width = weights.shape[0] if flipped else weights.shape[1]
     wide = width + (0 if extra is None else 128)
@@ -1309,11 +1431,35 @@
         return pltpu.VMEM((*shape, half, wide), dtype)
 
     anywhere, inside = pl.BlockSpec(memory_space=pl.ANY), pl.BlockSpec(memory_space=pltpu.VMEM)
-    total = pl.pallas_call(
-        functools.partial(product_sum_kernel, line, flipped, extra is not None),
-        out_shape=jax.ShapeDtypeStruct((2, half, wide), jnp.float32),
-        in_specs=[anywhere, inside] + ([] if extra is None else [anywhere]),
-        out_specs=inside,
+    out_shape = [jax.ShapeDtypeStruct((2, half, wide), jnp.float32)]
+    work_in, work_space = [], []
+    if grads is not None:
+        xn, tops, both, shape = grads
+        local, _, units = shape
+        work_in, span = [xn, tops, both], 256
+        up_down = [shape, shape, (local, units, width)]
+        out_shape += [jax.ShapeDtypeStruct(each, dtype) for each in up_down]
+        work_space = [
+            pltpu.VMEM((2, xn.shape[0], span), dtype),
+            pltpu.VMEM(both.shape, dtype),
+            pltpu.VMEM(blocks.shape, dtype),
+            pltpu.VMEM((span, both.shape[2]), jnp.float32),
+            pltpu.VMEM((span, both.shape[2]), dtype),
+            pltpu.VMEM((local, units, span), dtype),
+            sems((2,)),
+            sems((1,)),
+            sems((1,)),
+            sems((local,)),
+            sems((local,)),
+            sems((local,)),
+        ]
+    total, *work_out = pl.pallas_call(
+        functools.partial(product_sum_kernel, line, flipped, extra is not None, grads is not None),
+        out_shape=out_shape,
+        in_specs=[anywhere, inside]
+        + ([] if extra is None else [anywhere])
+        + [anywhere] * len(work_in),
+        out_specs=[inside] + [anywhere] * (len(out_shape) - 1),
         scratch_shapes=[
             space(4, line, 2, 2),
             pltpu.VMEM((2, rows, depth), dtype),
@@ -1334,13 +1480,323 @@
             sems((2, line)),
             sems((2, line, 2)),
             sems((2, line, 2)),
+            *work_space,
         ],
         compiler_params=pltpu.CompilerParams(
-            collective_id=number, has_side_effects=True, vmem_limit_bytes=60 << 20
+            collective_id=number, has_side_effects=True, vmem_limit_bytes=63 << 20
         ),
         name=name,
-    )(blocks, weights, *([] if extra is None else [extra]))
-    return total.reshape(2 * half, wide)
+    )(blocks, weights, *([] if extra is None else [extra]), *work_in)
+    return total.reshape(2 * half, wide), *work_out
+
+
+def closing_kernel(
+    line,
+    shared_rows,
+    parts_ref,
+    first_ref,
+    grad_ref,
+    unit_ref,
+    inverse_ref,
+    gain_ref,
+    output_ref,
+    summed_ref,
+    shared_ref,
+    outputs_ref,
+    grads_ref,
+    acc,
+    got_pair,
+    got_below,
+    got_above,
+    part,
+    got_x,
+    got_y,
+    got_far_x,
+    got_far_y,
+    grad_own,
+    small,
+    got_small,
+    load_sem,
+    pair_sem,
+    below_sem,
+    above_sem,
+    part_sem,
+    x_sem,
+    y_sem,
+    far_x_sem,
+    far_y_sem,
+    spread_sem,
+    arrive_sem,
+    own_sem,
+    small_sem,
+):
+    dp, place = lax.axis_index("dp"), lax.axis_index("expert")
+    z, c = place // 2, place % 2
+    side_x, side_y = corners(dp)
+    far = 3 - dp
+    to_x, to_y, to_pair = (side_x, place), (side_y, place), (dp, 2 * z + 1 - c)
+    to_up, to_down = (dp, place + 2), (dp, place - 2)
+    for device in (to_x, to_y, to_pair):
+        greet(device)
+    pl.when(z > 0)(lambda: greet(to_down))
+    pl.when(z < line - 1)(lambda: greet(to_up))
+    greeted = 3 + (z > 0).astype(jnp.int32) + (z < line - 1).astype(jnp.int32)
+    pl.semaphore_wait(pltpu.get_barrier_semaphore(), greeted)
+
+    def load(height, p):
+        return pltpu.make_async_copy(
+            parts_ref.at[height, c, p], acc.at[height, p], load_sem.at[height, p]
+        )
+
+    def hand(height, p):
+        at = (height, p)
+        source = parts_ref.at[height, 1 - c, p]
+        return send(source, got_pair.at[at], pair_sem.at[0, *at], pair_sem.at[1, *at], to_pair)
+
+    def climb(height, p):
+        at = (height, p)
+        return send(
+            acc.at[at], got_below.at[at], below_sem.at[0, *at], below_sem.at[1, *at], to_up
+        )
+
+    def descend(height, p):
+        at = (height, p)
+        return send(
+            acc.at[at], got_above.at[at], above_sem.at[0, *at], above_sem.at[1, *at], to_down
+        )
+
+    def start(k, carry):
+        height = farthest(line, z, k)
+        for p in (0, 1):
+            load(height, p).start()
+            hand(height, p).start()
+        return carry
+
+    def pair_sum(k, carry):
+        height = farthest(line, z, k)
+        for p in (0, 1):
+            load(height, p).wait()
+            hand(height, p).wait_recv()
+            acc[height, p] = acc[height, p] + got_pair[height, p]
+            pl.when((z == 0) & (height > z))(lambda: climb(height, p).start())
+            pl.when((z == line - 1) & (height < z))(lambda: descend(height, p).start())
+        return carry
+
+    def pass_on(k, carry):
+        height = farthest(line, z, k)
+        for p in (0, 1):
+
+            def upwards():
+                climb(height, p).wait_recv()
+                acc[height, p] = acc[height, p] + got_below[height, p]
+                climb(height, p).start()
+
+            def downwards():
+                descend(height, p).wait_recv()
+                acc[height, p] = acc[height, p] + got_above[height, p]
+                descend(height, p).start()
+
+            pl.when((height > z) & (z > 0))(upwards)
+            pl.when((height < z) & (z < line - 1))(downwards)
+        return carry
+
+    def first_load(q, p):
+        return pltpu.make_async_copy(first_ref.at[q, p], part.at[q, p], part_sem.at[q, p])
+
+    def along_x(p):
+        return send(part.at[side_x, p], got_x.at[p], x_sem.at[0, p], x_sem.at[1, p], to_x)
+
+    def along_y(p):
+        return send(part.at[side_y, p], got_y.at[p], y_sem.at[0, p], y_sem.at[1, p], to_y)
+
+    def far_x():
+        return send(part.at[far, 0], got_far_x, far_x_sem.at[0], far_x_sem.at[1], to_x)
+
+    def far_y():
+        return send(part.at[far, 1], got_far_y, far_y_sem.at[0], far_y_sem.at[1], to_y)
+
+    spreads = ((output_ref, outputs_ref), (grad_own, grads_ref))
+
+    def spread(a, corner, p, way, source=None):
+        target = spreads[a][1].at[corner, p]
+        return send(
+            target if source is None else source,
+            target,
+            spread_sem.at[a, corner, p, way],
+            arrive_sem.at[a, corner, p],
+            (to_x, to_y)[way],
+        )
+
+    def own_copy(a, p):
+        return pltpu.make_async_copy(
+            spreads[a][0].at[p], spreads[a][1].at[dp, p], own_sem.at[a, p]
+        )
+
+    def spread_own(a, p):
+        own_copy(a, p).start()
+        for way in (0, 1):
+            spread(a, dp, p, way, spreads[a][0].at[p]).start()
+
+    def spread_far(a):
+        spread(a, side_x, 0, 0).wait_recv()
+        spread(a, side_x, 0, 1).start()
+        spread(a, side_y, 1, 0).wait_recv()
+        spread(a, side_y, 1, 0).start()
+
+    lax.fori_loop(0, 1, start, 0)
+    for q in (far, side_x, side_y, dp):
+        for p in (0, 1):
+            first_load(q, p).start()
+    lax.fori_loop(1, line, start, 0)
+    for q in (far, side_x, side_y, dp):
+        for p in (0, 1):
+            first_load(q, p).wait()
+    far_x().start()
+    far_y().start()
+    along_x(0).start()
+    along_y(1).start()
+    lax.fori_loop(0, 1, pair_sum, 0)
+    far_x().wait_recv()
+    part[side_y, 0] = part[side_y, 0] + got_far_x[...]
+    along_y(0).start()
+    far_y().wait_recv()
+    part[side_x, 1] = part[side_x, 1] + got_far_y[...]
+    along_x(1).start()
+    for p in (0, 1):
+        spread_own(0, p)
+    lax.fori_loop(1, line, pair_sum, 0)
+    for p in (0, 1):
+        along_x(p).wait_recv()
+        along_y(p).wait_recv()
+        total = part[dp, p].astype(jnp.float32)
+        total = total + got_x[p].astype(jnp.float32) + got_y[p].astype(jnp.float32)
+        total = total * gain_ref[...]
+        unit = unit_ref[p]
+        mean = jnp.sum(total * unit, axis=1, keepdims=True) * (1.0 / unit.shape[1])
+        rows = grad_ref[p] + inverse_ref[p] * (total - unit * mean)
+        grad_own[p] = rows.astype(grad_own.dtype)
+        spread_own(1, p)
+    lax.fori_loop(0, 1, pass_on, 0)
+    spread_far(0)
+    lax.fori_loop(1, 2, pass_on, 0)
+    spread_far(1)
+    lax.fori_loop(2, line, pass_on, 0)
+    for p in (0, 1):
+        summed_ref[p] = acc[z, p].astype(jnp.float32)
+
+        def from_below():
+            climb(z, p).wait_recv()
+            summed_ref[p] = summed_ref[p] + got_below[z, p].astype(jnp.float32)
+
+        def from_above():
+            descend(z, p).wait_recv()
+            summed_ref[p] = summed_ref[p] + got_above[z, p].astype(jnp.float32)
+
+        pl.when(z > 0)(from_below)
+        pl.when(z < line - 1)(from_above)
+
+    last = summed_ref.shape[1] - shared_rows
+    for side, device in enumerate((to_x, to_y)):
+        value = summed_ref[1, last:, :] if side == 0 else shared_ref[...]
+        small[side] = value.astype(small.dtype)
+        spread(side, side_x, 1, 0).wait_recv()
+        spread(side, side_y, 0, 0).wait_recv()
+        for p in (0, 1):
+            spread(side, far, p, 0).wait_recv()
+            for way in (0, 1):
+                spread(side, dp, p, way).wait_send()
+            own_copy(side, p).wait()
+        spread(side, side_x, 0, 1).wait_send()
+        spread(side, side_y, 1, 0).wait_send()
+        exchange = send(
+            small.at[side], got_small.at[side], small_sem.at[0, side], small_sem.at[1, side], device
+        )
+        exchange.start()
+        exchange.wait_recv()
+        shared_ref[...] = small[side].astype(jnp.float32) + got_small[side].astype(jnp.float32)
+        exchange.wait_send()
+
+    far_x().wait_send()
+    far_y().wait_send()
+    for p in (0, 1):
+        along_x(p).wait_send()
+        along_y(p).wait_send()
+
+    def finish(height, carry):
+        for p in (0, 1):
+            hand(height, p).wait_send()
+            pl.when(height > z)(lambda: climb(height, p).wait_send())
+            pl.when(height < z)(lambda: descend(height, p).wait_send())
+        return carry
+
+    lax.fori_loop(0, line, finish, 0)
+
+
+def closing(parts, first, grad, unit, inverse, gain, output, shared_rows, line):
+    _, rows, wide = parts.shape
+    own, width = output.shape
+    high, half = rows // 2, own // 2
+    sems = pltpu.SemaphoreType.DMA
+    dtype = parts.dtype
+    single = jnp.float32
+    anywhere, inside = pl.BlockSpec(memory_space=pl.ANY), pl.BlockSpec(memory_space=pltpu.VMEM)
+    everyone = jax.ShapeDtypeStruct((4, 2, half, width), dtype)
+    summed, shared, outputs, grads = pl.pallas_call(
+        functools.partial(closing_kernel, line, shared_rows),
+        out_shape=[
+            jax.ShapeDtypeStruct((2, high, wide), single),
+            jax.ShapeDtypeStruct((shared_rows, wide), single),
+            everyone,
+            everyone,
+        ],
+        in_specs=[anywhere, anywhere] + [inside] * 5,
+        out_specs=[inside, inside, anywhere, anywhere],
+        scratch_shapes=[
+            pltpu.VMEM((line, 2, high, wide), dtype),
+            pltpu.VMEM((line, 2, high, wide), dtype),
+            pltpu.VMEM((line, 2, high, wide), dtype),
+            pltpu.VMEM((line, 2, high, wide), dtype),
+            pltpu.VMEM((4, 2, half, width), dtype),
+            pltpu.VMEM((2, half, width), dtype),
+            pltpu.VMEM((2, half, width), dtype),
+            pltpu.VMEM((half, width), dtype),
+            pltpu.VMEM((half, width), dtype),
+            pltpu.VMEM((2, half, width), dtype),
+            pltpu.VMEM((2, shared_rows, wide), dtype),
+            pltpu.VMEM((2, shared_rows, wide), dtype),
+            sems((line, 2)),
+            sems((2, line, 2)),
+            sems((2, line, 2)),
+            sems((2, line, 2)),
+            sems((4, 2)),
+            sems((2, 2)),
+            sems((2, 2)),
+            sems((2,)),
+            sems((2,)),
+            sems((2, 4, 2, 2)),
+            sems((2, 4, 2)),
+            sems((2, 2)),
+            sems((2, 2)),
+        ],
+        compiler_params=pltpu.CompilerParams(
+            collective_id=5, has_side_effects=True, vmem_limit_bytes=60 << 20
+        ),
+        name="closing",
+    )(
+        parts.reshape(line, 2, 2, high, wide),
+        first.reshape(4, 2, half, width),
+        grad.reshape(2, half, width),
+        unit.reshape(2, half, width),
+        inverse.reshape(2, half, 1),
+        gain.reshape(1, width),
+        output.reshape(2, half, width),
+    )
+    return (
+        summed.reshape(rows, wide),
+        shared,
+        outputs.reshape(4 * own, width),
+        grads.reshape(4 * own, width),
+    )
 
 
 def head_totals(first_sum, second_sum):
@@ -1446,28 +1902,19 @@
     xn_all, grad_units, scaled, gate_part = gate_act(
         own_tokens, top_all, w_gate, w_up, w_down, line
     )
-    token_count = pack_count * pack_span
     w_both = jnp.concatenate([*w_gate, *w_up], axis=1)
-    grad_tokens = product_sum(grad_units, w_both, True, gate_part, line, "grad_tokens", 4)
-    grad_units = grad_units.reshape(token_count, -1)
-    scaled = scaled.reshape(token_count, -1)
-    units = w_gate.shape[2]
-    moe_part = jnp.dot(
-        scaled, w_down.reshape(-1, model_width), preferred_element_type=jnp.float32
-    )
-    grad_down = contract(scaled, top_all, 0, 0).reshape(w_down.shape)
-    grad_both = [
-        contract(xn_all, grad_units[:, at : at + units], 0, 0)
-        for at in range(0, grad_units.shape[1], units)
-    ]
-    grad_gate = jnp.stack(grad_both[:local_experts])
-    grad_up = jnp.stack(grad_both[local_experts:])
-
-    moe_out = lax.psum_scatter(
-        moe_part.astype(jnp.bfloat16), ALL, scatter_dimension=0, tiled=True
-    ).astype(jnp.float32)
-    output = gather_dp((hidden_state + moe_out).astype(jnp.bfloat16))[None]
-
+    (grad_tokens,) = product_sum(grad_units, w_both, True, gate_part, line, "grad_tokens", 4)
+    moe_out, grad_gate, grad_up, grad_down = product_sum(
+        scaled,
+        w_down.reshape(-1, model_width),
+        False,
+        None,
+        line,
+        "expert_sum",
+        2,
+        (xn_all, top_all, grad_units, w_gate.shape),
+    )
+    output = (hidden_state + moe_out).astype(jnp.bfloat16)
     grad_xn_exp = grad_tokens[:, :model_width]
     gate_sums = grad_tokens[:, model_width : model_width + experts]
     grad_router_probs = jnp.where(named, gate_sums, 0.0)
@@ -1528,15 +1975,7 @@
     grad_first_normed_input = grad_first_normed_input + jnp.einsum(
         "psk,dk->psd", grad_v_raw, w_value, preferred_element_type=jnp.float32
     )
-    grad_first = scatter_dp(grad_first_normed_input[0].astype(jnp.bfloat16))
-    unit_own = own_rows(first_unit_input[0])
-    grad_attn_gain = jnp.sum(grad_first * unit_own, axis=0)
-    grad_first = grad_first * attention_norm_gain
-    grad_input = grad_hidden + own_rows(first_inverse_norm[0]) * (
-        grad_first - unit_own * jnp.mean(grad_first * unit_own, axis=-1, keepdims=True)
-    )
-    grad_input = gather_dp(grad_input.astype(jnp.bfloat16)).astype(jnp.float32)[None]
-
+    grad_attn_gain = jnp.sum(grad_first_normed_input[0] * first_unit_input[0], axis=0)
     wide = grad_projections.shape[1]
     small = jnp.concatenate(
         [
@@ -1558,19 +1997,27 @@
         ],
         axis=1,
     )
-    summed = scatter_expert(parts, line)
+    summed, shared, outputs, grad_input = closing(
+        parts,
+        grad_first_normed_input[0].astype(jnp.bfloat16),
+        grad_hidden,
+        own_rows(first_unit_input[0]),
+        own_rows(first_inverse_norm[0]),
+        attention_norm_gain,
+        output,
+        small_rows,
+        line,
+    )
     large_rows = summed.shape[0] - small_rows
-    small = summed[large_rows:].reshape(-1)
     gain_size, norm_size = local_width // groups, model_width // groups
-    own_gains = small[: 2 * gain_size]
-    shared = lax.psum(small[2 * gain_size : filled].astype(jnp.bfloat16), "dp")
-    shared = shared.astype(jnp.float32)
+    own_gains = summed[large_rows:].reshape(-1)[: 2 * gain_size]
+    shared = shared.reshape(-1)[2 * gain_size : filled]
     grad_out = lax.psum_scatter(
         grad_out.astype(jnp.bfloat16), "expert", scatter_dimension=0, tiled=True
     ).astype(jnp.float32)
     return (
-        output,
-        grad_input,
+        outputs[None],
+        grad_input.astype(jnp.float32)[None],
         shared[:norm_size],
         summed[:large_rows, :local_width],
         summed[:large_rows, local_width : 2 * local_width],
@@ -1580,9 +2027,9 @@
         own_gains[gain_size:],
         shared[norm_size : 2 * norm_size],
         shared[2 * norm_size :].reshape(norm_size, experts),
-        grad_gate,
-        grad_up,
-        grad_down,
+        grad_gate.astype(jnp.float32),
+        grad_up.astype(jnp.float32),
+        grad_down.astype(jnp.float32),
     )
 
 

time: 883 us -> 755 us (0.86)
  matrix products: 101 us -> 41.2 us
  Pallas kernels: 606 us -> 579 us
  blocking collectives: 35.8 us -> 19.2 us
  local copies, waits for them, and re-layouts: 53.4 us -> 38.8 us
  other arithmetic: 64.8 us -> 54.7 us
    pallas_call x3 -> x1, Pallas kernels: 160 us -> 22.2 us  [reduce_to(): pl.pallas_call(functools.partial(reduce_kernel, square, line, paired), ou...]
    pallas_call x1 -> x2, Pallas kernels: 95.8 us -> 196 us  [product_sum(): pl.pallas_call(functools.partial(product_sum_kernel, line, flipped, extra...]
    pallas_call x0 -> x1, Pallas kernels: none -> 77.3 us  [closing(): pl.pallas_call(functools.partial(closing_kernel, line, shared_rows), out_...]
    dot_general x6 -> x0, matrix products: 61.7 us -> none  [the longest x5 46.8 us: contract(): lax.dot_general(a, b, (((a_dim,), (b_dim,)), ((), ())), preferred_element...]
    pallas_call x3 -> x1, Pallas kernels: 61.8 us -> 23.4 us  [gather_dp(): pl.pallas_call(gather_square_kernel, out_shape=jax.ShapeDtypeStruct((4, 2...]
    pallas_call x2, Pallas kernels: 83.8 us -> 58.5 us  [to_tokens(): pl.pallas_call(functools.partial(to_tokens_kernel, line, summed), out_sha...]
    psum x1 -> x0, blocking collectives: 15.6 us -> none  [per_device(): shared = lax.psum(small[2 * gain_size:filled].astype(jnp.bfloat16), 'dp')]
  transfers between devices with their start and end apart: 3 -> 2, of which waited for: 0 -> 0; matrix products, arithmetic and copies ran while one was open for 22% -> 13% of each run, Pallas kernels for 41% -> 40%
where the time goes in v5:
time: 755 us; the launch traced here: 748 us
  Pallas kernels  579 us (77%)
  other arithmetic  54.7 us (7%)
  matrix products  41.2 us (5%)
  local copies, waits for them, and re-layouts  38.8 us (5%)
  blocking collectives  19.2 us (3%)
  between operations  14.9 us (2%)
    pallas_call x2, Pallas kernels, product_sum(): pl.pallas_call(functools.partial(product_sum_kernel, line, flipped, extra...  196 us
    pallas_call x1, Pallas kernels, gate_act(): pl.pallas_call(functools.partial(gate_act_kernel, line), out_shape=[jax.S...  85.9 us
    pallas_call x2, Pallas kernels, to_heads(): pl.pallas_call(functools.partial(to_heads_kernel, line, shared), out_shap...  83.4 us
    pallas_call x1, Pallas kernels, closing(): pl.pallas_call(functools.partial(closing_kernel, line, shared_rows), out_...  77.3 us
    pallas_call x2, Pallas kernels, to_tokens(): pl.pallas_call(functools.partial(to_tokens_kernel, line, summed), out_sha...  58.5 us
    pallas_call x1, Pallas kernels, gather_dp(): pl.pallas_call(gather_square_kernel, out_shape=jax.ShapeDtypeStruct((4, 2...  23.4 us
    pallas_call x1, Pallas kernels, reduce_to(): pl.pallas_call(functools.partial(reduce_kernel, square, line, paired), ou...  22.2 us
    psum x2, blocking collectives, head_totals(): return lax.psum((first_sum, second_sum), 'dp')  19.2 us
  transfers between devices with their start and end apart: 2, of which 0 were waited for; matrix products, arithmetic and copies ran while one was open for 13% of the time, Pallas kernels for 40%

profile of v5, /device:TPU:24, one launch (start us, length us, event | category | flops | bytes accessed | tf_op | source)
XLA Modules:
  0.0 748.1 jit_solution(9585862456792412385)
XLA Ops:
  9.2 4.3 convert_element_type.126
  19.1 4.4 multiply_reduce_fusion.7
  23.6 10.1 %all-reduce.4 = (f32[1,512]{1,0:T(1,128)S(1)}, f32[1,512]{1,0:T(1,128)S(1)}) all-reduce(f32[1,512]{1,0:T(1,128)S(1)} %bitcast.173, f32[1,512]{1,0:T(1,128)S(1)} %bitcast.174), channel_id=1, replica_groups=mesh['dp'=4,'expert'=8] {'dp'}, use_global_device_ids=true, to_apply=%region_2.3 | all-reduce | flops 1024 | bytes 8192 | tf_op jit(solution)/shard_map/psum | solution.py:1803
  45.0 3.9 subtract_convert_fusion
  52.1 3.7 convolution_convert_fusion.5.refs_2_
  55.8 68.3 %scatter_heads.1 = (bf16[4,512,128]{2,1,0:T(8,128)(2,1)}, bf16[4,2,512,128]{3,2,1,0:T(8,128)(2,1)}, bf16[4,2,512,128]{3,2,1,0:T(8,128)(2,1)}) custom-call(bf16[512,512]{1,0:T(8,128)(2,1)} %bitcast.152, bf16[512,512]{1,0:T(8,128)(2,1)} %bitcast.151, bf16[512,512]{1,0:T(8,128)(2,1)} %convolution_convert_fusion.5.refs_2_), custom_call_target="tpu_custom_call" | custom-call | tf_op jit(solution)/shard_map/scatter_heads/pallas_call | solution.py:488
  125.0 13.8 %attend.1 = (bf16[4,512,128]{2,1,0:T(8,128)(2,1)}, f32[4,1,512]{2,1,0:T(1,128)}) custom-call(s32[3,4]{1,0:T(4,128)} %pad_add_fusion.bounds, bf16[4,512,128]{2,1,0:T(8,128)(2,1)} %get-tuple-element.37.q_ref, bf16[4096,128]{1,0:T(8,128)(2,1)} %bitcast.141, bf16[4096,128]{1,0:T(8,128)(2,1)} %bitcast.143, s32[4,1,512]{2,1,0:T(1,128)} %copy-done.35), custom_call_target="tpu_custom_call" | custom-call | tf_op jit(solution)/shard_map/attend/pallas_call | solution.py:686
  138.7 18.2 %gather_heads.1 = bf16[512,512]{1,0:T(8,128)(2,1)} custom-call(bf16[4,512,128]{2,1,0:T(8,128)(2,1)} %get-tuple-element.41.refs_0_), custom_call_target="tpu_custom_call" | custom-call | tf_op jit(solution)/shard_map/gather_heads/pallas_call | solution.py:589
  156.9 4.3 convolution_convert_fusion.2
  161.3 22.2 %scatter_dp.1 = f32[2,64,2048]{2,1,0:T(8,128)} custom-call(bf16[4,1,1,2,64,2048]{5,4,3,2,1,0:T(8,128)(2,1)} %bitcast.155), custom_call_target="tpu_custom_call" | custom-call | tf_op jit(solution)/shard_map/scatter_dp/pallas_call | solution.py:363
  197.4 85.9 %gate_act.1 = (bf16[32,2,64,2048]{3,2,1,0:T(8,128)(2,1)}, bf16[16,256,1024]{2,1,0:T(8,128)(2,1)}, bf16[16,256,512]{2,1,0:T(8,128)(2,1)}, bf16[16,256,128]{2,1,0:T(8,128)(2,1)}) custom-call(bf16[2,64,2176]{2,1,0:T(8,128)(2,1)} %bitcast.146, bf16[16,256,2048]{2,1,0:T(8,128)(2,1)} %bitcast.127, bf16[2,2048,256]{2,1,0:T(8,128)(2,1)} %wg_ref.1, ...), custom_call_target="tpu_custom_call" | custom-call | tf_op jit(solution)/shard_map/gate_act/pallas_call | solution.py:1031
  283.3 95.8 %grad_tokens.1 = f32[2,64,2176]{2,1,0:T(8,128)} custom-call(bf16[16,256,1024]{2,1,0:T(8,128)(2,1)} %get-tuple-element.42.refs_0_.refs_4_, bf16[2048,1024]{1,0:T(8,128)(2,1)} %pad_maximum_fusion.1.refs_1_, bf16[16,256,128]{2,1,0:T(8,128)(2,1)} %get-tuple-element.43.refs_2_), custom_call_target="tpu_custom_call" | custom-call | tf_op jit(solution)/shard_map/grad_tokens/pallas_call | solution.py:1456
  380.2 2.9 multiply_reduce_fusion.1
  385.7 23.4 %gather_dp.1 = bf16[4,2,64,2048]{3,2,1,0:T(8,128)(2,1)} custom-call(bf16[2,64,2048]{2,1,0:T(8,128)(2,1)} %bitcast.148), custom_call_target="tpu_custom_call" | custom-call | tf_op jit(solution)/shard_map/gather_dp/pallas_call | solution.py:122
  409.2 4.5 convolution_convert_fusion.4.refs_0_
  416.2 15.1 %scatter_grads.1.d_ref = bf16[4,512,128]{2,1,0:T(8,128)(2,1)} custom-call(bf16[512,512]{1,0:T(8,128)(2,1)} %convolution_convert_fusion.4.refs_0_), custom_call_target="tpu_custom_call" | custom-call | tf_op jit(solution)/shard_map/scatter_grads/pallas_call | solution.py:488
  433.5 18.3 %attend_back.1 = (bf16[4,512,128]{2,1,0:T(8,128)(2,1)}, bf16[4096,128]{1,0:T(8,128)(2,1)}, bf16[4096,128]{1,0:T(8,128)(2,1)}) custom-call(s32[3,4]{1,0:T(4,128)} %pad_add_fusion.bounds, bf16[4,512,128]{2,1,0:T(8,128)(2,1)} %get-tuple-element.37.q_ref, bf16[4096,128]{1,0:T(8,128)(2,1)} %bitcast.142, bf16[4096,128]{1,0:T(8,128)(2,1)} %bitcast.144, ...), custom_call_target="tpu_custom_call" | custom-call | tf_op jit(solution)/shard_map/attend_back/pallas_call | solution.py:708
  451.8 40.3 %gather_grads.1 = (bf16[512,512]{1,0:T(8,128)(2,1)}, bf16[512,512]{1,0:T(8,128)(2,1)}, bf16[512,512]{1,0:T(8,128)(2,1)}) custom-call(bf16[4,512,128]{2,1,0:T(8,128)(2,1)} %get-tuple-element.44.refs_0_, bf16[4,2,512,128]{3,2,1,0:T(8,128)(2,1)} %bitcast.162, bf16[4,2,512,128]{3,2,1,0:T(8,128)(2,1)} %bitcast.163), custom_call_target="tpu_custom_call" | custom-call | tf_op jit(solution)/shard_map/gather_grads/pallas_call | solution.py:589
  501.0 9.1 %all-reduce.3 = (f32[512]{0:T(512)S(1)}, f32[512]{0:T(512)S(1)}) all-reduce(f32[512]{0:T(512)S(1)} %get-tuple-element.104, f32[512]{0:T(512)S(1)} %get-tuple-element.102), channel_id=1, replica_groups=mesh['dp'=4,'expert'=8] {'dp'}, use_global_device_ids=true, to_apply=%region_16.17 | all-reduce | flops 1024 | bytes 8192 | tf_op jit(solution)/shard_map/psum | solution.py:1803
  525.3 100.5 %expert_sum.1 = (f32[2,64,2048]{2,1,0:T(8,128)}, bf16[2,2048,256]{2,1,0:T(8,128)(2,1)}, bf16[2,2048,256]{2,1,0:T(8,128)(2,1)}, bf16[2,256,2048]{2,1,0:T(8,128)(2,1)}) custom-call(bf16[16,256,512]{2,1,0:T(8,128)(2,1)} %get-tuple-element.50.refs_0_, bf16[512,2048]{1,0:T(8,128)(2,1)} %bitcast.135, bf16[4096,2048]{1,0:T(8,128)(2,1)} %bitcast.130, ...), custom_call_target="tpu_custom_call" | custom-call | tf_op jit(solution)/shard_map/expert_sum/pallas_call | solution.py:1456
  625.8 8.1 %convolution_convert_fusion = bf16[2048,1536]{1,0:T(8,128)(2,1)} fusion(bf16[512,512]{1,0:T(8,128)(2,1)} %get-tuple-element.49, bf16[512,512]{1,0:T(8,128)(2,1)S(1)} %copy-done.18, bf16[512,512]{1,0:T(8,128)(2,1)} %copy-done.19, f32[2048]{0:T(1024)S(1)} %copy-done.38, f32[512]{0:T(512)S(1)} %add_rsqrt_fusion.2, bf16[1,512,2048]{2,1,0:T(8,128)(2,1)} %param.16), kind=kOutput, calls=%fused_computation | convolution fusion | flops 3233284096 | bytes 9971712 | tf_op jit(solution)/shard_map/sd,sk->dk/dot_general | solution.py:1966
  634.0 6.5 pad_maximum_fusion
  641.5 77.3 %closing.1 = (f32[2,144,1536]{2,1,0:T(8,128)}, f32[32,1536]{1,0:T(8,128)}, bf16[4,2,64,2048]{3,2,1,0:T(8,128)(2,1)}, bf16[4,2,64,2048]{3,2,1,0:T(8,128)(2,1)}) custom-call(bf16[4,2,2,144,1536]{4,3,2,1,0:T(8,128)(2,1)} %bitcast.129, bf16[4,2,64,2048]{3,2,1,0:T(8,128)(2,1)} %bitcast.136, f32[2,64,2048]{2,1,0:T(8,128)} %bitcast.139, f32[2,64,2048]{2,1,0:T(8,128)} %bitcast.140, ...), custom_call_target="tpu_custom_call" | custom-call | tf_op jit(solution)/shard_map/closing/pallas_call | solution.py:1744
  722.4 4.3 convert.47
  (177 shorter events, 88.0 us)
Async XLA Ops:
  7.2 179.0 %copy-start = (f32[2048,16]{0,1:T(8,128)S(1)}, f32[2048,16]{0,1:T(8,128)}, u32[]{:S(2)}) copy-start(f32[2048,16]{0,1:T(8,128)} %param.25) | copy-start | bytes 393220
  7.2 190.2 %all-gather.3.cloned.1.call-start = ((), (), s32[]{:S(2)}) async-start(), calls=%async_computation.2 | async-start | bytes 17301504 | tf_op jit(solution)/shard_map/all_gather | solution.py:1889
  9.2 728.7 %reduce-scatter.2.cloned.1.call-start = ((), (), s32[]{:S(2)}) async-start(), calls=%async_computation.1 | async-start | bytes 2359296 | tf_op jit(solution)/shard_map/reduce_scatter | solution.py:2015
  9.2 4.3 copy-start.4
  9.2 4.9 copy-start.38
  19.1 14.6 %copy-start.6 = (f32[512,512]{1,0:T(8,128)}, f32[512,512]{1,0:T(8,128)S(1)}, u32[]{:S(2)}) copy-start(f32[512,512]{1,0:T(8,128)S(1)} %copy.52) | copy-start | bytes 3145732
  19.1 14.6 %copy-start.37 = (f32[512]{0:T(512)S(1)}, f32[512]{0:T(512)}, u32[]{:S(2)}) copy-start(f32[512]{0:T(512)} %param.22) | copy-start | bytes 6148
  34.8 4.1 copy-start.36
  38.9 3.8 copy-start.8
  38.9 3.8 copy-start.39
  45.0 3.9 copy-start.20
  186.2 6.0 copy-start.2
  379.1 4.1 copy-start.3
  409.1 4.5 copy-start.24
  409.1 4.5 copy-start.33
  512.4 2.8 copy-start.12
  525.3 100.6 %copy-start.18 = (bf16[512,512]{1,0:T(8,128)(2,1)S(1)}, bf16[512,512]{1,0:T(8,128)(2,1)}, u32[]{:S(2)}) copy-start(bf16[512,512]{1,0:T(8,128)(2,1)} %multiply_convert_fusion.1) | copy-start | bytes 1572868
  634.0 6.6 copy-start.10
  634.0 6.6 copy-start.16
  634.0 6.6 copy-start.31
  722.3 4.3 slice-start
  722.4 5.9 copy-start.23
  733.0 3.7 copy-start.30
  735.6 4.1 copy-start.25
  (19 other events, 32.8 us)
Sparse Core Ops, SparseCore 0:
  11.6 138.8 all-gather.2
  512.6 32.0 reduce-scatter.1

commit v6 on v5

--- a/solution.py
+++ b/solution.py
@@ -1067,6 +1067,119 @@
     return xn.reshape(slots * count, width), grads, scaled, gates
 
 
+def column_products(left_ref, right_ref, chunk_buf, right_buf, total, chunk_sem, right_sem, store):
+    span = chunk_buf.shape[2]
+    blocks, rows, _ = right_buf.shape
+    joined = max(1, min(blocks, 1024 // rows))
+    depth = joined * rows
+    turns = left_ref.shape[1] // span
+
+    def at(n):
+        return pl.ds(pl.multiple_of(n * span, span), span)
+
+    def chunk(n):
+        return pltpu.make_async_copy(
+            left_ref.at[:, at(n)], chunk_buf.at[n % 2], chunk_sem.at[n % 2]
+        )
+
+    right_load = pltpu.make_async_copy(right_ref, right_buf, right_sem.at[0])
+    chunk(0).start()
+    right_load.start()
+
+    def turn(n):
+        pl.when(n + 1 < turns)(lambda: chunk(n + 1).start())
+        chunk(n).wait()
+        pl.when(n == 0)(right_load.wait)
+        total[...] = jnp.zeros_like(total)
+
+        def part(k, carry):
+            left = chunk_buf[n % 2, pl.ds(pl.multiple_of(k * depth, depth), depth), :]
+            right = right_buf[pl.ds(k * joined, joined)].reshape(depth, right_buf.shape[2])
+            total[...] += contract(left, right, 0, 0)
+            return carry
+
+        lax.fori_loop(0, blocks // joined, part, 0)
+        store(n, at(n))
+
+    return turn, turns
+
+
+def gate_up_grads(
+    xn_ref, units_ref, gate_ref, up_ref, chunk_buf, units_buf, total, both, chunk_sem, units_sem, out_sem
+):
+    local, _, units = gate_ref.shape
+    outs = (gate_ref, up_ref)
+
+    def copies(at):
+        return [
+            pltpu.make_async_copy(
+                both.at[:, pl.ds((kind * local + e) * units, units)],
+                outs[kind].at[e, at, :],
+                out_sem.at[kind, e],
+            )
+            for kind in (0, 1)
+            for e in range(local)
+        ]
+
+    start = pl.ds(0, chunk_buf.shape[2])
+
+    def store(n, at):
+        @pl.when(n > 0)
+        def _():
+            for copy in copies(start):
+                copy.wait()
+
+        both[...] = total[...].astype(both.dtype)
+        for copy in copies(at):
+            copy.start()
+
+    def end():
+        for copy in copies(start):
+            copy.wait()
+
+    turn, turns = column_products(
+        xn_ref, units_ref, chunk_buf, units_buf, total, chunk_sem, units_sem, store
+    )
+    return turn, end, turns
+
+
+def down_grads(
+    top_ref, scaled_ref, down_ref, chunk_buf, scaled_buf, total, out, chunk_sem, scaled_sem, out_sem
+):
+    local, units, _ = down_ref.shape
+
+    def copies(at):
+        return [
+            pltpu.make_async_copy(out.at[e], down_ref.at[e, :, at], out_sem.at[e])
+            for e in range(local)
+        ]
+
+    start = pl.ds(0, chunk_buf.shape[2])
+
+    def store(n, at):
+        @pl.when(n > 0)
+        def _():
+            for copy in copies(start):
+                copy.wait()
+
+        for e in range(local):
+            out[e] = total[:, e * units : (e + 1) * units].T.astype(out.dtype)
+        for copy in copies(at):
+            copy.start()
+
+    def end():
+        for copy in copies(start):
+            copy.wait()
+
+    turn, turns = column_products(
+        top_ref, scaled_ref, chunk_buf, scaled_buf, total, chunk_sem, scaled_sem, store
+    )
+    return turn, end, turns
+
+
+SPAN = 256
+
+
 def product_sum_kernel(
     line,
     flipped,
@@ -1078,7 +1191,7 @@
     e_ref = refs[2] if extra else None
     refs = refs[3:] if extra else refs[2:]
     if grads:
-        work_refs, refs = (*refs[:3], *refs[4:7], *refs[-12:]), (refs[3], *refs[7:-12])
+        work_refs, refs = (*refs[:2], *refs[3:5], *refs[-7:]), (refs[2], *refs[5:-7])
     (
         out_ref,
         made,
@@ -1256,7 +1369,7 @@
             pl.when((height < z) & (z < line - 1))(downwards)
 
     start_load(0)
-    work, work_end, turns = weight_grads(a_ref, *work_refs) if grads else (None, None, 1)
+    work, work_end, turns = gate_up_grads(*work_refs) if grads else (None, None, 1)
 
     def step(i, carry):
         k, j, _, _ = decode(i)
@@ -1302,123 +1415,6 @@
     lax.fori_loop(0, line, finish, 0)
 
 
-def weight_grads(
-    scaled_ref,
-    xn_ref,
-    top_ref,
-    units_ref,
-    gate_ref,
-    up_ref,
-    down_ref,
-    chunk_buf,
-    units_buf,
-    scaled_buf,
-    total,
-    both_out,
-    down_out,
-    chunk_sem,
-    units_sem,
-    scaled_sem,
-    gate_sem,
-    up_sem,
-    down_sem,
-):
-    local, width, units = gate_ref.shape
-    span = chunk_buf.shape[2]
-    blocks, rows, _ = units_buf.shape
-    step_blocks = max(1, min(blocks, 1024 // rows))
-    turns = 2 * (width // span)
-
-    def at(n):
-        return pl.ds(pl.multiple_of(n // 2 * span, span), span)
-
-    def chunk(n, source):
-        return pltpu.make_async_copy(
-            source.at[:, at(n)], chunk_buf.at[n % 2], chunk_sem.at[n % 2]
-        )
-
-    def start_chunk(n):
-        pl.when(n % 2 == 0)(lambda: chunk(n, xn_ref).start())
-        pl.when(n % 2 == 1)(lambda: chunk(n, top_ref).start())
-
-    def both(n, e):
-        gate = pltpu.make_async_copy(
-            both_out.at[:, pl.ds(e * units, units)], gate_ref.at[e, at(n), :], gate_sem.at[e]
-        )
-        up = pltpu.make_async_copy(
-            both_out.at[:, pl.ds((local + e) * units, units)],
-            up_ref.at[e, at(n), :],
-            up_sem.at[e],
-        )
-        return gate, up
-
-    def down(n, e):
-        return pltpu.make_async_copy(down_out.at[e], down_ref.at[e, :, at(n)], down_sem.at[e])
-
-    units_load = pltpu.make_async_copy(units_ref, units_buf, units_sem.at[0])
-    scaled_load = pltpu.make_async_copy(scaled_ref, scaled_buf, scaled_sem.at[0])
-    start_chunk(0)
-    units_load.start()
-    scaled_load.start()
-
-    def add_up(n, right, lanes):
-        total[:, :lanes] = jnp.zeros((span, lanes), jnp.float32)
-
-        def part(k, carry):
-            depth = step_blocks * rows
-            left = chunk_buf[n % 2, pl.ds(pl.multiple_of(k * depth, depth), depth), :]
-            with_rows = right[pl.ds(k * step_blocks, step_blocks)].reshape(depth, lanes)
-            total[:, :lanes] += contract(left, with_rows, 0, 0)
-            return carry
-
-        lax.fori_loop(0, blocks // step_blocks, part, 0)
-
-    def turn(n):
-        pl.when(n + 1 < turns)(lambda: start_chunk(n + 1))
-
-        def even():
-            chunk(n, xn_ref).wait()
-            pl.when(n == 0)(units_load.wait)
-            add_up(n, units_buf, 2 * local * units)
-
-            @pl.when(n > 1)
-            def _():
-                for e in range(local):
-                    for copy in both(n - 2, e):
-                        copy.wait()
-
-            both_out[...] = total[...].astype(both_out.dtype)
-            for e in range(local):
-                for copy in both(n, e):
-                    copy.start()
-
-        def odd():
-            chunk(n, top_ref).wait()
-            pl.when(n == 1)(scaled_load.wait)
-            add_up(n, scaled_buf, local * units)
-
-            @pl.when(n > 2)
-            def _():
-                for e in range(local):
-                    down(n - 2, e).wait()
-
-            for e in range(local):
-                value = total[:, e * units : (e + 1) * units].T
-                down_out[e] = value.astype(down_out.dtype)
-                down(n, e).start()
-
-        pl.when(n % 2 == 0)(even)
-        pl.when(n % 2 == 1)(odd)
-
-    def end():
-        for e in range(local):
-            for copy in both(turns - 2, e):
-                copy.wait()
-            down(turns - 1, e).wait()
-
-    return turn, end, turns
-
-
 def product_sum(blocks, weights, flipped, extra, line, name, number, grads=None):
     count, rows, depth = blocks.shape
     width = weights.shape[0] if flipped else weights.shape[1]
@@ -1434,24 +1430,17 @@
     out_shape = [jax.ShapeDtypeStruct((2, half, wide), jnp.float32)]
     work_in, work_space = [], []
     if grads is not None:
-        xn, tops, both, shape = grads
-        local, _, units = shape
-        work_in, span = [xn, tops, both], 256
-        up_down = [shape, shape, (local, units, width)]
-        out_shape += [jax.ShapeDtypeStruct(each, dtype) for each in up_down]
+        xn, both, shape = grads
+        work_in = [xn, both]
+        out_shape += [jax.ShapeDtypeStruct(shape, dtype)] * 2
         work_space = [
-            pltpu.VMEM((2, xn.shape[0], span), dtype),
+            pltpu.VMEM((2, xn.shape[0], SPAN), dtype),
             pltpu.VMEM(both.shape, dtype),
-            pltpu.VMEM(blocks.shape, dtype),
-            pltpu.VMEM((span, both.shape[2]), jnp.float32),
-            pltpu.VMEM((span, both.shape[2]), dtype),
-            pltpu.VMEM((local, units, span), dtype),
+            pltpu.VMEM((SPAN, both.shape[2]), jnp.float32),
+            pltpu.VMEM((SPAN, both.shape[2]), dtype),
             sems((2,)),
             sems((1,)),
-            sems((1,)),
-            sems((local,)),
-            sems((local,)),
-            sems((local,)),
+            sems((2, shape[0])),
         ]
     total, *work_out = pl.pallas_call(
         functools.partial(product_sum_kernel, line, flipped, extra is not None, grads is not None),
@@ -1494,16 +1483,20 @@
     line,
     shared_rows,
     parts_ref,
+    small_ref,
     first_ref,
     grad_ref,
     unit_ref,
     inverse_ref,
     gain_ref,
     output_ref,
+    top_ref,
+    scaled_ref,
     summed_ref,
     shared_ref,
     outputs_ref,
     grads_ref,
+    down_ref,
     acc,
     got_pair,
     got_below,
@@ -1518,6 +1511,8 @@
     got_small,
     load_sem,
     pair_sem,
+    load_small_sem,
+    pair_small_sem,
     below_sem,
     above_sem,
     part_sem,
@@ -1529,6 +1524,7 @@
     arrive_sem,
     own_sem,
     small_sem,
+    *work_refs,
 ):
     dp, place = lax.axis_index("dp"), lax.axis_index("expert")
     z, c = place // 2, place % 2
@@ -1543,15 +1539,37 @@
     greeted = 3 + (z > 0).astype(jnp.int32) + (z < line - 1).astype(jnp.int32)
     pl.semaphore_wait(pltpu.get_barrier_semaphore(), greeted)
 
-    def load(height, p):
-        return pltpu.make_async_copy(
-            parts_ref.at[height, c, p], acc.at[height, p], load_sem.at[height, p]
-        )
-
-    def hand(height, p):
+    large = parts_ref.shape[3]
+    top_rows, low_rows = pl.ds(0, large), pl.ds(large, shared_rows // 2)
+
+    def loads(height, p):
+        return (
+            pltpu.make_async_copy(
+                parts_ref.at[height, c, p], acc.at[height, p, top_rows], load_sem.at[height, p]
+            ),
+            pltpu.make_async_copy(
+                small_ref.at[height, c, p], acc.at[height, p, low_rows], load_small_sem.at[height, p]
+            ),
+        )
+
+    def hands(height, p):
         at = (height, p)
-        source = parts_ref.at[height, 1 - c, p]
-        return send(source, got_pair.at[at], pair_sem.at[0, *at], pair_sem.at[1, *at], to_pair)
+        return (
+            send(
+                parts_ref.at[height, 1 - c, p],
+                got_pair.at[height, p, top_rows],
+                pair_sem.at[0, *at],
+                pair_sem.at[1, *at],
+                to_pair,
+            ),
+            send(
+                small_ref.at[height, 1 - c, p],
+                got_pair.at[height, p, low_rows],
+                pair_small_sem.at[0, *at],
+                pair_small_sem.at[1, *at],
+                to_pair,
+            ),
+        )
 
     def climb(height, p):
         at = (height, p)
@@ -1568,15 +1586,17 @@
     def start(k, carry):
         height = farthest(line, z, k)
         for p in (0, 1):
-            load(height, p).start()
-            hand(height, p).start()
+            for copy in (*loads(height, p), *hands(height, p)):
+                copy.start()
         return carry
 
     def pair_sum(k, carry):
         height = farthest(line, z, k)
         for p in (0, 1):
-            load(height, p).wait()
-            hand(height, p).wait_recv()
+            for copy in loads(height, p):
+                copy.wait()
+            for copy in hands(height, p):
+                copy.wait_recv()
             acc[height, p] = acc[height, p] + got_pair[height, p]
             pl.when((z == 0) & (height > z))(lambda: climb(height, p).start())
             pl.when((z == line - 1) & (height < z))(lambda: descend(height, p).start())
@@ -1642,6 +1662,16 @@
         spread(a, side_x, 0, 1).start()
         spread(a, side_y, 1, 0).wait_recv()
         spread(a, side_y, 1, 0).start()
+
+    work, work_end, turns = down_grads(top_ref, scaled_ref, down_ref, *work_refs)
+    pauses = 4
+
+    def meanwhile(i):
+        def turn(n, carry):
+            work(n)
+            return carry
+
+        lax.fori_loop(turns * i // pauses, turns * (i + 1) // pauses, turn, 0)
 
     lax.fori_loop(0, 1, start, 0)
     for q in (far, side_x, side_y, dp):
@@ -1665,6 +1695,8 @@
     for p in (0, 1):
         spread_own(0, p)
     lax.fori_loop(1, line, pair_sum, 0)
+    meanwhile(0)
+    lax.fori_loop(0, 1, pass_on, 0)
     for p in (0, 1):
         along_x(p).wait_recv()
         along_y(p).wait_recv()
@@ -1676,11 +1708,13 @@
         rows = grad_ref[p] + inverse_ref[p] * (total - unit * mean)
         grad_own[p] = rows.astype(grad_own.dtype)
         spread_own(1, p)
-    lax.fori_loop(0, 1, pass_on, 0)
+    meanwhile(1)
     spread_far(0)
     lax.fori_loop(1, 2, pass_on, 0)
     spread_far(1)
+    meanwhile(2)
     lax.fori_loop(2, line, pass_on, 0)
+    meanwhile(3)
     for p in (0, 1):
         summed_ref[p] = acc[z, p].astype(jnp.float32)
 
@@ -1695,9 +1729,8 @@
         pl.when(z > 0)(from_below)
         pl.when(z < line - 1)(from_above)
 
-    last = summed_ref.shape[1] - shared_rows
     for side, device in enumerate((to_x, to_y)):
-        value = summed_ref[1, last:, :] if side == 0 else shared_ref[...]
+        value = summed_ref[:, large:, :] if side == 0 else shared_ref[...]
         small[side] = value.astype(small.dtype)
         spread(side, side_x, 1, 0).wait_recv()
         spread(side, side_y, 0, 0).wait_recv()
@@ -1724,33 +1757,38 @@
 
     def finish(height, carry):
         for p in (0, 1):
-            hand(height, p).wait_send()
+            for copy in hands(height, p):
+                copy.wait_send()
             pl.when(height > z)(lambda: climb(height, p).wait_send())
             pl.when(height < z)(lambda: descend(height, p).wait_send())
         return carry
 
     lax.fori_loop(0, line, finish, 0)
-
-
-def closing(parts, first, grad, unit, inverse, gain, output, shared_rows, line):
+    work_end()
+
+
+def closing(parts, small, first, grad, unit, inverse, gain, output, tops, scaled, shape, line):
     _, rows, wide = parts.shape
+    shared_rows = small.shape[1]
     own, width = output.shape
-    high, half = rows // 2, own // 2
+    high, half = (rows + shared_rows) // 2, own // 2
+    local, units, _ = shape
     sems = pltpu.SemaphoreType.DMA
     dtype = parts.dtype
     single = jnp.float32
     anywhere, inside = pl.BlockSpec(memory_space=pl.ANY), pl.BlockSpec(memory_space=pltpu.VMEM)
     everyone = jax.ShapeDtypeStruct((4, 2, half, width), dtype)
-    summed, shared, outputs, grads = pl.pallas_call(
+    summed, shared, outputs, grads, down = pl.pallas_call(
         functools.partial(closing_kernel, line, shared_rows),
         out_shape=[
             jax.ShapeDtypeStruct((2, high, wide), single),
-            jax.ShapeDtypeStruct((shared_rows, wide), single),
+            jax.ShapeDtypeStruct((2, shared_rows // 2, wide), single),
             everyone,
             everyone,
+            jax.ShapeDtypeStruct(shape, dtype),
         ],
-        in_specs=[anywhere, anywhere] + [inside] * 5,
-        out_specs=[inside, inside, anywhere, anywhere],
+        in_specs=[anywhere] * 3 + [inside] * 5 + [anywhere] * 2,
+        out_specs=[inside, inside, anywhere, anywhere, anywhere],
         scratch_shapes=[
             pltpu.VMEM((line, 2, high, wide), dtype),
             pltpu.VMEM((line, 2, high, wide), dtype),
@@ -1762,8 +1800,10 @@
             pltpu.VMEM((half, width), dtype),
             pltpu.VMEM((half, width), dtype),
             pltpu.VMEM((2, half, width), dtype),
-            pltpu.VMEM((2, shared_rows, wide), dtype),
-            pltpu.VMEM((2, shared_rows, wide), dtype),
+            pltpu.VMEM((2, 2, shared_rows // 2, wide), dtype),
+            pltpu.VMEM((2, 2, shared_rows // 2, wide), dtype),
+            sems((line, 2)),
+            sems((2, line, 2)),
             sems((line, 2)),
             sems((2, line, 2)),
             sems((2, line, 2)),
@@ -1777,25 +1817,37 @@
             sems((2, 4, 2)),
             sems((2, 2)),
             sems((2, 2)),
+            pltpu.VMEM((2, tops.shape[0], SPAN), dtype),
+            pltpu.VMEM(scaled.shape, dtype),
+            pltpu.VMEM((SPAN, local * units), single),
+            pltpu.VMEM((local, units, SPAN), dtype),
+            sems((2,)),
+            sems((1,)),
+            sems((local,)),
         ],
         compiler_params=pltpu.CompilerParams(
             collective_id=5, has_side_effects=True, vmem_limit_bytes=60 << 20
         ),
         name="closing",
     )(
-        parts.reshape(line, 2, 2, high, wide),
+        parts.reshape(line, 2, 2, rows // 2, wide),
+        small.reshape(line, 2, 2, shared_rows // 2, wide),
         first.reshape(4, 2, half, width),
         grad.reshape(2, half, width),
         unit.reshape(2, half, width),
         inverse.reshape(2, half, 1),
         gain.reshape(1, width),
         output.reshape(2, half, width),
+        tops,
+        scaled,
     )
     return (
-        summed.reshape(rows, wide),
+        summed[:, : rows // 2].reshape(rows, wide),
+        summed[:, rows // 2 :],
         shared,
         outputs.reshape(4 * own, width),
         grads.reshape(4 * own, width),
+        down,
     )
 
 
@@ -1886,7 +1938,8 @@
     expert_range = jnp.arange(experts, dtype=jnp.int32)
     named = jnp.any(chosen[:, :, None] == expert_range, axis=1)
     top_own = own_rows(d_output[0])
-    top_all = lax.all_gather(top_own, ALL, axis=0, tiled=True)
+    top_all = lax.all_gather(top_own, "expert", axis=0, tiled=True)
+    top_all = lax.all_gather(top_all, "dp", axis=0, tiled=True)
     gate_table = jnp.where(named, router, 0.0)
     gate_high = gate_table.astype(jnp.bfloat16)
     gate_low = (gate_table - gate_high.astype(jnp.float32)).astype(jnp.bfloat16)
@@ -1904,7 +1957,7 @@
     )
     w_both = jnp.concatenate([*w_gate, *w_up], axis=1)
     (grad_tokens,) = product_sum(grad_units, w_both, True, gate_part, line, "grad_tokens", 4)
-    moe_out, grad_gate, grad_up, grad_down = product_sum(
+    moe_out, grad_gate, grad_up = product_sum(
         scaled,
         w_down.reshape(-1, model_width),
         False,
@@ -1912,7 +1965,7 @@
         line,
         "expert_sum",
         2,
-        (xn_all, top_all, grad_units, w_gate.shape),
+        (xn_all, grad_units, w_gate.shape),
     )
     output = (hidden_state + moe_out).astype(jnp.bfloat16)
     grad_xn_exp = grad_tokens[:, :model_width]
@@ -1990,27 +2043,22 @@
     small_rows = 32
     filled = small.shape[1]
     small = jnp.pad(small, ((0, 0), (0, small_rows * wide - filled)))
-    parts = jnp.concatenate(
-        [
-            grad_projections.astype(jnp.bfloat16).reshape(groups, -1, wide),
-            small.astype(jnp.bfloat16).reshape(groups, small_rows, wide),
-        ],
-        axis=1,
-    )
-    summed, shared, outputs, grad_input = closing(
-        parts,
+    summed, own_small, shared, outputs, grad_input, grad_down = closing(
+        grad_projections.astype(jnp.bfloat16).reshape(groups, -1, wide),
+        small.astype(jnp.bfloat16).reshape(groups, small_rows, wide),
         grad_first_normed_input[0].astype(jnp.bfloat16),
         grad_hidden,
         own_rows(first_unit_input[0]),
         own_rows(first_inverse_norm[0]),
         attention_norm_gain,
         output,
-        small_rows,
+        top_all,
+        scaled,
+        w_down.shape,
         line,
     )
-    large_rows = summed.shape[0] - small_rows
     gain_size, norm_size = local_width // groups, model_width // groups
-    own_gains = summed[large_rows:].reshape(-1)[: 2 * gain_size]
+    own_gains = own_small.reshape(-1)[: 2 * gain_size]
     shared = shared.reshape(-1)[2 * gain_size : filled]
     grad_out = lax.psum_scatter(
         grad_out.astype(jnp.bfloat16), "expert", scatter_dimension=0, tiled=True
@@ -2019,9 +2067,9 @@
         outputs[None],
         grad_input.astype(jnp.float32)[None],
         shared[:norm_size],
-        summed[:large_rows, :local_width],
-        summed[:large_rows, local_width : 2 * local_width],
-        summed[:large_rows, 2 * local_width :],
+        summed[:, :local_width],
+        summed[:, local_width : 2 * local_width],
+        summed[:, 2 * local_width :],
         grad_out,
         own_gains[:gain_size],
         own_gains[gain_size:],

time: 755 us -> 792 us (1.049)
  waiting for transfers between devices: 0.04 us -> 47.7 us
  Pallas kernels: 579 us -> 570 us
    all_gather x1 -> x2, waiting for transfers between devices: 0.01 us -> 47.6 us  [the longest x1 46.9 us: per_device(): top_all = lax.all_gather(top_own, 'expert', axis=0, tiled=True)]
    pallas_call x2, Pallas kernels: 83.4 us -> 55.6 us  [to_heads(): pl.pallas_call(functools.partial(to_heads_kernel, line, shared), out_shap...]
    pallas_call x1, Pallas kernels: 22.2 us -> 39.8 us  [reduce_to(): pl.pallas_call(functools.partial(reduce_kernel, square, line, paired), ou...]
  transfers between devices with their start and end apart: 2 -> 3, of which waited for: 0 -> 2; matrix products, arithmetic and copies ran while one was open for 13% -> 12% of each run, Pallas kernels for 40% -> 38%
where the time goes in v6:
time: 792 us; the launch traced here: 783 us
  Pallas kernels  570 us (72%)
  other arithmetic  49.6 us (6%)
  waiting for transfers between devices  47.7 us (6%)
  local copies, waits for them, and re-layouts  42.9 us (5%)
  matrix products  38.8 us (5%)
  blocking collectives  19.3 us (2%)
  between operations  14.6 us (2%)
    pallas_call x2, Pallas kernels, product_sum(): pl.pallas_call(functools.partial(product_sum_kernel, line, flipped, extra...  195 us
    pallas_call x1, Pallas kernels, gate_act(): pl.pallas_call(functools.partial(gate_act_kernel, line), out_shape=[jax.S...  85.8 us
    pallas_call x1, Pallas kernels, closing(): pl.pallas_call(functools.partial(closing_kernel, line, shared_rows), out_...  84.1 us
    pallas_call x2, Pallas kernels, to_tokens(): pl.pallas_call(functools.partial(to_tokens_kernel, line, summed), out_sha...  58.8 us
    pallas_call x2, Pallas kernels, to_heads(): pl.pallas_call(functools.partial(to_heads_kernel, line, shared), out_shap...  55.6 us
    all_gather x1, waiting for transfers between devices, per_device(): top_all = lax.all_gather(top_own, 'expert', axis=0, tiled=True)  46.9 us
    pallas_call x1, Pallas kernels, reduce_to(): pl.pallas_call(functools.partial(reduce_kernel, square, line, paired), ou...  39.8 us
    pallas_call x1, Pallas kernels, gather_dp(): pl.pallas_call(gather_square_kernel, out_shape=jax.ShapeDtypeStruct((4, 2...  23.7 us
  transfers between devices with their start and end apart: 3, of which 2 were waited for; matrix products, arithmetic and copies ran while one was open for 12% of the time, Pallas kernels for 38%

profile of v6, /device:TPU:24, one launch (start us, length us, event | category | flops | bytes accessed | tf_op | source)
XLA Modules:
  0.0 782.6 jit_solution(13562395949667981197)
XLA Ops:
  9.2 46.9 %all-gather.5.cloned.1.call-done = bf16[1,1024,2048]{2,1,0:T(8,128)(2,1)} async-done(((bf16[1,128,2048]{2,1,0:T(8,128)(2,1)}), bf16[1,1024,2048]{2,1,0:T(8,128)(2,1)}) %all-gather.5.cloned.1.call-update) | async-done | bytes 4194320 | tf_op jit(solution)/shard_map/all_gather | solution.py:1941
  65.9 4.8 multiply_reduce_fusion.7
  70.7 10.2 %all-reduce.4 = (f32[1,512]{1,0:T(1,128)S(1)}, f32[1,512]{1,0:T(1,128)S(1)}) all-reduce(f32[1,512]{1,0:T(1,128)S(1)} %bitcast.173, f32[1,512]{1,0:T(1,128)S(1)} %bitcast.174), channel_id=1, replica_groups=mesh['dp'=4,'expert'=8] {'dp'}, use_global_device_ids=true, to_apply=%region_2.3 | all-reduce | flops 1024 | bytes 8192 | tf_op jit(solution)/shard_map/psum | solution.py:1855
  92.3 3.9 subtract_convert_fusion
  99.4 3.7 convolution_convert_fusion.5.refs_2_
  103.1 40.5 %scatter_heads.1 = (bf16[4,512,128]{2,1,0:T(8,128)(2,1)}, bf16[4,2,512,128]{3,2,1,0:T(8,128)(2,1)}, bf16[4,2,512,128]{3,2,1,0:T(8,128)(2,1)}) custom-call(bf16[512,512]{1,0:T(8,128)(2,1)} %bitcast.154, bf16[512,512]{1,0:T(8,128)(2,1)} %bitcast.153, bf16[512,512]{1,0:T(8,128)(2,1)} %convolution_convert_fusion.5.refs_2_), custom_call_target="tpu_custom_call" | custom-call | tf_op jit(solution)/shard_map/scatter_heads/pallas_call | solution.py:488
  144.4 11.3 %attend.1 = (bf16[4,512,128]{2,1,0:T(8,128)(2,1)}, f32[4,1,512]{2,1,0:T(1,128)}) custom-call(s32[3,4]{1,0:T(4,128)} %pad_add_fusion.bounds, bf16[4,512,128]{2,1,0:T(8,128)(2,1)} %get-tuple-element.37.q_ref, bf16[4096,128]{1,0:T(8,128)(2,1)} %bitcast.142, bf16[4096,128]{1,0:T(8,128)(2,1)} %bitcast.144, s32[4,1,512]{2,1,0:T(1,128)} %copy-done.35), custom_call_target="tpu_custom_call" | custom-call | tf_op jit(solution)/shard_map/attend/pallas_call | solution.py:686
  155.7 18.5 %gather_heads.1 = bf16[512,512]{1,0:T(8,128)(2,1)} custom-call(bf16[4,512,128]{2,1,0:T(8,128)(2,1)} %get-tuple-element.41.refs_0_), custom_call_target="tpu_custom_call" | custom-call | tf_op jit(solution)/shard_map/gather_heads/pallas_call | solution.py:589
  174.2 4.3 convolution_convert_fusion.2
  178.6 39.8 %scatter_dp.1 = f32[2,64,2048]{2,1,0:T(8,128)} custom-call(bf16[4,1,1,2,64,2048]{5,4,3,2,1,0:T(8,128)(2,1)} %bitcast.157), custom_call_target="tpu_custom_call" | custom-call | tf_op jit(solution)/shard_map/scatter_dp/pallas_call | solution.py:363
  233.0 85.8 %gate_act.1 = (bf16[32,2,64,2048]{3,2,1,0:T(8,128)(2,1)}, bf16[16,256,1024]{2,1,0:T(8,128)(2,1)}, bf16[16,256,512]{2,1,0:T(8,128)(2,1)}, bf16[16,256,128]{2,1,0:T(8,128)(2,1)}) custom-call(bf16[2,64,2176]{2,1,0:T(8,128)(2,1)} %bitcast.148, bf16[16,256,2048]{2,1,0:T(8,128)(2,1)} %bitcast.128, bf16[2,2048,256]{2,1,0:T(8,128)(2,1)} %wg_ref.1, ...), custom_call_target="tpu_custom_call" | custom-call | tf_op jit(solution)/shard_map/gate_act/pallas_call | solution.py:1031
  318.8 95.8 %grad_tokens.1 = f32[2,64,2176]{2,1,0:T(8,128)} custom-call(bf16[16,256,1024]{2,1,0:T(8,128)(2,1)} %get-tuple-element.42.refs_0_.refs_3_, bf16[2048,1024]{1,0:T(8,128)(2,1)} %pad_maximum_fusion.refs_1_, bf16[16,256,128]{2,1,0:T(8,128)(2,1)} %get-tuple-element.43.refs_2_), custom_call_target="tpu_custom_call" | custom-call | tf_op jit(solution)/shard_map/grad_tokens/pallas_call | solution.py:1445
  423.3 23.7 %gather_dp.1 = bf16[4,2,64,2048]{3,2,1,0:T(8,128)(2,1)} custom-call(bf16[2,64,2048]{2,1,0:T(8,128)(2,1)} %bitcast.150), custom_call_target="tpu_custom_call" | custom-call | tf_op jit(solution)/shard_map/gather_dp/pallas_call | solution.py:122
  447.0 3.8 convolution_convert_fusion.4.refs_0_
  454.5 15.1 %scatter_grads.1.d_ref = bf16[4,512,128]{2,1,0:T(8,128)(2,1)} custom-call(bf16[512,512]{1,0:T(8,128)(2,1)} %convolution_convert_fusion.4.refs_0_), custom_call_target="tpu_custom_call" | custom-call | tf_op jit(solution)/shard_map/scatter_grads/pallas_call | solution.py:488
  471.7 15.3 %attend_back.1 = (bf16[4,512,128]{2,1,0:T(8,128)(2,1)}, bf16[4096,128]{1,0:T(8,128)(2,1)}, bf16[4096,128]{1,0:T(8,128)(2,1)}) custom-call(s32[3,4]{1,0:T(4,128)} %pad_add_fusion.bounds, bf16[4,512,128]{2,1,0:T(8,128)(2,1)} %get-tuple-element.37.q_ref, bf16[4096,128]{1,0:T(8,128)(2,1)} %bitcast.143, bf16[4096,128]{1,0:T(8,128)(2,1)} %bitcast.145, ...), custom_call_target="tpu_custom_call" | custom-call | tf_op jit(solution)/shard_map/attend_back/pallas_call | solution.py:708
  486.9 40.3 %gather_grads.1 = (bf16[512,512]{1,0:T(8,128)(2,1)}, bf16[512,512]{1,0:T(8,128)(2,1)}, bf16[512,512]{1,0:T(8,128)(2,1)}) custom-call(bf16[4,512,128]{2,1,0:T(8,128)(2,1)} %get-tuple-element.44.refs_0_, bf16[4,2,512,128]{3,2,1,0:T(8,128)(2,1)} %bitcast.162, bf16[4,2,512,128]{3,2,1,0:T(8,128)(2,1)} %bitcast.163), custom_call_target="tpu_custom_call" | custom-call | tf_op jit(solution)/shard_map/gather_grads/pallas_call | solution.py:589
  537.5 9.1 %all-reduce.3 = (f32[512]{0:T(512)S(1)}, f32[512]{0:T(512)S(1)}) all-reduce(f32[512]{0:T(512)S(1)} %get-tuple-element.103, f32[512]{0:T(512)S(1)} %get-tuple-element.105), channel_id=1, replica_groups=mesh['dp'=4,'expert'=8] {'dp'}, use_global_device_ids=true, to_apply=%region_18.19 | all-reduce | flops 1024 | bytes 8192 | tf_op jit(solution)/shard_map/psum | solution.py:1855
  557.2 99.4 %expert_sum.1 = (f32[2,64,2048]{2,1,0:T(8,128)}, bf16[2,2048,256]{2,1,0:T(8,128)(2,1)}, bf16[2,2048,256]{2,1,0:T(8,128)(2,1)}) custom-call(bf16[16,256,512]{2,1,0:T(8,128)(2,1)} %get-tuple-element.50.refs_0_.scaled_ref, bf16[512,2048]{1,0:T(8,128)(2,1)} %bitcast.136, bf16[4096,2048]{1,0:T(8,128)(2,1)} %bitcast.130, ...), custom_call_target="tpu_custom_call" | custom-call | tf_op jit(solution)/shard_map/expert_sum/pallas_call | solution.py:1445
  659.6 5.6 convolution_convert_fusion
  665.3 84.1 %closing.1 = (f32[2,144,1536]{2,1,0:T(8,128)}, f32[2,16,1536]{2,1,0:T(8,128)}, bf16[4,2,64,2048]{3,2,1,0:T(8,128)(2,1)}, bf16[4,2,64,2048]{3,2,1,0:T(8,128)(2,1)}, bf16[2,256,2048]{2,1,0:T(8,128)(2,1)}) custom-call(bf16[4,2,2,128,1536]{4,3,2,1,0:T(8,128)(2,1)} %bitcast.137, bf16[4,2,2,16,1536]{4,3,2,1,0:T(8,128)(2,1)} %bitcast.147, ...), custom_call_target="tpu_custom_call" | custom-call | tf_op jit(solution)/shard_map/closing/pallas_call | solution.py:1781
  753.8 4.3 convert.47
  761.3 4.1 convert_element_type.153
  772.6 3.2 copy.78
  (181 shorter events, 94.5 us)
Async XLA Ops:
  7.2 213.8 %copy-start = (f32[2048,16]{0,1:T(8,128)S(1)}, f32[2048,16]{0,1:T(8,128)}, u32[]{:S(2)}) copy-start(f32[2048,16]{0,1:T(8,128)} %param.25) | copy-start | bytes 393220
  7.2 48.9 %all-gather.5.cloned.1.call-start = ((), (), s32[]{:S(2)}) async-start(), calls=%async_computation.2 | async-start | bytes 4718592 | tf_op jit(solution)/shard_map/all_gather | solution.py:1941
  9.2 223.8 %all-gather.7.cloned.1.call-start = ((), (), s32[]{:S(2)}) async-start(), calls=%async_computation.3 | async-start | bytes 20971520 | tf_op jit(solution)/shard_map/all_gather | solution.py:1942
  56.1 714.7 %reduce-scatter.2.cloned.1.call-start = ((), (), s32[]{:S(2)}) async-start(), calls=%async_computation.1 | async-start | bytes 2359296 | tf_op jit(solution)/shard_map/reduce_scatter | solution.py:2063
  57.7 3.1 copy-start.38
  65.9 15.1 %copy-start.7 = (f32[512,512]{1,0:T(8,128)}, f32[512,512]{1,0:T(8,128)S(1)}, u32[]{:S(2)}) copy-start(f32[512,512]{1,0:T(8,128)S(1)} %copy.50) | copy-start | bytes 3145732
  65.9 15.1 %copy-start.36 = (f32[512]{0:T(512)S(1)}, f32[512]{0:T(512)}, u32[]{:S(2)}) copy-start(f32[512]{0:T(512)} %param.22) | copy-start | bytes 6148
  82.1 4.1 copy-start.37
  86.2 3.8 copy-start.9
  86.2 3.8 copy-start.40
  92.3 3.9 copy-start.19
  221.0 5.9 copy-start.2
  414.6 6.1 copy-start.3
  423.2 23.7 %copy-start.39 = (bf16[512,2048]{1,0:T(8,128)(2,1)S(1)}, bf16[512,2048]{1,0:T(8,128)(2,1)}, u32[]{:S(2)}) copy-start(bf16[512,2048]{1,0:T(8,128)(2,1)} %param.21) | copy-start | bytes 6291460
  447.0 3.8 copy-start.23
  447.0 3.8 copy-start.33
  453.5 16.2 %copy-start.24 = (bf16[4,512,128]{2,1,0:T(8,128)(2,1)S(1)}, bf16[4,512,128]{2,1,0:T(8,128)(2,1)}, u32[]{:S(2)}) copy-start(bf16[4,512,128]{2,1,0:T(8,128)(2,1)} %get-tuple-element.41.refs_0_) | copy-start | bytes 1572868
  533.9 3.2 copy-start.10
  546.9 3.1 copy-start.15
  749.4 3.2 copy-start.30
  753.8 4.3 copy-start.22
  758.1 3.2 copy-start.31
  761.3 4.1 copy-start.21
  772.6 3.2 copy-start.1
  (20 other events, 40.6 us)
Sparse Core Ops, SparseCore 0:
  10.2 45.8 all-gather.4
  57.9 174.9 all-gather.6
  534.0 32.3 reduce-scatter.1

commit v7 on v6

--- a/solution.py
+++ b/solution.py
@@ -29,22 +29,8 @@
     half_size = head_size // 2
     frequency = rope_base ** (-2.0 * jnp.arange(half_size, dtype=jnp.float32) / head_size)
     angles = positions.astype(jnp.float32)[..., None] * frequency
-    return (jnp.cos(angles), jnp.sin(angles))
-
-
-def rotate(heads_in, cos_table, sin_table):
-    half_size = heads_in.shape[-1] // 2
-    first_half = heads_in[..., :half_size]
-    second_half = heads_in[..., half_size:]
-    cos_head = cos_table[..., None, :]
-    sin_head = sin_table[..., None, :]
-    return jnp.concatenate(
-        [
-            first_half * cos_head - second_half * sin_head,
-            second_half * cos_head + first_half * sin_head,
-        ],
-        axis=-1,
-    )
+    cos, sin = jnp.cos(angles), jnp.sin(angles)
+    return jnp.concatenate([cos, cos], axis=-1), jnp.concatenate([-sin, sin], axis=-1)
 
 
 ALL = ("dp", "expert")
@@ -1325,19 +1311,23 @@
             far_x(height).start()
             far_y(height).start()
 
+        pl.when(j == 0)(opposite)
+        pl.when(j == 1)(lambda: along_x(height, 0).start())
+        pl.when(j == 2)(lambda: along_y(height, 1).start())
+
+    def settle_far(i):
+        _, j, _, height = decode(i)
+
         def side_of_x():
-            along_x(height, 0).start()
             far_y(height).wait_recv()
             add(side_x, height, 1, got_far_y.at[height])
             along_x(height, 1).start()
 
         def side_of_y():
-            along_y(height, 1).start()
             far_x(height).wait_recv()
             add(side_y, height, 0, got_far_x.at[height])
             along_y(height, 0).start()
 
-        pl.when(j == 0)(opposite)
         pl.when(j == 1)(side_of_x)
         pl.when(j == 2)(side_of_y)
 
@@ -1378,9 +1368,9 @@
         if grads:
             every = count // turns
             pl.when((i < count) & (i % every == 0))(lambda: work(i // every))
-        late = farthest(line, z, k - 2)
-        pl.when((k >= 2) & (j == 0))(lambda: column(late))
-        pl.when((k >= 2) & (j == 3))(lambda: pass_on(late))
+        pl.when((i >= 4) & (i < count + 4))(lambda: settle_far(i - 4))
+        pl.when((k >= 3) & (j == 2))(lambda: pass_on(farthest(line, z, k - 3)))
+        pl.when((k >= 2) & (j == 3))(lambda: column(farthest(line, z, k - 2)))
         return carry
 
     lax.fori_loop(0, count + 8, step, 0)
@@ -1851,8 +1841,149 @@
     )
 
 
-def head_totals(first_sum, second_sum):
-    return lax.psum((first_sum, second_sum), "dp")
+def square_sum(values, got, sem, side, device):
+    copy = send(values.at[side], got.at[side], sem.at[0, side], sem.at[1, side], device)
+    copy.start()
+    copy.wait()
+    return values[side] + got[side]
+
+
+def as_rows(column):
+    return jnp.broadcast_to(column, (column.shape[0], 128)).T[:8]
+
+
+def as_column(rows):
+    return jnp.broadcast_to(rows[:1], (128, rows.shape[1])).T[:, :1]
+
+
+def meet_square(dp, place):
+    side_x, side_y = corners(dp)
+    devices = ((side_x, place), (side_y, place))
+    for device in devices:
+        greet(device)
+    pl.semaphore_wait(pltpu.get_barrier_semaphore(), 2)
+    return devices
+
+
+def normed_heads_kernel(
+    model_width, q_ref, k_ref, q_gain, k_gain, cos_ref, sin_ref, queries, keys, inverse, sums, got, sem
+):
+    devices = meet_square(lax.axis_index("dp"), lax.axis_index("expert"))
+    raws, gains, outs = (q_ref, k_ref), (q_gain, k_gain), (queries, keys)
+    for i, raw in enumerate(raws):
+        total = jnp.sum(raw[...] * raw[...], axis=1, keepdims=True)
+        sums[0, 8 * i : 8 * i + 8] = as_rows(total)
+    sums[1] = square_sum(sums, got, sem, 0, devices[0])
+    total = square_sum(sums, got, sem, 1, devices[1])
+    inverse[...] = lax.rsqrt(total * (1.0 / model_width) + epsilon)
+    for i, raw in enumerate(raws):
+        scale = as_column(inverse[8 * i : 8 * i + 8])
+        for at in range(0, raw.shape[1], HD):
+            head = raw[:, at : at + HD] * scale * gains[i][:, at : at + HD]
+            turned = head * cos_ref[...] + pltpu.roll(head, HD // 2, 1) * sin_ref[...]
+            outs[i][:, at : at + HD] = turned.astype(outs[i].dtype)
+
+
+def normed_heads(q_raw, k_raw, q_gain, k_gain, cos, sin, model_width):
+    rows, width = q_raw.shape
+    head = jax.ShapeDtypeStruct((rows, width), jnp.bfloat16)
+    return pl.pallas_call(
+        functools.partial(normed_heads_kernel, model_width),
+        out_shape=[head, head, jax.ShapeDtypeStruct((16, rows), jnp.float32)],
+        in_specs=[pl.BlockSpec(memory_space=pltpu.VMEM)] * 6,
+        out_specs=[pl.BlockSpec(memory_space=pltpu.VMEM)] * 3,
+        scratch_shapes=[
+            pltpu.VMEM((2, 16, rows), jnp.float32),
+            pltpu.VMEM((2, 16, rows), jnp.float32),
+            pltpu.SemaphoreType.DMA((2, 2)),
+        ],
+        compiler_params=pltpu.CompilerParams(
+            collective_id=11, has_side_effects=True, vmem_limit_bytes=40 << 20
+        ),
+        name="normed_heads",
+    )(q_raw, k_raw, q_gain.reshape(1, width), k_gain.reshape(1, width), cos, sin)
+
+
+def normed_heads_back_kernel(
+    model_width,
+    dq_ref,
+    dk_ref,
+    dv_ref,
+    q_ref,
+    k_ref,
+    q_gain,
+    k_gain,
+    cos_ref,
+    sin_ref,
+    inverse,
+    grads,
+    gain_grads,
+    sums,
+    got,
+    sem,
+):
+    devices = meet_square(lax.axis_index("dp"), lax.axis_index("expert"))
+    raws, gains, news = (q_ref, k_ref), (q_gain, k_gain), (dq_ref, dk_ref)
+    rows, width = q_ref.shape
+
+    def parts(i, at):
+        cut = slice(at, at + HD)
+        new = news[i][:, cut].astype(jnp.float32)
+        back = new * cos_ref[...] - pltpu.roll(new, HD // 2, 1) * sin_ref[...]
+        unit = raws[i][:, cut] * as_column(inverse[8 * i : 8 * i + 8])
+        return back, unit, back * gains[i][:, cut]
+
+    for i in (0, 1):
+        total = jnp.zeros((rows, 1), jnp.float32)
+        for at in range(0, width, HD):
+            back, unit, scaled = parts(i, at)
+            gain_grad = jnp.sum(back * unit, axis=0, keepdims=True)
+            gain_grads[8 * i : 8 * i + 8, at : at + HD] = jnp.broadcast_to(gain_grad, (8, HD))
+            total = total + jnp.sum(scaled * unit, axis=1, keepdims=True)
+        sums[0, 8 * i : 8 * i + 8] = as_rows(total)
+    sums[1] = square_sum(sums, got, sem, 0, devices[0])
+    dots = square_sum(sums, got, sem, 1, devices[1]) * (1.0 / model_width)
+    for i in (0, 1):
+        dot = as_column(dots[8 * i : 8 * i + 8])
+        scale = as_column(inverse[8 * i : 8 * i + 8])
+        for at in range(0, width, HD):
+            _, unit, scaled = parts(i, at)
+            value = scale * (scaled - unit * dot)
+            grads[:, i * width + at : i * width + at + HD] = value.astype(grads.dtype)
+    grads[:, 2 * width :] = dv_ref[...]
+
+
+def normed_heads_back(dq, dk, dv, q_raw, k_raw, q_gain, k_gain, cos, sin, inverse, model_width):
+    rows, width = q_raw.shape
+    return pl.pallas_call(
+        functools.partial(normed_heads_back_kernel, model_width),
+        out_shape=[
+            jax.ShapeDtypeStruct((rows, 3 * width), jnp.bfloat16),
+            jax.ShapeDtypeStruct((16, width), jnp.float32),
+        ],
+        in_specs=[pl.BlockSpec(memory_space=pltpu.VMEM)] * 10,
+        out_specs=[pl.BlockSpec(memory_space=pltpu.VMEM)] * 2,
+        scratch_shapes=[
+            pltpu.VMEM((2, 16, rows), jnp.float32),
+            pltpu.VMEM((2, 16, rows), jnp.float32),
+            pltpu.SemaphoreType.DMA((2, 2)),
+        ],
+        compiler_params=pltpu.CompilerParams(
+            collective_id=12, has_side_effects=True, vmem_limit_bytes=40 << 20
+        ),
+        name="normed_heads_back",
+    )(
+        dq,
+        dk,
+        dv,
+        q_raw,
+        k_raw,
+        q_gain.reshape(1, width),
+        k_gain.reshape(1, width),
+        cos,
+        sin,
+        inverse,
+    )
 
 
 def per_device(
@@ -1884,38 +2015,27 @@
     offset_rows = lax.axis_index("expert") * seg_rows
     segment, positions = doc_layout(lengths, pack_span)
     pos_query = lax.dynamic_slice_in_dim(positions, offset_rows, seg_rows, 1)
-    cos_table, sin_table = rope_tables(pos_query, HD)
-    head_shape = (pack_count, seg_rows, local_heads, HD)
+    cos_table, sin_table = rope_tables(pos_query[0], HD)
     inputs_single_float = inputs.astype(jnp.float32)
     first_inverse_norm = lax.rsqrt(
         jnp.mean(inputs_single_float * inputs_single_float, axis=-1, keepdims=True) + epsilon
     )
     first_unit_input = inputs_single_float * first_inverse_norm
     first_normed_input = (first_unit_input * attention_norm_gain).astype(jnp.bfloat16)
-    q_raw = jnp.dot(first_normed_input, w_query, preferred_element_type=jnp.float32)
-    k_raw = jnp.dot(first_normed_input, w_key, preferred_element_type=jnp.float32)
-    value_rows = jnp.dot(first_normed_input, w_value, preferred_element_type=jnp.float32).astype(
+    q_raw = jnp.dot(first_normed_input[0], w_query, preferred_element_type=jnp.float32)
+    k_raw = jnp.dot(first_normed_input[0], w_key, preferred_element_type=jnp.float32)
+    value_rows = jnp.dot(first_normed_input[0], w_value, preferred_element_type=jnp.float32).astype(
         jnp.bfloat16
     )
-    q_sum, k_sum = head_totals(jnp.sum(q_raw * q_raw, axis=-1), jnp.sum(k_raw * k_raw, axis=-1))
-    q_inv = lax.rsqrt(q_sum[..., None] / model_width + epsilon)
-    k_inv = lax.rsqrt(k_sum[..., None] / model_width + epsilon)
-    q_hat = q_raw * q_inv
-    k_hat = k_raw * k_inv
-    queries = rotate((q_hat * q_gain).reshape(head_shape), cos_table, sin_table).astype(
-        jnp.bfloat16
-    )
-    key_rows = (
-        rotate((k_hat * k_gain).reshape(head_shape), cos_table, sin_table)
-        .astype(jnp.bfloat16)
-        .reshape(pack_count, seg_rows, local_width)
+    queries, keys, head_inverse = normed_heads(
+        q_raw, k_raw, q_gain, k_gain, cos_table, sin_table, model_width
     )
     layout = (segment, positions)
     if local_heads == line:
         attention = by_head(layout, line)
     else:
         attention = by_query(layout, offset_rows)
-    attended, kept = attention[0](queries.reshape(seg_rows, local_width), key_rows[0], value_rows[0])
+    attended, kept = attention[0](queries, keys, value_rows)
     attn_part = jnp.dot(
         attended, w_out, preferred_element_type=jnp.float32
     )
@@ -1938,8 +2058,7 @@
     expert_range = jnp.arange(experts, dtype=jnp.int32)
     named = jnp.any(chosen[:, :, None] == expert_range, axis=1)
     top_own = own_rows(d_output[0])
-    top_all = lax.all_gather(top_own, "expert", axis=0, tiled=True)
-    top_all = lax.all_gather(top_all, "dp", axis=0, tiled=True)
+    top_all = lax.all_gather(top_own, ALL, axis=0, tiled=True)
     gate_table = jnp.where(named, router, 0.0)
     gate_high = gate_table.astype(jnp.bfloat16)
     gate_low = (gate_table - gate_high.astype(jnp.float32)).astype(jnp.bfloat16)
@@ -1993,42 +2112,28 @@
         "sd,kd->sk", grad_attn, w_out, preferred_element_type=jnp.float32
     ).astype(jnp.bfloat16)
     grad_queries, grad_keys, grad_values = attention[1](kept, grad_heads)
-    grad_queries = grad_queries.astype(jnp.float32).reshape(head_shape)
-    grad_q_normed = rotate(grad_queries, cos_table, -sin_table).reshape(
-        pack_count, seg_rows, local_width
-    )
-    grad_k_normed = rotate(
-        grad_keys.astype(jnp.float32).reshape(head_shape), cos_table, -sin_table).reshape(
-        pack_count, seg_rows, local_width
-    )
-    grad_q_gain = jnp.sum(grad_q_normed * q_hat, axis=(0, 1))
-    grad_k_gain = jnp.sum(grad_k_normed * k_hat, axis=(0, 1))
-    grad_q_hat = grad_q_normed * q_gain
-    grad_k_hat = grad_k_normed * k_gain
-    q_dot, k_dot = head_totals(
-        jnp.sum(grad_q_hat * q_hat, axis=-1), jnp.sum(grad_k_hat * k_hat, axis=-1)
-    )
-    grad_q_raw = (q_inv * (grad_q_hat - q_hat * q_dot[..., None] / model_width)).astype(
-        jnp.bfloat16
-    )
-    grad_k_raw = (k_inv * (grad_k_hat - k_hat * k_dot[..., None] / model_width)).astype(
-        jnp.bfloat16
-    )
-    grad_v_raw = grad_values.astype(jnp.bfloat16)[None]
-    grad_heads_raw = jnp.concatenate([grad_q_raw[0], grad_k_raw[0], grad_v_raw[0]], axis=1)
+    grad_heads_raw, gain_grads = normed_heads_back(
+        grad_queries.astype(jnp.bfloat16),
+        grad_keys,
+        grad_values,
+        q_raw,
+        k_raw,
+        q_gain,
+        k_gain,
+        cos_table,
+        sin_table,
+        head_inverse,
+        model_width,
+    )
+    grad_q_gain, grad_k_gain = gain_grads[0], gain_grads[8]
     grad_projections = jnp.einsum(
         "sd,sk->dk", first_normed_input[0], grad_heads_raw, preferred_element_type=jnp.float32
     )
-    grad_first_normed_input = jnp.einsum(
-        "psk,dk->psd", grad_q_raw, w_query, preferred_element_type=jnp.float32
-    )
-    grad_first_normed_input = grad_first_normed_input + jnp.einsum(
-        "psk,dk->psd", grad_k_raw, w_key, preferred_element_type=jnp.float32
-    )
-    grad_first_normed_input = grad_first_normed_input + jnp.einsum(
-        "psk,dk->psd", grad_v_raw, w_value, preferred_element_type=jnp.float32
-    )
-    grad_attn_gain = jnp.sum(grad_first_normed_input[0] * first_unit_input[0], axis=0)
+    grad_first_normed_input = sum(
+        contract(grad_heads_raw[:, i * local_width : (i + 1) * local_width], weight, 1, 1)
+        for i, weight in enumerate((w_query, w_key, w_value))
+    )
+    grad_attn_gain = jnp.sum(grad_first_normed_input * first_unit_input[0], axis=0)
     wide = grad_projections.shape[1]
     small = jnp.concatenate(
         [
@@ -2046,7 +2151,7 @@
     summed, own_small, shared, outputs, grad_input, grad_down = closing(
         grad_projections.astype(jnp.bfloat16).reshape(groups, -1, wide),
         small.astype(jnp.bfloat16).reshape(groups, small_rows, wide),
-        grad_first_normed_input[0].astype(jnp.bfloat16),
+        grad_first_normed_input.astype(jnp.bfloat16),
         grad_hidden,
         own_rows(first_unit_input[0]),
         own_rows(first_inverse_norm[0]),

time: 792 us -> 720 us (0.909)
  waiting for transfers between devices: 47.7 us -> 0.04 us
  Pallas kernels: 570 us -> 595 us
  blocking collectives: 19.3 us -> 0 us
  local copies, waits for them, and re-layouts: 42.9 us -> 27.3 us
  other arithmetic: 49.6 us -> 38.9 us
    all_gather x2 -> x1, waiting for transfers between devices: 47.6 us -> 0.01 us  [per_device(): top_all = lax.all_gather(top_own, ALL, axis=0, tiled=True)]
    pallas_call x2, Pallas kernels: 55.6 us -> 85 us  [to_heads(): pl.pallas_call(functools.partial(to_heads_kernel, line, shared), out_shap...]
    pallas_call x2, Pallas kernels: 195 us -> 172 us  [product_sum(): pl.pallas_call(functools.partial(product_sum_kernel, line, flipped, extra...]
    pallas_call x0 -> x2, Pallas kernels: none -> 21 us  [the longest x1 11.8 us: normed_heads_back(): pl.pallas_call(functools.partial(normed_heads_back_kernel, model_width),...]
    psum x2 -> x0, blocking collectives: 19.3 us -> none  [head_totals(): return lax.psum((first_sum, second_sum), 'dp')]
    pallas_call x1, Pallas kernels: 39.8 us -> 23.1 us  [reduce_to(): pl.pallas_call(functools.partial(reduce_kernel, square, line, paired), ou...]
    pallas_call x2, Pallas kernels: 58.8 us -> 74 us  [to_tokens(): pl.pallas_call(functools.partial(to_tokens_kernel, line, summed), out_sha...]
    reshape x6 -> x0, local copies, waits for them, and re-layouts: 8.04 us -> none  [the longest x1 2.54 us: per_device(): (q_hat * q_gain).reshape(head_shape)]
  transfers between devices with their start and end apart: 3 -> 2, of which waited for: 2 -> 0; matrix products, arithmetic and copies ran while one was open for 12% -> 11% of each run, Pallas kernels for 38% -> 57%
where the time goes in v7:
time: 720 us; the launch traced here: 710 us
  Pallas kernels  595 us (83%)
  other arithmetic  38.9 us (5%)
  matrix products  33.5 us (5%)
  local copies, waits for them, and re-layouts  27.3 us (4%)
  between operations  15.1 us (2%)
    pallas_call x2, Pallas kernels, product_sum(): pl.pallas_call(functools.partial(product_sum_kernel, line, flipped, extra...  172 us
    pallas_call x1, Pallas kernels, gate_act(): pl.pallas_call(functools.partial(gate_act_kernel, line), out_shape=[jax.S...  85.2 us
    pallas_call x2, Pallas kernels, to_heads(): pl.pallas_call(functools.partial(to_heads_kernel, line, shared), out_shap...  85 us
    pallas_call x1, Pallas kernels, closing(): pl.pallas_call(functools.partial(closing_kernel, line, shared_rows), out_...  81.2 us
    pallas_call x2, Pallas kernels, to_tokens(): pl.pallas_call(functools.partial(to_tokens_kernel, line, summed), out_sha...  74 us
    pallas_call x1, Pallas kernels, reduce_to(): pl.pallas_call(functools.partial(reduce_kernel, square, line, paired), ou...  23.1 us
    pallas_call x1, Pallas kernels, gather_dp(): pl.pallas_call(gather_square_kernel, out_shape=jax.ShapeDtypeStruct((4, 2...  21.8 us
    pallas_call x1, Pallas kernels, attend_back(): pl.pallas_call(attend_back_kernel, grid_spec=pltpu.PrefetchScalarGridSpec...  18.3 us
  transfers between devices with their start and end apart: 2, of which 0 were waited for; matrix products, arithmetic and copies ran while one was open for 11% of the time, Pallas kernels for 57%

profile of v7, /device:TPU:24, one launch (start us, length us, event | category | flops | bytes accessed | tf_op | source)
XLA Modules:
  0.0 709.7 jit_solution(17862900021607274113)
XLA Ops:
  11.0 4.3 convert_element_type.104
  20.4 9.2 %normed_heads.1 = (bf16[512,512]{1,0:T(8,128)(2,1)S(1)}, bf16[512,512]{1,0:T(8,128)(2,1)S(1)}, f32[16,512]{1,0:T(8,128)S(1)}) custom-call(f32[512,512]{1,0:T(8,128)S(1)} %fusion.28.q_ref, f32[512,512]{1,0:T(8,128)S(1)} %fusion.26.k_ref, f32[1,512]{1,0:T(1,128)S(1)} %bitcast.88, f32[1,512]{1,0:T(1,128)S(1)} %bitcast.90, ...), custom_call_target="tpu_custom_call" | custom-call | tf_op jit(solution)/shard_map/normed_heads/pallas_call | solution.py:1890
  31.7 62.2 %scatter_heads.1 = (bf16[4,512,128]{2,1,0:T(8,128)(2,1)}, bf16[4,2,512,128]{3,2,1,0:T(8,128)(2,1)}, bf16[4,2,512,128]{3,2,1,0:T(8,128)(2,1)}) custom-call(bf16[512,512]{1,0:T(8,128)(2,1)} %copy-done.11, bf16[512,512]{1,0:T(8,128)(2,1)} %copy-done.12, bf16[512,512]{1,0:T(8,128)(2,1)} %convolution_convert_fusion.5.refs_2_), custom_call_target="tpu_custom_call" | custom-call | tf_op jit(solution)/shard_map/scatter_heads/pallas_call | solution.py:474
  94.8 13.6 %attend.1 = (bf16[4,512,128]{2,1,0:T(8,128)(2,1)}, f32[4,1,512]{2,1,0:T(1,128)}) custom-call(s32[3,4]{1,0:T(4,128)} %pad_add_fusion.bounds, bf16[4,512,128]{2,1,0:T(8,128)(2,1)} %get-tuple-element.44.q_ref, bf16[4096,128]{1,0:T(8,128)(2,1)} %bitcast.102, bf16[4096,128]{1,0:T(8,128)(2,1)} %bitcast.104, s32[4,1,512]{2,1,0:T(1,128)} %copy-done.35), custom_call_target="tpu_custom_call" | custom-call | tf_op jit(solution)/shard_map/attend/pallas_call | solution.py:672
  108.4 33.2 %gather_heads.1 = bf16[512,512]{1,0:T(8,128)(2,1)} custom-call(bf16[4,512,128]{2,1,0:T(8,128)(2,1)} %get-tuple-element.48.refs_0_), custom_call_target="tpu_custom_call" | custom-call | tf_op jit(solution)/shard_map/gather_heads/pallas_call | solution.py:575
  141.6 3.6 convolution_convert_fusion.2
  145.3 23.1 %scatter_dp.1 = f32[2,64,2048]{2,1,0:T(8,128)} custom-call(bf16[4,1,1,2,64,2048]{5,4,3,2,1,0:T(8,128)(2,1)} %bitcast.113), custom_call_target="tpu_custom_call" | custom-call | tf_op jit(solution)/shard_map/scatter_dp/pallas_call | solution.py:349
  182.0 85.2 %gate_act.1 = (bf16[32,2,64,2048]{3,2,1,0:T(8,128)(2,1)}, bf16[16,256,1024]{2,1,0:T(8,128)(2,1)}, bf16[16,256,512]{2,1,0:T(8,128)(2,1)}, bf16[16,256,128]{2,1,0:T(8,128)(2,1)}) custom-call(bf16[2,64,2176]{2,1,0:T(8,128)(2,1)} %bitcast.108, bf16[16,256,2048]{2,1,0:T(8,128)(2,1)} %bitcast.92, bf16[2,2048,256]{2,1,0:T(8,128)(2,1)} %wg_ref.1, ...), custom_call_target="tpu_custom_call" | custom-call | tf_op jit(solution)/shard_map/gate_act/pallas_call | solution.py:1017
  267.2 86.3 %grad_tokens.1 = f32[2,64,2176]{2,1,0:T(8,128)} custom-call(bf16[16,256,1024]{2,1,0:T(8,128)(2,1)} %get-tuple-element.49.refs_0_.refs_3_, bf16[2048,1024]{1,0:T(8,128)(2,1)} %pad_maximum_fusion.refs_1_, bf16[16,256,128]{2,1,0:T(8,128)(2,1)} %get-tuple-element.50.refs_2_), custom_call_target="tpu_custom_call" | custom-call | tf_op jit(solution)/shard_map/grad_tokens/pallas_call | solution.py:1435
  360.1 21.8 %gather_dp.1 = bf16[4,2,64,2048]{3,2,1,0:T(8,128)(2,1)} custom-call(bf16[2,64,2048]{2,1,0:T(8,128)(2,1)} %bitcast.110), custom_call_target="tpu_custom_call" | custom-call | tf_op jit(solution)/shard_map/gather_dp/pallas_call | solution.py:108
  381.9 4.2 convolution_convert_fusion.1
  388.9 4.4 convolution_convert_fusion.4.refs_0_
  393.2 22.8 %scatter_grads.1.d_ref = bf16[4,512,128]{2,1,0:T(8,128)(2,1)} custom-call(bf16[512,512]{1,0:T(8,128)(2,1)} %convolution_convert_fusion.4.refs_0_), custom_call_target="tpu_custom_call" | custom-call | tf_op jit(solution)/shard_map/scatter_grads/pallas_call | solution.py:474
  418.0 18.3 %attend_back.1 = (bf16[4,512,128]{2,1,0:T(8,128)(2,1)}, bf16[4096,128]{1,0:T(8,128)(2,1)}, bf16[4096,128]{1,0:T(8,128)(2,1)}) custom-call(s32[3,4]{1,0:T(4,128)} %pad_add_fusion.bounds, bf16[4,512,128]{2,1,0:T(8,128)(2,1)} %get-tuple-element.44.q_ref, bf16[4096,128]{1,0:T(8,128)(2,1)} %bitcast.103, bf16[4096,128]{1,0:T(8,128)(2,1)} %bitcast.105, ...), custom_call_target="tpu_custom_call" | custom-call | tf_op jit(solution)/shard_map/attend_back/pallas_call | solution.py:694
  436.3 40.8 %gather_grads.1 = (bf16[512,512]{1,0:T(8,128)(2,1)}, bf16[512,512]{1,0:T(8,128)(2,1)}, bf16[512,512]{1,0:T(8,128)(2,1)}) custom-call(bf16[4,512,128]{2,1,0:T(8,128)(2,1)} %get-tuple-element.51.refs_0_, bf16[4,2,512,128]{3,2,1,0:T(8,128)(2,1)} %bitcast.118, bf16[4,2,512,128]{3,2,1,0:T(8,128)(2,1)} %bitcast.119), custom_call_target="tpu_custom_call" | custom-call | tf_op jit(solution)/shard_map/gather_grads/pallas_call | solution.py:575
  480.3 11.8 %normed_heads_back.1 = (bf16[512,1536]{1,0:T(8,128)(2,1)S(1)}, f32[16,512]{1,0:T(8,128)S(1)}) custom-call(bf16[512,512]{1,0:T(8,128)(2,1)S(1)} %copy-done.8, bf16[512,512]{1,0:T(8,128)(2,1)S(1)} %copy-done.9, bf16[512,512]{1,0:T(8,128)(2,1)S(1)} %copy-done.10, f32[512,512]{1,0:T(8,128)S(1)} %copy-done.5, f32[512,512]{1,0:T(8,128)S(1)} %copy-done.3, ...), custom_call_target="tpu_custom_call" | custom-call | tf_op jit(solution)/shard_map/normed_heads_back/pallas_call | solution.py:1958
  496.5 3.0 fusion.31
  501.0 85.3 %expert_sum.1 = (f32[2,64,2048]{2,1,0:T(8,128)}, bf16[2,2048,256]{2,1,0:T(8,128)(2,1)}, bf16[2,2048,256]{2,1,0:T(8,128)(2,1)}) custom-call(bf16[16,256,512]{2,1,0:T(8,128)(2,1)} %get-tuple-element.60.refs_0_.scaled_ref, bf16[512,2048]{1,0:T(8,128)(2,1)} %bitcast.96, bf16[4096,2048]{1,0:T(8,128)(2,1)} %bitcast.94, ...), custom_call_target="tpu_custom_call" | custom-call | tf_op jit(solution)/shard_map/expert_sum/pallas_call | solution.py:1435
  586.2 3.0 add_convert_fusion.output_ref
  589.2 5.5 convolution_convert_fusion
  594.8 81.2 %closing.1 = (f32[2,144,1536]{2,1,0:T(8,128)}, f32[2,16,1536]{2,1,0:T(8,128)}, bf16[4,2,64,2048]{3,2,1,0:T(8,128)(2,1)}, bf16[4,2,64,2048]{3,2,1,0:T(8,128)(2,1)}, bf16[2,256,2048]{2,1,0:T(8,128)(2,1)}) custom-call(bf16[4,2,2,128,1536]{4,3,2,1,0:T(8,128)(2,1)} %bitcast.97, bf16[4,2,2,16,1536]{4,3,2,1,0:T(8,128)(2,1)} %bitcast.107, ...), custom_call_target="tpu_custom_call" | custom-call | tf_op jit(solution)/shard_map/closing/pallas_call | solution.py:1771
  680.4 4.3 convert.28
  687.9 4.1 convert_element_type.127
  699.2 3.2 copy.56
  (154 shorter events, 60.4 us)
Async XLA Ops:
  7.2 163.9 %copy-start = (f32[2048,16]{0,1:T(8,128)S(1)}, f32[2048,16]{0,1:T(8,128)}, u32[]{:S(2)}) copy-start(f32[2048,16]{0,1:T(8,128)} %param.25) | copy-start | bytes 393220
  7.2 174.8 %all-gather.3.cloned.1.call-start = ((), (), s32[]{:S(2)}) async-start(), calls=%async_computation.2 | async-start | bytes 17301504 | tf_op jit(solution)/shard_map/all_gather | solution.py:2061
  9.2 688.3 %reduce-scatter.2.cloned.1.call-start = ((), (), s32[]{:S(2)}) async-start(), calls=%async_computation.1 | async-start | bytes 2359296 | tf_op jit(solution)/shard_map/reduce_scatter | solution.py:2168
  11.0 4.3 copy-start.17
  20.4 11.4 %copy-start.4 = (f32[512,512]{1,0:T(8,128)}, f32[512,512]{1,0:T(8,128)S(1)}, u32[]{:S(2)}) copy-start(f32[512,512]{1,0:T(8,128)S(1)} %fusion.28.q_ref) | copy-start | bytes 3145732
  20.4 9.2 %copy-start.29 = (bf16[2048,512]{1,0:T(8,128)(2,1)S(1)}, bf16[2048,512]{1,0:T(8,128)(2,1)}, u32[]{:S(2)}) copy-start(bf16[2048,512]{1,0:T(8,128)(2,1)} %param.20) | copy-start | bytes 6291460
  94.0 47.6 %copy-start.37 = (bf16[512,2048]{1,0:T(8,128)(2,1)S(1)}, bf16[512,2048]{1,0:T(8,128)(2,1)}, u32[]{:S(2)}) copy-start(bf16[512,2048]{1,0:T(8,128)(2,1)} %param.21) | copy-start | bytes 6291460
  168.4 2.7 copy-start.34
  171.0 4.3 copy-start.15
  175.3 3.2 copy-start.21
  353.5 4.0 copy-start.16
  360.1 21.8 %copy-start.33 = (bf16[512,512]{1,0:T(8,128)(2,1)S(1)}, bf16[512,512]{1,0:T(8,128)(2,1)}, u32[]{:S(2)}) copy-start(bf16[512,512]{1,0:T(8,128)(2,1)} %gather_heads.1) | copy-start | bytes 1572868
  388.9 27.1 %copy-start.24 = (bf16[4,512,128]{2,1,0:T(8,128)(2,1)S(1)}, bf16[4,512,128]{2,1,0:T(8,128)(2,1)}, u32[]{:S(2)}) copy-start(bf16[4,512,128]{2,1,0:T(8,128)(2,1)} %get-tuple-element.48.refs_0_) | copy-start | bytes 1572868
  436.3 40.8 %copy-start.3 = (f32[512,512]{1,0:T(8,128)S(1)}, f32[512,512]{1,0:T(8,128)}, u32[]{:S(2)}) copy-start(f32[512,512]{1,0:T(8,128)} %copy-done.2) | copy-start | bytes 3145732
  436.3 40.9 %copy-start.5 = (f32[512,512]{1,0:T(8,128)S(1)}, f32[512,512]{1,0:T(8,128)}, u32[]{:S(2)}) copy-start(f32[512,512]{1,0:T(8,128)} %copy-done.4) | copy-start | bytes 3145732
  480.3 11.8 %copy-start.26 = (bf16[2048,512]{1,0:T(8,128)(2,1)S(1)}, bf16[2048,512]{1,0:T(8,128)(2,1)}, u32[]{:S(2)}) copy-start(bf16[2048,512]{1,0:T(8,128)(2,1)} %param.18) | copy-start | bytes 6291460
  492.1 3.5 copy-start.6
  586.2 3.0 copy-start.7
  586.2 3.0 copy-start.19
  675.9 3.2 copy-start.31
  680.4 4.3 copy-start.23
  684.7 3.2 copy-start.32
  687.9 4.1 copy-start.22
  699.2 3.2 copy-start.1
  (16 other events, 25.1 us)
Sparse Core Ops, SparseCore 0:
  11.6 146.7 all-gather.2
  386.2 40.2 reduce-scatter.1

commit v8 on v7

--- a/solution.py
+++ b/solution.py
@@ -706,7 +706,268 @@
     )(bounds, queries, keys, values, starts, total, delta, grad)
 
 
-def by_head(layout, line):
+def out_sum_kernel(
+    line,
+    o_ref,
+    w_ref,
+    attended_ref,
+    out_ref,
+    att,
+    made,
+    got_x,
+    got_y,
+    got_far_x,
+    got_far_y,
+    sent,
+    arrived,
+    own_sem,
+    att_sem,
+    x_sem,
+    y_sem,
+    far_x_sem,
+    far_y_sem,
+):
+    dp, place = lax.axis_index("dp"), lax.axis_index("expert")
+    z, c = place // 2, place % 2
+    side_x, side_y = corners(dp)
+    far = 3 - dp
+    to_x, to_y = (side_x, place), (side_y, place)
+    visit_others(line, z, lambda other: greet((dp, 2 * other + c)))
+    greet(to_x)
+    greet(to_y)
+    pl.semaphore_wait(pltpu.get_barrier_semaphore(), line + 1)
+    rows, half, width = att.shape[1], made.shape[2], made.shape[3]
+    chunk = 512
+    order = (far, side_x, side_y, dp)
+
+    def block(q):
+        return pl.ds(pl.multiple_of(q * rows, rows), rows)
+
+    def out(q, other):
+        device = (dp, 2 * other + c)
+        source, target = o_ref.at[other, block(q)], att.at[q, :, columns(z)]
+        return send(source, target, sent.at[q, other], arrived.at[q, z], device)
+
+    def into(q, origin):
+        part = att.at[q, :, columns(origin)]
+        return send(part, part, sent.at[q, origin], arrived.at[q, origin], to_x)
+
+    def own(q):
+        return pltpu.make_async_copy(
+            o_ref.at[z, block(q)], att.at[q, :, columns(z)], own_sem.at[q]
+        )
+
+    def att_out(q):
+        return pltpu.make_async_copy(att.at[q], attended_ref.at[block(q)], att_sem.at[q])
+
+    def along_x(p):
+        return send(made.at[side_x, p], got_x.at[p], x_sem.at[0, p], x_sem.at[1, p], to_x)
+
+    def along_y(p):
+        return send(made.at[side_y, p], got_y.at[p], y_sem.at[0, p], y_sem.at[1, p], to_y)
+
+    def far_x():
+        return send(made.at[far, 0], got_far_x, far_x_sem.at[0], far_x_sem.at[1], to_x)
+
+    def far_y():
+        return send(made.at[far, 1], got_far_y, far_y_sem.at[0], far_y_sem.at[1], to_y)
+
+    for q in order:
+        visit_others(line, z, lambda other: out(q, other).start())
+        own(q).start()
+    for i, q in enumerate(order):
+        visit_others(line, z, lambda origin: into(q, origin).wait_recv())
+        own(q).wait()
+        att_out(q).start()
+        for at in range(0, width, chunk):
+            part = contract(att[q], w_ref[:, at : at + chunk], 1, 0).astype(made.dtype)
+            made[q, :, :, at : at + chunk] = part.reshape(2, half, chunk)
+        if i == 0:
+            far_x().start()
+            far_y().start()
+        if i == 1:
+            along_x(0).start()
+        if i == 2:
+            along_y(1).start()
+    far_y().wait_recv()
+    made[side_x, 1] = made[side_x, 1] + got_far_y[...]
+    along_x(1).start()
+    far_x().wait_recv()
+    made[side_y, 0] = made[side_y, 0] + got_far_x[...]
+    along_y(0).start()
+    for p in (0, 1):
+        along_x(p).wait_recv()
+        along_y(p).wait_recv()
+        total = made[dp, p].astype(jnp.float32)
+        out_ref[p] = total + got_x[p].astype(jnp.float32) + got_y[p].astype(jnp.float32)
+    far_x().wait_send()
+    far_y().wait_send()
+    for p in (0, 1):
+        along_x(p).wait_send()
+        along_y(p).wait_send()
+    for q in order:
+        visit_others(line, z, lambda other: out(q, other).wait_send())
+        att_out(q).wait()
+
+
+def out_sum(heads, w_out, line):
+    rows = heads.shape[1]
+    depth, width = w_out.shape
+    quarter, half = rows // 4, rows // 8
+    sems = pltpu.SemaphoreType.DMA
+    dtype = heads.dtype
+    anywhere, inside = pl.BlockSpec(memory_space=pl.ANY), pl.BlockSpec(memory_space=pltpu.VMEM)
+    attended, total = pl.pallas_call(
+        functools.partial(out_sum_kernel, line),
+        out_shape=[
+            jax.ShapeDtypeStruct((rows, depth), dtype),
+            jax.ShapeDtypeStruct((2, half, width), jnp.float32),
+        ],
+        in_specs=[anywhere, inside],
+        out_specs=[anywhere, inside],
+        scratch_shapes=[
+            pltpu.VMEM((4, quarter, depth), dtype),
+            pltpu.VMEM((4, 2, half, width), dtype),
+            pltpu.VMEM((2, half, width), dtype),
+            pltpu.VMEM((2, half, width), dtype),
+            pltpu.VMEM((half, width), dtype),
+            pltpu.VMEM((half, width), dtype),
+            sems((4, line)),
+            sems((4, line)),
+            sems((4,)),
+            sems((4,)),
+            sems((2, 2)),
+            sems((2, 2)),
+            sems((2,)),
+            sems((2,)),
+        ],
+        compiler_params=pltpu.CompilerParams(
+            collective_id=7, has_side_effects=True, vmem_limit_bytes=40 << 20
+        ),
+        name="out_sum",
+    )(heads, w_out)
+    return attended, total.reshape(quarter, width)
+
+
+def out_back_kernel(
+    line, x_ref, w_ref, all_ref, grad_ref, buf, grads, spread_sem, arrive_sem, own_sem, all_sem, sent, arrived, mine_sem
+):
+    dp, place = lax.axis_index("dp"), lax.axis_index("expert")
+    z, c = place // 2, place % 2
+    side_x, side_y = corners(dp)
+    far = 3 - dp
+    devices = ((side_x, place), (side_y, place))
+    visit_others(line, z, lambda other: greet((dp, 2 * other + c)))
+    for device in devices:
+        greet(device)
+    pl.semaphore_wait(pltpu.get_barrier_semaphore(), line + 1)
+    rows = grads.shape[1]
+
+    def spread(corner, p, way, source=None):
+        target = buf.at[corner, p]
+        return send(
+            target if source is None else source,
+            target,
+            spread_sem.at[corner, p, way],
+            arrive_sem.at[corner, p],
+            devices[way],
+        )
+
+    def own(p):
+        return pltpu.make_async_copy(x_ref.at[p], buf.at[dp, p], own_sem.at[p])
+
+    def all_out(q):
+        return pltpu.make_async_copy(buf.at[q], all_ref.at[q], all_sem.at[q])
+
+    def block(q):
+        return pl.ds(pl.multiple_of(q * rows, rows), rows)
+
+    def out(q, other):
+        device = (dp, 2 * other + c)
+        source, target = grads.at[q, :, columns(other)], grad_ref.at[z, block(q)]
+        return send(source, target, sent.at[q, other], arrived.at[q, z], device)
+
+    def into(q, origin):
+        part = grad_ref.at[origin, block(q)]
+        return send(part, part, sent.at[q, origin], arrived.at[q, origin], devices[0])
+
+    def mine(q):
+        return pltpu.make_async_copy(
+            grads.at[q, :, columns(z)], grad_ref.at[z, block(q)], mine_sem.at[q]
+        )
+
+    def product(q):
+        all_out(q).start()
+        value = contract(buf[q].reshape(rows, buf.shape[3]), w_ref[...], 1, 1)
+        grads[q] = value.astype(grads.dtype)
+        visit_others(line, z, lambda other: out(q, other).start())
+        mine(q).start()
+
+    for p in (0, 1):
+        spread(dp, p, 0, x_ref.at[p]).start()
+        spread(dp, 1 - p, 1, x_ref.at[1 - p]).start()
+        own(p).start()
+    for p in (0, 1):
+        own(p).wait()
+    product(dp)
+    spread(side_x, 0, 0).wait_recv()
+    spread(side_x, 0, 1).start()
+    spread(side_y, 1, 0).wait_recv()
+    spread(side_y, 1, 0).start()
+    spread(side_x, 1, 0).wait_recv()
+    product(side_x)
+    spread(side_y, 0, 0).wait_recv()
+    product(side_y)
+    for p in (0, 1):
+        spread(far, p, 0).wait_recv()
+    product(far)
+    for q in (dp, side_x, side_y, far):
+        visit_others(line, z, lambda origin: into(q, origin).wait_recv())
+        visit_others(line, z, lambda other: out(q, other).wait_send())
+        mine(q).wait()
+        all_out(q).wait()
+    for p in (0, 1):
+        for way in (0, 1):
+            spread(dp, p, way).wait_send()
+    spread(side_x, 0, 1).wait_send()
+    spread(side_y, 1, 0).wait_send()
+
+
+def out_back(own, w_out, line):
+    quarter, width = own.shape
+    depth = w_out.shape[0]
+    half = quarter // 2
+    sems = pltpu.SemaphoreType.DMA
+    dtype = own.dtype
+    anywhere, inside = pl.BlockSpec(memory_space=pl.ANY), pl.BlockSpec(memory_space=pltpu.VMEM)
+    everyone, grad = pl.pallas_call(
+        functools.partial(out_back_kernel, line),
+        out_shape=[
+            jax.ShapeDtypeStruct((4, 2, half, width), dtype),
+            jax.ShapeDtypeStruct((line, 4 * quarter, HD), dtype),
+        ],
+        in_specs=[inside, inside],
+        out_specs=[anywhere, anywhere],
+        scratch_shapes=[
+            pltpu.VMEM((4, 2, half, width), dtype),
+            pltpu.VMEM((4, quarter, depth), dtype),
+            sems((4, 2, 2)),
+            sems((4, 2)),
+            sems((2,)),
+            sems((4,)),
+            sems((4, line)),
+            sems((4, line)),
+            sems((4,)),
+        ],
+        compiler_params=pltpu.CompilerParams(
+            collective_id=8, has_side_effects=True, vmem_limit_bytes=40 << 20
+        ),
+        name="out_back",
+    )(own.reshape(2, half, width), w_out)
+    return everyone.reshape(4 * quarter, width), grad
+
+
+def by_head(layout, w_out, line):
     positions = layout[1][0]
     pack = positions.shape[0]
     span = pack // (2 * line)
@@ -724,27 +985,27 @@
         )
         k, v = k.reshape(pack, HD), v.reshape(pack, HD)
         out, total = attend(bounds, q, k, v, starts)
-        (attended,) = to_tokens([out], (False,), line, "gather_heads", 7)
-        return attended, (q, k, v, out, total)
-
-    def backward(kept, grad):
+        return *out_sum(out, w_out, line), (q, k, v, out, total)
+
+    def backward(kept, grad_own):
         q, k, v, out, total = kept
-        (grad,) = to_heads([grad], (False,), line, "scatter_grads", 8)
+        grad_all, grad = out_back(grad_own, w_out, line)
         delta = jnp.sum(grad.astype(jnp.float32) * out.astype(jnp.float32), axis=-1)
         dq, dk, dv = attend_back(bounds, q, k, v, starts, total, delta[:, None, :], grad)
         shape = (line, 2, span, HD)
-        return to_tokens(
+        grads = to_tokens(
             [dq, dk.reshape(shape), dv.reshape(shape)],
             (False, True, True),
             line,
             "gather_grads",
             9,
         )
+        return grad_all, *grads
 
     return forward, backward
 
 
-def by_query(layout, offset_rows):
+def by_query(layout, w_out, offset_rows):
     segment = layout[0][0]
     pack = segment.shape[0]
 
@@ -771,10 +1032,14 @@
         total = largest + jnp.log(jnp.sum(jnp.exp(scores - largest), axis=-1, keepdims=True))
         weights = jnp.exp(scores - total).astype(jnp.bfloat16)
         attended = jnp.einsum("hsl,lhd->shd", weights, v, preferred_element_type=jnp.float32)
-        return attended.astype(jnp.bfloat16).reshape(queries.shape), (q, k, v, total)
-
-    def backward(kept, grad):
+        attended = attended.astype(jnp.bfloat16).reshape(queries.shape)
+        projected = scatter_dp(contract(attended, w_out, 1, 0).astype(jnp.bfloat16))
+        return attended, projected, (q, k, v, total)
+
+    def backward(kept, grad_own):
         q, k, v, total = kept
+        grad_all = gather_dp(grad_own)
+        grad = contract(grad_all, w_out, 1, 1).astype(jnp.bfloat16)
         shape = grad.shape
         grad = heads(grad)
         weights = jnp.exp(score_block(q, k) - total)
@@ -791,7 +1056,8 @@
             return lax.psum_scatter(part, "expert", scatter_dimension=0, tiled=True)
 
         scale = HD ** (-0.5)
-        return (dq * scale).reshape(shape), to_owner(dk * scale), to_owner(dv)
+        dq = (dq * scale).reshape(shape)
+        return grad_all, dq, to_owner(dk * scale), to_owner(dv)
 
     return forward, backward
 
@@ -2032,20 +2298,17 @@
     )
     layout = (segment, positions)
     if local_heads == line:
-        attention = by_head(layout, line)
+        attention = by_head(layout, w_out, line)
     else:
-        attention = by_query(layout, offset_rows)
-    attended, kept = attention[0](queries, keys, value_rows)
-    attn_part = jnp.dot(
-        attended, w_out, preferred_element_type=jnp.float32
-    )
+        attention = by_query(layout, w_out, offset_rows)
+    attended, projected, kept = attention[0](queries, keys, value_rows)
     own = lax.axis_index("dp")
     part_rows = seg_rows // lax.axis_size("dp")
 
     def own_rows(rows):
         return lax.dynamic_slice_in_dim(rows, own * part_rows, part_rows, 0)
 
-    hidden_state = own_rows(inputs_single_float[0]) + scatter_dp(attn_part.astype(jnp.bfloat16))
+    hidden_state = own_rows(inputs_single_float[0]) + projected
     second_inverse_norm = lax.rsqrt(
         jnp.mean(hidden_state * hidden_state, axis=-1, keepdims=True) + epsilon
     )
@@ -2106,12 +2369,10 @@
         - second_unit_input
         * jnp.mean(grad_second_unit_input * second_unit_input, axis=-1, keepdims=True)
     )
-    grad_attn = gather_dp(grad_hidden.astype(jnp.bfloat16))
+    grad_attn, grad_queries, grad_keys, grad_values = attention[1](
+        kept, grad_hidden.astype(jnp.bfloat16)
+    )
     grad_out = jnp.einsum("sk,sd->kd", attended, grad_attn, preferred_element_type=jnp.float32)
-    grad_heads = jnp.einsum(
-        "sd,kd->sk", grad_attn, w_out, preferred_element_type=jnp.float32
-    ).astype(jnp.bfloat16)
-    grad_queries, grad_keys, grad_values = attention[1](kept, grad_heads)
     grad_heads_raw, gain_grads = normed_heads_back(
         grad_queries.astype(jnp.bfloat16),
         grad_keys,

time: 720 us -> 677 us (0.940)
  Pallas kernels: 595 us -> 562 us
  matrix products: 33.5 us -> 23.9 us
    pallas_call x2 -> x1, Pallas kernels: 74 us -> 40.6 us  [to_tokens(): pl.pallas_call(functools.partial(to_tokens_kernel, line, summed), out_sha...]
    pallas_call x2 -> x1, Pallas kernels: 85 us -> 62.5 us  [to_heads(): pl.pallas_call(functools.partial(to_heads_kernel, line, shared), out_shap...]
    pallas_call x2, Pallas kernels: 44.9 us -> 66.8 us  [the longest x1 40.3 us: out_sum(): pl.pallas_call(functools.partial(out_sum_kernel, line), out_shape=[jax.Sh...]
    dot_general x2 -> x0, matrix products: 7.98 us -> none  [the longest x1 4.36 us: per_device(): jnp.einsum('sd,kd->sk', grad_attn, w_out, preferred_element_type=jnp.floa...]
  transfers between devices with their start and end apart: 2 -> 2, of which waited for: 0 -> 0; matrix products, arithmetic and copies ran while one was open for 11% -> 11% of each run, Pallas kernels for 57% -> 54%
where the time goes in v8:
time: 677 us; the launch traced here: 670 us
  Pallas kernels  562 us (83%)
  other arithmetic  38.5 us (6%)
  local copies, waits for them, and re-layouts  31.3 us (5%)
  matrix products  23.9 us (4%)
  between operations  15 us (2%)
    pallas_call x2, Pallas kernels, product_sum(): pl.pallas_call(functools.partial(product_sum_kernel, line, flipped, extra...  171 us
    pallas_call x1, Pallas kernels, gate_act(): pl.pallas_call(functools.partial(gate_act_kernel, line), out_shape=[jax.S...  86.5 us
    pallas_call x1, Pallas kernels, closing(): pl.pallas_call(functools.partial(closing_kernel, line, shared_rows), out_...  81.5 us
    pallas_call x1, Pallas kernels, to_heads(): pl.pallas_call(functools.partial(to_heads_kernel, line, shared), out_shap...  62.5 us
    pallas_call x1, Pallas kernels, to_tokens(): pl.pallas_call(functools.partial(to_tokens_kernel, line, summed), out_sha...  40.6 us
    pallas_call x1, Pallas kernels, out_sum(): pl.pallas_call(functools.partial(out_sum_kernel, line), out_shape=[jax.Sh...  40.3 us
    pallas_call x1, Pallas kernels, out_back(): pl.pallas_call(functools.partial(out_back_kernel, line), out_shape=[jax.S...  26.5 us
    pallas_call x1, Pallas kernels, attend_back(): pl.pallas_call(attend_back_kernel, grid_spec=pltpu.PrefetchScalarGridSpec...  18.3 us
  transfers between devices with their start and end apart: 2, of which 0 were waited for; matrix products, arithmetic and copies ran while one was open for 11% of the time, Pallas kernels for 54%

profile of v8, /device:TPU:24, one launch (start us, length us, event | category | flops | bytes accessed | tf_op | source)
XLA Modules:
  0.0 670.2 jit_solution(1660688864661108811)
XLA Ops:
  11.0 4.3 convert_element_type.98
  20.4 9.2 %normed_heads.1 = (bf16[512,512]{1,0:T(8,128)(2,1)S(1)}, bf16[512,512]{1,0:T(8,128)(2,1)S(1)}, f32[16,512]{1,0:T(8,128)S(1)}) custom-call(f32[512,512]{1,0:T(8,128)S(1)} %fusion.28.q_ref, f32[512,512]{1,0:T(8,128)S(1)} %fusion.26.k_ref, f32[1,512]{1,0:T(1,128)S(1)} %bitcast.84, f32[1,512]{1,0:T(1,128)S(1)} %bitcast.86, ...), custom_call_target="tpu_custom_call" | custom-call | tf_op jit(solution)/shard_map/normed_heads/pallas_call | solution.py:2156
  31.8 62.5 %scatter_heads.1 = (bf16[4,512,128]{2,1,0:T(8,128)(2,1)}, bf16[4,2,512,128]{3,2,1,0:T(8,128)(2,1)}, bf16[4,2,512,128]{3,2,1,0:T(8,128)(2,1)}) custom-call(bf16[512,512]{1,0:T(8,128)(2,1)} %copy-done.17, bf16[512,512]{1,0:T(8,128)(2,1)} %copy-done.18, bf16[512,512]{1,0:T(8,128)(2,1)} %convolution_convert_fusion.3.refs_2_), custom_call_target="tpu_custom_call" | custom-call | tf_op jit(solution)/shard_map/scatter_heads/pallas_call | solution.py:474
  95.1 13.6 %attend.1 = (bf16[4,512,128]{2,1,0:T(8,128)(2,1)}, f32[4,1,512]{2,1,0:T(1,128)}) custom-call(s32[3,4]{1,0:T(4,128)} %pad_add_fusion.bounds, bf16[4,512,128]{2,1,0:T(8,128)(2,1)} %get-tuple-element.48.q_ref, bf16[4096,128]{1,0:T(8,128)(2,1)} %bitcast.99, bf16[4096,128]{1,0:T(8,128)(2,1)} %bitcast.101, s32[4,1,512]{2,1,0:T(1,128)} %copy-done.41), custom_call_target="tpu_custom_call" | custom-call | tf_op jit(solution)/shard_map/attend/pallas_call | solution.py:672
  109.8 40.3 %out_sum.1 = (bf16[512,512]{1,0:T(8,128)(2,1)S(1)}, f32[2,64,2048]{2,1,0:T(8,128)S(1)}) custom-call(bf16[4,512,128]{2,1,0:T(8,128)(2,1)S(1)} %copy-done.11, bf16[512,2048]{1,0:T(8,128)(2,1)S(1)} %copy-done.2), custom_call_target="tpu_custom_call" | custom-call | tf_op jit(solution)/shard_map/out_sum/pallas_call | solution.py:820
  150.1 2.9 multiply_reduce_fusion.4
  157.3 2.7 slice_bitcast_fusion.1
  164.7 86.5 %gate_act.1 = (bf16[32,2,64,2048]{3,2,1,0:T(8,128)(2,1)}, bf16[16,256,1024]{2,1,0:T(8,128)(2,1)}, bf16[16,256,512]{2,1,0:T(8,128)(2,1)}, bf16[16,256,128]{2,1,0:T(8,128)(2,1)}) custom-call(bf16[2,64,2176]{2,1,0:T(8,128)(2,1)} %bitcast.105, bf16[16,256,2048]{2,1,0:T(8,128)(2,1)} %bitcast.89, bf16[2,2048,256]{2,1,0:T(8,128)(2,1)} %wg_ref.1, ...), custom_call_target="tpu_custom_call" | custom-call | tf_op jit(solution)/shard_map/gate_act/pallas_call | solution.py:1283
  251.3 84.9 %grad_tokens.1 = f32[2,64,2176]{2,1,0:T(8,128)} custom-call(bf16[16,256,1024]{2,1,0:T(8,128)(2,1)} %get-tuple-element.54.refs_0_.refs_3_, bf16[2048,1024]{1,0:T(8,128)(2,1)} %pad_maximum_fusion.refs_1_, bf16[16,256,128]{2,1,0:T(8,128)(2,1)} %get-tuple-element.55.refs_2_), custom_call_target="tpu_custom_call" | custom-call | tf_op jit(solution)/shard_map/grad_tokens/pallas_call | solution.py:1701
  337.3 2.9 multiply_reduce_fusion.1
  342.7 26.5 %out_back.1 = (bf16[4,2,64,2048]{3,2,1,0:T(8,128)(2,1)S(1)}, bf16[4,512,128]{2,1,0:T(8,128)(2,1)S(1)}) custom-call(bf16[2,64,2048]{2,1,0:T(8,128)(2,1)S(1)} %bitcast.83, bf16[512,2048]{1,0:T(8,128)(2,1)S(1)} %copy-done.3), custom_call_target="tpu_custom_call" | custom-call | tf_op jit(solution)/shard_map/out_back/pallas_call | solution.py:943
  369.3 2.6 convolution_convert_fusion.1
  378.1 18.3 %attend_back.1 = (bf16[4,512,128]{2,1,0:T(8,128)(2,1)}, bf16[4096,128]{1,0:T(8,128)(2,1)}, bf16[4096,128]{1,0:T(8,128)(2,1)}) custom-call(s32[3,4]{1,0:T(4,128)} %pad_add_fusion.bounds, bf16[4,512,128]{2,1,0:T(8,128)(2,1)} %get-tuple-element.48.q_ref, bf16[4096,128]{1,0:T(8,128)(2,1)} %bitcast.100, bf16[4096,128]{1,0:T(8,128)(2,1)} %bitcast.102, ...), custom_call_target="tpu_custom_call" | custom-call | tf_op jit(solution)/shard_map/attend_back/pallas_call | solution.py:694
  396.4 40.6 %gather_grads.1 = (bf16[512,512]{1,0:T(8,128)(2,1)}, bf16[512,512]{1,0:T(8,128)(2,1)}, bf16[512,512]{1,0:T(8,128)(2,1)}) custom-call(bf16[4,512,128]{2,1,0:T(8,128)(2,1)} %get-tuple-element.57.refs_0_, bf16[4,2,512,128]{3,2,1,0:T(8,128)(2,1)} %bitcast.111, bf16[4,2,512,128]{3,2,1,0:T(8,128)(2,1)} %bitcast.112), custom_call_target="tpu_custom_call" | custom-call | tf_op jit(solution)/shard_map/gather_grads/pallas_call | solution.py:575
  440.2 11.9 %normed_heads_back.1 = (bf16[512,1536]{1,0:T(8,128)(2,1)S(1)}, f32[16,512]{1,0:T(8,128)S(1)}) custom-call(bf16[512,512]{1,0:T(8,128)(2,1)S(1)} %copy-done.14, bf16[512,512]{1,0:T(8,128)(2,1)S(1)} %copy-done.15, bf16[512,512]{1,0:T(8,128)(2,1)S(1)} %copy-done.16, f32[512,512]{1,0:T(8,128)S(1)} %copy-done.8, f32[512,512]{1,0:T(8,128)S(1)} %copy-done.6, ...), custom_call_target="tpu_custom_call" | custom-call | tf_op jit(solution)/shard_map/normed_heads_back/pallas_call | solution.py:2224
  456.5 2.9 fusion.31
  460.9 85.7 %expert_sum.1 = (f32[2,64,2048]{2,1,0:T(8,128)}, bf16[2,2048,256]{2,1,0:T(8,128)(2,1)}, bf16[2,2048,256]{2,1,0:T(8,128)(2,1)}) custom-call(bf16[16,256,512]{2,1,0:T(8,128)(2,1)} %get-tuple-element.66.refs_0_.scaled_ref, bf16[512,2048]{1,0:T(8,128)(2,1)} %bitcast.93, bf16[4096,2048]{1,0:T(8,128)(2,1)} %bitcast.91, ...), custom_call_target="tpu_custom_call" | custom-call | tf_op jit(solution)/shard_map/expert_sum/pallas_call | solution.py:1701
  546.6 3.0 add_convert_fusion.output_ref
  549.6 5.5 convolution_convert_fusion
  555.1 81.5 %closing.1 = (f32[2,144,1536]{2,1,0:T(8,128)}, f32[2,16,1536]{2,1,0:T(8,128)}, bf16[4,2,64,2048]{3,2,1,0:T(8,128)(2,1)}, bf16[4,2,64,2048]{3,2,1,0:T(8,128)(2,1)}, bf16[2,256,2048]{2,1,0:T(8,128)(2,1)}) custom-call(bf16[4,2,2,128,1536]{4,3,2,1,0:T(8,128)(2,1)} %bitcast.94, bf16[4,2,2,16,1536]{4,3,2,1,0:T(8,128)(2,1)} %bitcast.104, ...), custom_call_target="tpu_custom_call" | custom-call | tf_op jit(solution)/shard_map/closing/pallas_call | solution.py:2037
  641.1 4.3 convert.28
  645.4 2.5 convert_element_type.121
  648.6 4.1 convert_element_type.119
  659.9 3.2 copy.56
  (160 shorter events, 52.8 us)
Async XLA Ops:
  7.2 145.8 %copy-start = (f32[2048,16]{0,1:T(8,128)S(1)}, f32[2048,16]{0,1:T(8,128)}, u32[]{:S(2)}) copy-start(f32[2048,16]{0,1:T(8,128)} %param.25) | copy-start | bytes 393220
  7.2 157.5 %all-gather.3.cloned.1.call-start = ((), (), s32[]{:S(2)}) async-start(), calls=%async_computation.2 | async-start | bytes 17301504 | tf_op jit(solution)/shard_map/all_gather | solution.py:2324
  9.2 649.0 %reduce-scatter.2.cloned.1.call-start = ((), (), s32[]{:S(2)}) async-start(), calls=%async_computation.1 | async-start | bytes 2359296 | tf_op jit(solution)/shard_map/reduce_scatter | solution.py:2429
  11.0 4.3 copy-start.26
  20.4 11.4 %copy-start.7 = (f32[512,512]{1,0:T(8,128)}, f32[512,512]{1,0:T(8,128)S(1)}, u32[]{:S(2)}) copy-start(f32[512,512]{1,0:T(8,128)S(1)} %fusion.28.q_ref) | copy-start | bytes 3145732
  20.4 9.2 %copy-start.36 = (bf16[2048,512]{1,0:T(8,128)(2,1)S(1)}, bf16[2048,512]{1,0:T(8,128)(2,1)}, u32[]{:S(2)}) copy-start(bf16[2048,512]{1,0:T(8,128)(2,1)} %param.20) | copy-start | bytes 6291460
  31.7 77.0 %copy-start.2 = (bf16[512,2048]{1,0:T(8,128)(2,1)S(1)}, bf16[512,2048]{1,0:T(8,128)(2,1)}, u32[]{:S(2)}) copy-start(bf16[512,2048]{1,0:T(8,128)(2,1)} %w_ref.3) | copy-start | bytes 6291460
  150.0 3.0 copy-start.40
  153.0 4.3 copy-start.23
  336.1 4.0 copy-start.24
  342.7 26.6 %copy-start.22 = (bf16[512,512]{1,0:T(8,128)(2,1)S(1)}, bf16[512,512]{1,0:T(8,128)(2,1)}, u32[]{:S(2)}) copy-start(bf16[512,512]{1,0:T(8,128)(2,1)} %copy-done.21) | copy-start | bytes 1572868
  369.3 7.8 %copy-start.13 = (bf16[4,512,128]{2,1,0:T(8,128)(2,1)}, bf16[4,512,128]{2,1,0:T(8,128)(2,1)S(1)}, u32[]{:S(2)}) copy-start(bf16[4,512,128]{2,1,0:T(8,128)(2,1)S(1)} %get-tuple-element.56.d_ref) | copy-start | bytes 1572868
  371.9 5.2 copy-start.12
  396.4 40.7 %copy-start.6 = (f32[512,512]{1,0:T(8,128)S(1)}, f32[512,512]{1,0:T(8,128)}, u32[]{:S(2)}) copy-start(f32[512,512]{1,0:T(8,128)} %copy-done.5) | copy-start | bytes 3145732
  396.4 40.7 %copy-start.8 = (f32[512,512]{1,0:T(8,128)S(1)}, f32[512,512]{1,0:T(8,128)}, u32[]{:S(2)}) copy-start(f32[512,512]{1,0:T(8,128)} %copy-done.7) | copy-start | bytes 3145732
  440.2 11.9 %copy-start.33 = (bf16[2048,512]{1,0:T(8,128)(2,1)S(1)}, bf16[2048,512]{1,0:T(8,128)(2,1)}, u32[]{:S(2)}) copy-start(bf16[2048,512]{1,0:T(8,128)(2,1)} %param.18) | copy-start | bytes 6291460
  452.1 3.5 copy-start.9
  546.6 3.0 copy-start.10
  546.6 3.0 copy-start.29
  636.6 3.2 copy-start.38
  641.1 4.3 copy-start.31
  645.4 3.2 copy-start.39
  648.6 4.1 copy-start.30
  659.9 3.2 copy-start.1
  (21 other events, 37.4 us)
Sparse Core Ops, SparseCore 0:
  11.6 148.0 all-gather.2
  372.0 32.5 reduce-scatter.1

commit v9 on v8

--- a/solution.py
+++ b/solution.py
@@ -1432,6 +1432,175 @@
 SPAN = 256
 
 
+def line_sum(
+    line,
+    parts_ref,
+    small_ref,
+    summed_ref,
+    shared_ref,
+    acc,
+    got_pair,
+    got_below,
+    got_above,
+    small,
+    got_small,
+    load_sem,
+    pair_sem,
+    load_small_sem,
+    pair_small_sem,
+    below_sem,
+    above_sem,
+    small_sem,
+    summed_sem,
+):
+    dp, place = lax.axis_index("dp"), lax.axis_index("expert")
+    z, c = place // 2, place % 2
+    side_x, side_y = corners(dp)
+    to_pair, to_up, to_down = (dp, 2 * z + 1 - c), (dp, place + 2), (dp, place - 2)
+    large = parts_ref.shape[3]
+    top_rows, low_rows = pl.ds(0, large), pl.ds(large, small_ref.shape[3])
+
+    def loads(height, p):
+        return (
+            pltpu.make_async_copy(
+                parts_ref.at[height, c, p], acc.at[height, p, top_rows], load_sem.at[height, p]
+            ),
+            pltpu.make_async_copy(
+                small_ref.at[height, c, p], acc.at[height, p, low_rows], load_small_sem.at[height, p]
+            ),
+        )
+
+    def hands(height, p):
+        at = (height, p)
+        return (
+            send(
+                parts_ref.at[height, 1 - c, p],
+                got_pair.at[height, p, top_rows],
+                pair_sem.at[0, *at],
+                pair_sem.at[1, *at],
+                to_pair,
+            ),
+            send(
+                small_ref.at[height, 1 - c, p],
+                got_pair.at[height, p, low_rows],
+                pair_small_sem.at[0, *at],
+                pair_small_sem.at[1, *at],
+                to_pair,
+            ),
+        )
+
+    def climb(height, p):
+        at = (height, p)
+        return send(
+            acc.at[at], got_below.at[at], below_sem.at[0, *at], below_sem.at[1, *at], to_up
+        )
+
+    def descend(height, p):
+        at = (height, p)
+        return send(
+            acc.at[at], got_above.at[at], above_sem.at[0, *at], above_sem.at[1, *at], to_down
+        )
+
+    def start(k, carry):
+        height = farthest(line, z, k)
+        for p in (0, 1):
+            for copy in (*loads(height, p), *hands(height, p)):
+                copy.start()
+        return carry
+
+    def pair_sum(k, carry):
+        height = farthest(line, z, k)
+        for p in (0, 1):
+            for copy in loads(height, p):
+                copy.wait()
+            for copy in hands(height, p):
+                copy.wait_recv()
+            acc[height, p] = acc[height, p] + got_pair[height, p]
+            pl.when((z == 0) & (height > z))(lambda: climb(height, p).start())
+            pl.when((z == line - 1) & (height < z))(lambda: descend(height, p).start())
+        return carry
+
+    def pass_on(k, carry):
+        height = farthest(line, z, k)
+        for p in (0, 1):
+
+            def upwards():
+                climb(height, p).wait_recv()
+                acc[height, p] = acc[height, p] + got_below[height, p]
+                climb(height, p).start()
+
+            def downwards():
+                descend(height, p).wait_recv()
+                acc[height, p] = acc[height, p] + got_above[height, p]
+                descend(height, p).start()
+
+            pl.when((height > z) & (z > 0))(upwards)
+            pl.when((height < z) & (z < line - 1))(downwards)
+        return carry
+
+    def summed_out(p):
+        return pltpu.make_async_copy(acc.at[z, p], summed_ref.at[p], summed_sem.at[p])
+
+    def end():
+        for p in (0, 1):
+
+            def from_below():
+                climb(z, p).wait_recv()
+                acc[z, p] = acc[z, p] + got_below[z, p]
+
+            def from_above():
+                descend(z, p).wait_recv()
+                acc[z, p] = acc[z, p] + got_above[z, p]
+
+            pl.when(z > 0)(from_below)
+            pl.when(z < line - 1)(from_above)
+        small[0] = acc[z, :, large:, :]
+
+        def finish(height, carry):
+            for p in (0, 1):
+                for copy in hands(height, p):
+                    copy.wait_send()
+                pl.when(height > z)(lambda: climb(height, p).wait_send())
+                pl.when(height < z)(lambda: descend(height, p).wait_send())
+            return carry
+
+        lax.fori_loop(0, line, finish, 0)
+        for side, device in enumerate(((side_x, place), (side_y, place))):
+            exchange = send(
+                small.at[side],
+                got_small.at[side],
+                small_sem.at[0, side],
+                small_sem.at[1, side],
+                device,
+            )
+            exchange.start()
+            exchange.wait_recv()
+            total = small[side].astype(jnp.float32) + got_small[side].astype(jnp.float32)
+            if side == 0:
+                small[1] = total.astype(small.dtype)
+                for p in (0, 1):
+                    summed_out(p).start()
+            else:
+                shared_ref[...] = total
+            exchange.wait_send()
+        for p in (0, 1):
+            summed_out(p).wait()
+
+    return start, pair_sum, pass_on, end
+
+
+def line_sum_space(line, rows, small_rows, wide, dtype):
+    high = (rows + small_rows) // 2
+    sems = pltpu.SemaphoreType.DMA
+    return (
+        [pltpu.VMEM((line, 2, high, wide), dtype)] * 4
+        + [pltpu.VMEM((2, 2, small_rows // 2, wide), dtype)] * 2
+        + [sems((line, 2)), sems((2, line, 2))] * 2
+        + [sems((2, line, 2))] * 2
+        + [sems((2, 2)), sems((2,))]
+    )
+
+
 def product_sum_kernel(
     line,
     flipped,
@@ -1443,7 +1612,8 @@
     e_ref = refs[2] if extra else None
     refs = refs[3:] if extra else refs[2:]
     if grads:
-        work_refs, refs = (*refs[:2], *refs[3:5], *refs[-7:]), (refs[2], *refs[5:-7])
+        top_ref, parts_ref, small_ref, out_ref, down_ref, summed_ref, shared_ref = refs[:7]
+        refs, work_refs, sum_refs = (out_ref, *refs[7:-21]), refs[-21:-14], refs[-14:]
     (
         out_ref,
         made,
@@ -1625,7 +1795,12 @@
             pl.when((height < z) & (z < line - 1))(downwards)
 
     start_load(0)
-    work, work_end, turns = gate_up_grads(*work_refs) if grads else (None, None, 1)
+    if grads:
+        work, work_end, turns = down_grads(top_ref, a_ref, down_ref, *work_refs)
+        line_start, line_pair, line_pass, line_end = line_sum(
+            line, parts_ref, small_ref, summed_ref, shared_ref, *sum_refs
+        )
+        lax.fori_loop(0, line, line_start, 0)
 
     def step(i, carry):
         k, j, _, _ = decode(i)
@@ -1634,6 +1809,15 @@
         if grads:
             every = count // turns
             pl.when((i < count) & (i % every == 0))(lambda: work(i // every))
+
+            @pl.when(i < line)
+            def _():
+                line_pair(i, 0)
+
+            @pl.when((i >= 6) & (i % 4 == 2) & (i < 6 + 4 * line))
+            def _():
+                line_pass((i - 6) // 4, 0)
+
         pl.when((i >= 4) & (i < count + 4))(lambda: settle_far(i - 4))
         pl.when((k >= 3) & (j == 2))(lambda: pass_on(farthest(line, z, k - 3)))
         pl.when((k >= 2) & (j == 3))(lambda: column(farthest(line, z, k - 2)))
@@ -1641,6 +1825,7 @@
 
     lax.fori_loop(0, count + 8, step, 0)
     if grads:
+        line_end()
         work_end()
     for p in (0, 1):
         out_ref[p] = made[dp, z, c, p].astype(jnp.float32)
@@ -1686,17 +1871,30 @@
     out_shape = [jax.ShapeDtypeStruct((2, half, wide), jnp.float32)]
     work_in, work_space = [], []
     if grads is not None:
-        xn, both, shape = grads
-        work_in = [xn, both]
-        out_shape += [jax.ShapeDtypeStruct(shape, dtype)] * 2
+        tops, parts, small, shape = grads
+        local, units, _ = shape
+        _, large, wider = parts.shape
+        small_rows = small.shape[1]
+        span = SPAN if large >= 8 * small_rows else SPAN // 2
+        work_in = [
+            tops,
+            parts.reshape(line, 2, 2, large // 2, wider),
+            small.reshape(line, 2, 2, small_rows // 2, wider),
+        ]
+        out_shape += [
+            jax.ShapeDtypeStruct(shape, dtype),
+            jax.ShapeDtypeStruct((2, (large + small_rows) // 2, wider), dtype),
+            jax.ShapeDtypeStruct((2, small_rows // 2, wider), jnp.float32),
+        ]
         work_space = [
-            pltpu.VMEM((2, xn.shape[0], SPAN), dtype),
-            pltpu.VMEM(both.shape, dtype),
-            pltpu.VMEM((SPAN, both.shape[2]), jnp.float32),
-            pltpu.VMEM((SPAN, both.shape[2]), dtype),
+            pltpu.VMEM((2, tops.shape[0], span), dtype),
+            pltpu.VMEM(blocks.shape, dtype),
+            pltpu.VMEM((span, local * units), jnp.float32),
+            pltpu.VMEM((local, units, span), dtype),
             sems((2,)),
             sems((1,)),
-            sems((2, shape[0])),
+            sems((local,)),
+            *line_sum_space(line, large, small_rows, wider, dtype),
         ]
     total, *work_out = pl.pallas_call(
         functools.partial(product_sum_kernel, line, flipped, extra is not None, grads is not None),
@@ -1704,7 +1902,7 @@
         in_specs=[anywhere, inside]
         + ([] if extra is None else [anywhere])
         + [anywhere] * len(work_in),
-        out_specs=[inside] + [anywhere] * (len(out_shape) - 1),
+        out_specs=[inside] + ([] if grads is None else [anywhere, anywhere, inside]),
         scratch_shapes=[
             space(4, line, 2, 2),
             pltpu.VMEM((2, rows, depth), dtype),
@@ -1736,41 +1934,24 @@
 
 
 def closing_kernel(
-    line,
-    shared_rows,
-    parts_ref,
-    small_ref,
     first_ref,
     grad_ref,
     unit_ref,
     inverse_ref,
     gain_ref,
     output_ref,
-    top_ref,
-    scaled_ref,
-    summed_ref,
-    shared_ref,
+    xn_ref,
+    units_ref,
     outputs_ref,
     grads_ref,
-    down_ref,
-    acc,
-    got_pair,
-    got_below,
-    got_above,
+    gate_ref,
+    up_ref,
     part,
     got_x,
     got_y,
     got_far_x,
     got_far_y,
     grad_own,
-    small,
-    got_small,
-    load_sem,
-    pair_sem,
-    load_small_sem,
-    pair_small_sem,
-    below_sem,
-    above_sem,
     part_sem,
     x_sem,
     y_sem,
@@ -1779,102 +1960,12 @@
     spread_sem,
     arrive_sem,
     own_sem,
-    small_sem,
     *work_refs,
 ):
     dp, place = lax.axis_index("dp"), lax.axis_index("expert")
-    z, c = place // 2, place % 2
     side_x, side_y = corners(dp)
     far = 3 - dp
-    to_x, to_y, to_pair = (side_x, place), (side_y, place), (dp, 2 * z + 1 - c)
-    to_up, to_down = (dp, place + 2), (dp, place - 2)
-    for device in (to_x, to_y, to_pair):
-        greet(device)
-    pl.when(z > 0)(lambda: greet(to_down))
-    pl.when(z < line - 1)(lambda: greet(to_up))
-    greeted = 3 + (z > 0).astype(jnp.int32) + (z < line - 1).astype(jnp.int32)
-    pl.semaphore_wait(pltpu.get_barrier_semaphore(), greeted)
-
-    large = parts_ref.shape[3]
-    top_rows, low_rows = pl.ds(0, large), pl.ds(large, shared_rows // 2)
-
-    def loads(height, p):
-        return (
-            pltpu.make_async_copy(
-                parts_ref.at[height, c, p], acc.at[height, p, top_rows], load_sem.at[height, p]
-            ),
-            pltpu.make_async_copy(
-                small_ref.at[height, c, p], acc.at[height, p, low_rows], load_small_sem.at[height, p]
-            ),
-        )
-
-    def hands(height, p):
-        at = (height, p)
-        return (
-            send(
-                parts_ref.at[height, 1 - c, p],
-                got_pair.at[height, p, top_rows],
-                pair_sem.at[0, *at],
-                pair_sem.at[1, *at],
-                to_pair,
-            ),
-            send(
-                small_ref.at[height, 1 - c, p],
-                got_pair.at[height, p, low_rows],
-                pair_small_sem.at[0, *at],
-                pair_small_sem.at[1, *at],
-                to_pair,
-            ),
-        )
-
-    def climb(height, p):
-        at = (height, p)
-        return send(
-            acc.at[at], got_below.at[at], below_sem.at[0, *at], below_sem.at[1, *at], to_up
-        )
-
-    def descend(height, p):
-        at = (height, p)
-        return send(
-            acc.at[at], got_above.at[at], above_sem.at[0, *at], above_sem.at[1, *at], to_down
-        )
-
-    def start(k, carry):
-        height = farthest(line, z, k)
-        for p in (0, 1):
-            for copy in (*loads(height, p), *hands(height, p)):
-                copy.start()
-        return carry
-
-    def pair_sum(k, carry):
-        height = farthest(line, z, k)
-        for p in (0, 1):
-            for copy in loads(height, p):
-                copy.wait()
-            for copy in hands(height, p):
-                copy.wait_recv()
-            acc[height, p] = acc[height, p] + got_pair[height, p]
-            pl.when((z == 0) & (height > z))(lambda: climb(height, p).start())
-            pl.when((z == line - 1) & (height < z))(lambda: descend(height, p).start())
-        return carry
-
-    def pass_on(k, carry):
-        height = farthest(line, z, k)
-        for p in (0, 1):
-
-            def upwards():
-                climb(height, p).wait_recv()
-                acc[height, p] = acc[height, p] + got_below[height, p]
-                climb(height, p).start()
-
-            def downwards():
-                descend(height, p).wait_recv()
-                acc[height, p] = acc[height, p] + got_above[height, p]
-                descend(height, p).start()
-
-            pl.when((height > z) & (z > 0))(upwards)
-            pl.when((height < z) & (z < line - 1))(downwards)
-        return carry
+    to_x, to_y = meet_square(dp, place)
 
     def first_load(q, p):
         return pltpu.make_async_copy(first_ref.at[q, p], part.at[q, p], part_sem.at[q, p])
@@ -1919,7 +2010,7 @@
         spread(a, side_y, 1, 0).wait_recv()
         spread(a, side_y, 1, 0).start()
 
-    work, work_end, turns = down_grads(top_ref, scaled_ref, down_ref, *work_refs)
+    work, work_end, turns = gate_up_grads(xn_ref, units_ref, gate_ref, up_ref, *work_refs)
     pauses = 4
 
     def meanwhile(i):
@@ -1929,11 +2020,9 @@
 
         lax.fori_loop(turns * i // pauses, turns * (i + 1) // pauses, turn, 0)
 
-    lax.fori_loop(0, 1, start, 0)
     for q in (far, side_x, side_y, dp):
         for p in (0, 1):
             first_load(q, p).start()
-    lax.fori_loop(1, line, start, 0)
     for q in (far, side_x, side_y, dp):
         for p in (0, 1):
             first_load(q, p).wait()
@@ -1941,18 +2030,16 @@
     far_y().start()
     along_x(0).start()
     along_y(1).start()
-    lax.fori_loop(0, 1, pair_sum, 0)
+    for p in (0, 1):
+        spread_own(0, p)
     far_x().wait_recv()
     part[side_y, 0] = part[side_y, 0] + got_far_x[...]
     along_y(0).start()
     far_y().wait_recv()
     part[side_x, 1] = part[side_x, 1] + got_far_y[...]
     along_x(1).start()
-    for p in (0, 1):
-        spread_own(0, p)
-    lax.fori_loop(1, line, pair_sum, 0)
     meanwhile(0)
-    lax.fori_loop(0, 1, pass_on, 0)
+    spread_far(0)
     for p in (0, 1):
         along_x(p).wait_recv()
         along_y(p).wait_recv()
@@ -1965,105 +2052,47 @@
         grad_own[p] = rows.astype(grad_own.dtype)
         spread_own(1, p)
     meanwhile(1)
-    spread_far(0)
-    lax.fori_loop(1, 2, pass_on, 0)
+    meanwhile(2)
     spread_far(1)
-    meanwhile(2)
-    lax.fori_loop(2, line, pass_on, 0)
     meanwhile(3)
-    for p in (0, 1):
-        summed_ref[p] = acc[z, p].astype(jnp.float32)
-
-        def from_below():
-            climb(z, p).wait_recv()
-            summed_ref[p] = summed_ref[p] + got_below[z, p].astype(jnp.float32)
-
-        def from_above():
-            descend(z, p).wait_recv()
-            summed_ref[p] = summed_ref[p] + got_above[z, p].astype(jnp.float32)
-
-        pl.when(z > 0)(from_below)
-        pl.when(z < line - 1)(from_above)
-
-    for side, device in enumerate((to_x, to_y)):
-        value = summed_ref[:, large:, :] if side == 0 else shared_ref[...]
-        small[side] = value.astype(small.dtype)
-        spread(side, side_x, 1, 0).wait_recv()
-        spread(side, side_y, 0, 0).wait_recv()
+    for a in (0, 1):
+        spread(a, side_x, 1, 0).wait_recv()
+        spread(a, side_y, 0, 0).wait_recv()
         for p in (0, 1):
-            spread(side, far, p, 0).wait_recv()
+            spread(a, far, p, 0).wait_recv()
             for way in (0, 1):
-                spread(side, dp, p, way).wait_send()
-            own_copy(side, p).wait()
-        spread(side, side_x, 0, 1).wait_send()
-        spread(side, side_y, 1, 0).wait_send()
-        exchange = send(
-            small.at[side], got_small.at[side], small_sem.at[0, side], small_sem.at[1, side], device
-        )
-        exchange.start()
-        exchange.wait_recv()
-        shared_ref[...] = small[side].astype(jnp.float32) + got_small[side].astype(jnp.float32)
-        exchange.wait_send()
-
+                spread(a, dp, p, way).wait_send()
+            own_copy(a, p).wait()
+        spread(a, side_x, 0, 1).wait_send()
+        spread(a, side_y, 1, 0).wait_send()
     far_x().wait_send()
     far_y().wait_send()
     for p in (0, 1):
         along_x(p).wait_send()
         along_y(p).wait_send()
-
-    def finish(height, carry):
-        for p in (0, 1):
-            for copy in hands(height, p):
-                copy.wait_send()
-            pl.when(height > z)(lambda: climb(height, p).wait_send())
-            pl.when(height < z)(lambda: descend(height, p).wait_send())
-        return carry
-
-    lax.fori_loop(0, line, finish, 0)
     work_end()
 
 
-def closing(parts, small, first, grad, unit, inverse, gain, output, tops, scaled, shape, line):
-    _, rows, wide = parts.shape
-    shared_rows = small.shape[1]
+def closing(first, grad, unit, inverse, gain, output, xn, units, shape):
     own, width = output.shape
-    high, half = (rows + shared_rows) // 2, own // 2
-    local, units, _ = shape
+    half = own // 2
     sems = pltpu.SemaphoreType.DMA
-    dtype = parts.dtype
-    single = jnp.float32
+    dtype = output.dtype
     anywhere, inside = pl.BlockSpec(memory_space=pl.ANY), pl.BlockSpec(memory_space=pltpu.VMEM)
     everyone = jax.ShapeDtypeStruct((4, 2, half, width), dtype)
-    summed, shared, outputs, grads, down = pl.pallas_call(
-        functools.partial(closing_kernel, line, shared_rows),
-        out_shape=[
-            jax.ShapeDtypeStruct((2, high, wide), single),
-            jax.ShapeDtypeStruct((2, shared_rows // 2, wide), single),
-            everyone,
-            everyone,
-            jax.ShapeDtypeStruct(shape, dtype),
-        ],
-        in_specs=[anywhere] * 3 + [inside] * 5 + [anywhere] * 2,
-        out_specs=[inside, inside, anywhere, anywhere, anywhere],
+    weight = jax.ShapeDtypeStruct(shape, dtype)
+    outputs, grads, gate, up = pl.pallas_call(
+        closing_kernel,
+        out_shape=[everyone, everyone, weight, weight],
+        in_specs=[anywhere] + [inside] * 5 + [anywhere] * 2,
+        out_specs=[anywhere] * 4,
         scratch_shapes=[
-            pltpu.VMEM((line, 2, high, wide), dtype),
-            pltpu.VMEM((line, 2, high, wide), dtype),
-            pltpu.VMEM((line, 2, high, wide), dtype),
-            pltpu.VMEM((line, 2, high, wide), dtype),
             pltpu.VMEM((4, 2, half, width), dtype),
             pltpu.VMEM((2, half, width), dtype),
             pltpu.VMEM((2, half, width), dtype),
             pltpu.VMEM((half, width), dtype),
             pltpu.VMEM((half, width), dtype),
             pltpu.VMEM((2, half, width), dtype),
-            pltpu.VMEM((2, 2, shared_rows // 2, wide), dtype),
-            pltpu.VMEM((2, 2, shared_rows // 2, wide), dtype),
-            sems((line, 2)),
-            sems((2, line, 2)),
-            sems((line, 2)),
-            sems((2, line, 2)),
-            sems((2, line, 2)),
-            sems((2, line, 2)),
             sems((4, 2)),
             sems((2, 2)),
             sems((2, 2)),
@@ -2072,39 +2101,29 @@
             sems((2, 4, 2, 2)),
             sems((2, 4, 2)),
             sems((2, 2)),
-            sems((2, 2)),
-            pltpu.VMEM((2, tops.shape[0], SPAN), dtype),
-            pltpu.VMEM(scaled.shape, dtype),
-            pltpu.VMEM((SPAN, local * units), single),
-            pltpu.VMEM((local, units, SPAN), dtype),
+            pltpu.VMEM((2, xn.shape[0], SPAN), dtype),
+            pltpu.VMEM(units.shape, dtype),
+            pltpu.VMEM((SPAN, units.shape[2]), jnp.float32),
+            pltpu.VMEM((SPAN, units.shape[2]), dtype),
             sems((2,)),
             sems((1,)),
-            sems((local,)),
+            sems((2, shape[0])),
         ],
         compiler_params=pltpu.CompilerParams(
             collective_id=5, has_side_effects=True, vmem_limit_bytes=60 << 20
         ),
         name="closing",
     )(
-        parts.reshape(line, 2, 2, rows // 2, wide),
-        small.reshape(line, 2, 2, shared_rows // 2, wide),
         first.reshape(4, 2, half, width),
         grad.reshape(2, half, width),
         unit.reshape(2, half, width),
         inverse.reshape(2, half, 1),
         gain.reshape(1, width),
         output.reshape(2, half, width),
-        tops,
-        scaled,
-    )
-    return (
-        summed[:, : rows // 2].reshape(rows, wide),
-        summed[:, rows // 2 :],
-        shared,
-        outputs.reshape(4 * own, width),
-        grads.reshape(4 * own, width),
-        down,
-    )
+        xn,
+        units,
+    )
+    return outputs.reshape(4 * own, width), grads.reshape(4 * own, width), gate, up
 
 
 def square_sum(values, got, sem, side, device):
@@ -2339,17 +2358,6 @@
     )
     w_both = jnp.concatenate([*w_gate, *w_up], axis=1)
     (grad_tokens,) = product_sum(grad_units, w_both, True, gate_part, line, "grad_tokens", 4)
-    moe_out, grad_gate, grad_up = product_sum(
-        scaled,
-        w_down.reshape(-1, model_width),
-        False,
-        None,
-        line,
-        "expert_sum",
-        2,
-        (xn_all, grad_units, w_gate.shape),
-    )
-    output = (hidden_state + moe_out).astype(jnp.bfloat16)
     grad_xn_exp = grad_tokens[:, :model_width]
     gate_sums = grad_tokens[:, model_width : model_width + experts]
     grad_router_probs = jnp.where(named, gate_sums, 0.0)
@@ -2409,19 +2417,35 @@
     small_rows = 32
     filled = small.shape[1]
     small = jnp.pad(small, ((0, 0), (0, small_rows * wide - filled)))
-    summed, own_small, shared, outputs, grad_input, grad_down = closing(
-        grad_projections.astype(jnp.bfloat16).reshape(groups, -1, wide),
-        small.astype(jnp.bfloat16).reshape(groups, small_rows, wide),
+    moe_out, grad_down, summed, shared = product_sum(
+        scaled,
+        w_down.reshape(-1, model_width),
+        False,
+        None,
+        line,
+        "expert_sum",
+        2,
+        (
+            top_all,
+            grad_projections.astype(jnp.bfloat16).reshape(groups, -1, wide),
+            small.astype(jnp.bfloat16).reshape(groups, small_rows, wide),
+            w_down.shape,
+        ),
+    )
+    large = summed.shape[1] - small_rows // 2
+    own_small = summed[:, large:].astype(jnp.float32)
+    summed = summed[:, :large].reshape(2 * large, wide).astype(jnp.float32)
+    output = (hidden_state + moe_out).astype(jnp.bfloat16)
+    outputs, grad_input, grad_gate, grad_up = closing(
         grad_first_normed_input.astype(jnp.bfloat16),
         grad_hidden,
         own_rows(first_unit_input[0]),
         own_rows(first_inverse_norm[0]),
         attention_norm_gain,
         output,
-        top_all,
-        scaled,
-        w_down.shape,
-        line,
+        xn_all,
+        grad_units,
+        w_gate.shape,
     )
     gain_size, norm_size = local_width // groups, model_width // groups
     own_gains = own_small.reshape(-1)[: 2 * gain_size]

time: 677 us -> 681 us (level)
    pallas_call x2, Pallas kernels: 171 us -> 190 us  [product_sum(): pl.pallas_call(functools.partial(product_sum_kernel, line, flipped, extra...]
    pallas_call x1, Pallas kernels: 81.5 us -> 63.6 us  [closing(): pl.pallas_call(closing_kernel, out_shape=[everyone, everyone, weight, wei...]
  transfers between devices with their start and end apart: 2 -> 2, of which waited for: 0 -> 0; matrix products, arithmetic and copies ran while one was open for 11% -> 10% of each run, Pallas kernels for 54% -> 55%
where the time goes in v9:
time: 681 us; the launch traced here: 673 us
  Pallas kernels  567 us (83%)
  other arithmetic  34.7 us (5%)
  matrix products  29.4 us (4%)
  local copies, waits for them, and re-layouts  27.6 us (4%)
  between operations  14.9 us (2%)
    pallas_call x2, Pallas kernels, product_sum(): pl.pallas_call(functools.partial(product_sum_kernel, line, flipped, extra...  190 us
    pallas_call x1, Pallas kernels, gate_act(): pl.pallas_call(functools.partial(gate_act_kernel, line), out_shape=[jax.S...  86.2 us
    pallas_call x1, Pallas kernels, closing(): pl.pallas_call(closing_kernel, out_shape=[everyone, everyone, weight, wei...  63.6 us
    pallas_call x1, Pallas kernels, to_heads(): pl.pallas_call(functools.partial(to_heads_kernel, line, shared), out_shap...  62.4 us
    pallas_call x1, Pallas kernels, to_tokens(): pl.pallas_call(functools.partial(to_tokens_kernel, line, summed), out_sha...  42.9 us
    pallas_call x1, Pallas kernels, out_sum(): pl.pallas_call(functools.partial(out_sum_kernel, line), out_shape=[jax.Sh...  37.1 us
    pallas_call x1, Pallas kernels, out_back(): pl.pallas_call(functools.partial(out_back_kernel, line), out_shape=[jax.S...  25.6 us
    pallas_call x1, Pallas kernels, attend_back(): pl.pallas_call(attend_back_kernel, grid_spec=pltpu.PrefetchScalarGridSpec...  21.3 us
  transfers between devices with their start and end apart: 2, of which 0 were waited for; matrix products, arithmetic and copies ran while one was open for 10% of the time, Pallas kernels for 55%

profile of v9, /device:TPU:24, one launch (start us, length us, event | category | flops | bytes accessed | tf_op | source)
XLA Modules:
  0.0 673.4 jit_solution(16262172105648693341)
XLA Ops:
  10.1 4.3 convert_element_type.106
  21.4 9.4 %normed_heads.1 = (bf16[512,512]{1,0:T(8,128)(2,1)S(1)}, bf16[512,512]{1,0:T(8,128)(2,1)S(1)}, f32[16,512]{1,0:T(8,128)S(1)}) custom-call(f32[512,512]{1,0:T(8,128)S(1)} %fusion.28.q_ref, f32[512,512]{1,0:T(8,128)S(1)} %fusion.26.k_ref, f32[1,512]{1,0:T(1,128)S(1)} %bitcast.86, f32[1,512]{1,0:T(1,128)S(1)} %bitcast.88, ...), custom_call_target="tpu_custom_call" | custom-call | tf_op jit(solution)/shard_map/normed_heads/pallas_call | solution.py:2175
  32.9 62.4 %scatter_heads.1 = (bf16[4,512,128]{2,1,0:T(8,128)(2,1)}, bf16[4,2,512,128]{3,2,1,0:T(8,128)(2,1)}, bf16[4,2,512,128]{3,2,1,0:T(8,128)(2,1)}) custom-call(bf16[512,512]{1,0:T(8,128)(2,1)} %copy-done.18, bf16[512,512]{1,0:T(8,128)(2,1)} %copy-done.19, bf16[512,512]{1,0:T(8,128)(2,1)} %convolution_convert_fusion.3.refs_2_), custom_call_target="tpu_custom_call" | custom-call | tf_op jit(solution)/shard_map/scatter_heads/pallas_call | solution.py:474
  96.1 15.9 %attend.1 = (bf16[4,512,128]{2,1,0:T(8,128)(2,1)}, f32[4,1,512]{2,1,0:T(1,128)}) custom-call(s32[3,4]{1,0:T(4,128)} %pad_add_fusion.bounds, bf16[4,512,128]{2,1,0:T(8,128)(2,1)} %get-tuple-element.48.q_ref, bf16[4096,128]{1,0:T(8,128)(2,1)} %bitcast.100, bf16[4096,128]{1,0:T(8,128)(2,1)} %bitcast.102, s32[4,1,512]{2,1,0:T(1,128)} %copy-done.44), custom_call_target="tpu_custom_call" | custom-call | tf_op jit(solution)/shard_map/attend/pallas_call | solution.py:672
  113.0 37.1 %out_sum.1 = (bf16[512,512]{1,0:T(8,128)(2,1)S(1)}, f32[2,64,2048]{2,1,0:T(8,128)S(1)}) custom-call(bf16[4,512,128]{2,1,0:T(8,128)(2,1)S(1)} %copy-done.12, bf16[512,2048]{1,0:T(8,128)(2,1)S(1)} %copy-done.2), custom_call_target="tpu_custom_call" | custom-call | tf_op jit(solution)/shard_map/out_sum/pallas_call | solution.py:820
  150.2 2.9 multiply_reduce_fusion.4
  162.7 86.2 %gate_act.1 = (bf16[32,2,64,2048]{3,2,1,0:T(8,128)(2,1)}, bf16[16,256,1024]{2,1,0:T(8,128)(2,1)}, bf16[16,256,512]{2,1,0:T(8,128)(2,1)}, bf16[16,256,128]{2,1,0:T(8,128)(2,1)}) custom-call(bf16[2,64,2176]{2,1,0:T(8,128)(2,1)} %bitcast.106, bf16[16,256,2048]{2,1,0:T(8,128)(2,1)} %bitcast.91, bf16[2,2048,256]{2,1,0:T(8,128)(2,1)} %wg_ref.1, ...), custom_call_target="tpu_custom_call" | custom-call | tf_op jit(solution)/shard_map/gate_act/pallas_call | solution.py:1283
  248.8 86.6 %grad_tokens.1 = f32[2,64,2176]{2,1,0:T(8,128)} custom-call(bf16[16,256,1024]{2,1,0:T(8,128)(2,1)} %get-tuple-element.54.refs_0_.units_ref, bf16[2048,1024]{1,0:T(8,128)(2,1)} %pad_maximum_fusion.refs_1_, bf16[16,256,128]{2,1,0:T(8,128)(2,1)} %get-tuple-element.55.refs_2_), custom_call_target="tpu_custom_call" | custom-call | tf_op jit(solution)/shard_map/grad_tokens/pallas_call | solution.py:1899
  336.6 2.9 multiply_reduce_fusion.1
  339.5 2.5 fusion.30
  342.0 25.6 %out_back.1 = (bf16[4,2,64,2048]{3,2,1,0:T(8,128)(2,1)S(1)}, bf16[4,512,128]{2,1,0:T(8,128)(2,1)S(1)}) custom-call(bf16[2,64,2048]{2,1,0:T(8,128)(2,1)S(1)} %bitcast.85, bf16[512,2048]{1,0:T(8,128)(2,1)S(1)} %copy-done.3), custom_call_target="tpu_custom_call" | custom-call | tf_op jit(solution)/shard_map/out_back/pallas_call | solution.py:943
  368.7 2.6 convolution_convert_fusion.1
  371.4 21.3 %attend_back.1 = (bf16[4,512,128]{2,1,0:T(8,128)(2,1)}, bf16[4096,128]{1,0:T(8,128)(2,1)}, bf16[4096,128]{1,0:T(8,128)(2,1)}) custom-call(s32[3,4]{1,0:T(4,128)} %pad_add_fusion.bounds, bf16[4,512,128]{2,1,0:T(8,128)(2,1)} %get-tuple-element.48.q_ref, bf16[4096,128]{1,0:T(8,128)(2,1)} %bitcast.101, bf16[4096,128]{1,0:T(8,128)(2,1)} %bitcast.103, ...), custom_call_target="tpu_custom_call" | custom-call | tf_op jit(solution)/shard_map/attend_back/pallas_call | solution.py:694
  392.7 42.9 %gather_grads.1 = (bf16[512,512]{1,0:T(8,128)(2,1)}, bf16[512,512]{1,0:T(8,128)(2,1)}, bf16[512,512]{1,0:T(8,128)(2,1)}) custom-call(bf16[4,512,128]{2,1,0:T(8,128)(2,1)} %get-tuple-element.57.refs_0_, bf16[4,2,512,128]{3,2,1,0:T(8,128)(2,1)} %bitcast.112, bf16[4,2,512,128]{3,2,1,0:T(8,128)(2,1)} %bitcast.113), custom_call_target="tpu_custom_call" | custom-call | tf_op jit(solution)/shard_map/gather_grads/pallas_call | solution.py:575
  438.7 12.0 %normed_heads_back.1 = (bf16[512,1536]{1,0:T(8,128)(2,1)S(1)}, f32[16,512]{1,0:T(8,128)S(1)}) custom-call(bf16[512,512]{1,0:T(8,128)(2,1)S(1)} %copy-done.15, bf16[512,512]{1,0:T(8,128)(2,1)S(1)} %copy-done.16, bf16[512,512]{1,0:T(8,128)(2,1)S(1)} %copy-done.17, f32[512,512]{1,0:T(8,128)S(1)} %copy-done.9, f32[512,512]{1,0:T(8,128)S(1)} %copy-done.7, ...), custom_call_target="tpu_custom_call" | custom-call | tf_op jit(solution)/shard_map/normed_heads_back/pallas_call | solution.py:2243
  450.8 3.3 fusion.8
  457.1 3.2 fusion.10
  461.1 4.5 fusion
  467.6 5.5 convolution_convert_fusion
  473.1 103.8 %expert_sum.1 = (f32[2,64,2048]{2,1,0:T(8,128)}, bf16[2,256,2048]{2,1,0:T(8,128)(2,1)}, bf16[2,144,1536]{2,1,0:T(8,128)(2,1)}, f32[2,16,1536]{2,1,0:T(8,128)}) custom-call(bf16[16,256,512]{2,1,0:T(8,128)(2,1)} %get-tuple-element.65.refs_0_, bf16[512,2048]{1,0:T(8,128)(2,1)} %bitcast.94, bf16[4096,2048]{1,0:T(8,128)(2,1)} %bitcast.92, ...), custom_call_target="tpu_custom_call" | custom-call | tf_op jit(solution)/shard_map/expert_sum/pallas_call | solution.py:1899
  578.0 2.6 slice.83
  582.9 63.6 %closing.1 = (bf16[4,2,64,2048]{3,2,1,0:T(8,128)(2,1)}, bf16[4,2,64,2048]{3,2,1,0:T(8,128)(2,1)}, bf16[2,2048,256]{2,1,0:T(8,128)(2,1)}, bf16[2,2048,256]{2,1,0:T(8,128)(2,1)}) custom-call(bf16[4,2,64,2048]{3,2,1,0:T(8,128)(2,1)} %bitcast.95, f32[2,64,2048]{2,1,0:T(8,128)} %bitcast.98, f32[2,64,2048]{2,1,0:T(8,128)} %bitcast.99, ...), custom_call_target="tpu_custom_call" | custom-call | tf_op jit(solution)/shard_map/closing/pallas_call | solution.py:2084
  650.1 2.5 convert.31
  657.3 2.5 convert_element_type.130
  (170 shorter events, 52.3 us)
Async XLA Ops:
  7.2 145.9 %copy-start = (f32[2048,16]{0,1:T(8,128)S(1)}, f32[2048,16]{0,1:T(8,128)}, u32[]{:S(2)}) copy-start(f32[2048,16]{0,1:T(8,128)} %param.25) | copy-start | bytes 393220
  7.2 155.5 %all-gather.3.cloned.1.call-start = ((), (), s32[]{:S(2)}) async-start(), calls=%async_computation.2 | async-start | bytes 17301504 | tf_op jit(solution)/shard_map/all_gather | solution.py:2343
  9.2 654.0 %reduce-scatter.2.cloned.1.call-start = ((), (), s32[]{:S(2)}) async-start(), calls=%async_computation.1 | async-start | bytes 2359296 | tf_op jit(solution)/shard_map/reduce_scatter | solution.py:2453
  10.1 4.3 copy-start.27
  14.3 3.8 copy-start.45
  21.3 11.6 %copy-start.8 = (f32[512,512]{1,0:T(8,128)}, f32[512,512]{1,0:T(8,128)S(1)}, u32[]{:S(2)}) copy-start(f32[512,512]{1,0:T(8,128)S(1)} %fusion.28.q_ref) | copy-start | bytes 3145732
  21.4 9.4 %copy-start.42 = (bf16[2048,512]{1,0:T(8,128)(2,1)S(1)}, bf16[2048,512]{1,0:T(8,128)(2,1)}, u32[]{:S(2)}) copy-start(bf16[2048,512]{1,0:T(8,128)(2,1)} %param.20) | copy-start | bytes 6291460
  32.9 79.1 %copy-start.2 = (bf16[512,2048]{1,0:T(8,128)(2,1)S(1)}, bf16[512,2048]{1,0:T(8,128)(2,1)}, u32[]{:S(2)}) copy-start(bf16[512,2048]{1,0:T(8,128)(2,1)} %w_ref.3) | copy-start | bytes 6291460
  155.7 3.4 copy-start.32
  335.5 4.0 copy-start.25
  342.0 25.7 %copy-start.13 = (bf16[4,512,128]{2,1,0:T(8,128)(2,1)S(1)}, bf16[4,512,128]{2,1,0:T(8,128)(2,1)}, u32[]{:S(2)}) copy-start(bf16[4,512,128]{2,1,0:T(8,128)(2,1)} %get-tuple-element.52.o_ref) | copy-start | bytes 1572868
  342.0 26.6 %copy-start.23 = (bf16[512,512]{1,0:T(8,128)(2,1)S(1)}, bf16[512,512]{1,0:T(8,128)(2,1)}, u32[]{:S(2)}) copy-start(bf16[512,512]{1,0:T(8,128)(2,1)} %copy-done.22) | copy-start | bytes 1572868
  367.7 3.6 copy-start.14
  392.6 42.9 %copy-start.7 = (f32[512,512]{1,0:T(8,128)S(1)}, f32[512,512]{1,0:T(8,128)}, u32[]{:S(2)}) copy-start(f32[512,512]{1,0:T(8,128)} %copy-done.6) | copy-start | bytes 3145732
  392.6 42.9 %copy-start.9 = (f32[512,512]{1,0:T(8,128)S(1)}, f32[512,512]{1,0:T(8,128)}, u32[]{:S(2)}) copy-start(f32[512,512]{1,0:T(8,128)} %copy-done.8) | copy-start | bytes 3145732
  438.7 12.1 %copy-start.40 = (bf16[2048,512]{1,0:T(8,128)(2,1)S(1)}, bf16[2048,512]{1,0:T(8,128)(2,1)}, u32[]{:S(2)}) copy-start(bf16[2048,512]{1,0:T(8,128)(2,1)} %param.19) | copy-start | bytes 6291460
  450.8 3.3 copy-start.10
  450.8 3.3 copy-start.26
  457.0 3.2 copy-start.11
  457.1 3.2 copy-start.28
  457.1 4.1 copy-start.30
  576.9 3.7 copy-start.5
  576.9 3.7 copy-start.33
  646.4 3.6 copy-start.37
  (26 other events, 50.4 us)
Sparse Core Ops, SparseCore 0:
  11.6 146.6 all-gather.2
  371.5 34.3 reduce-scatter.1

commit v10 on v9

--- a/solution.py
+++ b/solution.py
@@ -485,8 +485,11 @@
     )(*arrays)
 
 
-def to_tokens_kernel(line, summed, *refs):
+def to_tokens_kernel(line, summed, working, *refs):
     count, sums = len(summed), sum(summed)
+    if working:
+        work_in, work_out, work_refs = refs[count : count + 2], refs[2 * count + 2], refs[-7:]
+        refs = (*refs[:count], *refs[count + 2 : 2 * count + 2], *refs[2 * count + 3 : -7])
     ins, outs = refs[:count], refs[count : 2 * count]
     mine, theirs = refs[2 * count : 2 * count + 2]
     sent, arrived, pair_sem, load_sem, own_sem = refs[2 * count + 2 :]
@@ -551,6 +554,15 @@
     for i in range(count):
         add(i, z)
         own(i).start()
+    if working:
+        work, work_end, turns = unit_grads(0, *work_in, work_out, *work_refs)
+
+        def turn(n, carry):
+            work(n)
+            return carry
+
+        lax.fori_loop(0, turns, turn, 0)
+        work_end()
 
     def finish(other):
         for i in range(count):
@@ -566,17 +578,22 @@
             hand(i, z).wait_send()
 
 
-def to_tokens(arrays, summed, line, name, number):
+def to_tokens(arrays, summed, line, name, number, work=None):
     rows = arrays[0].shape[-2]
     count, sums = len(arrays), max(sum(summed), 1)
     sems = pltpu.SemaphoreType.DMA
     dtype = arrays[0].dtype
     held = (sums, line, rows, HD) if sum(summed) else (1, 1, 16, HD)
+    work_in, work_shape, work_space = [], [], []
+    if work is not None:
+        xn, units, shape = work
+        work_in, work_space = [xn, units], unit_grads_space(xn, units, shape)
+        work_shape = [jax.ShapeDtypeStruct(shape, dtype)]
     return pl.pallas_call(
-        functools.partial(to_tokens_kernel, line, summed),
-        out_shape=[jax.ShapeDtypeStruct((rows, line * HD), dtype)] * count,
-        in_specs=[pl.BlockSpec(memory_space=pl.ANY)] * count,
-        out_specs=[pl.BlockSpec(memory_space=pl.ANY)] * count,
+        functools.partial(to_tokens_kernel, line, summed, work is not None),
+        out_shape=[jax.ShapeDtypeStruct((rows, line * HD), dtype)] * count + work_shape,
+        in_specs=[pl.BlockSpec(memory_space=pl.ANY)] * (count + len(work_in)),
+        out_specs=[pl.BlockSpec(memory_space=pl.ANY)] * (count + len(work_shape)),
         scratch_shapes=[pltpu.VMEM(held, dtype)] * 2
         + [
             sems((count, line)),
@@ -584,10 +601,13 @@
             sems((2, sums, line)),
             sems((sums, line)),
             sems((count,)),
+            *work_space,
         ],
-        compiler_params=pltpu.CompilerParams(collective_id=number, has_side_effects=True),
+        compiler_params=pltpu.CompilerParams(
+            collective_id=number, has_side_effects=True, vmem_limit_bytes=40 << 20
+        ),
         name=name,
-    )(*arrays)
+    )(*arrays, *work_in)
 
 
 KEY_TILE = 512
@@ -987,7 +1007,7 @@
         out, total = attend(bounds, q, k, v, starts)
         return *out_sum(out, w_out, line), (q, k, v, out, total)
 
-    def backward(kept, grad_own):
+    def backward(kept, grad_own, work):
         q, k, v, out, total = kept
         grad_all, grad = out_back(grad_own, w_out, line)
         delta = jnp.sum(grad.astype(jnp.float32) * out.astype(jnp.float32), axis=-1)
@@ -999,6 +1019,7 @@
             line,
             "gather_grads",
             9,
+            work,
         )
         return grad_all, *grads
 
@@ -1036,7 +1057,7 @@
         projected = scatter_dp(contract(attended, w_out, 1, 0).astype(jnp.bfloat16))
         return attended, projected, (q, k, v, total)
 
-    def backward(kept, grad_own):
+    def backward(kept, grad_own, work):
         q, k, v, total = kept
         grad_all = gather_dp(grad_own)
         grad = contract(grad_all, w_out, 1, 1).astype(jnp.bfloat16)
@@ -1057,7 +1078,10 @@
 
         scale = HD ** (-0.5)
         dq = (dq * scale).reshape(shape)
-        return grad_all, dq, to_owner(dk * scale), to_owner(dv)
+        xn, units, (local, _, width) = work
+        units = units.reshape(pack, -1)
+        gate = [contract(xn, units[:, e * width : (e + 1) * width], 0, 0) for e in range(local)]
+        return grad_all, dq, to_owner(dk * scale), to_owner(dv), jnp.stack(gate)
 
     return forward, backward
 
@@ -1356,24 +1380,21 @@
     return turn, turns
 
 
-def gate_up_grads(
-    xn_ref, units_ref, gate_ref, up_ref, chunk_buf, units_buf, total, both, chunk_sem, units_sem, out_sem
+def unit_grads(
+    kind, xn_ref, units_ref, out_ref, chunk_buf, units_buf, total, made, chunk_sem, units_sem, out_sem
 ):
-    local, _, units = gate_ref.shape
-    outs = (gate_ref, up_ref)
+    local, _, units = out_ref.shape
+    span = chunk_buf.shape[2]
 
     def copies(at):
         return [
             pltpu.make_async_copy(
-                both.at[:, pl.ds((kind * local + e) * units, units)],
-                outs[kind].at[e, at, :],
-                out_sem.at[kind, e],
+                made.at[:, pl.ds(e * units, units)], out_ref.at[e, at, :], out_sem.at[e]
             )
-            for kind in (0, 1)
             for e in range(local)
         ]
 
-    start = pl.ds(0, chunk_buf.shape[2])
+    start = pl.ds(0, span)
 
     def store(n, at):
         @pl.when(n > 0)
@@ -1381,7 +1402,7 @@
             for copy in copies(start):
                 copy.wait()
 
-        both[...] = total[...].astype(both.dtype)
+        made[...] = total[...].astype(made.dtype)
         for copy in copies(at):
             copy.start()
 
@@ -1389,10 +1410,26 @@
         for copy in copies(start):
             copy.wait()
 
+    side = units_ref.at[:, :, pl.ds(kind * local * units, local * units)]
     turn, turns = column_products(
-        xn_ref, units_ref, chunk_buf, units_buf, total, chunk_sem, units_sem, store
+        xn_ref, side, chunk_buf, units_buf, total, chunk_sem, units_sem, store
     )
     return turn, end, turns
+
+
+def unit_grads_space(xn, units, shape):
+    local, _, width = shape
+    blocks, rows, _ = units.shape
+    sems = pltpu.SemaphoreType.DMA
+    return [
+        pltpu.VMEM((2, xn.shape[0], SPAN), xn.dtype),
+        pltpu.VMEM((blocks, rows, local * width), xn.dtype),
+        pltpu.VMEM((SPAN, local * width), jnp.float32),
+        pltpu.VMEM((SPAN, local * width), xn.dtype),
+        sems((2,)),
+        sems((1,)),
+        sems((local,)),
+    ]
 
 
 def down_grads(
@@ -1611,6 +1648,18 @@
     a_ref, w_ref = refs[0], refs[1]
     e_ref = refs[2] if extra else None
     refs = refs[3:] if extra else refs[2:]
+    w_loads = []
+    if flipped:
+        up_ref, *refs, w_buf, w_sem = refs
+        experts, _, units = w_ref.shape
+        for kind, source in enumerate((w_ref, up_ref)):
+            for e in range(experts):
+                at = kind * experts + e
+                target = w_buf.at[:, at * units : (at + 1) * units]
+                w_loads.append(pltpu.make_async_copy(source.at[e], target, w_sem.at[at]))
+        w_ref = w_buf
+        for copy in w_loads:
+            copy.start()
     if grads:
         top_ref, parts_ref, small_ref, out_ref, down_ref, summed_ref, shared_ref = refs[:7]
         refs, work_refs, sum_refs = (out_ref, *refs[7:-21]), refs[-21:-14], refs[-14:]
@@ -1795,6 +1844,8 @@
             pl.when((height < z) & (z < line - 1))(downwards)
 
     start_load(0)
+    for copy in w_loads:
+        copy.wait()
     if grads:
         work, work_end, turns = down_grads(top_ref, a_ref, down_ref, *work_refs)
         line_start, line_pair, line_pass, line_end = line_sum(
@@ -1858,7 +1909,7 @@
 
 def product_sum(blocks, weights, flipped, extra, line, name, number, grads=None):
     count, rows, depth = blocks.shape
-    width = weights.shape[0] if flipped else weights.shape[1]
+    width = weights[0].shape[1] if flipped else weights.shape[1]
     wide = width + (0 if extra is None else 128)
     half = rows // 4
     sems = pltpu.SemaphoreType.DMA
@@ -1899,9 +1950,9 @@
     total, *work_out = pl.pallas_call(
         functools.partial(product_sum_kernel, line, flipped, extra is not None, grads is not None),
         out_shape=out_shape,
-        in_specs=[anywhere, inside]
+        in_specs=[anywhere, anywhere if flipped else inside]
         + ([] if extra is None else [anywhere])
-        + [anywhere] * len(work_in),
+        + [anywhere] * (len(work_in) + flipped),
         out_specs=[inside] + ([] if grads is None else [anywhere, anywhere, inside]),
         scratch_shapes=[
             space(4, line, 2, 2),
@@ -1924,12 +1975,19 @@
             sems((2, line, 2)),
             sems((2, line, 2)),
             *work_space,
+            *([pltpu.VMEM((width, depth), dtype), sems((2 * weights[0].shape[0],))] if flipped else []),
         ],
         compiler_params=pltpu.CompilerParams(
             collective_id=number, has_side_effects=True, vmem_limit_bytes=63 << 20
         ),
         name=name,
-    )(blocks, weights, *([] if extra is None else [extra]), *work_in)
+    )(
+        blocks,
+        weights[0] if flipped else weights,
+        *([] if extra is None else [extra]),
+        *([weights[1]] if flipped else []),
+        *work_in,
+    )
     return total.reshape(2 * half, wide), *work_out
 
 
@@ -1944,7 +2002,6 @@
     units_ref,
     outputs_ref,
     grads_ref,
-    gate_ref,
     up_ref,
     part,
     got_x,
@@ -2010,7 +2067,7 @@
         spread(a, side_y, 1, 0).wait_recv()
         spread(a, side_y, 1, 0).start()
 
-    work, work_end, turns = gate_up_grads(xn_ref, units_ref, gate_ref, up_ref, *work_refs)
+    work, work_end, turns = unit_grads(1, xn_ref, units_ref, up_ref, *work_refs)
     pauses = 4
 
     def meanwhile(i):
@@ -2081,11 +2138,11 @@
     anywhere, inside = pl.BlockSpec(memory_space=pl.ANY), pl.BlockSpec(memory_space=pltpu.VMEM)
     everyone = jax.ShapeDtypeStruct((4, 2, half, width), dtype)
     weight = jax.ShapeDtypeStruct(shape, dtype)
-    outputs, grads, gate, up = pl.pallas_call(
+    outputs, grads, up = pl.pallas_call(
         closing_kernel,
-        out_shape=[everyone, everyone, weight, weight],
+        out_shape=[everyone, everyone, weight],
         in_specs=[anywhere] + [inside] * 5 + [anywhere] * 2,
-        out_specs=[anywhere] * 4,
+        out_specs=[anywhere] * 3,
         scratch_shapes=[
             pltpu.VMEM((4, 2, half, width), dtype),
             pltpu.VMEM((2, half, width), dtype),
@@ -2101,13 +2158,7 @@
             sems((2, 4, 2, 2)),
             sems((2, 4, 2)),
             sems((2, 2)),
-            pltpu.VMEM((2, xn.shape[0], SPAN), dtype),
-            pltpu.VMEM(units.shape, dtype),
-            pltpu.VMEM((SPAN, units.shape[2]), jnp.float32),
-            pltpu.VMEM((SPAN, units.shape[2]), dtype),
-            sems((2,)),
-            sems((1,)),
-            sems((2, shape[0])),
+            *unit_grads_space(xn, units, shape),
         ],
         compiler_params=pltpu.CompilerParams(
             collective_id=5, has_side_effects=True, vmem_limit_bytes=60 << 20
@@ -2123,7 +2174,7 @@
         xn,
         units,
     )
-    return outputs.reshape(4 * own, width), grads.reshape(4 * own, width), gate, up
+    return outputs.reshape(4 * own, width), grads.reshape(4 * own, width), up
 
 
 def square_sum(values, got, sem, side, device):
@@ -2356,8 +2407,8 @@
     xn_all, grad_units, scaled, gate_part = gate_act(
         own_tokens, top_all, w_gate, w_up, w_down, line
     )
-    w_both = jnp.concatenate([*w_gate, *w_up], axis=1)
-    (grad_tokens,) = product_sum(grad_units, w_both, True, gate_part, line, "grad_tokens", 4)
+    (grad_tokens,) = product_sum(
+        grad_units, (w_gate, w_up), True, gate_part, line, "grad_tokens", 4)
     grad_xn_exp = grad_tokens[:, :model_width]
     gate_sums = grad_tokens[:, model_width : model_width + experts]
     grad_router_probs = jnp.where(named, gate_sums, 0.0)
@@ -2377,8 +2428,8 @@
         - second_unit_input
         * jnp.mean(grad_second_unit_input * second_unit_input, axis=-1, keepdims=True)
     )
-    grad_attn, grad_queries, grad_keys, grad_values = attention[1](
-        kept, grad_hidden.astype(jnp.bfloat16)
+    grad_attn, grad_queries, grad_keys, grad_values, grad_gate = attention[1](
+        kept, grad_hidden.astype(jnp.bfloat16), (xn_all, grad_units, w_gate.shape)
     )
     grad_out = jnp.einsum("sk,sd->kd", attended, grad_attn, preferred_element_type=jnp.float32)
     grad_heads_raw, gain_grads = normed_heads_back(
@@ -2436,7 +2487,7 @@
     own_small = summed[:, large:].astype(jnp.float32)
     summed = summed[:, :large].reshape(2 * large, wide).astype(jnp.float32)
     output = (hidden_state + moe_out).astype(jnp.bfloat16)
-    outputs, grad_input, grad_gate, grad_up = closing(
+    outputs, grad_input, grad_up = closing(
         grad_first_normed_input.astype(jnp.bfloat16),
         grad_hidden,
         own_rows(first_unit_input[0]),

time: 681 us -> 671 us (0.985)
  Pallas kernels: 567 us -> 556 us
  transfers between devices with their start and end apart: 2 -> 2, of which waited for: 0 -> 1; matrix products, arithmetic and copies ran while one was open for 10% -> 9% of each run, Pallas kernels for 55% -> 44%
where the time goes in v10:
time: 671 us; the launch traced here: 662 us
  Pallas kernels  556 us (83%)
  other arithmetic  34.7 us (5%)
  matrix products  27.8 us (4%)
  local copies, waits for them, and re-layouts  27.2 us (4%)
  between operations  14.9 us (2%)
    pallas_call x2, Pallas kernels, product_sum(): pl.pallas_call(functools.partial(product_sum_kernel, line, flipped, extra...  193 us
    pallas_call x1, Pallas kernels, gate_act(): pl.pallas_call(functools.partial(gate_act_kernel, line), out_shape=[jax.S...  86.9 us
    pallas_call x1, Pallas kernels, to_heads(): pl.pallas_call(functools.partial(to_heads_kernel, line, shared), out_shap...  62.5 us
    pallas_call x1, Pallas kernels, closing(): pl.pallas_call(closing_kernel, out_shape=[everyone, everyone, weight], in...  60.1 us
    pallas_call x1, Pallas kernels, to_tokens(): pl.pallas_call(functools.partial(to_tokens_kernel, line, summed, work is...  40.1 us
    pallas_call x1, Pallas kernels, out_sum(): pl.pallas_call(functools.partial(out_sum_kernel, line), out_shape=[jax.Sh...  39.6 us
    pallas_call x1, Pallas kernels, out_back(): pl.pallas_call(functools.partial(out_back_kernel, line), out_shape=[jax.S...  25.3 us
    pallas_call x1, Pallas kernels, attend_back(): pl.pallas_call(attend_back_kernel, grid_spec=pltpu.PrefetchScalarGridSpec...  15.3 us
  transfers between devices with their start and end apart: 2, of which 1 were waited for; matrix products, arithmetic and copies ran while one was open for 9% of the time, Pallas kernels for 44%

profile of v10, /device:TPU:24, one launch (start us, length us, event | category | flops | bytes accessed | tf_op | source)
XLA Modules:
  0.0 662.2 jit_solution(16853813182550290583)
XLA Ops:
  11.0 4.3 convert_element_type.106
  20.4 9.2 %normed_heads.1 = (bf16[512,512]{1,0:T(8,128)(2,1)S(1)}, bf16[512,512]{1,0:T(8,128)(2,1)S(1)}, f32[16,512]{1,0:T(8,128)S(1)}) custom-call(f32[512,512]{1,0:T(8,128)S(1)} %fusion.28.q_ref, f32[512,512]{1,0:T(8,128)S(1)} %fusion.26.k_ref, f32[1,512]{1,0:T(1,128)S(1)} %bitcast.80, f32[1,512]{1,0:T(1,128)S(1)} %bitcast.82, ...), custom_call_target="tpu_custom_call" | custom-call | tf_op jit(solution)/shard_map/normed_heads/pallas_call | solution.py:2226
  31.8 62.5 %scatter_heads.1 = (bf16[4,512,128]{2,1,0:T(8,128)(2,1)}, bf16[4,2,512,128]{3,2,1,0:T(8,128)(2,1)}, bf16[4,2,512,128]{3,2,1,0:T(8,128)(2,1)}) custom-call(bf16[512,512]{1,0:T(8,128)(2,1)} %copy-done.18, bf16[512,512]{1,0:T(8,128)(2,1)} %copy-done.19, bf16[512,512]{1,0:T(8,128)(2,1)} %convolution_convert_fusion.3.refs_2_), custom_call_target="tpu_custom_call" | custom-call | tf_op jit(solution)/shard_map/scatter_heads/pallas_call | solution.py:474
  95.1 11.4 %attend.1 = (bf16[4,512,128]{2,1,0:T(8,128)(2,1)}, f32[4,1,512]{2,1,0:T(1,128)}) custom-call(s32[3,4]{1,0:T(4,128)} %pad_add_fusion.bounds, bf16[4,512,128]{2,1,0:T(8,128)(2,1)} %get-tuple-element.48.q_ref, bf16[4096,128]{1,0:T(8,128)(2,1)} %bitcast.95, bf16[4096,128]{1,0:T(8,128)(2,1)} %bitcast.97, s32[4,1,512]{2,1,0:T(1,128)} %copy-done.44), custom_call_target="tpu_custom_call" | custom-call | tf_op jit(solution)/shard_map/attend/pallas_call | solution.py:692
  107.5 39.6 %out_sum.1 = (bf16[512,512]{1,0:T(8,128)(2,1)S(1)}, f32[2,64,2048]{2,1,0:T(8,128)S(1)}) custom-call(bf16[4,512,128]{2,1,0:T(8,128)(2,1)S(1)} %copy-done.12, bf16[512,2048]{1,0:T(8,128)(2,1)S(1)} %copy-done.2), custom_call_target="tpu_custom_call" | custom-call | tf_op jit(solution)/shard_map/out_sum/pallas_call | solution.py:840
  147.1 3.1 multiply_reduce_fusion.4
  159.4 86.9 %gate_act.1 = (bf16[32,2,64,2048]{3,2,1,0:T(8,128)(2,1)}, bf16[16,256,1024]{2,1,0:T(8,128)(2,1)}, bf16[16,256,512]{2,1,0:T(8,128)(2,1)}, bf16[16,256,128]{2,1,0:T(8,128)(2,1)}) custom-call(bf16[2,64,2176]{2,1,0:T(8,128)(2,1)} %bitcast.101, bf16[16,256,2048]{2,1,0:T(8,128)(2,1)} %bitcast.85, bf16[2,2048,256]{2,1,0:T(8,128)(2,1)} %refs_1_.1, ...), custom_call_target="tpu_custom_call" | custom-call | tf_op jit(solution)/shard_map/gate_act/pallas_call | solution.py:1307
  246.3 84.8 %grad_tokens.1 = f32[2,64,2176]{2,1,0:T(8,128)} custom-call(bf16[16,256,1024]{2,1,0:T(8,128)(2,1)} %get-tuple-element.54.refs_0_.refs_4_.units_ref, bf16[2,2048,256]{2,1,0:T(8,128)(2,1)} %refs_1_.1, bf16[16,256,128]{2,1,0:T(8,128)(2,1)} %get-tuple-element.55.refs_2_, bf16[2,2048,256]{2,1,0:T(8,128)(2,1)} %refs_3_.1), custom_call_target="tpu_custom_call" | custom-call | tf_op jit(solution)/shard_map/grad_tokens/pallas_call | solution.py:1950
  332.2 2.9 multiply_reduce_fusion.1
  335.2 2.6 fusion.30
  337.8 25.3 %out_back.1 = (bf16[4,2,64,2048]{3,2,1,0:T(8,128)(2,1)S(1)}, bf16[4,512,128]{2,1,0:T(8,128)(2,1)S(1)}) custom-call(bf16[2,64,2048]{2,1,0:T(8,128)(2,1)S(1)} %bitcast.77, bf16[512,2048]{1,0:T(8,128)(2,1)S(1)} %copy-done.3), custom_call_target="tpu_custom_call" | custom-call | tf_op jit(solution)/shard_map/out_back/pallas_call | solution.py:963
  364.3 15.3 %attend_back.1 = (bf16[4,512,128]{2,1,0:T(8,128)(2,1)}, bf16[4096,128]{1,0:T(8,128)(2,1)}, bf16[4096,128]{1,0:T(8,128)(2,1)}) custom-call(s32[3,4]{1,0:T(4,128)} %pad_add_fusion.bounds, bf16[4,512,128]{2,1,0:T(8,128)(2,1)} %get-tuple-element.48.q_ref, bf16[4096,128]{1,0:T(8,128)(2,1)} %bitcast.96, bf16[4096,128]{1,0:T(8,128)(2,1)} %bitcast.98, ...), custom_call_target="tpu_custom_call" | custom-call | tf_op jit(solution)/shard_map/attend_back/pallas_call | solution.py:714
  383.1 40.1 %gather_grads.1 = (bf16[512,512]{1,0:T(8,128)(2,1)S(1)}, bf16[512,512]{1,0:T(8,128)(2,1)S(1)}, bf16[512,512]{1,0:T(8,128)(2,1)S(1)}, bf16[2,2048,256]{2,1,0:T(8,128)(2,1)S(1)}) custom-call(bf16[4,512,128]{2,1,0:T(8,128)(2,1)S(1)} %copy-done.17, bf16[4,2,512,128]{3,2,1,0:T(8,128)(2,1)S(1)} %bitcast.78, bf16[4,2,512,128]{3,2,1,0:T(8,128)(2,1)S(1)} %bitcast.79, ...), custom_call_target="tpu_custom_call" | custom-call | tf_op jit(solution)/shard_map/gather_grads/pallas_call | solution.py:592
  424.5 12.4 %normed_heads_back.1 = (bf16[512,1536]{1,0:T(8,128)(2,1)S(1)}, f32[16,512]{1,0:T(8,128)S(1)}) custom-call(bf16[512,512]{1,0:T(8,128)(2,1)S(1)} %get-tuple-element.61.dq_ref, bf16[512,512]{1,0:T(8,128)(2,1)S(1)} %get-tuple-element.62.dk_ref, bf16[512,512]{1,0:T(8,128)(2,1)S(1)} %get-tuple-element.63.dv_ref, f32[512,512]{1,0:T(8,128)S(1)} %copy-done.9, ...), custom_call_target="tpu_custom_call" | custom-call | tf_op jit(solution)/shard_map/normed_heads_back/pallas_call | solution.py:2294
  437.0 3.3 fusion.10
  440.3 2.7 convolution_convert_fusion.1
  446.9 3.0 fusion.8
  451.2 2.9 fusion
  456.2 5.7 convolution_convert_fusion
  462.0 108.2 %expert_sum.1 = (f32[2,64,2048]{2,1,0:T(8,128)}, bf16[2,256,2048]{2,1,0:T(8,128)(2,1)}, bf16[2,144,1536]{2,1,0:T(8,128)(2,1)}, f32[2,16,1536]{2,1,0:T(8,128)}) custom-call(bf16[16,256,512]{2,1,0:T(8,128)(2,1)} %get-tuple-element.66.refs_0_, bf16[512,2048]{1,0:T(8,128)(2,1)} %bitcast.89, bf16[4096,2048]{1,0:T(8,128)(2,1)} %bitcast.86, ...), custom_call_target="tpu_custom_call" | custom-call | tf_op jit(solution)/shard_map/expert_sum/pallas_call | solution.py:1950
  570.2 2.8 slice.83
  576.1 60.1 %closing.1 = (bf16[4,2,64,2048]{3,2,1,0:T(8,128)(2,1)}, bf16[4,2,64,2048]{3,2,1,0:T(8,128)(2,1)}, bf16[2,2048,256]{2,1,0:T(8,128)(2,1)}) custom-call(bf16[4,2,64,2048]{3,2,1,0:T(8,128)(2,1)} %bitcast.90, f32[2,64,2048]{2,1,0:T(8,128)} %bitcast.93, f32[2,64,2048]{2,1,0:T(8,128)} %bitcast.94, f32[2,64,1]{2,1,0:T(8,128)} %reshape.491.inverse_ref, ...), custom_call_target="tpu_custom_call" | custom-call | tf_op jit(solution)/shard_map/closing/pallas_call | solution.py:2141
  636.2 4.3 convert.31
  642.9 2.5 convert_element_type.130
  (166 shorter events, 51.6 us)
Async XLA Ops:
  7.2 143.0 %copy-start = (f32[2048,16]{0,1:T(8,128)S(1)}, f32[2048,16]{0,1:T(8,128)}, u32[]{:S(2)}) copy-start(f32[2048,16]{0,1:T(8,128)} %param.25) | copy-start | bytes 393220
  7.2 152.2 %all-gather.3.cloned.1.call-start = ((), (), s32[]{:S(2)}) async-start(), calls=%async_computation.2 | async-start | bytes 17301504 | tf_op jit(solution)/shard_map/all_gather | solution.py:2394
  9.2 642.9 %reduce-scatter.2.cloned.1.call-start = ((), (), s32[]{:S(2)}) async-start(), calls=%async_computation.1 | async-start | bytes 2359296 | tf_op jit(solution)/shard_map/reduce_scatter | solution.py:2504
  11.0 4.3 copy-start.29
  20.4 11.4 %copy-start.8 = (f32[512,512]{1,0:T(8,128)}, f32[512,512]{1,0:T(8,128)S(1)}, u32[]{:S(2)}) copy-start(f32[512,512]{1,0:T(8,128)S(1)} %fusion.28.q_ref) | copy-start | bytes 3145732
  20.4 9.2 %copy-start.40 = (bf16[2048,512]{1,0:T(8,128)(2,1)S(1)}, bf16[2048,512]{1,0:T(8,128)(2,1)}, u32[]{:S(2)}) copy-start(bf16[2048,512]{1,0:T(8,128)(2,1)} %param.20) | copy-start | bytes 6291460
  31.7 74.7 %copy-start.2 = (bf16[512,2048]{1,0:T(8,128)(2,1)S(1)}, bf16[512,2048]{1,0:T(8,128)(2,1)}, u32[]{:S(2)}) copy-start(bf16[512,2048]{1,0:T(8,128)(2,1)} %w_ref.3) | copy-start | bytes 6291460
  147.0 3.1 copy-start.4
  147.0 3.1 copy-start.24
  147.1 3.1 copy-start.43
  150.2 7.4 %copy-start.26 = (f32[128,2048]{1,0:T(8,128)}, f32[128,2048]{1,0:T(8,128)S(1)}, u32[]{:S(2)}) copy-start(f32[128,2048]{1,0:T(8,128)S(1)} %get-tuple-element.127) | copy-start | bytes 3145732
  331.1 4.0 copy-start.27
  337.7 25.3 %copy-start.13 = (bf16[4,512,128]{2,1,0:T(8,128)(2,1)S(1)}, bf16[4,512,128]{2,1,0:T(8,128)(2,1)}, u32[]{:S(2)}) copy-start(bf16[4,512,128]{2,1,0:T(8,128)(2,1)} %get-tuple-element.52.o_ref) | copy-start | bytes 1572868
  363.1 16.6 %copy-start.22 = (bf16[4,2,64,2048]{3,2,1,0:T(8,128)(2,1)}, bf16[4,2,64,2048]{3,2,1,0:T(8,128)(2,1)S(1)}, u32[]{:S(2)}) copy-start(bf16[4,2,64,2048]{3,2,1,0:T(8,128)(2,1)S(1)} %get-tuple-element.74) | copy-start | bytes 6291460
  383.1 41.4 %copy-start.7 = (f32[512,512]{1,0:T(8,128)S(1)}, f32[512,512]{1,0:T(8,128)}, u32[]{:S(2)}) copy-start(f32[512,512]{1,0:T(8,128)} %copy-done.6) | copy-start | bytes 3145732
  383.1 41.4 %copy-start.9 = (f32[512,512]{1,0:T(8,128)S(1)}, f32[512,512]{1,0:T(8,128)}, u32[]{:S(2)}) copy-start(f32[512,512]{1,0:T(8,128)} %copy-done.8) | copy-start | bytes 3145732
  424.5 12.4 %copy-start.38 = (bf16[2048,512]{1,0:T(8,128)(2,1)S(1)}, bf16[2048,512]{1,0:T(8,128)(2,1)}, u32[]{:S(2)}) copy-start(bf16[2048,512]{1,0:T(8,128)(2,1)} %param.18) | copy-start | bytes 6291460
  436.9 3.3 copy-start.23
  436.9 3.3 copy-start.25
  446.9 3.6 copy-start.32
  446.9 4.3 copy-start.41
  570.1 3.7 copy-start.5
  570.1 3.7 copy-start.33
  636.2 4.3 copy-start.35
  (25 other events, 43.5 us)
Sparse Core Ops, SparseCore 0:
  11.6 147.7 all-gather.2
  443.1 33.3 reduce-scatter.1

commit v11 on v8

--- a/solution.py
+++ b/solution.py
@@ -485,15 +485,13 @@
     )(*arrays)
 
 
-def to_tokens_kernel(line, summed, *refs):
-    count, sums = len(summed), sum(summed)
-    ins, outs = refs[:count], refs[count : 2 * count]
-    mine, theirs = refs[2 * count : 2 * count + 2]
-    sent, arrived, pair_sem, load_sem, own_sem = refs[2 * count + 2 :]
+def head_return(
+    line, summed, ins, outs, mine, theirs, sent, arrived, pair_sem, load_sem, own_sem
+):
+    count = len(summed)
     dp, place = lax.axis_index("dp"), lax.axis_index("expert")
     z, c = place // 2, place % 2
     pair = (dp, 2 * z + 1 - c)
-    greet_line(line, dp, z, c)
     at_sum = [sum(summed[:i]) for i in range(count)]
 
     def load(i, other):
@@ -539,18 +537,22 @@
             s = at_sum[i]
             mine[s, other] = mine[s, other] + theirs[s, other]
 
-    def dispatch(other):
+    def begin():
+        visit_others(line, z, prepare)
+        prepare(z)
+
+    def dispatch(k):
+        other = (z + 1 + k) % line
         for i in range(count):
             add(i, other)
-            out(i, other).start()
-
-    if sums:
-        visit_others(line, z, prepare)
-        prepare(z)
-    visit_others(line, z, dispatch)
-    for i in range(count):
-        add(i, z)
-        own(i).start()
+
+            @pl.when(k < line - 1)
+            def _():
+                out(i, other).start()
+
+            @pl.when(k == line - 1)
+            def _():
+                own(i).start()
 
     def finish(other):
         for i in range(count):
@@ -559,35 +561,27 @@
             if summed[i]:
                 hand(i, other).wait_send()
 
-    visit_others(line, z, finish)
-    for i in range(count):
-        own(i).wait()
-        if summed[i]:
-            hand(i, z).wait_send()
-
-
-def to_tokens(arrays, summed, line, name, number):
-    rows = arrays[0].shape[-2]
-    count, sums = len(arrays), max(sum(summed), 1)
+    def end():
+        visit_others(line, z, finish)
+        for i in range(count):
+            own(i).wait()
+            if summed[i]:
+                hand(i, z).wait_send()
+
+    return begin, dispatch, end
+
+
+def head_return_space(arrays, summed, line):
+    rows, dtype = arrays[0].shape[-2], arrays[0].dtype
+    count, sums = len(arrays), sum(summed)
     sems = pltpu.SemaphoreType.DMA
-    dtype = arrays[0].dtype
-    held = (sums, line, rows, HD) if sum(summed) else (1, 1, 16, HD)
-    return pl.pallas_call(
-        functools.partial(to_tokens_kernel, line, summed),
-        out_shape=[jax.ShapeDtypeStruct((rows, line * HD), dtype)] * count,
-        in_specs=[pl.BlockSpec(memory_space=pl.ANY)] * count,
-        out_specs=[pl.BlockSpec(memory_space=pl.ANY)] * count,
-        scratch_shapes=[pltpu.VMEM(held, dtype)] * 2
-        + [
-            sems((count, line)),
-            sems((count, line)),
-            sems((2, sums, line)),
-            sems((sums, line)),
-            sems((count,)),
-        ],
-        compiler_params=pltpu.CompilerParams(collective_id=number, has_side_effects=True),
-        name=name,
-    )(*arrays)
+    return [pltpu.VMEM((sums, line, rows, HD), dtype)] * 2 + [
+        sems((count, line)),
+        sems((count, line)),
+        sems((2, sums, line)),
+        sems((sums, line)),
+        sems((count,)),
+    ]
 
 
 KEY_TILE = 512
@@ -993,14 +987,7 @@
         delta = jnp.sum(grad.astype(jnp.float32) * out.astype(jnp.float32), axis=-1)
         dq, dk, dv = attend_back(bounds, q, k, v, starts, total, delta[:, None, :], grad)
         shape = (line, 2, span, HD)
-        grads = to_tokens(
-            [dq, dk.reshape(shape), dv.reshape(shape)],
-            (False, True, True),
-            line,
-            "gather_grads",
-            9,
-        )
-        return grad_all, *grads
+        return grad_all, [dq, dk.reshape(shape), dv.reshape(shape)], []
 
     return forward, backward
 
@@ -1057,7 +1044,8 @@
 
         scale = HD ** (-0.5)
         dq = (dq * scale).reshape(shape)
-        return grad_all, dq, to_owner(dk * scale), to_owner(dv)
+        dq = dq.astype(jnp.bfloat16)
+        return grad_all, [], [dq, to_owner(dk * scale), to_owner(dv)]
 
     return forward, backward
 
@@ -1437,11 +1425,29 @@
     flipped,
     extra,
     grads,
+    summed,
     *refs,
 ):
     a_ref, w_ref = refs[0], refs[1]
     e_ref = refs[2] if extra else None
     refs = refs[3:] if extra else refs[2:]
+    w_loads = []
+    if flipped:
+        up_ref, *refs, w_buf, w_sem = refs
+        experts, _, units = w_ref.shape
+        for kind, source in enumerate((w_ref, up_ref)):
+            for e in range(experts):
+                at = kind * experts + e
+                target = w_buf.at[:, at * units : (at + 1) * units]
+                w_loads.append(pltpu.make_async_copy(source.at[e], target, w_sem.at[at]))
+        w_ref = w_buf
+        for copy in w_loads:
+            copy.start()
+    heads = len(summed)
+    if heads:
+        head_ins, head_refs = refs[2 : 2 + heads], refs[-7:]
+        head_outs = refs[5 + heads : 5 + 2 * heads]
+        refs = (*refs[:2], *refs[2 + heads : 5 + heads], *refs[5 + 2 * heads : -7])
     if grads:
         work_refs, refs = (*refs[:2], *refs[3:5], *refs[-7:]), (refs[2], *refs[5:-7])
     (
@@ -1474,9 +1480,13 @@
     to_up, to_down = (dp, place + 2), (dp, place - 2)
     for device in (to_x, to_y, to_pair):
         greet(device)
-    pl.when(z > 0)(lambda: greet(to_down))
-    pl.when(z < line - 1)(lambda: greet(to_up))
-    greeted = 3 + (z > 0).astype(jnp.int32) + (z < line - 1).astype(jnp.int32)
+    if heads:
+        visit_others(line, z, lambda other: greet((dp, 2 * other + c)))
+        greeted = 2 + line
+    else:
+        pl.when(z > 0)(lambda: greet(to_down))
+        pl.when(z < line - 1)(lambda: greet(to_up))
+        greeted = 3 + (z > 0).astype(jnp.int32) + (z < line - 1).astype(jnp.int32)
     pl.semaphore_wait(pltpu.get_barrier_semaphore(), greeted)
     count = 4 * line
     width = w_ref.shape[0] if flipped else w_ref.shape[1]
@@ -1625,6 +1635,11 @@
             pl.when((height < z) & (z < line - 1))(downwards)
 
     start_load(0)
+    for copy in w_loads:
+        copy.wait()
+    if heads:
+        begin, dispatch, heads_end = head_return(line, summed, head_ins, head_outs, *head_refs)
+        begin()
     work, work_end, turns = gate_up_grads(*work_refs) if grads else (None, None, 1)
 
     def step(i, carry):
@@ -1634,12 +1649,16 @@
         if grads:
             every = count // turns
             pl.when((i < count) & (i % every == 0))(lambda: work(i // every))
+        if heads:
+            pl.when(i < line)(lambda: dispatch(i))
         pl.when((i >= 4) & (i < count + 4))(lambda: settle_far(i - 4))
         pl.when((k >= 3) & (j == 2))(lambda: pass_on(farthest(line, z, k - 3)))
         pl.when((k >= 2) & (j == 3))(lambda: column(farthest(line, z, k - 2)))
         return carry
 
     lax.fori_loop(0, count + 8, step, 0)
+    if heads:
+        heads_end()
     if grads:
         work_end()
     for p in (0, 1):
@@ -1671,9 +1690,11 @@
     lax.fori_loop(0, line, finish, 0)
 
 
-def product_sum(blocks, weights, flipped, extra, line, name, number, grads=None):
+def product_sum(
+    blocks, weights, flipped, extra, line, name, number, grads=None, heads=(), summed=()
+):
     count, rows, depth = blocks.shape
-    width = weights.shape[0] if flipped else weights.shape[1]
+    width = weights[0].shape[1] if flipped else weights.shape[1]
     wide = width + (0 if extra is None else 128)
     half = rows // 4
     sems = pltpu.SemaphoreType.DMA
@@ -1698,12 +1719,19 @@
             sems((1,)),
             sems((2, shape[0])),
         ]
+    if heads:
+        tokens = jax.ShapeDtypeStruct((heads[0].shape[-2], line * HD), dtype)
+        work_in += heads
+        out_shape += [tokens] * len(heads)
+        work_space += head_return_space(heads, summed, line)
     total, *work_out = pl.pallas_call(
-        functools.partial(product_sum_kernel, line, flipped, extra is not None, grads is not None),
+        functools.partial(
+            product_sum_kernel, line, flipped, extra is not None, grads is not None, summed
+        ),
         out_shape=out_shape,
-        in_specs=[anywhere, inside]
+        in_specs=[anywhere, anywhere if flipped else inside]
         + ([] if extra is None else [anywhere])
-        + [anywhere] * len(work_in),
+        + [anywhere] * (len(work_in) + flipped),
         out_specs=[inside] + [anywhere] * (len(out_shape) - 1),
         scratch_shapes=[
             space(4, line, 2, 2),
@@ -1726,12 +1754,23 @@
             sems((2, line, 2)),
             sems((2, line, 2)),
             *work_space,
+            *(
+                [pltpu.VMEM((width, depth), dtype), sems((2 * weights[0].shape[0],))]
+                if flipped
+                else []
+            ),
         ],
         compiler_params=pltpu.CompilerParams(
             collective_id=number, has_side_effects=True, vmem_limit_bytes=63 << 20
         ),
         name=name,
-    )(blocks, weights, *([] if extra is None else [extra]), *work_in)
+    )(
+        blocks,
+        weights[0] if flipped else weights,
+        *([] if extra is None else [extra]),
+        *([weights[1]] if flipped else []),
+        *work_in,
+    )
     return total.reshape(2 * half, wide), *work_out
 
 
@@ -2337,9 +2376,29 @@
     xn_all, grad_units, scaled, gate_part = gate_act(
         own_tokens, top_all, w_gate, w_up, w_down, line
     )
-    w_both = jnp.concatenate([*w_gate, *w_up], axis=1)
-    (grad_tokens,) = product_sum(grad_units, w_both, True, gate_part, line, "grad_tokens", 4)
-    moe_out, grad_gate, grad_up = product_sum(
+    (grad_tokens,) = product_sum(
+        grad_units, (w_gate, w_up), True, gate_part, line, "grad_tokens", 4)
+    grad_xn_exp = grad_tokens[:, :model_width]
+    gate_sums = grad_tokens[:, model_width : model_width + experts]
+    grad_router_probs = jnp.where(named, gate_sums, 0.0)
+    grad_logits = router * (
+        grad_router_probs - jnp.sum(router * grad_router_probs, axis=-1, keepdims=True)
+    )
+    grad_second_normed_input = grad_xn_exp + jnp.einsum(
+        "se,de->sd", grad_logits, w_router, precision=lax.Precision.HIGHEST
+    )
+    grad_router = jnp.einsum(
+        "sd,se->de", second_normed_input, grad_logits, precision=lax.Precision.HIGHEST
+    )
+    grad_expert_norm_gain = jnp.sum(grad_second_normed_input * second_unit_input, axis=0)
+    grad_second_unit_input = grad_second_normed_input * expert_norm_gain
+    grad_hidden = top_own.astype(jnp.float32) + second_inverse_norm * (
+        grad_second_unit_input
+        - second_unit_input
+        * jnp.mean(grad_second_unit_input * second_unit_input, axis=-1, keepdims=True)
+    )
+    grad_attn, by_heads, by_tokens = attention[1](kept, grad_hidden.astype(jnp.bfloat16))
+    moe_out, grad_gate, grad_up, *returned = product_sum(
         scaled,
         w_down.reshape(-1, model_width),
         False,
@@ -2348,33 +2407,14 @@
         "expert_sum",
         2,
         (xn_all, grad_units, w_gate.shape),
-    )
+        by_heads,
+        (False, True, True) if by_heads else (),
+    )
+    grad_queries, grad_keys, grad_values = returned or by_tokens
     output = (hidden_state + moe_out).astype(jnp.bfloat16)
-    grad_xn_exp = grad_tokens[:, :model_width]
-    gate_sums = grad_tokens[:, model_width : model_width + experts]
-    grad_router_probs = jnp.where(named, gate_sums, 0.0)
-    grad_logits = router * (
-        grad_router_probs - jnp.sum(router * grad_router_probs, axis=-1, keepdims=True)
-    )
-    grad_second_normed_input = grad_xn_exp + jnp.einsum(
-        "se,de->sd", grad_logits, w_router, precision=lax.Precision.HIGHEST
-    )
-    grad_router = jnp.einsum(
-        "sd,se->de", second_normed_input, grad_logits, precision=lax.Precision.HIGHEST
-    )
-    grad_expert_norm_gain = jnp.sum(grad_second_normed_input * second_unit_input, axis=0)
-    grad_second_unit_input = grad_second_normed_input * expert_norm_gain
-    grad_hidden = top_own.astype(jnp.float32) + second_inverse_norm * (
-        grad_second_unit_input
-        - second_unit_input
-        * jnp.mean(grad_second_unit_input * second_unit_input, axis=-1, keepdims=True)
-    )
-    grad_attn, grad_queries, grad_keys, grad_values = attention[1](
-        kept, grad_hidden.astype(jnp.bfloat16)
-    )
     grad_out = jnp.einsum("sk,sd->kd", attended, grad_attn, preferred_element_type=jnp.float32)
     grad_heads_raw, gain_grads = normed_heads_back(
-        grad_queries.astype(jnp.bfloat16),
+        grad_queries,
         grad_keys,
         grad_values,
         q_raw,

time: 677 us -> 643 us (0.950)
  Pallas kernels: 562 us -> 522 us
    pallas_call x1 -> x0, Pallas kernels: 40.6 us -> none  [to_tokens(): pl.pallas_call(functools.partial(to_tokens_kernel, line, summed), out_sha...]
    unnamed x89 -> x87, local copies, waits for them, and re-layouts: 11.8 us -> 13.9 us
  transfers between devices with their start and end apart: 2 -> 2, of which waited for: 0 -> 0; matrix products, arithmetic and copies ran while one was open for 11% -> 11% of each run, Pallas kernels for 54% -> 51%
where the time goes in v11:
time: 643 us; the launch traced here: 631 us
  Pallas kernels  522 us (81%)
  other arithmetic  36.6 us (6%)
  local copies, waits for them, and re-layouts  32.1 us (5%)
  matrix products  25.6 us (4%)
  between operations  14.9 us (2%)
    pallas_call x2, Pallas kernels, product_sum(): pl.pallas_call(functools.partial(product_sum_kernel, line, flipped, extra...  174 us
    pallas_call x1, Pallas kernels, gate_act(): pl.pallas_call(functools.partial(gate_act_kernel, line), out_shape=[jax.S...  86.5 us
    pallas_call x1, Pallas kernels, closing(): pl.pallas_call(functools.partial(closing_kernel, line, shared_rows), out_...  81.2 us
    pallas_call x1, Pallas kernels, to_heads(): pl.pallas_call(functools.partial(to_heads_kernel, line, shared), out_shap...  62.1 us
    pallas_call x1, Pallas kernels, out_sum(): pl.pallas_call(functools.partial(out_sum_kernel, line), out_shape=[jax.Sh...  39.6 us
    pallas_call x1, Pallas kernels, out_back(): pl.pallas_call(functools.partial(out_back_kernel, line), out_shape=[jax.S...  25.9 us
    pallas_call x1, Pallas kernels, attend_back(): pl.pallas_call(attend_back_kernel, grid_spec=pltpu.PrefetchScalarGridSpec...  18.3 us
    unnamed x87, local copies, waits for them, and re-layouts  13.9 us
  transfers between devices with their start and end apart: 2, of which 0 were waited for; matrix products, arithmetic and copies ran while one was open for 11% of the time, Pallas kernels for 51%

profile of v11, /device:TPU:24, one launch (start us, length us, event | category | flops | bytes accessed | tf_op | source)
XLA Modules:
  0.0 631.3 jit_solution(7322629295617905364)
XLA Ops:
  10.1 4.3 convert_element_type.98
  21.4 9.4 %normed_heads.1 = (bf16[512,512]{1,0:T(8,128)(2,1)S(1)}, bf16[512,512]{1,0:T(8,128)(2,1)S(1)}, f32[16,512]{1,0:T(8,128)S(1)}) custom-call(f32[512,512]{1,0:T(8,128)S(1)} %fusion.28.q_ref, f32[512,512]{1,0:T(8,128)S(1)} %fusion.26.k_ref, f32[1,512]{1,0:T(1,128)S(1)} %bitcast.76, f32[1,512]{1,0:T(1,128)S(1)} %bitcast.78, ...), custom_call_target="tpu_custom_call" | custom-call | tf_op jit(solution)/shard_map/normed_heads/pallas_call | solution.py:2195
  32.9 62.1 %scatter_heads.1 = (bf16[4,512,128]{2,1,0:T(8,128)(2,1)}, bf16[4,2,512,128]{3,2,1,0:T(8,128)(2,1)}, bf16[4,2,512,128]{3,2,1,0:T(8,128)(2,1)}) custom-call(bf16[512,512]{1,0:T(8,128)(2,1)} %copy-done.16, bf16[512,512]{1,0:T(8,128)(2,1)} %copy-done.17, bf16[512,512]{1,0:T(8,128)(2,1)} %convolution_convert_fusion.3.refs_2_), custom_call_target="tpu_custom_call" | custom-call | tf_op jit(solution)/shard_map/scatter_heads/pallas_call | solution.py:474
  95.9 13.6 %attend.1 = (bf16[4,512,128]{2,1,0:T(8,128)(2,1)}, f32[4,1,512]{2,1,0:T(1,128)}) custom-call(s32[3,4]{1,0:T(4,128)} %pad_add_fusion.bounds, bf16[4,512,128]{2,1,0:T(8,128)(2,1)} %get-tuple-element.48.q_ref, bf16[4096,128]{1,0:T(8,128)(2,1)} %bitcast.91, bf16[4096,128]{1,0:T(8,128)(2,1)} %bitcast.93, s32[4,1,512]{2,1,0:T(1,128)} %copy-done.39), custom_call_target="tpu_custom_call" | custom-call | tf_op jit(solution)/shard_map/attend/pallas_call | solution.py:666
  110.5 39.6 %out_sum.1 = (bf16[512,512]{1,0:T(8,128)(2,1)S(1)}, f32[2,64,2048]{2,1,0:T(8,128)S(1)}) custom-call(bf16[4,512,128]{2,1,0:T(8,128)(2,1)S(1)} %copy-done.10, bf16[512,2048]{1,0:T(8,128)(2,1)S(1)} %copy-done.2), custom_call_target="tpu_custom_call" | custom-call | tf_op jit(solution)/shard_map/out_sum/pallas_call | solution.py:814
  150.1 2.9 multiply_reduce_fusion.4
  155.7 4.2 broadcast_multiply_fusion
  159.9 86.5 %gate_act.1 = (bf16[32,2,64,2048]{3,2,1,0:T(8,128)(2,1)}, bf16[16,256,1024]{2,1,0:T(8,128)(2,1)}, bf16[16,256,512]{2,1,0:T(8,128)(2,1)}, bf16[16,256,128]{2,1,0:T(8,128)(2,1)}) custom-call(bf16[2,64,2176]{2,1,0:T(8,128)(2,1)} %bitcast.97, bf16[16,256,2048]{2,1,0:T(8,128)(2,1)} %bitcast.81, bf16[2,2048,256]{2,1,0:T(8,128)(2,1)} %refs_1_.1, ...), custom_call_target="tpu_custom_call" | custom-call | tf_op jit(solution)/shard_map/gate_act/pallas_call | solution.py:1271
  246.4 84.8 %grad_tokens.1 = f32[2,64,2176]{2,1,0:T(8,128)} custom-call(bf16[16,256,1024]{2,1,0:T(8,128)(2,1)} %get-tuple-element.55.refs_0_.refs_3_, bf16[2,2048,256]{2,1,0:T(8,128)(2,1)} %refs_1_.1, bf16[16,256,128]{2,1,0:T(8,128)(2,1)} %get-tuple-element.57.refs_2_, bf16[2,2048,256]{2,1,0:T(8,128)(2,1)} %refs_3_.1), custom_call_target="tpu_custom_call" | custom-call | tf_op jit(solution)/shard_map/grad_tokens/pallas_call | solution.py:1727
  332.3 2.9 multiply_reduce_fusion.1
  335.2 2.5 fusion.30
  337.8 25.9 %out_back.1 = (bf16[4,2,64,2048]{3,2,1,0:T(8,128)(2,1)S(1)}, bf16[4,512,128]{2,1,0:T(8,128)(2,1)S(1)}) custom-call(bf16[2,64,2048]{2,1,0:T(8,128)(2,1)S(1)} %bitcast.75, bf16[512,2048]{1,0:T(8,128)(2,1)S(1)} %copy-done.3), custom_call_target="tpu_custom_call" | custom-call | tf_op jit(solution)/shard_map/out_back/pallas_call | solution.py:937
  363.7 2.6 convolution_convert_fusion.1
  372.5 18.3 %attend_back.1 = (bf16[4,512,128]{2,1,0:T(8,128)(2,1)}, bf16[4096,128]{1,0:T(8,128)(2,1)}, bf16[4096,128]{1,0:T(8,128)(2,1)}) custom-call(s32[3,4]{1,0:T(4,128)} %pad_add_fusion.bounds, bf16[4,512,128]{2,1,0:T(8,128)(2,1)} %get-tuple-element.48.q_ref, bf16[4096,128]{1,0:T(8,128)(2,1)} %bitcast.92, bf16[4096,128]{1,0:T(8,128)(2,1)} %bitcast.94, ...), custom_call_target="tpu_custom_call" | custom-call | tf_op jit(solution)/shard_map/attend_back/pallas_call | solution.py:688
  390.8 88.8 %expert_sum.1 = (f32[2,64,2048]{2,1,0:T(8,128)}, bf16[2,2048,256]{2,1,0:T(8,128)(2,1)}, bf16[2,2048,256]{2,1,0:T(8,128)(2,1)}, bf16[512,512]{1,0:T(8,128)(2,1)},...) custom-call(bf16[16,256,512]{2,1,0:T(8,128)(2,1)} %get-tuple-element.53.refs_0_.scaled_ref, ...), custom_call_target="tpu_custom_call" | custom-call | tf_op jit(solution)/shard_map/expert_sum/pallas_call | solution.py:1727
  485.2 11.9 %normed_heads_back.1 = (bf16[512,1536]{1,0:T(8,128)(2,1)S(1)}, f32[16,512]{1,0:T(8,128)S(1)}) custom-call(bf16[512,512]{1,0:T(8,128)(2,1)S(1)} %copy-done.13, bf16[512,512]{1,0:T(8,128)(2,1)S(1)} %copy-done.14, bf16[512,512]{1,0:T(8,128)(2,1)S(1)} %copy-done.15, f32[512,512]{1,0:T(8,128)S(1)} %copy-done.9, f32[512,512]{1,0:T(8,128)S(1)} %copy-done.7, ...), custom_call_target="tpu_custom_call" | custom-call | tf_op jit(solution)/shard_map/normed_heads_back/pallas_call | solution.py:2263
  497.3 3.0 fusion.8
  502.5 2.9 fusion.31
  509.6 5.6 convolution_convert_fusion
  515.2 81.2 %closing.1 = (f32[2,144,1536]{2,1,0:T(8,128)}, f32[2,16,1536]{2,1,0:T(8,128)}, bf16[4,2,64,2048]{3,2,1,0:T(8,128)(2,1)}, bf16[4,2,64,2048]{3,2,1,0:T(8,128)(2,1)}, bf16[2,256,2048]{2,1,0:T(8,128)(2,1)}) custom-call(bf16[4,2,2,128,1536]{4,3,2,1,0:T(8,128)(2,1)} %bitcast.86, bf16[4,2,2,16,1536]{4,3,2,1,0:T(8,128)(2,1)} %bitcast.96, ...), custom_call_target="tpu_custom_call" | custom-call | tf_op jit(solution)/shard_map/closing/pallas_call | solution.py:2076
  600.8 4.1 convert_element_type.119
  608.6 4.3 convert.28
  612.9 2.5 convert_element_type.121
  621.0 3.2 copy.56
  (155 shorter events, 49.5 us)
Async XLA Ops:
  7.2 145.9 %copy-start = (f32[2048,16]{0,1:T(8,128)S(1)}, f32[2048,16]{0,1:T(8,128)}, u32[]{:S(2)}) copy-start(f32[2048,16]{0,1:T(8,128)} %param.25) | copy-start | bytes 393220
  7.2 152.7 %all-gather.3.cloned.1.call-start = ((), (), s32[]{:S(2)}) async-start(), calls=%async_computation.2 | async-start | bytes 17301504 | tf_op jit(solution)/shard_map/all_gather | solution.py:2363
  9.2 610.1 %reduce-scatter.2.cloned.1.call-start = ((), (), s32[]{:S(2)}) async-start(), calls=%async_computation.1 | async-start | bytes 2359296 | tf_op jit(solution)/shard_map/reduce_scatter | solution.py:2469
  10.1 4.3 copy-start.25
  14.3 3.8 copy-start.40
  21.4 11.6 %copy-start.8 = (f32[512,512]{1,0:T(8,128)}, f32[512,512]{1,0:T(8,128)S(1)}, u32[]{:S(2)}) copy-start(f32[512,512]{1,0:T(8,128)S(1)} %fusion.28.q_ref) | copy-start | bytes 3145732
  21.4 9.4 %copy-start.34 = (bf16[2048,512]{1,0:T(8,128)(2,1)S(1)}, bf16[2048,512]{1,0:T(8,128)(2,1)}, u32[]{:S(2)}) copy-start(bf16[2048,512]{1,0:T(8,128)(2,1)} %param.20) | copy-start | bytes 6291460
  32.9 76.5 %copy-start.2 = (bf16[512,2048]{1,0:T(8,128)(2,1)S(1)}, bf16[512,2048]{1,0:T(8,128)(2,1)}, u32[]{:S(2)}) copy-start(bf16[512,2048]{1,0:T(8,128)(2,1)} %w_ref.3) | copy-start | bytes 6291460
  150.1 3.0 copy-start.4
  150.1 3.0 copy-start.20
  150.1 3.0 copy-start.38
  153.0 2.6 copy-start.22
  331.2 4.0 copy-start.23
  335.2 2.5 copy-start.3
  337.8 25.9 %copy-start.21 = (bf16[512,512]{1,0:T(8,128)(2,1)S(1)}, bf16[512,512]{1,0:T(8,128)(2,1)}, u32[]{:S(2)}) copy-start(bf16[512,512]{1,0:T(8,128)(2,1)} %copy-done.20) | copy-start | bytes 1572868
  363.6 7.9 %copy-start.12 = (bf16[4,512,128]{2,1,0:T(8,128)(2,1)}, bf16[4,512,128]{2,1,0:T(8,128)(2,1)S(1)}, u32[]{:S(2)}) copy-start(bf16[4,512,128]{2,1,0:T(8,128)(2,1)S(1)} %get-tuple-element.58.d_ref) | copy-start | bytes 1572868
  366.3 2.5 copy-start.24
  366.3 5.2 copy-start.11
  497.3 3.0 copy-start.33
  506.7 2.9 copy-start.27
  596.3 3.2 copy-start.36
  600.8 4.1 copy-start.29
  608.6 4.3 copy-start.30
  621.0 3.2 copy-start.1
  (20 other events, 29.6 us)
Sparse Core Ops, SparseCore 0:
  11.6 146.4 all-gather.2
  366.4 32.1 reduce-scatter.1
